TPU v7x, 8 devices: a whole 2x2x1 slice. The times are simulated.
8 devices in a mesh: sub: 4 (over z, y, x), fsdp: 2 (over core).
Axes of the slice: x: 2, y: 2, z: 1, core: 2. Of those that a mesh axis runs over, the one named last changes fastest.
Arguments:
- x_in: bfloat16 [16, 512, 1536], P(('sub', 'fsdp'))
- w_q: bfloat16 [2, 1536, 12, 128], P(None, ('sub', 'fsdp'))
- w_k: bfloat16 [2, 1536, 2, 128], P(None, ('sub', 'fsdp'))
- w_v: bfloat16 [2, 1536, 2, 128], P(None, ('sub', 'fsdp'))
- w_o: bfloat16 [2, 1536, 12, 128], P(None, ('sub', 'fsdp'))
- w_up: bfloat16 [2, 1536, 8960], P(None, ('sub', 'fsdp'))
- w_down: bfloat16 [2, 8960, 1536], P(None, ('sub', 'fsdp'))
- grad_out: bfloat16 [16, 512, 1536], P(('sub', 'fsdp'))
Outputs:
- output 1: bfloat16 [16, 512, 1536], P(('sub', 'fsdp'))
- output 2: bfloat16 [16, 512, 1536], P(('sub', 'fsdp'))
- output 3: float32 [2, 1536, 12, 128], P(None, ('sub', 'fsdp'))
- output 4: float32 [2, 1536, 2, 128], P(None, ('sub', 'fsdp'))
- output 5: float32 [2, 1536, 2, 128], P(None, ('sub', 'fsdp'))
- output 6: float32 [2, 1536, 12, 128], P(None, ('sub', 'fsdp'))
- output 7: float32 [2, 1536, 8960], P(None, ('sub', 'fsdp'))
- output 8: float32 [2, 8960, 1536], P(None, ('sub', 'fsdp'))
All inputs are finite; a program needn't handle non-finite values.
Results may differ from a plain program's by a relative error of at most 0.02.
Values are sent between devices in bfloat16 or wider.
A program may use at most 1 GiB of HBM per device.

v0:
```python
import functools

import jax
import jax.numpy as jnp
from jax import lax
from jax.experimental import pallas as pl
from jax.experimental.layout import Layout, with_layout_constraint
from jax.experimental.pallas import tpu as pltpu
from jax.sharding import PartitionSpec as P


AXES = ("sub", "fsdp")
EPS = 1e-6
MASK_FILL = -1e30
GELU_A = (2.0 / 3.141592653589793) ** 0.5
GELU_B = 0.044715
CORES = 2
QUERY_BLOCK = 256


def rms_norm(values):
    return values * lax.rsqrt(jnp.mean(values * values, axis=-1, keepdims=True) + EPS)


def norm_bf16(x_loc):
    return rms_norm(x_loc.astype(jnp.float32)).astype(jnp.bfloat16)


def norm_back(x_loc, grad_norm):
    _, pull_back = jax.vjp(rms_norm, x_loc.astype(jnp.float32))
    return pull_back(grad_norm)[0]


def mixed(form, left, right):
    return jnp.einsum(form, left, right, preferred_element_type=jnp.float32)


def swap(value):
    return lax.ppermute(value, "fsdp", [(0, 1), (1, 0)])


def by_core(core, mine, other):
    return jnp.where(core == 0, mine, other), jnp.where(core == 0, other, mine)


def to_columns(core, halves):
    keep = jnp.where(core == 0, halves[0], halves[1])
    send = jnp.where(core == 0, halves[1], halves[0])
    first, second = by_core(core, keep, swap(send))
    return jnp.concatenate([first, second], axis=0)


def to_rows(core, grad):
    rows = grad.shape[0] // CORES
    grad = grad.reshape((CORES, rows) + grad.shape[1:])
    keep = lax.dynamic_index_in_dim(grad, core, 0, keepdims=False)
    send = lax.dynamic_index_in_dim(grad, 1 - core, 0, keepdims=False)
    return by_core(core, keep, swap(send))


def gather(piece):
    return lax.all_gather(piece, "sub", axis=0, tiled=True)


def scatter_sum(grad_full):
    return lax.psum_scatter(grad_full, "sub", scatter_dimension=0, tiled=True)


def pair_rows(value):
    return jnp.concatenate([value, swap(value)], axis=0)


def causal_blocks(seq):
    return [(start, start + QUERY_BLOCK) for start in range(0, seq, QUERY_BLOCK)]


def dot(left, right, contract):
    return lax.dot_general(left, right, (contract, ((), ())), preferred_element_type=jnp.float32)


def probabilities(k_blk, q_blk, scale):
    scores = dot(k_blk, q_blk, ((1,), (1,))) * scale
    keys, queries = scores.shape
    key = lax.broadcasted_iota(jnp.int32, (queries, queries), 0)
    query = lax.broadcasted_iota(jnp.int32, (queries, queries), 1)
    last = jnp.where(key <= query, scores[keys - queries:], MASK_FILL)
    scores = last if keys == queries else jnp.concatenate([scores[:keys - queries], last], axis=0)
    powers = jnp.exp(scores - jnp.max(scores, axis=0, keepdims=True))
    return powers * (1.0 / jnp.sum(powers, axis=0, keepdims=True))


def attn_fwd_kernel(q_width, head, qkv_ref, o_ref):
    seq = qkv_ref.shape[0]
    k_all = qkv_ref[:, q_width:q_width + head]
    v_flip = jnp.transpose(qkv_ref[:, q_width + head:].astype(jnp.float32)).astype(jnp.bfloat16)
    for col in range(0, q_width, head):
        for start, end in causal_blocks(seq):
            probs = probabilities(k_all[:end], qkv_ref[start:end, col:col + head], head ** -0.5)
            o_flip = dot(v_flip[:, :end], probs.astype(jnp.bfloat16), ((1,), (0,)))
            o_ref[start:end, col:col + head] = jnp.transpose(o_flip).astype(jnp.bfloat16)


def attn_bwd_kernel(q_width, head, qkv_ref, d_o_ref, out_ref, d_k_ref, d_v_ref):
    seq = qkv_ref.shape[0]
    scale = head ** -0.5
    k_all = qkv_ref[:, q_width:q_width + head]
    v_all = qkv_ref[:, q_width + head:]
    k_flip = jnp.transpose(k_all.astype(jnp.float32)).astype(jnp.bfloat16)
    d_k_ref[...] = jnp.zeros_like(d_k_ref)
    d_v_ref[...] = jnp.zeros_like(d_v_ref)
    for col in range(0, q_width, head):
        for start, end in causal_blocks(seq):
            q_blk = qkv_ref[start:end, col:col + head]
            d_o_blk = d_o_ref[start:end, col:col + head]
            probs = probabilities(k_all[:end], q_blk, scale)
            d_p = dot(v_all[:end], d_o_blk, ((1,), (1,)))
            d_v_ref[:end] += dot(probs.astype(jnp.bfloat16), d_o_blk, ((1,), (0,)))
            d_s = probs * (d_p - jnp.sum(probs * d_p, axis=0, keepdims=True))
            d_s = (d_s * scale).astype(jnp.bfloat16)
            d_k_ref[:end] += dot(d_s, q_blk, ((1,), (0,)))
            d_q_flip = dot(k_flip[:, :end], d_s, ((1,), (0,)))
            out_ref[start:end, col:col + head] = jnp.transpose(d_q_flip).astype(jnp.bfloat16)
    out_ref[:, q_width:q_width + head] = d_k_ref[...].astype(jnp.bfloat16)
    out_ref[:, q_width + head:] = d_v_ref[...].astype(jnp.bfloat16)


def by_sequence(kernel, seq, q_width, head, args, width, scratch, flops):
    rows = args[0].shape[0]
    return pl.pallas_call(
        functools.partial(kernel, q_width, head),
        grid=(rows // seq,),
        in_specs=[pl.BlockSpec((seq, arg.shape[1]), lambda i: (i, 0)) for arg in args],
        out_specs=pl.BlockSpec((seq, width), lambda i: (i, 0)),
        out_shape=jax.ShapeDtypeStruct((rows, width), jnp.bfloat16),
        scratch_shapes=[pltpu.VMEM((seq, head), jnp.float32)] * scratch,
        cost_estimate=pl.CostEstimate(flops=flops, bytes_accessed=0, transcendentals=0),
    )(*args)


def attn_forward(x_own, weight, q_width, head, seq):
    normed = pair_rows(norm_bf16(x_own))
    qkv = mixed("td,de->te", normed, weight[:, :q_width + 2 * head]).astype(jnp.bfloat16)
    o_act = by_sequence(attn_fwd_kernel, seq, q_width, head, (qkv,), q_width, 0, 20_000_000_000)
    o_weight = weight[:, q_width + 2 * head:]
    rows = x_own.shape[0]
    other = swap(mixed("te,de->td", o_act[rows:], o_weight))
    proj = mixed("te,de->td", o_act[:rows], o_weight) + other
    y_own = (x_own.astype(jnp.float32) + proj).astype(jnp.bfloat16)
    return y_own, (x_own, normed, qkv, o_act)


def attn_backward(saved, weight, q_width, head, seq, grad_own):
    x_own, normed, qkv, o_act = saved
    rows = grad_own.shape[0]
    grad_y = pair_rows(grad_own)
    d_o = mixed("td,de->te", grad_y, weight[:, q_width + 2 * head:]).astype(jnp.bfloat16)
    d_qkv = by_sequence(attn_bwd_kernel, seq, q_width, head, (qkv, d_o), qkv.shape[1], 2, 40_000_000_000)
    w_qkv = weight[:, :q_width + 2 * head]
    other = swap(mixed("te,de->td", d_qkv[rows:], w_qkv))
    d_norm = mixed("te,de->td", d_qkv[:rows], w_qkv) + other
    grad_x = (grad_own.astype(jnp.float32) + norm_back(x_own, d_norm)).astype(jnp.bfloat16)
    return grad_x, mixed("td,te->de", normed, d_qkv), mixed("td,te->de", grad_y, o_act)


def gelu_parts(hidden):
    square = hidden * hidden
    half = 0.5 + 0.5 * jnp.tanh(hidden * (GELU_A + GELU_A * GELU_B * square))
    value = hidden * half
    slope = half + value * (1.0 - half) * (2.0 * GELU_A + 6.0 * GELU_A * GELU_B * square)
    return value.astype(jnp.bfloat16), slope


def mlp_hidden(normed, up_weight):
    return lax.optimization_barrier(gelu_parts(mixed("td,df->tf", normed, up_weight)))


def mlp_output(x_own, gelu_act, down_weight):
    rows = x_own.shape[0]
    other = swap(mixed("tf,fd->td", gelu_act[rows:], down_weight))
    proj = mixed("tf,fd->td", gelu_act[:rows], down_weight) + other
    return (x_own.astype(jnp.float32) + proj).astype(jnp.bfloat16)


def grad_hidden(slope, grad_y, down_weight):
    return (mixed("td,fd->tf", grad_y, down_weight) * slope).astype(jnp.bfloat16)


def mlp_backward(x_own, slope, up_weight, down_weight, grad_own):
    rows = grad_own.shape[0]
    d_hid = grad_hidden(slope, pair_rows(grad_own), down_weight)
    other = swap(mixed("tf,df->td", d_hid[rows:], up_weight))
    d_norm = mixed("tf,df->td", d_hid[:rows], up_weight) + other
    return (grad_own.astype(jnp.float32) + norm_back(x_own, d_norm)).astype(jnp.bfloat16)


def all_rows(value):
    mine = gather(value)
    return mine, swap(mine)


def mlp_weight_grads(norms, grads, up_block, down_block):
    d_up, d_down = 0.0, 0.0
    for normed, grad_y in zip(norms, grads):
        gelu_act, slope = mlp_hidden(normed, up_block)
        d_down = d_down + mixed("tf,td->fd", gelu_act, grad_y)
        d_hid = lax.optimization_barrier(grad_hidden(slope, grad_y, down_block))
        d_up = d_up + mixed("td,tf->df", normed, d_hid)
    return d_up, d_down


def up_rows(core, chip, chips, d_up):
    grid = with_layout_constraint(d_up.reshape((chips, -1) + d_up.shape[1:]), Layout(major_to_minor=(0, 1, 2)))
    parts = []
    for step in range(chips):
        part = lax.dynamic_index_in_dim(grid, chip ^ step, 0, keepdims=False)
        parts.append(lax.ppermute(part, "sub", [(i, i ^ step) for i in range(chips)]) if step else part)
    grid = jnp.stack(parts)
    grid = grid.reshape(chips, CORES, grid.shape[1] // CORES, grid.shape[2])
    keep = lax.dynamic_index_in_dim(grid, core, 1, keepdims=False)
    other = swap(lax.dynamic_index_in_dim(grid, 1 - core, 1, keepdims=False))
    both = by_core(core, keep, other)
    cols = [lax.dynamic_index_in_dim(part, chip ^ i, 0, keepdims=False) for i in range(chips) for part in both]
    return jnp.concatenate(cols, axis=1)


def solution(mesh):
    row_spec = P(AXES)
    weight_spec = P(None, AXES)
    chips = mesh.shape["sub"]

    def body(x_loc, w_q, w_k, w_v, w_o, w_up, w_down, grad_out):
        core = lax.axis_index("fsdp")
        chip = lax.axis_index("sub")
        pairs, shard, heads, head = w_q.shape
        seqs, seq, width = x_loc.shape
        q_width = heads // CORES * head
        block = w_down.shape[1]

        def attn_piece(layer):
            halves = []
            for part in range(CORES):
                cols = [w[layer].reshape(shard, CORES, -1)[:, part] for w in (w_q, w_k, w_v, w_o)]
                halves.append(jnp.concatenate(cols, axis=1))
            return to_columns(core, halves)

        def up_piece(layer):
            grid = w_up[layer].reshape(shard, chips, CORES, block)
            return to_columns(core, [grid[:, :, part].reshape(shard, chips * block) for part in range(CORES)])

        attn_full, up_full, down_full, up_block = [], [], [], []
        for layer in range(pairs):
            attn_full.append(gather(attn_piece(layer)))
            up_full.append(gather(up_piece(layer)))
            down_full.append(gather(w_down[layer]))
            up_block.append(lax.select_n(chip, *[up_full[layer][:, i * block:(i + 1) * block] for i in range(chips)]))
        carry_x = x_loc.reshape(seqs * seq, width)
        grad_x = grad_out.reshape(seqs * seq, width)
        attn_saved, mlp_saved = [], []
        for layer in range(pairs):
            x_own, saved = attn_forward(carry_x, attn_full[layer], q_width, head, seq)
            attn_saved.append(saved)
            n_own = norm_bf16(x_own)
            gelu_act, slope = mlp_hidden(pair_rows(n_own), up_full[layer])
            norms = all_rows(n_own)
            if layer == pairs - 1:
                mlp_grads = mlp_weight_grads(norms, all_rows(grad_x), up_block[layer], w_down[layer])
                down_full[layer], mlp_grads = lax.optimization_barrier((down_full[layer], mlp_grads))
            carry_x = mlp_output(x_own, gelu_act, down_full[layer])
            mlp_saved.append((x_own, norms, slope))
        y_loc = carry_x.reshape(x_loc.shape)
        grad_lists = ([], [], [], [], [], [])
        for layer in reversed(range(pairs)):
            x_own, norms, slope = mlp_saved[layer]
            if layer < pairs - 1:
                mlp_grads = mlp_weight_grads(norms, all_rows(grad_x), up_block[layer], w_down[layer])
            grad_lists[5].append(mlp_grads[1])
            grad_lists[4].append(up_rows(core, chip, chips, mlp_grads[0]))
            grad_x = mlp_backward(x_own, slope, up_full[layer], down_full[layer], grad_x)
            grad_x, d_qkv, d_o = attn_backward(attn_saved[layer], attn_full[layer], q_width, head, seq, grad_x)
            grad_x, d_qkv, d_o = lax.optimization_barrier((grad_x, d_qkv, d_o))
            parts = to_rows(core, scatter_sum(d_o))
            grad_lists[3].append(jnp.concatenate(parts, axis=1).reshape(shard, heads, head))
            parts = to_rows(core, scatter_sum(d_qkv))
            grad_lists[0].append(jnp.concatenate([part[:, :q_width] for part in parts], axis=1)
                                 .reshape(shard, heads, head))
            grad_lists[1].append(jnp.stack([part[:, q_width:q_width + head] for part in parts], axis=1))
            grad_lists[2].append(jnp.stack([part[:, q_width + head:] for part in parts], axis=1))
        return (y_loc, grad_x.reshape(x_loc.shape)) + tuple(jnp.stack(grad_list[::-1]) for grad_list in grad_lists)

    return jax.shard_map(body, mesh=mesh, in_specs=(row_spec,) + (weight_spec,) * 6 + (row_spec,),
                         out_specs=(row_spec, row_spec) + (weight_spec,) * 6, check_vma=False)
```

profile of v0, /device:TPU:0, one launch (start us, length us, event | category | flops | bytes accessed | tf_op | source)
XLA Modules:
  0.0 1838.6 jit_solution(9611053298271373382)
XLA Ops:
  42.6 8.0 fusion.149
  87.4 15.2 all-gather.13.cloned.1.call-done
  102.6 11.6 fusion.94.qkv_ref
  114.2 17.3 shard_map.143
  131.5 7.5 fusion.121
  157.0 7.7 fusion.44
  172.8 58.2 %all-gather.15.cloned.1.call-done = bf16[1536,4480]{1,0:T(8,128)(2,1)} async-done(((bf16[384,4480]{1,0:T(8,128)(2,1)}), bf16[1536,4480]{1,0:T(8,128)(2,1)}) %all-gather.15.cloned.1.call-update) | async-done | bytes 13762576 | tf_op jit(solution)/shard_map/all_gather | solution.py:62
  231.0 51.3 %multiply_add_fusion.2 = (f32[2048,4480]{1,0:T(8,128)}, bf16[2048,4480]{1,0:T(8,128)(2,1)}) fusion(bf16[1536,4480]{1,0:T(8,128)(2,1)} %all-gather.15.cloned.1.call-done, bf16[1024,1536]{1,0:T(8,128)(2,1)} %collective-permute-done.3, bf16[1024,1536]{1,0:T(8,128)(2,1)S(1)} %fusion.45), kind=kOutput, calls=%fused_computation.6 | convolution fusion | flops 28326756352 | bytes 75104256 | tf_op jit(solution)/shard_map/td,df->tf/dot_general | solution.py:35
  282.3 77.7 %all-gather.29.cloned.1.call-done = bf16[1,4480,1536]{2,1,0:T(8,128)(2,1)} async-done(((bf16[1,1120,1536]{2,1,0:T(8,128)(2,1)}), bf16[1,4480,1536]{2,1,0:T(8,128)(2,1)}) %all-gather.29.cloned.1.call-update) | async-done | bytes 13762576 | tf_op jit(solution)/shard_map/all_gather | solution.py:62
  360.1 21.4 %fusion.17 = f32[1024,1536]{1,0:T(8,128)} fusion(bf16[1,4480,1536]{2,1,0:T(8,128)(2,1)} %all-gather.29.cloned.1.call-done, bf16[2048,4480]{1,0:T(8,128)(2,1)} %get-tuple-element.29), kind=kOutput, calls=%fused_computation.37 | convolution fusion | flops 14092861440 | bytes 29229056 | tf_op jit(solution)/shard_map/tf,fd->td/dot_general | solution.py:35
  385.9 8.6 collective-permute-done.10
  399.3 21.5 %fusion.48 = (f32[1024]{0:T(1024)S(1)}, bf16[1024,1536]{1,0:T(8,128)(2,1)S(1)}) fusion(f32[1024,1536]{1,0:T(8,128)} %collective-permute-done.5, bf16[1,4480,1536]{2,1,0:T(8,128)(2,1)} %all-gather.29.cloned.1.call-done, bf16[2048,4480]{1,0:T(8,128)(2,1)} %get-tuple-element.29, bf16[1024,1536]{1,0:T(8,128)(2,1)S(1)} %copy-done.12), kind=kOutput, calls=%fused_computation.93 | convolution fusion | flops 14103870464 | bytes 35524608 | tf_op jit(solution)/shard_map/tf,fd->td/dot_general | solution.py:35
  428.9 10.9 fusion.95.qkv_ref
  439.9 17.1 shard_map.144
  462.0 10.1 collective-permute-done.8
  482.0 56.1 %all-gather.23.cloned.1.call-done = bf16[4096,1536]{1,0:T(8,128)(2,1)} async-done(((bf16[1024,1536]{1,0:T(8,128)(2,1)}), bf16[4096,1536]{1,0:T(8,128)(2,1)}) %all-gather.23.cloned.1.call-update) | async-done | bytes 12582928 | tf_op jit(solution)/shard_map/all_gather | solution.py:62
  538.1 128.9 %all-gather.19.cloned.1.call-done = bf16[1536,4480]{1,0:T(8,128)(2,1)} async-done(((bf16[384,4480]{1,0:T(8,128)(2,1)}), bf16[1536,4480]{1,0:T(8,128)(2,1)}) %all-gather.19.cloned.1.call-update) | async-done | bytes 13762576 | tf_op jit(solution)/shard_map/all_gather | solution.py:62
  667.0 8.3 fusion.97
  675.3 53.1 %multiply_add_fusion = (f32[2048,4480]{1,0:T(8,128)}, bf16[2048,4480]{1,0:T(8,128)(2,1)}) fusion(bf16[1536,4480]{1,0:T(8,128)(2,1)} %all-gather.19.cloned.1.call-done, bf16[1024,1536]{1,0:T(8,128)(2,1)} %collective-permute-done.9, bf16[1024,1536]{1,0:T(8,128)(2,1)S(1)} %copy-done.19), kind=kOutput, calls=%fused_computation.2 | convolution fusion | flops 28326756352 | bytes 75104256 | tf_op jit(solution)/shard_map/td,df->tf/dot_general | solution.py:35
  728.4 57.8 %all-gather.21.cloned.1.call-done = bf16[4096,1536]{1,0:T(8,128)(2,1)} async-done(((bf16[1024,1536]{1,0:T(8,128)(2,1)}), bf16[4096,1536]{1,0:T(8,128)(2,1)}) %all-gather.21.cloned.1.call-update) | async-done | bytes 12582928 | tf_op jit(solution)/shard_map/all_gather | solution.py:62
  786.2 31.0 %multiply_add_fusion.10 = (f32[4096,1120]{0,1:T(8,128)}, bf16[4096,1120]{0,1:T(8,128)(2,1)}) fusion(bf16[4096,1536]{1,0:T(8,128)(2,1)} %all-gather.21.cloned.1.call-done, bf16[1536,1120]{1,0:T(8,128)(2,1)} %fusion.97), kind=kOutput, calls=%fused_computation.26 | convolution fusion | flops 14157086720 | bytes 43548672 | tf_op jit(solution)/shard_map/td,df->tf/dot_general | solution.py:35
  817.2 25.3 %fusion.12 = bf16[4096,1120]{0,1:T(8,128)(2,1)} fusion(f32[4096,1120]{0,1:T(8,128)} %get-tuple-element.31, bf16[4096,1536]{1,0:T(8,128)(2,1)} %all-gather.23.cloned.1.call-done, bf16[2,1120,1536]{2,1,0:T(8,128)(2,1)} %param.14), kind=kOutput, calls=%fused_computation.30 | convolution fusion | flops 14102036480 | bytes 43548672 | tf_op jit(solution)/shard_map/td,fd->tf/dot_general | solution.py:35
  842.6 21.3 %fusion.164 = f32[1536,1120]{0,1:T(8,128)} fusion(bf16[4096,1120]{0,1:T(8,128)(2,1)} %fusion.12, bf16[4096,1536]{1,0:T(8,128)(2,1)} %all-gather.21.cloned.1.call-done), kind=kOutput, calls=%fused_computation.326 | convolution fusion | flops 14092861440 | bytes 28639232 | tf_op jit(solution)/shard_map/td,tf->df/dot_general | solution.py:35
  863.9 18.8 %fusion.161 = f32[1120,1536]{1,0:T(8,128)} fusion(bf16[4096,1120]{0,1:T(8,128)(2,1)S(1)} %copy-done.68, bf16[4096,1536]{1,0:T(8,128)(2,1)} %all-gather.23.cloned.1.call-done), kind=kOutput, calls=%fused_computation.323 | convolution fusion | flops 14092861440 | bytes 28639232 | tf_op jit(solution)/shard_map/tf,td->fd/dot_general | solution.py:35
  882.7 30.0 %multiply_add_fusion.8 = (f32[4096,1120]{0,1:T(8,128)}, bf16[4096,1120]{0,1:T(8,128)(2,1)}) fusion(bf16[4096,1536]{1,0:T(8,128)(2,1)} %collective-permute-done.11, bf16[1536,1120]{1,0:T(8,128)(2,1)S(1)} %copy-done.25), kind=kOutput, calls=%fused_computation.22 | convolution fusion | flops 14157086720 | bytes 43548672 | tf_op jit(solution)/shard_map/td,df->tf/dot_general | solution.py:35
  912.7 24.9 %fusion.13 = bf16[4096,1120]{0,1:T(8,128)(2,1)} fusion(f32[4096,1120]{0,1:T(8,128)} %get-tuple-element.32, bf16[4096,1536]{1,0:T(8,128)(2,1)} %collective-permute-done.12, bf16[2,1120,1536]{2,1,0:T(8,128)(2,1)} %param.14), kind=kOutput, calls=%fused_computation.31 | convolution fusion | flops 14102036480 | bytes 43548672 | tf_op jit(solution)/shard_map/td,fd->tf/dot_general | solution.py:35
  937.6 22.0 %convolution_add_fusion.1 = f32[1536,1120]{0,1:T(8,128)} fusion(f32[1536,1120]{0,1:T(8,128)} %fusion.164, bf16[4096,1120]{0,1:T(8,128)(2,1)} %fusion.13, bf16[4096,1536]{1,0:T(8,128)(2,1)} %collective-permute-done.11), kind=kOutput, calls=%fused_computation.57 | convolution fusion | flops 14094581760 | bytes 35520512 | tf_op jit(solution)/shard_map/td,tf->df/dot_general | solution.py:35
  959.6 18.4 %convolution_add_fusion.3 = f32[1120,1536]{1,0:T(8,128)} fusion(f32[1120,1536]{1,0:T(8,128)S(1)} %copy-done.67, bf16[4096,1120]{0,1:T(8,128)(2,1)S(1)} %copy-done.66, bf16[4096,1536]{1,0:T(8,128)(2,1)} %collective-permute-done.12), kind=kOutput, calls=%fused_computation.59 | convolution fusion | flops 14094581760 | bytes 35520512 | tf_op jit(solution)/shard_map/tf,td->fd/dot_general | solution.py:35
  978.0 41.8 %multiply_convert_fusion.1 = bf16[2048,4480]{1,0:T(8,128)(2,1)} fusion(f32[2048,4480]{1,0:T(8,128)} %get-tuple-element.36, bf16[4480,1536]{1,0:T(8,128)(2,1)} %bitcast.276, bf16[1024,1536]{1,0:T(8,128)(2,1)} %collective-permute-done.14, bf16[1024,1536]{1,0:T(8,128)(2,1)} %bitcast.21), kind=kOutput, calls=%fused_computation.1 | convolution fusion | flops 28216655872 | bytes 75104256 | tf_op jit(solution)/shard_map/td,fd->tf/dot_general | solution.py:35
  1019.8 21.6 %fusion.25 = f32[1024,1536]{1,0:T(8,128)} fusion(bf16[1536,4480]{1,0:T(8,128)(2,1)} %all-gather.19.cloned.1.call-done, bf16[2048,4480]{1,0:T(8,128)(2,1)} %multiply_convert_fusion.1), kind=kOutput, calls=%fused_computation.68 | convolution fusion | flops 14092861440 | bytes 29229056 | tf_op jit(solution)/shard_map/tf,df->td/dot_general | solution.py:35
  1042.0 10.0 collective-permute-done.15
  1052.1 22.9 %fusion.55 = (f32[1024]{0:T(1024)S(1)}, f32[1024,1536]{1,0:T(8,128)}) fusion(bf16[1024,1536]{1,0:T(8,128)(2,1)S(1)} %copy-done.9, f32[1024,1536]{1,0:T(8,128)} %collective-permute-done.15, bf16[1536,4480]{1,0:T(8,128)(2,1)} %all-gather.19.cloned.1.call-done, bf16[2048,4480]{1,0:T(8,128)(2,1)} %multiply_convert_fusion.1), kind=kOutput, calls=%fused_computation.100 | convolution fusion | flops 14099151872 | bytes 38670336 | tf_op jit(solution)/shard_map/tf,df->td/dot_general | solution.py:35
  1087.1 10.0 fusion.102.d_o_ref
  1097.1 27.8 %shard_map.145 = bf16[2048,1024]{1,0:T(8,128)(2,1)} custom-call(bf16[2048,1024]{1,0:T(8,128)(2,1)} %fusion.95.qkv_ref, bf16[2048,768]{1,0:T(8,128)(2,1)} %fusion.102.d_o_ref), custom_call_target="tpu_custom_call" | custom-call | flops 40000000000 | tf_op jit(solution)/shard_map/pallas_call | solution.py:129
  1124.9 8.8 fusion.104
  1141.0 12.4 fusion.90
  1153.4 8.2 fusion.51
  1169.4 40.8 %multiply_convert_fusion = bf16[2048,4480]{1,0:T(8,128)(2,1)} fusion(f32[2048,4480]{1,0:T(8,128)} %get-tuple-element.38, bf16[1,4480,1536]{2,1,0:T(8,128)(2,1)} %all-gather.29.cloned.1.call-done, bf16[1024,1536]{1,0:T(8,128)(2,1)} %collective-permute-done.18, bf16[1024,1536]{1,0:T(8,128)(2,1)S(1)} %fusion.39), kind=kOutput, calls=%fused_computation | convolution fusion | flops 28216655872 | bytes 75104256 | tf_op jit(solution)/shard_map/td,fd->tf/dot_general | solution.py:35
  1210.2 21.8 %fusion.21 = f32[1024,1536]{1,0:T(8,128)} fusion(bf16[1536,4480]{1,0:T(8,128)(2,1)} %all-gather.15.cloned.1.call-done, bf16[2048,4480]{1,0:T(8,128)(2,1)} %multiply_convert_fusion), kind=kOutput, calls=%fused_computation.64 | convolution fusion | flops 14092861440 | bytes 29229056 | tf_op jit(solution)/shard_map/tf,df->td/dot_general | solution.py:35
  1239.6 31.0 %multiply_add_fusion.6 = (f32[4096,1120]{0,1:T(8,128)}, bf16[4096,1120]{0,1:T(8,128)(2,1)}) fusion(bf16[4096,1536]{1,0:T(8,128)(2,1)} %all-gather.25.cloned.1.call-done, bf16[1536,1120]{1,0:T(8,128)(2,1)S(1)} %fusion.96), kind=kOutput, calls=%fused_computation.18 | convolution fusion | flops 14157086720 | bytes 43548672 | tf_op jit(solution)/shard_map/td,df->tf/dot_general | solution.py:35
  1270.6 7.8 copy.145
  1293.7 24.9 %fusion.47 = (f32[1024]{0:T(1024)S(1)}, f32[1024,1536]{1,0:T(8,128)}) fusion(bf16[1024,1536]{1,0:T(8,128)(2,1)} %copy-done.11, f32[1024,1536]{1,0:T(8,128)} %collective-permute-done.19, bf16[1536,4480]{1,0:T(8,128)(2,1)} %all-gather.15.cloned.1.call-done, bf16[2048,4480]{1,0:T(8,128)(2,1)} %multiply_convert_fusion), kind=kOutput, calls=%fused_computation.92 | convolution fusion | flops 14099151872 | bytes 38670336 | tf_op jit(solution)/shard_map/tf,df->td/dot_general | solution.py:35
  1323.6 30.6 %multiply_add_fusion.4 = (f32[4096,1120]{0,1:T(8,128)}, bf16[4096,1120]{0,1:T(8,128)(2,1)}) fusion(bf16[4096,1536]{1,0:T(8,128)(2,1)} %collective-permute-done.26, bf16[1536,1120]{1,0:T(8,128)(2,1)} %copy-done.24), kind=kOutput, calls=%fused_computation.14 | convolution fusion | flops 14157086720 | bytes 43548672 | tf_op jit(solution)/shard_map/td,df->tf/dot_general | solution.py:35
  1356.4 42.1 %collective-permute-done.33 = f32[384,1120]{0,1:T(8,128)} collective-permute-done((f32[384,1120]{0,1:T(8,128)}, f32[384,1120]{0,1:T(8,128)}, u32[]{:S(2)}, u32[]{:S(2)}) %collective-permute-start.33) | collective-permute-done | bytes 1720352 | tf_op jit(solution)/shard_map/ppermute | solution.py:216
  1411.2 10.2 fusion.103.d_o_ref
  1421.4 27.8 %shard_map.146 = bf16[2048,1024]{1,0:T(8,128)(2,1)} custom-call(bf16[2048,1024]{1,0:T(8,128)(2,1)} %fusion.94.qkv_ref, bf16[2048,768]{1,0:T(8,128)(2,1)} %fusion.103.d_o_ref), custom_call_target="tpu_custom_call" | custom-call | flops 40000000000 | tf_op jit(solution)/shard_map/pallas_call | solution.py:129
  1449.2 8.8 fusion.108
  1458.6 21.7 %fusion.29 = f32[1024,1536]{1,0:T(8,128)} fusion(bf16[4480,1536]{1,0:T(8,128)(2,1)} %bitcast.277, bf16[2048,4480]{1,0:T(8,128)(2,1)} %get-tuple-element.30), kind=kOutput, calls=%fused_computation.72 | convolution fusion | flops 14092861440 | bytes 29229056 | tf_op jit(solution)/shard_map/tf,fd->td/dot_general | solution.py:35
  1483.2 7.9 concatenate.89
  1495.7 9.6 fusion.86
  1505.3 12.3 fusion.92
  1518.1 8.0 fusion.73
  1530.7 23.2 %fusion.54 = bf16[1024,1536]{1,0:T(8,128)(2,1)} fusion(bf16[1024,1536]{1,0:T(8,128)(2,1)} %copy-done.8, f32[1024,1536]{1,0:T(8,128)} %collective-permute-done.13, bf16[4480,1536]{1,0:T(8,128)(2,1)} %bitcast.278, bf16[2048,4480]{1,0:T(8,128)(2,1)} %get-tuple-element.30), kind=kOutput, calls=%fused_computation.99 | convolution fusion | flops 14099152896 | bytes 35520512 | tf_op jit(solution)/shard_map/tf,fd->td/dot_general | solution.py:35
  1561.3 25.4 %fusion.14 = bf16[4096,1120]{0,1:T(8,128)(2,1)} fusion(f32[4096,1120]{0,1:T(8,128)} %get-tuple-element.44, bf16[4096,1536]{1,0:T(8,128)(2,1)} %all-gather.27.cloned.1.call-done, bf16[2,1120,1536]{2,1,0:T(8,128)(2,1)} %param.14), kind=kOutput, calls=%fused_computation.32 | convolution fusion | flops 14102036480 | bytes 43548672 | tf_op jit(solution)/shard_map/td,fd->tf/dot_general | solution.py:35
  1586.6 23.4 %fusion.162 = f32[1536,1120]{1,0:T(8,128)} fusion(bf16[4096,1536]{1,0:T(8,128)(2,1)} %all-gather.25.cloned.1.call-done, bf16[4096,1120]{0,1:T(8,128)(2,1)} %fusion.14), kind=kOutput, calls=%fused_computation.324 | convolution fusion | flops 14092861440 | bytes 28639232 | tf_op jit(solution)/shard_map/td,tf->df/dot_general | solution.py:35
  1612.1 25.5 %fusion.15 = bf16[4096,1120]{0,1:T(8,128)(2,1)} fusion(f32[4096,1120]{0,1:T(8,128)} %get-tuple-element.45, bf16[4096,1536]{1,0:T(8,128)(2,1)} %collective-permute-done.27, bf16[2,1120,1536]{2,1,0:T(8,128)(2,1)} %param.14), kind=kOutput, calls=%fused_computation.33 | convolution fusion | flops 14102036480 | bytes 43548672 | tf_op jit(solution)/shard_map/td,fd->tf/dot_general | solution.py:35
  1637.6 22.9 %convolution_add_fusion = f32[1536,1120]{1,0:T(8,128)S(1)} fusion(f32[1536,1120]{1,0:T(8,128)} %fusion.162, bf16[4096,1536]{1,0:T(8,128)(2,1)} %collective-permute-done.26, bf16[4096,1120]{0,1:T(8,128)(2,1)} %fusion.15), kind=kOutput, calls=%fused_computation.56 | convolution fusion | flops 14094581760 | bytes 35520512 | tf_op jit(solution)/shard_map/td,tf->df/dot_general | solution.py:35
  1672.5 21.3 %fusion.163 = f32[1120,1536]{1,0:T(8,128)} fusion(bf16[4096,1120]{0,1:T(8,128)(2,1)} %get-tuple-element.47, bf16[4096,1536]{1,0:T(8,128)(2,1)} %all-gather.27.cloned.1.call-done), kind=kOutput, calls=%fused_computation.325 | convolution fusion | flops 14092861440 | bytes 28639232 | tf_op jit(solution)/shard_map/tf,td->fd/dot_general | solution.py:35
  1700.0 11.6 collective-permute-done.30
  1713.9 33.5 %collective-permute-done.29 = f32[384,1120]{0,1:T(8,128)} collective-permute-done((f32[384,1120]{0,1:T(8,128)}, f32[384,1120]{0,1:T(8,128)}, u32[]{:S(2)}, u32[]{:S(2)}) %collective-permute-start.29) | collective-permute-done | bytes 1720352 | tf_op jit(solution)/shard_map/ppermute | solution.py:216
  1759.5 22.0 %fusion.35 = f32[1,1120,1536]{2,1,0:T(8,128)} fusion(f32[1120,1536]{1,0:T(8,128)} %fusion.163, bf16[4096,1120]{0,1:T(8,128)(2,1)} %get-tuple-element.48, bf16[4096,1536]{1,0:T(8,128)(2,1)} %collective-permute-done.27), kind=kOutput, calls=%fused_computation.78 | convolution fusion | flops 14094581760 | bytes 35520512 | tf_op jit(solution)/shard_map/tf,td->fd/dot_general | solution.py:35
  1784.0 11.6 pad_maximum_fusion.1
  1812.7 8.0 concatenate.88
  1820.7 11.0 pad_maximum_fusion
  (379 shorter events, 274.7 us)
Async XLA Ops:
  7.2 95.4 %all-gather.13.cloned.1.call-start = ((), (), s32[]{:S(2)}) async-start(), calls=%async_computation.4 | async-start | bytes 6881280 | tf_op jit(solution)/shard_map/all_gather | solution.py:62
  19.6 19.8 %collective-permute-start.1 = (bf16[192,1792]{1,0:T(8,128)(2,1)}, bf16[192,1792]{1,0:T(8,128)(2,1)}, u32[]{:S(2)}, u32[]{:S(2)}) collective-permute-start(bf16[192,1792]{1,0:T(8,128)(2,1)} %broadcast_select_fusion.14), channel_id=1, source_target_pairs={{0,1},{1,0},{2,3},{3,2},{4,5},{5,4},{6,7},{7,6}} | collective-permute-start | bytes 2064392 | tf_op jit(solution)/shard_map/ppermute | solution.py:39
  42.4 188.6 %all-gather.15.cloned.1.call-start = ((), (), s32[]{:S(2)}) async-start(), calls=%async_computation.5 | async-start | bytes 17203200 | tf_op jit(solution)/shard_map/all_gather | solution.py:62
  63.0 4.0 collective-permute-start.4
  70.7 289.3 %all-gather.29.cloned.1.call-start = ((), (), s32[]{:S(2)}) async-start(), calls=%async_computation.16 | async-start | bytes 17203200 | tf_op jit(solution)/shard_map/all_gather | solution.py:62
  77.7 345.6 %all-gather.17.cloned.1.call-start = ((), (), s32[]{:S(2)}) async-start(), calls=%async_computation.6 | async-start | bytes 6881280 | tf_op jit(solution)/shard_map/all_gather | solution.py:62
  81.6 5.8 collective-permute-start
  139.0 18.0 collective-permute-start.2
  153.1 2.3 collective-permute-start.7
  157.0 381.1 %all-gather.23.cloned.1.call-start = ((), (), s32[]{:S(2)}) async-start(), calls=%async_computation.9 | async-start | bytes 15728640 | tf_op jit(solution)/shard_map/all_gather | solution.py:62
  167.0 115.4 %copy-start.18 = (bf16[1024,1536]{1,0:T(8,128)(2,1)}, bf16[1024,1536]{1,0:T(8,128)(2,1)S(1)}, u32[]{:S(2)}) copy-start(bf16[1024,1536]{1,0:T(8,128)(2,1)S(1)} %fusion.45) | copy-start | bytes 9437188
  167.0 5.8 collective-permute-start.3
  167.4 499.6 %all-gather.19.cloned.1.call-start = ((), (), s32[]{:S(2)}) async-start(), calls=%async_computation.7 | async-start | bytes 17203200 | tf_op jit(solution)/shard_map/all_gather | solution.py:62
  282.3 99.2 %copy-start.21 = (bf16[192,4,1,1120]{3,1,0,2:T(4,128)(2,1)S(1)}, bf16[192,4,1,1120]{3,1,0,2:T(4,128)(2,1)}, u32[]{:S(2)}) copy-start(bf16[192,4,1,1120]{3,1,0,2:T(4,128)(2,1)} %get-tuple-element.123) | copy-start | bytes 5160964
  282.3 102.2 %copy-start.20 = (bf16[192,4,1,1120]{3,1,0,2:T(4,128)(2,1)S(1)}, bf16[192,4,1,1120]{3,1,0,2:T(4,128)(2,1)}, u32[]{:S(2)}) copy-start(bf16[192,4,1,1120]{3,1,0,2:T(4,128)(2,1)} %get-tuple-element.122) | copy-start | bytes 5160964
  381.5 16.8 collective-permute-start.5
  384.0 10.4 collective-permute-start.10
  398.2 388.0 %all-gather.21.cloned.1.call-start = ((), (), s32[]{:S(2)}) async-start(), calls=%async_computation.8 | async-start | bytes 15728640 | tf_op jit(solution)/shard_map/all_gather | solution.py:62
  423.1 5.8 collective-permute-start.6
  461.9 10.2 collective-permute-start.8
  481.2 496.8 %all-gather.31.cloned.1.call-start = ((), (), s32[]{:S(2)}) async-start(), calls=%async_computation.17 | async-start | bytes 17203200 | tf_op jit(solution)/shard_map/all_gather | solution.py:62
  481.2 194.0 %collective-permute-start.9 = (bf16[1024,1536]{1,0:T(8,128)(2,1)}, bf16[1024,1536]{1,0:T(8,128)(2,1)}, u32[]{:S(2)}, u32[]{:S(2)}) collective-permute-start(bf16[1024,1536]{1,0:T(8,128)(2,1)} %fusion.53), channel_id=1, source_target_pairs={{0,1},{1,0},{2,3},{3,2},{4,5},{5,4},{6,7},{7,6}} | collective-permute-start | bytes 9437192 | tf_op jit(solution)/shard_map/ppermute | solution.py:39
  481.4 496.6 %collective-permute-start.14 = (bf16[1024,1536]{1,0:T(8,128)(2,1)}, bf16[1024,1536]{1,0:T(8,128)(2,1)}, u32[]{:S(2)}, u32[]{:S(2)}) collective-permute-start(bf16[1024,1536]{1,0:T(8,128)(2,1)} %bitcast.21), channel_id=1, source_target_pairs={{0,1},{1,0},{2,3},{3,2},{4,5},{5,4},{6,7},{7,6}} | collective-permute-start | bytes 9437192 | tf_op jit(solution)/shard_map/ppermute | solution.py:39
  481.9 681.8 %all-gather.25.cloned.1.call-start = ((), (), s32[]{:S(2)}) async-start(), calls=%async_computation.14 | async-start | bytes 15728640 | tf_op jit(solution)/shard_map/all_gather | solution.py:62
  482.0 193.3 %copy-start.19 = (bf16[1024,1536]{1,0:T(8,128)(2,1)S(1)}, bf16[1024,1536]{1,0:T(8,128)(2,1)}, u32[]{:S(2)}) copy-start(bf16[1024,1536]{1,0:T(8,128)(2,1)} %fusion.53) | copy-start | bytes 9437188
  538.1 374.5 %collective-permute-start.12 = (bf16[4096,1536]{1,0:T(8,128)(2,1)}, bf16[4096,1536]{1,0:T(8,128)(2,1)}, u32[]{:S(2)}, u32[]{:S(2)}) collective-permute-start(bf16[4096,1536]{1,0:T(8,128)(2,1)} %all-gather.23.cloned.1.call-done), channel_id=1, source_target_pairs={{0,1},{1,0},{2,3},{3,2},{4,5},{5,4},{6,7},{7,6}} | collective-permute-start | bytes 37748744 | tf_op jit(solution)/shard_map/ppermute | solution.py:39
  786.2 96.5 %collective-permute-start.11 = (bf16[4096,1536]{1,0:T(8,128)(2,1)}, bf16[4096,1536]{1,0:T(8,128)(2,1)}, u32[]{:S(2)}, u32[]{:S(2)}) collective-permute-start(bf16[4096,1536]{1,0:T(8,128)(2,1)} %all-gather.21.cloned.1.call-done), channel_id=1, source_target_pairs={{0,1},{1,0},{2,3},{3,2},{4,5},{5,4},{6,7},{7,6}} | collective-permute-start | bytes 37748744 | tf_op jit(solution)/shard_map/ppermute | solution.py:39
  1019.8 32.2 %copy-start.9 = (bf16[1024,1536]{1,0:T(8,128)(2,1)S(1)}, bf16[1024,1536]{1,0:T(8,128)(2,1)}, u32[]{:S(2)}) copy-start(bf16[1024,1536]{1,0:T(8,128)(2,1)} %copy-done.8) | copy-start | bytes 9437188
  1041.5 10.6 collective-permute-start.15
  1042.0 33.0 %copy-start.61 = (f32[1024]{0:T(1024)S(1)}, f32[1024]{0:T(1024)}, u32[]{:S(2)}) copy-start(f32[1024]{0:T(1024)} %copy-done.60) | copy-start | bytes 12292
  1042.0 33.0 %copy-start.55 = (f32[1024]{0:T(1024)S(1)}, f32[1024]{0:T(1024)}, u32[]{:S(2)}) copy-start(f32[1024]{0:T(1024)} %copy-done.54) | copy-start | bytes 12292
  1042.0 449.1 %reduce-scatter.11.cloned.1.call-start = ((), (), s32[]{:S(2)}) async-start(), calls=%async_computation.13 | async-start | bytes 5898240 | tf_op jit(solution)/shard_map/reduce_scatter | solution.py:66
  1042.0 32.9 %copy-start.10 = (bf16[1024,1536]{1,0:T(8,128)(2,1)S(1)}, bf16[1024,1536]{1,0:T(8,128)(2,1)}, u32[]{:S(2)}) copy-start(bf16[1024,1536]{1,0:T(8,128)(2,1)} %copy-done.8) | copy-start | bytes 9437188
  1079.7 54.4 %copy-start.6 = (bf16[1024,1536]{1,0:T(8,128)(2,1)}, bf16[1024,1536]{1,0:T(8,128)(2,1)S(1)}, u32[]{:S(2)}) copy-start(bf16[1024,1536]{1,0:T(8,128)(2,1)S(1)} %fusion.37) | copy-start | bytes 9437188
  1079.7 5.7 collective-permute-start.16
  1133.7 19.6 %collective-permute-start.17 = (f32[1024,1536]{1,0:T(8,128)}, f32[1024,1536]{1,0:T(8,128)}, u32[]{:S(2)}, u32[]{:S(2)}) collective-permute-start(f32[1024,1536]{1,0:T(8,128)} %fusion.104), channel_id=1, source_target_pairs={{0,1},{1,0},{2,3},{3,2},{4,5},{5,4},{6,7},{7,6}} | collective-permute-start | bytes 18874376 | tf_op jit(solution)/shard_map/ppermute | solution.py:39
  1163.5 46.7 %copy-start.2 = (bf16[1024,1536]{1,0:T(8,128)(2,1)}, bf16[1024,1536]{1,0:T(8,128)(2,1)S(1)}, u32[]{:S(2)}) copy-start(bf16[1024,1536]{1,0:T(8,128)(2,1)S(1)} %fusion.39) | copy-start | bytes 9437188
  1163.5 330.0 %reduce-scatter.7.cloned.1.call-start = ((), (), s32[]{:S(2)}) async-start(), calls=%async_computation.11 | async-start | bytes 7864320 | tf_op jit(solution)/shard_map/reduce_scatter | solution.py:66
  1163.6 5.8 collective-permute-start.18
  1163.7 159.9 %collective-permute-start.26 = (bf16[4096,1536]{1,0:T(8,128)(2,1)}, bf16[4096,1536]{1,0:T(8,128)(2,1)}, u32[]{:S(2)}, u32[]{:S(2)}) collective-permute-start(bf16[4096,1536]{1,0:T(8,128)(2,1)} %all-gather.25.cloned.1.call-done), channel_id=1, source_target_pairs={{0,1},{1,0},{2,3},{3,2},{4,5},{5,4},{6,7},{7,6}} | collective-permute-start | bytes 37748744 | tf_op jit(solution)/shard_map/ppermute | solution.py:39
  1164.2 353.4 %all-gather.27.cloned.1.call-start = ((), (), s32[]{:S(2)}) async-start(), calls=%async_computation.15 | async-start | bytes 15728640 | tf_op jit(solution)/shard_map/all_gather | solution.py:62
  1231.9 61.7 %collective-permute-start.19 = (f32[1024,1536]{1,0:T(8,128)}, f32[1024,1536]{1,0:T(8,128)}, u32[]{:S(2)}, u32[]{:S(2)}) collective-permute-start(f32[1024,1536]{1,0:T(8,128)} %fusion.21), channel_id=1, source_target_pairs={{0,1},{1,0},{2,3},{3,2},{4,5},{5,4},{6,7},{7,6}} | collective-permute-start | bytes 18874376 | tf_op jit(solution)/shard_map/ppermute | solution.py:39
  1239.6 31.1 %copy-start.24 = (bf16[1536,1120]{1,0:T(8,128)(2,1)}, bf16[1536,1120]{1,0:T(8,128)(2,1)S(1)}, u32[]{:S(2)}) copy-start(bf16[1536,1120]{1,0:T(8,128)(2,1)S(1)} %fusion.96) | copy-start | bytes 10321924
  1286.6 67.6 %collective-permute-start.34 = (f32[384,1120]{0,1:T(8,128)}, f32[384,1120]{0,1:T(8,128)}, u32[]{:S(2)}, u32[]{:S(2)}) collective-permute-start(f32[384,1120]{0,1:T(8,128)} %bitcast.260), channel_id=1, source_target_pairs={{0,6},{2,4},{4,2},{6,0},{1,7},{3,5},{5,3},{7,1}} | collective-permute-start | bytes 5160968 | tf_op jit(solution)/shard_map/ppermute | solution.py:216
  1291.2 107.2 %collective-permute-start.33 = (f32[384,1120]{0,1:T(8,128)}, f32[384,1120]{0,1:T(8,128)}, u32[]{:S(2)}, u32[]{:S(2)}) collective-permute-start(f32[384,1120]{0,1:T(8,128)} %bitcast.261), channel_id=1, source_target_pairs={{0,4},{2,6},{4,0},{6,2},{1,5},{3,7},{5,1},{7,3}} | collective-permute-start | bytes 5160968 | tf_op jit(solution)/shard_map/ppermute | solution.py:216
  1293.2 107.6 %collective-permute-start.32 = (f32[384,1120]{0,1:T(8,128)}, f32[384,1120]{0,1:T(8,128)}, u32[]{:S(2)}, u32[]{:S(2)}) collective-permute-start(f32[384,1120]{0,1:T(8,128)} %bitcast.72), channel_id=1, source_target_pairs={{0,2},{2,0},{4,6},{6,4},{1,3},{3,1},{5,7},{7,5}} | collective-permute-start | bytes 5160968 | tf_op jit(solution)/shard_map/ppermute | solution.py:216
  1293.6 25.0 %copy-start.3 = (bf16[1024,1536]{1,0:T(8,128)(2,1)S(1)}, bf16[1024,1536]{1,0:T(8,128)(2,1)}, u32[]{:S(2)}) copy-start(bf16[1024,1536]{1,0:T(8,128)(2,1)} %copy-done.2) | copy-start | bytes 9437188
  1293.6 25.0 %copy-start.51 = (f32[1024]{0:T(1024)S(1)}, f32[1024]{0:T(1024)}, u32[]{:S(2)}) copy-start(f32[1024]{0:T(1024)} %copy-done.50) | copy-start | bytes 12292
  1293.6 316.5 %reduce-scatter.9.cloned.1.call-start = ((), (), s32[]{:S(2)}) async-start(), calls=%async_computation.12 | async-start | bytes 5898240 | tf_op jit(solution)/shard_map/reduce_scatter | solution.py:66
  1323.6 87.6 %collective-permute-start.20 = (bf16[1024,1536]{1,0:T(8,128)(2,1)}, bf16[1024,1536]{1,0:T(8,128)(2,1)}, u32[]{:S(2)}, u32[]{:S(2)}) collective-permute-start(bf16[1024,1536]{1,0:T(8,128)(2,1)} %fusion.41), channel_id=1, source_target_pairs={{0,1},{1,0},{2,3},{3,2},{4,5},{5,4},{6,7},{7,6}} | collective-permute-start | bytes 9437192 | tf_op jit(solution)/shard_map/ppermute | solution.py:39
  1411.2 69.1 %collective-permute-start.35 = (f32[4,192,1120]{2,1,0:T(8,128)}, f32[4,192,1120]{2,1,0:T(8,128)S(1)}, u32[]{:S(2)}, u32[]{:S(2)}) collective-permute-start(f32[4,192,1120]{2,1,0:T(8,128)} %dynamic-slice_bitcast_fusion), channel_id=1, source_target_pairs={{0,1},{1,0},{2,3},{3,2},{4,5},{5,4},{6,7},{7,6}} | collective-permute-start | bytes 10321928 | tf_op jit(solution)/shard_map/ppermute | solution.py:39
  1449.2 31.1 %slice-start.2 = ((s8[7077888]{0:T(1024)(128)(4,1)}), s8[4194304]{0:T(1024)(128)(4,1)S(1)}, s32[]{:S(2)}) async-start(s8[7077888]{0:T(1024)(128)(4,1)} %bitcast.244), calls=%async_computation.20 | async-start | bytes 8388608
  1458.1 60.0 %collective-permute-start.21 = (f32[1024,1536]{1,0:T(8,128)}, f32[1024,1536]{1,0:T(8,128)}, u32[]{:S(2)}, u32[]{:S(2)}) collective-permute-start(f32[1024,1536]{1,0:T(8,128)} %fusion.108), channel_id=1, source_target_pairs={{0,1},{1,0},{2,3},{3,2},{4,5},{5,4},{6,7},{7,6}} | collective-permute-start | bytes 18874376 | tf_op jit(solution)/shard_map/ppermute | solution.py:39
  1480.3 50.4 %collective-permute-start.13 = (f32[1024,1536]{1,0:T(8,128)}, f32[1024,1536]{1,0:T(8,128)}, u32[]{:S(2)}, u32[]{:S(2)}) collective-permute-start(f32[1024,1536]{1,0:T(8,128)} %fusion.29), channel_id=1, source_target_pairs={{0,1},{1,0},{2,3},{3,2},{4,5},{5,4},{6,7},{7,6}} | collective-permute-start | bytes 18874376 | tf_op jit(solution)/shard_map/ppermute | solution.py:39
  1493.1 60.8 %collective-permute-start.25 = (f32[192,768]{1,0:T(8,128)}, f32[192,768]{1,0:T(8,128)}, u32[]{:S(2)}, u32[]{:S(2)}) collective-permute-start(f32[192,768]{1,0:T(8,128)} %dynamic-slice_bitcast_fusion.20), channel_id=1, source_target_pairs={{0,1},{1,0},{2,3},{3,2},{4,5},{5,4},{6,7},{7,6}} | collective-permute-start | bytes 1769480 | tf_op jit(solution)/shard_map/ppermute | solution.py:39
  1495.6 60.9 %collective-permute-start.23 = (f32[192,1024]{1,0:T(8,128)}, f32[192,1024]{1,0:T(8,128)}, u32[]{:S(2)}, u32[]{:S(2)}) collective-permute-start(f32[192,1024]{1,0:T(8,128)} %dynamic-slice_bitcast_fusion.18), channel_id=1, source_target_pairs={{0,1},{1,0},{2,3},{3,2},{4,5},{5,4},{6,7},{7,6}} | collective-permute-start | bytes 2359304 | tf_op jit(solution)/shard_map/ppermute | solution.py:39
  1517.6 94.5 %collective-permute-start.27 = (bf16[4096,1536]{1,0:T(8,128)(2,1)}, bf16[4096,1536]{1,0:T(8,128)(2,1)}, u32[]{:S(2)}, u32[]{:S(2)}) collective-permute-start(bf16[4096,1536]{1,0:T(8,128)(2,1)} %all-gather.27.cloned.1.call-done), channel_id=1, source_target_pairs={{0,1},{1,0},{2,3},{3,2},{4,5},{5,4},{6,7},{7,6}} | collective-permute-start | bytes 37748744 | tf_op jit(solution)/shard_map/ppermute | solution.py:39
  1530.6 250.9 %reduce-scatter.5.cloned.1.call-start = ((), (), s32[]{:S(2)}) async-start(), calls=%async_computation.10 | async-start | bytes 7864320 | tf_op jit(solution)/shard_map/reduce_scatter | solution.py:66
  1612.0 81.8 %collective-permute-start.24 = (f32[192,768]{1,0:T(8,128)}, f32[192,768]{1,0:T(8,128)}, u32[]{:S(2)}, u32[]{:S(2)}) collective-permute-start(f32[192,768]{1,0:T(8,128)} %dynamic-slice_bitcast_fusion.21), channel_id=1, source_target_pairs={{0,1},{1,0},{2,3},{3,2},{4,5},{5,4},{6,7},{7,6}} | collective-permute-start | bytes 1769480 | tf_op jit(solution)/shard_map/ppermute | solution.py:39
  1665.6 46.0 %collective-permute-start.30 = (f32[384,1120]{0,1:T(8,128)}, f32[384,1120]{0,1:T(8,128)}, u32[]{:S(2)}, u32[]{:S(2)}) collective-permute-start(f32[384,1120]{0,1:T(8,128)} %bitcast.262), channel_id=1, source_target_pairs={{0,6},{2,4},{4,2},{6,0},{1,7},{3,5},{5,3},{7,1}} | collective-permute-start | bytes 5160968 | tf_op jit(solution)/shard_map/ppermute | solution.py:216
  1669.4 78.0 %collective-permute-start.29 = (f32[384,1120]{0,1:T(8,128)}, f32[384,1120]{0,1:T(8,128)}, u32[]{:S(2)}, u32[]{:S(2)}) collective-permute-start(f32[384,1120]{0,1:T(8,128)} %bitcast.263), channel_id=1, source_target_pairs={{0,4},{2,6},{4,0},{6,2},{1,5},{3,7},{5,1},{7,3}} | collective-permute-start | bytes 5160968 | tf_op jit(solution)/shard_map/ppermute | solution.py:216
  1671.9 77.6 %collective-permute-start.28 = (f32[384,1120]{0,1:T(8,128)}, f32[384,1120]{0,1:T(8,128)}, u32[]{:S(2)}, u32[]{:S(2)}) collective-permute-start(f32[384,1120]{0,1:T(8,128)} %bitcast.53), channel_id=1, source_target_pairs={{0,2},{2,0},{4,6},{6,4},{1,3},{3,1},{5,7},{7,5}} | collective-permute-start | bytes 5160968 | tf_op jit(solution)/shard_map/ppermute | solution.py:216
  1759.5 48.7 %collective-permute-start.31 = (f32[4,192,1120]{2,1,0:T(8,128)}, f32[4,192,1120]{2,1,0:T(8,128)}, u32[]{:S(2)}, u32[]{:S(2)}) collective-permute-start(f32[4,192,1120]{2,1,0:T(8,128)} %dynamic-slice_bitcast_fusion.1), channel_id=1, source_target_pairs={{0,1},{1,0},{2,3},{3,2},{4,5},{5,4},{6,7},{7,6}} | collective-permute-start | bytes 10321928 | tf_op jit(solution)/shard_map/ppermute | solution.py:39
  1783.5 12.1 collective-permute-start.22
  (59 other events, 476.1 us)
Sparse Core Ops, SparseCore 0:
  42.5 60.0 all-gather.12
  104.4 126.6 all-gather.14
  233.4 126.6 all-gather.28
  361.7 57.9 all-gather.16
  421.3 116.8 all-gather.22
  540.3 126.6 all-gather.18
  669.3 116.8 all-gather.20
  788.0 126.6 all-gather.30
  1042.1 117.2 all-gather.24
  1163.6 52.1 reduce-scatter.10
  1218.8 64.4 reduce-scatter.6
  1293.7 175.3 all-gather.26
  1530.7 52.0 reduce-scatter.8
  1610.2 104.5 reduce-scatter.4
where the time goes:
time: 1850 us; the launch traced here: 1840 us
  matrix products  903 us (49%)
  waiting for transfers between devices  542 us (29%)
  local copies, waits for them, and re-layouts  177 us (10%)
  other arithmetic  95.6 us (5%)
  Pallas kernels  90.1 us (5%)
    dot_general x44, matrix products, mixed(): return jnp.einsum(form, left, right, preferred_element_type=jnp.float32)  903 us
    all_gather x10, waiting for transfers between devices, gather(): return lax.all_gather(piece, 'sub', axis=0, tiled=True)  394 us
    pallas_call x4, Pallas kernels, by_sequence(): pl.pallas_call(functools.partial(kernel, q_width, head), grid=(rows // se...  90.1 us
    ppermute x6, waiting for transfers between devices, up_rows(): lax.ppermute(part, 'sub', [(i, i ^ step) for i in range(chips)])  87.2 us
    ppermute x30, waiting for transfers between devices, swap(): return lax.ppermute(value, 'fsdp', [(0, 1), (1, 0)])  59.9 us
  transfers between devices with their start and end apart: 50, of which 19 were waited for; matrix products, arithmetic and copies ran while one was open for 57% of the time, Pallas kernels for 5%

commit v1 on v0

--- a/solution.py
+++ b/solution.py
@@ -4,7 +4,6 @@
 import jax.numpy as jnp
 from jax import lax
 from jax.experimental import pallas as pl
-from jax.experimental.layout import Layout, with_layout_constraint
 from jax.experimental.pallas import tpu as pltpu
 from jax.sharding import PartitionSpec as P
 
@@ -14,8 +13,11 @@
 MASK_FILL = -1e30
 GELU_A = (2.0 / 3.141592653589793) ** 0.5
 GELU_B = 0.044715
+CHIPS = 4
 CORES = 2
 QUERY_BLOCK = 256
+TOKEN_TILE = 512
+ROW_TILE = 48
 
 
 def rms_norm(values):
@@ -159,7 +161,8 @@
     other = swap(mixed("te,de->td", d_qkv[rows:], w_qkv))
     d_norm = mixed("te,de->td", d_qkv[:rows], w_qkv) + other
     grad_x = (grad_own.astype(jnp.float32) + norm_back(x_own, d_norm)).astype(jnp.bfloat16)
-    return grad_x, mixed("td,te->de", normed, d_qkv), mixed("td,te->de", grad_y, o_act)
+    d_qkv_w = mixed("td,te->de", normed, d_qkv)
+    return grad_x, d_qkv_w, mixed("td,te->de", grad_y, o_act)
 
 
 def gelu_parts(hidden):
@@ -181,13 +184,10 @@
     return (x_own.astype(jnp.float32) + proj).astype(jnp.bfloat16)
 
 
-def grad_hidden(slope, grad_y, down_weight):
-    return (mixed("td,fd->tf", grad_y, down_weight) * slope).astype(jnp.bfloat16)
-
-
 def mlp_backward(x_own, slope, up_weight, down_weight, grad_own):
     rows = grad_own.shape[0]
-    d_hid = grad_hidden(slope, pair_rows(grad_own), down_weight)
+    grad_act = mixed("td,fd->tf", pair_rows(grad_own), down_weight)
+    d_hid = (grad_act * slope).astype(jnp.bfloat16)
     other = swap(mixed("tf,df->td", d_hid[rows:], up_weight))
     d_norm = mixed("tf,df->td", d_hid[:rows], up_weight) + other
     return (grad_own.astype(jnp.float32) + norm_back(x_own, d_norm)).astype(jnp.bfloat16)
@@ -198,29 +198,95 @@
     return mine, swap(mine)
 
 
-def mlp_weight_grads(norms, grads, up_block, down_block):
-    d_up, d_down = 0.0, 0.0
-    for normed, grad_y in zip(norms, grads):
-        gelu_act, slope = mlp_hidden(normed, up_block)
-        d_down = d_down + mixed("tf,td->fd", gelu_act, grad_y)
-        d_hid = lax.optimization_barrier(grad_hidden(slope, grad_y, down_block))
-        d_up = d_up + mixed("td,tf->df", normed, d_hid)
-    return d_up, d_down
-
-
-def up_rows(core, chip, chips, d_up):
-    grid = with_layout_constraint(d_up.reshape((chips, -1) + d_up.shape[1:]), Layout(major_to_minor=(0, 1, 2)))
-    parts = []
-    for step in range(chips):
-        part = lax.dynamic_index_in_dim(grid, chip ^ step, 0, keepdims=False)
-        parts.append(lax.ppermute(part, "sub", [(i, i ^ step) for i in range(chips)]) if step else part)
-    grid = jnp.stack(parts)
-    grid = grid.reshape(chips, CORES, grid.shape[1] // CORES, grid.shape[2])
-    keep = lax.dynamic_index_in_dim(grid, core, 1, keepdims=False)
-    other = swap(lax.dynamic_index_in_dim(grid, 1 - core, 1, keepdims=False))
-    both = by_core(core, keep, other)
-    cols = [lax.dynamic_index_in_dim(part, chip ^ i, 0, keepdims=False) for i in range(chips) for part in both]
-    return jnp.concatenate(cols, axis=1)
+def mlp_grads_kernel(half, place_ref, up_ref, down_ref, n0_ref, n1_ref, g0_ref, g1_ref, *rest):
+    d_down_ref, parts, d_up_ref, flip_ref = rest[-2 * CHIPS - 3], rest[-2 * CHIPS - 2:-2], rest[-2], rest[-1]
+    step = pl.program_id(0)
+    normed = jnp.where(step < half, n0_ref[...], n1_ref[...])
+    grad_y = jnp.where(step < half, g0_ref[...], g1_ref[...])
+
+    @pl.when(step == 0)
+    def _():
+        d_down_ref[...] = jnp.zeros_like(d_down_ref)
+        d_up_ref[...] = jnp.zeros_like(d_up_ref)
+
+    gelu_act, slope = gelu_parts(dot(up_ref[...], normed, ((1,), (1,))))
+    d_hid = (dot(down_ref[...], grad_y, ((1,), (1,))) * slope).astype(jnp.bfloat16)
+    d_down_ref[0] += dot(gelu_act, grad_y, ((1,), (0,)))
+    d_up_ref[...] += dot(d_hid, normed, ((1,), (0,)))
+
+    @pl.when(step == pl.num_programs(0) - 1)
+    def _():
+        rows = parts[0].shape[0]
+        for i in range(CHIPS):
+            start = pl.multiple_of((place_ref[0] ^ i) * (CORES * rows), CORES * rows)
+            flip_ref[...] = jnp.transpose(d_up_ref[:, pl.ds(start, CORES * rows)])
+            for j in range(CORES):
+                start = pl.multiple_of((place_ref[1] ^ j) * rows, rows)
+                parts[CORES * i + j][...] = flip_ref[pl.ds(start, rows), :]
+
+
+def mlp_weight_grads(place, layer, pairs, earlier, up_flip, down_block, norms, grads):
+    block, width = down_block.shape
+    half = norms[0].shape[0] // TOKEN_TILE
+    rows = width // (CHIPS * CORES)
+    once = pl.Buffered(1)
+    whole = pl.BlockSpec((block, width), lambda i, p: (0, 0), pipeline_mode=once)
+    mine = pl.BlockSpec((TOKEN_TILE, width), lambda i, p: (jnp.minimum(i, half - 1), 0))
+    others = pl.BlockSpec((TOKEN_TILE, width), lambda i, p: (jnp.maximum(i - half, 0), 0))
+    part = pl.BlockSpec((rows, block), lambda i, p: (0, 0), pipeline_mode=once)
+    args = [place, up_flip, down_block, norms[0], norms[1], grads[0], grads[1]] + earlier
+    outs = pl.pallas_call(
+        functools.partial(mlp_grads_kernel, half),
+        grid_spec=pltpu.PrefetchScalarGridSpec(
+            num_scalar_prefetch=1,
+            grid=(2 * half,),
+            in_specs=[whole, whole, mine, others, mine, others] + [pl.BlockSpec(memory_space=pl.ANY)] * len(earlier),
+            out_specs=[pl.BlockSpec((1, block, width), lambda i, p: (layer, 0, 0), pipeline_mode=once)]
+            + [part] * (CHIPS * CORES),
+            scratch_shapes=[pltpu.VMEM((block, width), jnp.float32), pltpu.VMEM((CORES * rows, block), jnp.float32)],
+        ),
+        out_shape=[jax.ShapeDtypeStruct((pairs, block, width), jnp.float32)]
+        + [jax.ShapeDtypeStruct((rows, block), jnp.float32)] * (CHIPS * CORES),
+        input_output_aliases={7: 0} if earlier else {},
+        compiler_params=pltpu.CompilerParams(vmem_limit_bytes=60 * 1024 * 1024),
+        cost_estimate=pl.CostEstimate(flops=8 * 2 * norms[0].shape[0] * block * width, bytes_accessed=0,
+                                      transcendentals=0),
+        name="mlp_grads",
+    )(*args)
+    return outs[0], outs[1:]
+
+
+def exchange(parts):
+    devices = range(CHIPS * CORES)
+    return [lax.ppermute(part, AXES, [(d, d ^ i) for d in devices]) if i else part for i, part in enumerate(parts)]
+
+
+def assemble_kernel(place_ref, *refs):
+    parts, out_ref = [ref[...] for ref in refs[:CHIPS * CORES]], refs[-1]
+    for bit in range(3):
+        swapped = ((place_ref[0] * CORES + place_ref[1]) >> bit) % 2 == 1
+        parts = [jnp.where(swapped, parts[i ^ (1 << bit)], part) for i, part in enumerate(parts)]
+    for i, part in enumerate(parts):
+        out_ref[0, :, i * part.shape[1]:(i + 1) * part.shape[1]] = part
+
+
+def assemble(place, layer, pairs, earlier, parts):
+    rows, block = parts[0].shape
+    out_width = block * len(parts)
+    return pl.pallas_call(
+        assemble_kernel,
+        grid_spec=pltpu.PrefetchScalarGridSpec(
+            num_scalar_prefetch=1,
+            grid=(rows // ROW_TILE,),
+            in_specs=[pl.BlockSpec((ROW_TILE, block), lambda i, p: (i, 0))] * len(parts)
+            + [pl.BlockSpec(memory_space=pl.ANY)] * len(earlier),
+            out_specs=pl.BlockSpec((1, ROW_TILE, out_width), lambda i, p: (layer, i, 0)),
+        ),
+        out_shape=jax.ShapeDtypeStruct((pairs, rows, out_width), jnp.float32),
+        input_output_aliases={1 + len(parts): 0} if earlier else {},
+        cost_estimate=pl.CostEstimate(flops=5_000_000_000, bytes_accessed=0, transcendentals=0),
+        name="assemble",
+    )(place, *parts, *earlier)
 
 
 def solution(mesh):
@@ -247,15 +313,21 @@
             grid = w_up[layer].reshape(shard, chips, CORES, block)
             return to_columns(core, [grid[:, :, part].reshape(shard, chips * block) for part in range(CORES)])
 
-        attn_full, up_full, down_full, up_block = [], [], [], []
+        attn_full, up_full, down_full, up_flip = [], [], [], []
         for layer in range(pairs):
             attn_full.append(gather(attn_piece(layer)))
             up_full.append(gather(up_piece(layer)))
             down_full.append(gather(w_down[layer]))
-            up_block.append(lax.select_n(chip, *[up_full[layer][:, i * block:(i + 1) * block] for i in range(chips)]))
+            up_flip.append(lax.select_n(chip, *[up_full[layer][:, i * block:(i + 1) * block] for i in range(chips)]).T)
+        place = jnp.stack([chip, core]).astype(jnp.int32)
         carry_x = x_loc.reshape(seqs * seq, width)
         grad_x = grad_out.reshape(seqs * seq, width)
-        attn_saved, mlp_saved = [], []
+        attn_saved, mlp_saved, d_up, d_down = [], [], [], []
+
+        def weight_grads(layer, norms, grads, d_down):
+            down, parts = mlp_weight_grads(place, layer, pairs, d_down, up_flip[layer], w_down[layer], norms, grads)
+            return exchange(parts), [down]
+
         for layer in range(pairs):
             x_own, saved = attn_forward(carry_x, attn_full[layer], q_width, head, seq)
             attn_saved.append(saved)
@@ -263,21 +335,18 @@
             gelu_act, slope = mlp_hidden(pair_rows(n_own), up_full[layer])
             norms = all_rows(n_own)
             if layer == pairs - 1:
-                mlp_grads = mlp_weight_grads(norms, all_rows(grad_x), up_block[layer], w_down[layer])
-                down_full[layer], mlp_grads = lax.optimization_barrier((down_full[layer], mlp_grads))
+                parts, d_down = weight_grads(layer, norms, all_rows(grad_x), d_down)
             carry_x = mlp_output(x_own, gelu_act, down_full[layer])
             mlp_saved.append((x_own, norms, slope))
         y_loc = carry_x.reshape(x_loc.shape)
-        grad_lists = ([], [], [], [], [], [])
+        grad_lists = ([], [], [], [])
         for layer in reversed(range(pairs)):
             x_own, norms, slope = mlp_saved[layer]
             if layer < pairs - 1:
-                mlp_grads = mlp_weight_grads(norms, all_rows(grad_x), up_block[layer], w_down[layer])
-            grad_lists[5].append(mlp_grads[1])
-            grad_lists[4].append(up_rows(core, chip, chips, mlp_grads[0]))
+                parts, d_down = weight_grads(layer, norms, all_rows(grad_x), d_down)
+            d_up = [assemble(place, layer, pairs, d_up, parts)]
             grad_x = mlp_backward(x_own, slope, up_full[layer], down_full[layer], grad_x)
             grad_x, d_qkv, d_o = attn_backward(attn_saved[layer], attn_full[layer], q_width, head, seq, grad_x)
-            grad_x, d_qkv, d_o = lax.optimization_barrier((grad_x, d_qkv, d_o))
             parts = to_rows(core, scatter_sum(d_o))
             grad_lists[3].append(jnp.concatenate(parts, axis=1).reshape(shard, heads, head))
             parts = to_rows(core, scatter_sum(d_qkv))
@@ -285,7 +354,8 @@
                                  .reshape(shard, heads, head))
             grad_lists[1].append(jnp.stack([part[:, q_width:q_width + head] for part in parts], axis=1))
             grad_lists[2].append(jnp.stack([part[:, q_width + head:] for part in parts], axis=1))
-        return (y_loc, grad_x.reshape(x_loc.shape)) + tuple(jnp.stack(grad_list[::-1]) for grad_list in grad_lists)
+        stacked = tuple(jnp.stack(grad_list[::-1]) for grad_list in grad_lists)
+        return (y_loc, grad_x.reshape(x_loc.shape)) + stacked + (d_up[0], d_down[0])
 
     return jax.shard_map(body, mesh=mesh, in_specs=(row_spec,) + (weight_spec,) * 6 + (row_spec,),
                          out_specs=(row_spec, row_spec) + (weight_spec,) * 6, check_vma=False)

time: 1850 us -> 1790 us (0.968)
  matrix products: 903 us -> 488 us
  Pallas kernels: 90.1 us -> 389 us
  waiting for transfers between devices: 542 us -> 672 us
  local copies, waits for them, and re-layouts: 177 us -> 131 us
  other arithmetic: 95.6 us -> 71.5 us
    dot_general x44 -> x28, matrix products: 903 us -> 488 us  [mixed(): return jnp.einsum(form, left, right, preferred_element_type=jnp.float32)]
    pallas_call x0 -> x4, Pallas kernels: none -> 298 us  [the longest x2 282 us: mlp_weight_grads(): pl.pallas_call(functools.partial(mlp_grads_kernel, half), grid_spec=pltpu...]
    ppermute x6 -> x14, waiting for transfers between devices: 87.2 us -> 151 us  [exchange(): lax.ppermute(part, AXES, [(d, d ^ i) for d in devices])]
    reduce_scatter x4, waiting for transfers between devices: 0.03 us -> 36.1 us  [scatter_sum(): return lax.psum_scatter(grad_full, 'sub', scatter_dimension=0, tiled=True)]
    unnamed x151 -> x175, local copies, waits for them, and re-layouts: 22.4 us -> 49.5 us
    another operation x12 -> x9, other arithmetic: 30 us -> 3.6 us  [the longest x8 2.96 us: body(): stacked = tuple((jnp.stack(grad_list[::-1]) for grad_list in grad_lists))]
    dynamic_slice x8 -> x0, local copies, waits for them, and re-layouts: 20.2 us -> none  [up_rows(): part = lax.dynamic_index_in_dim(grid, chip ^ step, 0, keepdims=False)]
    select_n x4 -> x0, other arithmetic: 18.9 us -> none  [the longest x2 15.7 us: body(): lax.select_n(chip, *[up_full[layer][:, i * block:(i + 1) * block] for i i...]
  transfers between devices with their start and end apart: 50 -> 56, of which waited for: 19 -> 26; matrix products, arithmetic and copies ran while one was open for 57% -> 37% of each run, Pallas kernels for 5% -> 21%
where the time goes in v1:
time: 1790 us
  waiting for transfers between devices  672 us (38%)
  matrix products  488 us (27%)
  Pallas kernels  389 us (22%)
  local copies, waits for them, and re-layouts  131 us (7%)
  other arithmetic  71.5 us (4%)
  starting transfers between devices  21.9 us (1%)
    dot_general x28, matrix products, mixed(): return jnp.einsum(form, left, right, preferred_element_type=jnp.float32)  488 us
    all_gather x10, waiting for transfers between devices, gather(): return lax.all_gather(piece, 'sub', axis=0, tiled=True)  408 us
    pallas_call x2, Pallas kernels, mlp_weight_grads(): pl.pallas_call(functools.partial(mlp_grads_kernel, half), grid_spec=pltpu...  282 us
    ppermute x14, waiting for transfers between devices, exchange(): lax.ppermute(part, AXES, [(d, d ^ i) for d in devices])  151 us
    pallas_call x4, Pallas kernels, by_sequence(): pl.pallas_call(functools.partial(kernel, q_width, head), grid=(rows // se...  90.2 us
    ppermute x28, waiting for transfers between devices, swap(): return lax.ppermute(value, 'fsdp', [(0, 1), (1, 0)])  76.8 us
    unnamed x175, local copies, waits for them, and re-layouts  49.5 us
    reduce_scatter x4, waiting for transfers between devices, scatter_sum(): return lax.psum_scatter(grad_full, 'sub', scatter_dimension=0, tiled=True)  36.1 us
  transfers between devices with their start and end apart: 56, of which 26 were waited for; matrix products, arithmetic and copies ran while one was open for 37% of the time, Pallas kernels for 21%

profile of v1, /device:TPU:0, one launch (start us, length us, event | category | flops | bytes accessed | tf_op | source)
XLA Modules:
  0.0 1788.1 jit_solution(16908566905089410016)
XLA Ops:
  20.9 6.4 fusion.133
  27.3 7.1 reshape_squeeze.31
  37.8 6.0 fusion.134
  43.8 9.2 copy.142
  53.1 5.7 copy.143
  65.3 7.2 reshape_squeeze.28
  72.5 6.0 fusion.135
  78.6 8.7 copy.134
  115.5 8.0 slice_bitcast_fusion.14
  146.9 11.6 fusion.86.qkv_ref
  158.5 17.1 shard_map.143
  180.9 10.0 collective-permute-done.2
  203.9 40.3 %all-gather.15.cloned.1.call-done = bf16[1536,4480]{0,1:T(8,128)(2,1)} async-done(((bf16[384,4480]{0,1:T(8,128)(2,1)}), bf16[1536,4480]{0,1:T(8,128)(2,1)}) %all-gather.15.cloned.1.call-update) | async-done | bytes 13762576 | tf_op jit(solution)/shard_map/all_gather | solution.py:64
  244.3 51.1 %multiply_add_fusion.2 = (f32[2048,4480]{1,0:T(8,128)}, bf16[2048,4480]{1,0:T(8,128)(2,1)}) fusion(bf16[1536,4480]{0,1:T(8,128)(2,1)} %all-gather.15.cloned.1.call-done, bf16[1024,1536]{1,0:T(8,128)(2,1)} %collective-permute-done.3, bf16[1024,1536]{1,0:T(8,128)(2,1)S(1)} %fusion.35), kind=kOutput, calls=%fused_computation.6 | convolution fusion | flops 28326756352 | bytes 75104256 | tf_op jit(solution)/shard_map/td,df->tf/dot_general | solution.py:37
  295.4 77.9 %all-gather.29.cloned.1.call-done = bf16[1,4480,1536]{2,1,0:T(8,128)(2,1)} async-done(((bf16[1,1120,1536]{2,1,0:T(8,128)(2,1)}), bf16[1,4480,1536]{2,1,0:T(8,128)(2,1)}) %all-gather.29.cloned.1.call-update) | async-done | bytes 13762576 | tf_op jit(solution)/shard_map/all_gather | solution.py:64
  373.3 18.8 %fusion.10 = f32[1024,1536]{1,0:T(8,128)S(1)} fusion(bf16[1,4480,1536]{2,1,0:T(8,128)(2,1)} %all-gather.29.cloned.1.call-done, bf16[2048,4480]{1,0:T(8,128)(2,1)} %get-tuple-element.30), kind=kOutput, calls=%fused_computation.16 | convolution fusion | flops 14092861440 | bytes 29229056 | tf_op jit(solution)/shard_map/tf,fd->td/dot_general | solution.py:37
  392.1 10.1 collective-permute-done.5
  402.2 20.8 %fusion.38 = (f32[1024]{0:T(1024)S(1)}, bf16[1024,1536]{1,0:T(8,128)(2,1)S(1)}) fusion(f32[1024,1536]{1,0:T(8,128)S(1)} %collective-permute-done.5, bf16[1,4480,1536]{2,1,0:T(8,128)(2,1)} %all-gather.29.cloned.1.call-done, bf16[2048,4480]{1,0:T(8,128)(2,1)} %get-tuple-element.30, bf16[1024,1536]{1,0:T(8,128)(2,1)S(1)} %copy-done.14), kind=kOutput, calls=%fused_computation.63 | convolution fusion | flops 14103870464 | bytes 35524608 | tf_op jit(solution)/shard_map/tf,fd->td/dot_general | solution.py:37
  425.8 7.1 all-gather.17.cloned.1.call-done
  432.9 10.6 fusion.87.qkv_ref
  443.5 17.1 shard_map.144
  465.6 10.1 collective-permute-done.8
  485.7 75.3 %all-gather.19.cloned.1.call-done = bf16[1536,4480]{0,1:T(8,128)(2,1)} async-done(((bf16[384,4480]{0,1:T(8,128)(2,1)}), bf16[1536,4480]{0,1:T(8,128)(2,1)}) %all-gather.19.cloned.1.call-update) | async-done | bytes 13762576 | tf_op jit(solution)/shard_map/all_gather | solution.py:64
  561.0 51.1 %multiply_add_fusion = (f32[2048,4480]{1,0:T(8,128)}, bf16[2048,4480]{1,0:T(8,128)(2,1)}) fusion(bf16[1536,4480]{0,1:T(8,128)(2,1)} %all-gather.19.cloned.1.call-done, bf16[1024,1536]{1,0:T(8,128)(2,1)} %collective-permute-done.9, bf16[1024,1536]{1,0:T(8,128)(2,1)} %fusion.43), kind=kOutput, calls=%fused_computation.2 | convolution fusion | flops 28326756352 | bytes 75104256 | tf_op jit(solution)/shard_map/td,df->tf/dot_general | solution.py:37
  612.2 77.7 %all-gather.31.cloned.1.call-done = bf16[1,4480,1536]{2,1,0:T(8,128)(2,1)} async-done(((bf16[1,1120,1536]{2,1,0:T(8,128)(2,1)}), bf16[1,4480,1536]{2,1,0:T(8,128)(2,1)}) %all-gather.31.cloned.1.call-update) | async-done | bytes 13762576 | tf_op jit(solution)/shard_map/all_gather | solution.py:64
  689.9 40.5 %multiply_convert_fusion.1 = bf16[2048,4480]{1,0:T(8,128)(2,1)} fusion(f32[2048,4480]{1,0:T(8,128)} %get-tuple-element.32, bf16[1,4480,1536]{2,1,0:T(8,128)(2,1)} %all-gather.31.cloned.1.call-done, bf16[1024,1536]{1,0:T(8,128)(2,1)} %collective-permute-done.12, bf16[1024,1536]{1,0:T(8,128)(2,1)S(1)} %bitcast.158), kind=kOutput, calls=%fused_computation.1 | convolution fusion | flops 28216655872 | bytes 75104256 | tf_op jit(solution)/shard_map/td,fd->tf/dot_general | solution.py:37
  730.4 21.4 %fusion.18 = f32[1024,1536]{1,0:T(8,128)} fusion(bf16[1536,4480]{0,1:T(8,128)(2,1)} %all-gather.19.cloned.1.call-done, bf16[2048,4480]{1,0:T(8,128)(2,1)} %multiply_convert_fusion.1), kind=kOutput, calls=%fused_computation.43 | convolution fusion | flops 14092861440 | bytes 29229056 | tf_op jit(solution)/shard_map/tf,df->td/dot_general | solution.py:37
  752.0 10.4 collective-permute-done.13
  762.3 21.8 %fusion.45 = (f32[1024]{0:T(1024)S(1)}, f32[1024,1536]{1,0:T(8,128)S(1)}) fusion(bf16[1024,1536]{1,0:T(8,128)(2,1)} %copy-done.10, f32[1024,1536]{1,0:T(8,128)} %collective-permute-done.13, bf16[1536,4480]{0,1:T(8,128)(2,1)} %all-gather.19.cloned.1.call-done, bf16[2048,4480]{1,0:T(8,128)(2,1)} %multiply_convert_fusion.1), kind=kOutput, calls=%fused_computation.70 | convolution fusion | flops 14099151872 | bytes 38670336 | tf_op jit(solution)/shard_map/tf,df->td/dot_general | solution.py:37
  793.8 10.0 fusion.92.d_o_ref
  803.9 27.8 %shard_map.145 = bf16[2048,1024]{1,0:T(8,128)(2,1)} custom-call(bf16[2048,1024]{1,0:T(8,128)(2,1)} %fusion.87.qkv_ref, bf16[2048,768]{1,0:T(8,128)(2,1)} %fusion.92.d_o_ref), custom_call_target="tpu_custom_call" | custom-call | flops 40000000000 | tf_op jit(solution)/shard_map/pallas_call | solution.py:131
  831.7 11.7 fusion.82
  843.5 6.1 fusion.94
  849.9 10.0 collective-permute-done.15
  859.9 6.2 fusion.41
  873.8 42.0 %multiply_convert_fusion = bf16[2048,4480]{1,0:T(8,128)(2,1)} fusion(f32[2048,4480]{1,0:T(8,128)} %get-tuple-element.33, bf16[1,4480,1536]{2,1,0:T(8,128)(2,1)} %all-gather.29.cloned.1.call-done, bf16[1024,1536]{1,0:T(8,128)(2,1)} %collective-permute-done.16, bf16[1024,1536]{1,0:T(8,128)(2,1)} %copy-done), kind=kOutput, calls=%fused_computation | convolution fusion | flops 28216655872 | bytes 75104256 | tf_op jit(solution)/shard_map/td,fd->tf/dot_general | solution.py:37
  915.8 21.6 %fusion.14 = f32[1024,1536]{1,0:T(8,128)} fusion(bf16[1536,4480]{0,1:T(8,128)(2,1)} %all-gather.15.cloned.1.call-done, bf16[2048,4480]{1,0:T(8,128)(2,1)} %multiply_convert_fusion), kind=kOutput, calls=%fused_computation.39 | convolution fusion | flops 14092861440 | bytes 29229056 | tf_op jit(solution)/shard_map/tf,df->td/dot_general | solution.py:37
  937.7 6.9 fusion.80
  947.9 21.6 %fusion.37 = (f32[1024]{0:T(1024)S(1)}, f32[1024,1536]{1,0:T(8,128)S(1)}) fusion(bf16[1024,1536]{1,0:T(8,128)(2,1)} %copy-done.13, f32[1024,1536]{1,0:T(8,128)} %collective-permute-done.17, bf16[1536,4480]{0,1:T(8,128)(2,1)} %all-gather.15.cloned.1.call-done, bf16[2048,4480]{1,0:T(8,128)(2,1)} %multiply_convert_fusion), kind=kOutput, calls=%fused_computation.62 | convolution fusion | flops 14099151872 | bytes 38670336 | tf_op jit(solution)/shard_map/tf,df->td/dot_general | solution.py:37
  973.8 8.8 fusion.89.up_ref
  982.8 62.9 %all-gather.25.cloned.1.call-done.n0_ref = bf16[4096,1536]{1,0:T(8,128)(2,1)} async-done(((bf16[1024,1536]{1,0:T(8,128)(2,1)}), bf16[4096,1536]{1,0:T(8,128)(2,1)}) %all-gather.25.cloned.1.call-update) | async-done | bytes 12582928 | tf_op jit(solution)/shard_map/all_gather | solution.py:64
  1045.8 9.2 fusion.78
  1055.0 21.8 %fusion.5 = f32[1024,1536]{1,0:T(8,128)} fusion(bf16[1,4480,1536]{2,1,0:T(8,128)(2,1)} %all-gather.31.cloned.1.call-done, bf16[2048,4480]{1,0:T(8,128)(2,1)} %get-tuple-element.31), kind=kOutput, calls=%fused_computation.11 | convolution fusion | flops 14092861440 | bytes 29229056 | tf_op jit(solution)/shard_map/tf,fd->td/dot_general | solution.py:37
  1077.6 36.0 %reduce-scatter.7.cloned.1.call-done = f32[384,1024]{1,0:T(8,128)} async-done(((f32[1536,1024]{1,0:T(8,128)}), f32[384,1024]{1,0:T(8,128)}) %reduce-scatter.7.cloned.1.call-update) | async-done | bytes 1572880 | tf_op jit(solution)/shard_map/reduce_scatter | solution.py:68
  1115.7 9.3 fusion.93.d_o_ref
  1125.1 28.2 %shard_map.146 = bf16[2048,1024]{1,0:T(8,128)(2,1)} custom-call(bf16[2048,1024]{1,0:T(8,128)(2,1)} %fusion.86.qkv_ref, bf16[2048,768]{1,0:T(8,128)(2,1)} %fusion.93.d_o_ref), custom_call_target="tpu_custom_call" | custom-call | flops 40000000000 | tf_op jit(solution)/shard_map/pallas_call | solution.py:131
  1153.3 12.1 fusion.84
  1165.5 66.8 %all-gather.23.cloned.1.call-done.g0_ref = bf16[4096,1536]{1,0:T(8,128)(2,1)} async-done(((bf16[1024,1536]{1,0:T(8,128)(2,1)}), bf16[4096,1536]{1,0:T(8,128)(2,1)}) %all-gather.23.cloned.1.call-update) | async-done | bytes 12582928 | tf_op jit(solution)/shard_map/all_gather | solution.py:64
  1232.3 141.0 %mlp_grads.2 = (f32[2,1120,1536]{2,1,0:T(8,128)}, f32[192,1120]{1,0:T(8,128)}, f32[192,1120]{1,0:T(8,128)}, f32[192,1120]{1,0:T(8,128)}, f32[192,1120]{1,0:T(8,1...) custom-call(s32[2]{0:T(128)} %pad_add_fusion.place_ref, ...), custom_call_target="tpu_custom_call" | custom-call | flops 112742891520 | tf_op jit(solution)/shard_map/mlp_grads/pallas_call | solution.py:238
  1375.0 8.9 fusion.98
  1386.1 8.7 fusion.91.up_ref
  1394.8 28.5 %collective-permute-done.36.refs_2_ = f32[192,1120]{1,0:T(8,128)S(1)} collective-permute-done((f32[192,1120]{1,0:T(8,128)S(1)}, f32[192,1120]{1,0:T(8,128)S(1)}, u32[]{:S(2)}, u32[]{:S(2)}) %collective-permute-start.36) | collective-permute-done | bytes 860192 | tf_op jit(solution)/shard_map/ppermute | solution.py:261
  1424.8 16.3 collective-permute-done.37.refs_3_
  1443.9 21.8 %fusion.44 = bf16[1024,1536]{1,0:T(8,128)(2,1)} fusion(bf16[1024,1536]{1,0:T(8,128)(2,1)S(1)} %copy-done.12, f32[1024,1536]{1,0:T(8,128)} %collective-permute-done.11, bf16[1,4480,1536]{2,1,0:T(8,128)(2,1)} %all-gather.31.cloned.1.call-done, bf16[2048,4480]{1,0:T(8,128)(2,1)} %get-tuple-element.31), kind=kOutput, calls=%fused_computation.69 | convolution fusion | flops 14099152896 | bytes 35520512 | tf_op jit(solution)/shard_map/tf,fd->td/dot_general | solution.py:37
  1473.9 18.7 %collective-permute-done.40.refs_6_ = f32[192,1120]{1,0:T(8,128)} collective-permute-done((f32[192,1120]{1,0:T(8,128)}, f32[192,1120]{1,0:T(8,128)}, u32[]{:S(2)}, u32[]{:S(2)}) %collective-permute-start.40) | collective-permute-done | bytes 860192 | tf_op jit(solution)/shard_map/ppermute | solution.py:261
  1492.6 16.4 collective-permute-done.41.refs_7_
  1509.0 8.1 assemble.2.refs_8_
  1517.2 10.6 fusion.63
  1530.1 5.8 fusion.33
  1540.0 141.4 %mlp_grads.3 = (f32[2,1120,1536]{2,1,0:T(8,128)}, f32[192,1120]{1,0:T(8,128)}, f32[192,1120]{1,0:T(8,128)}, f32[192,1120]{1,0:T(8,128)}, f32[192,1120]{1,0:T(8,1...) custom-call(s32[2]{0:T(128)} %pad_add_fusion.place_ref, ...), custom_call_target="tpu_custom_call", output_to_operand_aliasing={{0}: (7, {})} | custom-call | flops 112742891520 | tf_op jit(solution)/shard_map/mlp_grads/pallas_call | solution.py:238
  1696.9 7.8 collective-permute-done.29.refs_2_
  1708.8 13.0 collective-permute-done.30.refs_3_
  1721.9 50.4 %collective-permute-done.32.refs_5_ = f32[192,1120]{1,0:T(8,128)S(1)} collective-permute-done((f32[192,1120]{1,0:T(8,128)S(1)}, f32[192,1120]{1,0:T(8,128)S(1)}, u32[]{:S(2)}, u32[]{:S(2)}) %collective-permute-start.32) | collective-permute-done | bytes 860192 | tf_op jit(solution)/shard_map/ppermute | solution.py:261
  1773.5 7.9 assemble.3
  (373 shorter events, 182.6 us)
Async XLA Ops:
  7.2 139.7 %all-gather.13.cloned.1.call-start = ((), (), s32[]{:S(2)}) async-start(), calls=%async_computation.4 | async-start | bytes 6881280 | tf_op jit(solution)/shard_map/all_gather | solution.py:64
  20.1 14.3 collective-permute-start.1
  37.5 206.8 %all-gather.15.cloned.1.call-start = ((), (), s32[]{:S(2)}) async-start(), calls=%async_computation.5 | async-start | bytes 17203200 | tf_op jit(solution)/shard_map/all_gather | solution.py:64
  65.1 34.6 %collective-permute-start.10 = (bf16[192,4480]{1,0:T(8,128)(2,1)}, bf16[192,4480]{1,0:T(8,128)(2,1)}, u32[]{:S(2)}, u32[]{:S(2)}) collective-permute-start(bf16[192,4480]{1,0:T(8,128)(2,1)} %copy.127), channel_id=1, source_target_pairs={{0,1},{1,0},{2,3},{3,2},{4,5},{5,4},{6,7},{7,6}} | collective-permute-start | bytes 5160968 | tf_op jit(solution)/shard_map/ppermute | solution.py:41
  99.3 4.5 collective-permute-start.4
  115.4 257.9 %all-gather.29.cloned.1.call-start = ((), (), s32[]{:S(2)}) async-start(), calls=%async_computation.16 | async-start | bytes 17203200 | tf_op jit(solution)/shard_map/all_gather | solution.py:64
  123.6 309.3 %all-gather.17.cloned.1.call-start = ((), (), s32[]{:S(2)}) async-start(), calls=%async_computation.6 | async-start | bytes 6881280 | tf_op jit(solution)/shard_map/all_gather | solution.py:64
  127.5 2.2 collective-permute-start.7
  131.2 429.9 %all-gather.19.cloned.1.call-start = ((), (), s32[]{:S(2)}) async-start(), calls=%async_computation.7 | async-start | bytes 17203200 | tf_op jit(solution)/shard_map/all_gather | solution.py:64
  137.5 552.4 %all-gather.31.cloned.1.call-start = ((), (), s32[]{:S(2)}) async-start(), calls=%async_computation.17 | async-start | bytes 17203200 | tf_op jit(solution)/shard_map/all_gather | solution.py:64
  141.1 5.8 collective-permute-start
  180.7 10.2 collective-permute-start.2
  198.1 97.2 %copy-start.20 = (bf16[1024,1536]{1,0:T(8,128)(2,1)}, bf16[1024,1536]{1,0:T(8,128)(2,1)S(1)}, u32[]{:S(2)}) copy-start(bf16[1024,1536]{1,0:T(8,128)(2,1)S(1)} %fusion.35) | copy-start | bytes 9437188
  198.1 5.8 collective-permute-start.3
  198.3 775.2 %all-gather.27.cloned.1.call-start = ((), (), s32[]{:S(2)}) async-start(), calls=%async_computation.15 | async-start | bytes 15728640 | tf_op jit(solution)/shard_map/all_gather | solution.py:64
  295.4 106.9 %copy-start.14 = (bf16[1024,1536]{1,0:T(8,128)(2,1)S(1)}, bf16[1024,1536]{1,0:T(8,128)(2,1)}, u32[]{:S(2)}) copy-start(bf16[1024,1536]{1,0:T(8,128)(2,1)} %copy-done.13) | copy-start | bytes 9437188
  392.1 10.2 collective-permute-start.5
  425.3 7.6 collective-permute-start.6
  425.5 557.1 %all-gather.21.cloned.1.call-start = ((), (), s32[]{:S(2)}) async-start(), calls=%async_computation.12 | async-start | bytes 15728640 | tf_op jit(solution)/shard_map/all_gather | solution.py:64
  465.5 10.2 collective-permute-start.8
  484.7 76.3 %collective-permute-start.9 = (bf16[1024,1536]{1,0:T(8,128)(2,1)}, bf16[1024,1536]{1,0:T(8,128)(2,1)}, u32[]{:S(2)}, u32[]{:S(2)}) collective-permute-start(bf16[1024,1536]{1,0:T(8,128)(2,1)} %fusion.43), channel_id=1, source_target_pairs={{0,1},{1,0},{2,3},{3,2},{4,5},{5,4},{6,7},{7,6}} | collective-permute-start | bytes 9437192 | tf_op jit(solution)/shard_map/ppermute | solution.py:41
  484.9 127.3 %collective-permute-start.12 = (bf16[1024,1536]{1,0:T(8,128)(2,1)S(1)}, bf16[1024,1536]{1,0:T(8,128)(2,1)}, u32[]{:S(2)}, u32[]{:S(2)}) collective-permute-start(bf16[1024,1536]{1,0:T(8,128)(2,1)S(1)} %bitcast.157), channel_id=1, source_target_pairs={{0,1},{1,0},{2,3},{3,2},{4,5},{5,4},{6,7},{7,6}} | collective-permute-start | bytes 9437192 | tf_op jit(solution)/shard_map/ppermute | solution.py:41
  485.3 560.5 %all-gather.25.cloned.1.call-start = ((), (), s32[]{:S(2)}) async-start(), calls=%async_computation.14 | async-start | bytes 15728640 | tf_op jit(solution)/shard_map/all_gather | solution.py:64
  751.8 10.5 collective-permute-start.13
  751.9 32.3 %copy-start.69 = (f32[1024]{0:T(1024)S(1)}, f32[1024]{0:T(1024)}, u32[]{:S(2)}) copy-start(f32[1024]{0:T(1024)} %copy-done.68) | copy-start | bytes 12292
  751.9 32.3 %copy-start.63 = (f32[1024]{0:T(1024)S(1)}, f32[1024]{0:T(1024)}, u32[]{:S(2)}) copy-start(f32[1024]{0:T(1024)} %copy-done.62) | copy-start | bytes 12292
  751.9 361.7 %reduce-scatter.7.cloned.1.call-start = ((), (), s32[]{:S(2)}) async-start(), calls=%async_computation.9 | async-start | bytes 7864320 | tf_op jit(solution)/shard_map/reduce_scatter | solution.py:68
  786.3 5.7 collective-permute-start.14
  843.4 388.8 %all-gather.23.cloned.1.call-start = ((), (), s32[]{:S(2)}) async-start(), calls=%async_computation.13 | async-start | bytes 15728640 | tf_op jit(solution)/shard_map/all_gather | solution.py:64
  849.7 10.2 collective-permute-start.15
  868.0 5.8 collective-permute-start.16
  869.6 504.1 %reduce-scatter.11.cloned.1.call-start = ((), (), s32[]{:S(2)}) async-start(), calls=%async_computation.11 | async-start | bytes 5898240 | tf_op jit(solution)/shard_map/reduce_scatter | solution.py:68
  937.4 10.5 collective-permute-start.17
  944.6 583.2 %reduce-scatter.9.cloned.1.call-start = ((), (), s32[]{:S(2)}) async-start(), calls=%async_computation.10 | async-start | bytes 5898240 | tf_op jit(solution)/shard_map/reduce_scatter | solution.py:68
  972.6 73.2 %collective-permute-start.18 = (bf16[1024,1536]{1,0:T(8,128)(2,1)}, bf16[1024,1536]{1,0:T(8,128)(2,1)S(1)}, u32[]{:S(2)}, u32[]{:S(2)}) collective-permute-start(bf16[1024,1536]{1,0:T(8,128)(2,1)} %fusion.31), channel_id=1, source_target_pairs={{0,1},{1,0},{2,3},{3,2},{4,5},{5,4},{6,7},{7,6}} | collective-permute-start | bytes 9437192 | tf_op jit(solution)/shard_map/ppermute | solution.py:41
  973.5 191.9 %collective-permute-start.27 = (bf16[4096,1536]{1,0:T(8,128)(2,1)}, bf16[4096,1536]{1,0:T(8,128)(2,1)}, u32[]{:S(2)}, u32[]{:S(2)}) collective-permute-start(bf16[4096,1536]{1,0:T(8,128)(2,1)} %all-gather.27.cloned.1.call-done.g0_ref), channel_id=1, source_target_pairs={{0,1},{1,0},{2,3},{3,2},{4,5},{5,4},{6,7},{7,6}} | collective-permute-start | bytes 37748744 | tf_op jit(solution)/shard_map/ppermute | solution.py:41
  982.6 557.4 %collective-permute-start.24 = (bf16[4096,1536]{1,0:T(8,128)(2,1)}, bf16[4096,1536]{1,0:T(8,128)(2,1)}, u32[]{:S(2)}, u32[]{:S(2)}) collective-permute-start(bf16[4096,1536]{1,0:T(8,128)(2,1)} %all-gather.21.cloned.1.call-done.n0_ref), channel_id=1, source_target_pairs={{0,1},{1,0},{2,3},{3,2},{4,5},{5,4},{6,7},{7,6}} | collective-permute-start | bytes 37748744 | tf_op jit(solution)/shard_map/ppermute | solution.py:41
  1045.8 186.5 %collective-permute-start.26 = (bf16[4096,1536]{1,0:T(8,128)(2,1)}, bf16[4096,1536]{1,0:T(8,128)(2,1)}, u32[]{:S(2)}, u32[]{:S(2)}) collective-permute-start(bf16[4096,1536]{1,0:T(8,128)(2,1)} %all-gather.25.cloned.1.call-done.n0_ref), channel_id=1, source_target_pairs={{0,1},{1,0},{2,3},{3,2},{4,5},{5,4},{6,7},{7,6}} | collective-permute-start | bytes 37748744 | tf_op jit(solution)/shard_map/ppermute | solution.py:41
  1055.0 483.7 %reduce-scatter.5.cloned.1.call-start = ((), (), s32[]{:S(2)}) async-start(), calls=%async_computation.8 | async-start | bytes 7864320 | tf_op jit(solution)/shard_map/reduce_scatter | solution.py:68
  1076.8 298.1 %collective-permute-start.11 = (f32[1024,1536]{1,0:T(8,128)}, f32[1024,1536]{1,0:T(8,128)}, u32[]{:S(2)}, u32[]{:S(2)}) collective-permute-start(f32[1024,1536]{1,0:T(8,128)} %fusion.5), channel_id=1, source_target_pairs={{0,1},{1,0},{2,3},{3,2},{4,5},{5,4},{6,7},{7,6}} | collective-permute-start | bytes 18874376 | tf_op jit(solution)/shard_map/ppermute | solution.py:41
  1115.7 269.7 %collective-permute-start.21 = (f32[192,1024]{1,0:T(8,128)}, f32[192,1024]{1,0:T(8,128)}, u32[]{:S(2)}, u32[]{:S(2)}) collective-permute-start(f32[192,1024]{1,0:T(8,128)} %dynamic-slice_bitcast_fusion), channel_id=1, source_target_pairs={{0,1},{1,0},{2,3},{3,2},{4,5},{5,4},{6,7},{7,6}} | collective-permute-start | bytes 2359304 | tf_op jit(solution)/shard_map/ppermute | solution.py:41
  1232.3 307.7 %collective-permute-start.25 = (bf16[4096,1536]{1,0:T(8,128)(2,1)}, bf16[4096,1536]{1,0:T(8,128)(2,1)}, u32[]{:S(2)}, u32[]{:S(2)}) collective-permute-start(bf16[4096,1536]{1,0:T(8,128)(2,1)} %all-gather.23.cloned.1.call-done.g0_ref), channel_id=1, source_target_pairs={{0,1},{1,0},{2,3},{3,2},{4,5},{5,4},{6,7},{7,6}} | collective-permute-start | bytes 37748744 | tf_op jit(solution)/shard_map/ppermute | solution.py:41
  1373.3 12.4 collective-permute-start.35
  1374.9 9.0 collective-permute-start.23
  1383.9 39.4 %collective-permute-start.36 = (f32[192,1120]{1,0:T(8,128)S(1)}, f32[192,1120]{1,0:T(8,128)S(1)}, u32[]{:S(2)}, u32[]{:S(2)}) collective-permute-start(f32[192,1120]{1,0:T(8,128)S(1)} %copy-done.78), channel_id=1, source_target_pairs={{0,2},{1,3},{2,0},{3,1},{4,6},{5,7},{6,4},{7,5}} | collective-permute-start | bytes 2580488 | tf_op jit(solution)/shard_map/ppermute | solution.py:261
  1385.4 58.5 %copy-start.12 = (bf16[1024,1536]{1,0:T(8,128)(2,1)S(1)}, bf16[1024,1536]{1,0:T(8,128)(2,1)}, u32[]{:S(2)}) copy-start(bf16[1024,1536]{1,0:T(8,128)(2,1)} %copy-done.10) | copy-start | bytes 9437188
  1385.4 55.7 %collective-permute-start.37 = (f32[192,1120]{1,0:T(8,128)S(1)}, f32[192,1120]{1,0:T(8,128)S(1)}, u32[]{:S(2)}, u32[]{:S(2)}) collective-permute-start(f32[192,1120]{1,0:T(8,128)S(1)} %copy-done.77), channel_id=1, source_target_pairs={{0,3},{1,2},{2,1},{3,0},{4,7},{5,6},{6,5},{7,4}} | collective-permute-start | bytes 2580488 | tf_op jit(solution)/shard_map/ppermute | solution.py:261
  1385.7 131.5 %collective-permute-start.19 = (f32[1024,1536]{1,0:T(8,128)}, f32[1024,1536]{1,0:T(8,128)}, u32[]{:S(2)}, u32[]{:S(2)}) collective-permute-start(f32[1024,1536]{1,0:T(8,128)} %fusion.98), channel_id=1, source_target_pairs={{0,1},{1,0},{2,3},{3,2},{4,5},{5,4},{6,7},{7,6}} | collective-permute-start | bytes 18874376 | tf_op jit(solution)/shard_map/ppermute | solution.py:41
  1423.3 45.6 %collective-permute-start.38 = (f32[192,1120]{1,0:T(8,128)}, f32[192,1120]{1,0:T(8,128)}, u32[]{:S(2)}, u32[]{:S(2)}) collective-permute-start(f32[192,1120]{1,0:T(8,128)} %get-tuple-element.47), channel_id=1, source_target_pairs={{0,4},{1,5},{2,6},{3,7},{4,0},{5,1},{6,2},{7,3}} | collective-permute-start | bytes 2580488 | tf_op jit(solution)/shard_map/ppermute | solution.py:261
  1442.0 28.3 %collective-permute-start.39 = (f32[192,1120]{1,0:T(8,128)}, f32[192,1120]{1,0:T(8,128)}, u32[]{:S(2)}, u32[]{:S(2)}) collective-permute-start(f32[192,1120]{1,0:T(8,128)} %get-tuple-element.48), channel_id=1, source_target_pairs={{0,5},{1,4},{2,7},{3,6},{4,1},{5,0},{6,3},{7,2}} | collective-permute-start | bytes 2580488 | tf_op jit(solution)/shard_map/ppermute | solution.py:261
  1468.9 23.8 %collective-permute-start.40 = (f32[192,1120]{1,0:T(8,128)}, f32[192,1120]{1,0:T(8,128)}, u32[]{:S(2)}, u32[]{:S(2)}) collective-permute-start(f32[192,1120]{1,0:T(8,128)} %get-tuple-element.49), channel_id=1, source_target_pairs={{0,6},{1,7},{2,4},{3,5},{4,2},{5,3},{6,0},{7,1}} | collective-permute-start | bytes 2580488 | tf_op jit(solution)/shard_map/ppermute | solution.py:261
  1470.4 38.7 %collective-permute-start.41 = (f32[192,1120]{1,0:T(8,128)}, f32[192,1120]{1,0:T(8,128)}, u32[]{:S(2)}, u32[]{:S(2)}) collective-permute-start(f32[192,1120]{1,0:T(8,128)} %get-tuple-element.50), channel_id=1, source_target_pairs={{0,7},{1,6},{2,5},{3,4},{4,3},{5,2},{6,1},{7,0}} | collective-permute-start | bytes 2580488 | tf_op jit(solution)/shard_map/ppermute | solution.py:261
  1528.9 7.0 collective-permute-start.22
  1539.9 145.1 %collective-permute-start.20 = (f32[192,1024]{1,0:T(8,128)S(1)}, f32[192,1024]{1,0:T(8,128)}, u32[]{:S(2)}, u32[]{:S(2)}) collective-permute-start(f32[192,1024]{1,0:T(8,128)S(1)} %dynamic-slice_bitcast_fusion.1), channel_id=1, source_target_pairs={{0,1},{1,0},{2,3},{3,2},{4,5},{5,4},{6,7},{7,6}} | collective-permute-start | bytes 2359304 | tf_op jit(solution)/shard_map/ppermute | solution.py:41
  1540.0 142.7 %copy-start.22 = (f32[1,192,12,128]{3,2,1,0:T(8,128)S(1)}, f32[1,192,12,128]{3,2,1,0:T(8,128)}, u32[]{:S(2)}) copy-start(f32[1,192,12,128]{3,2,1,0:T(8,128)} %stack_reshape.15) | copy-start | bytes 3538948
  1681.4 14.1 collective-permute-start.28
  1681.8 22.8 %collective-permute-start.29 = (f32[192,1120]{1,0:T(8,128)}, f32[192,1120]{1,0:T(8,128)}, u32[]{:S(2)}, u32[]{:S(2)}) collective-permute-start(f32[192,1120]{1,0:T(8,128)} %get-tuple-element.37), channel_id=1, source_target_pairs={{0,2},{1,3},{2,0},{3,1},{4,6},{5,7},{6,4},{7,5}} | collective-permute-start | bytes 2580488 | tf_op jit(solution)/shard_map/ppermute | solution.py:261
  1692.7 29.1 %collective-permute-start.30 = (f32[192,1120]{1,0:T(8,128)S(1)}, f32[192,1120]{1,0:T(8,128)S(1)}, u32[]{:S(2)}, u32[]{:S(2)}) collective-permute-start(f32[192,1120]{1,0:T(8,128)S(1)} %copy-done.76), channel_id=1, source_target_pairs={{0,3},{1,2},{2,1},{3,0},{4,7},{5,6},{6,5},{7,4}} | collective-permute-start | bytes 2580488 | tf_op jit(solution)/shard_map/ppermute | solution.py:261
  1693.3 28.5 %collective-permute-start.31 = (f32[192,1120]{1,0:T(8,128)S(1)}, f32[192,1120]{1,0:T(8,128)S(1)}, u32[]{:S(2)}, u32[]{:S(2)}) collective-permute-start(f32[192,1120]{1,0:T(8,128)S(1)} %copy-done.75), channel_id=1, source_target_pairs={{0,4},{1,5},{2,6},{3,7},{4,0},{5,1},{6,2},{7,3}} | collective-permute-start | bytes 2580488 | tf_op jit(solution)/shard_map/ppermute | solution.py:261
  1694.1 78.1 %collective-permute-start.32 = (f32[192,1120]{1,0:T(8,128)S(1)}, f32[192,1120]{1,0:T(8,128)S(1)}, u32[]{:S(2)}, u32[]{:S(2)}) collective-permute-start(f32[192,1120]{1,0:T(8,128)S(1)} %copy-done.74), channel_id=1, source_target_pairs={{0,5},{1,4},{2,7},{3,6},{4,1},{5,0},{6,3},{7,2}} | collective-permute-start | bytes 2580488 | tf_op jit(solution)/shard_map/ppermute | solution.py:261
  1695.4 76.9 %collective-permute-start.33 = (f32[192,1120]{1,0:T(8,128)S(1)}, f32[192,1120]{1,0:T(8,128)S(1)}, u32[]{:S(2)}, u32[]{:S(2)}) collective-permute-start(f32[192,1120]{1,0:T(8,128)S(1)} %copy-done.73), channel_id=1, source_target_pairs={{0,6},{1,7},{2,4},{3,5},{4,2},{5,3},{6,0},{7,1}} | collective-permute-start | bytes 2580488 | tf_op jit(solution)/shard_map/ppermute | solution.py:261
  1704.7 67.6 %collective-permute-start.34 = (f32[192,1120]{1,0:T(8,128)S(1)}, f32[192,1120]{1,0:T(8,128)}, u32[]{:S(2)}, u32[]{:S(2)}) collective-permute-start(f32[192,1120]{1,0:T(8,128)S(1)} %copy-done.72), channel_id=1, source_target_pairs={{0,7},{1,6},{2,5},{3,4},{4,3},{5,2},{6,1},{7,0}} | collective-permute-start | bytes 2580488 | tf_op jit(solution)/shard_map/ppermute | solution.py:261
  1721.8 50.4 %copy-start.39 = (f32[192,1120]{1,0:T(8,128)}, f32[192,1120]{1,0:T(8,128)S(1)}, u32[]{:S(2)}) copy-start(f32[192,1120]{1,0:T(8,128)S(1)} %collective-permute-done.30.refs_3_) | copy-start | bytes 2580484
  1721.9 50.4 %copy-start.40 = (f32[192,1120]{1,0:T(8,128)}, f32[192,1120]{1,0:T(8,128)S(1)}, u32[]{:S(2)}) copy-start(f32[192,1120]{1,0:T(8,128)S(1)} %collective-permute-done.31.refs_4_) | copy-start | bytes 2580484
  (75 other events, 710.8 us)
Sparse Core Ops, SparseCore 0:
  37.6 60.0 all-gather.12
  115.5 128.6 all-gather.14
  246.6 126.6 all-gather.28
  374.9 57.9 all-gather.16
  434.5 126.5 all-gather.18
  563.2 126.6 all-gather.30
  691.7 116.8 all-gather.26
  810.3 116.8 all-gather.20
  928.9 116.8 all-gather.24
  1049.1 64.4 reduce-scatter.6
  1115.4 116.8 all-gather.22
  1235.0 51.3 reduce-scatter.10
  1289.4 51.4 reduce-scatter.8
  1343.6 81.4 reduce-scatter.4

commit v2 on v1

--- a/solution.py
+++ b/solution.py
@@ -66,6 +66,12 @@
 
 def scatter_sum(grad_full):
     return lax.psum_scatter(grad_full, "sub", scatter_dimension=0, tiled=True)
+
+
+def both_halves(left, right, rows, form):
+    other = swap(mixed(form, left[rows:], right))
+    own = lax.optimization_barrier(mixed(form, left[:rows], right))
+    return own + other
 
 
 def pair_rows(value):
@@ -145,8 +151,7 @@
     o_act = by_sequence(attn_fwd_kernel, seq, q_width, head, (qkv,), q_width, 0, 20_000_000_000)
     o_weight = weight[:, q_width + 2 * head:]
     rows = x_own.shape[0]
-    other = swap(mixed("te,de->td", o_act[rows:], o_weight))
-    proj = mixed("te,de->td", o_act[:rows], o_weight) + other
+    proj = both_halves(o_act, o_weight, rows, "te,de->td")
     y_own = (x_own.astype(jnp.float32) + proj).astype(jnp.bfloat16)
     return y_own, (x_own, normed, qkv, o_act)
 
@@ -158,8 +163,7 @@
     d_o = mixed("td,de->te", grad_y, weight[:, q_width + 2 * head:]).astype(jnp.bfloat16)
     d_qkv = by_sequence(attn_bwd_kernel, seq, q_width, head, (qkv, d_o), qkv.shape[1], 2, 40_000_000_000)
     w_qkv = weight[:, :q_width + 2 * head]
-    other = swap(mixed("te,de->td", d_qkv[rows:], w_qkv))
-    d_norm = mixed("te,de->td", d_qkv[:rows], w_qkv) + other
+    d_norm = both_halves(d_qkv, w_qkv, rows, "te,de->td")
     grad_x = (grad_own.astype(jnp.float32) + norm_back(x_own, d_norm)).astype(jnp.bfloat16)
     d_qkv_w = mixed("td,te->de", normed, d_qkv)
     return grad_x, d_qkv_w, mixed("td,te->de", grad_y, o_act)
@@ -179,8 +183,7 @@
 
 def mlp_output(x_own, gelu_act, down_weight):
     rows = x_own.shape[0]
-    other = swap(mixed("tf,fd->td", gelu_act[rows:], down_weight))
-    proj = mixed("tf,fd->td", gelu_act[:rows], down_weight) + other
+    proj = both_halves(gelu_act, down_weight, rows, "tf,fd->td")
     return (x_own.astype(jnp.float32) + proj).astype(jnp.bfloat16)
 
 
@@ -188,8 +191,7 @@
     rows = grad_own.shape[0]
     grad_act = mixed("td,fd->tf", pair_rows(grad_own), down_weight)
     d_hid = (grad_act * slope).astype(jnp.bfloat16)
-    other = swap(mixed("tf,df->td", d_hid[rows:], up_weight))
-    d_norm = mixed("tf,df->td", d_hid[:rows], up_weight) + other
+    d_norm = both_halves(d_hid, up_weight, rows, "tf,df->td")
     return (grad_own.astype(jnp.float32) + norm_back(x_own, d_norm)).astype(jnp.bfloat16)
 
 
@@ -318,7 +320,8 @@
             attn_full.append(gather(attn_piece(layer)))
             up_full.append(gather(up_piece(layer)))
             down_full.append(gather(w_down[layer]))
-            up_flip.append(lax.select_n(chip, *[up_full[layer][:, i * block:(i + 1) * block] for i in range(chips)]).T)
+            cols = [up_full[layer][:, i * block:(i + 1) * block] for i in range(chips)]
+            up_flip.append(lax.select_n(chip, *cols).T)
         place = jnp.stack([chip, core]).astype(jnp.int32)
         carry_x = x_loc.reshape(seqs * seq, width)
         grad_x = grad_out.reshape(seqs * seq, width)
@@ -336,9 +339,10 @@
             norms = all_rows(n_own)
             if layer == pairs - 1:
                 parts, d_down = weight_grads(layer, norms, all_rows(grad_x), d_down)
-            carry_x = mlp_output(x_own, gelu_act, down_full[layer])
             mlp_saved.append((x_own, norms, slope))
-        y_loc = carry_x.reshape(x_loc.shape)
+            if layer < pairs - 1:
+                carry_x = mlp_output(x_own, gelu_act, down_full[layer])
+        last = (x_own, gelu_act, down_full[-1])
         grad_lists = ([], [], [], [])
         for layer in reversed(range(pairs)):
             x_own, norms, slope = mlp_saved[layer]
@@ -354,6 +358,8 @@
                                  .reshape(shard, heads, head))
             grad_lists[1].append(jnp.stack([part[:, q_width:q_width + head] for part in parts], axis=1))
             grad_lists[2].append(jnp.stack([part[:, q_width + head:] for part in parts], axis=1))
+        last, d_down = lax.optimization_barrier((last, d_down))
+        y_loc = mlp_output(*last).reshape(x_loc.shape)
         stacked = tuple(jnp.stack(grad_list[::-1]) for grad_list in grad_lists)
         return (y_loc, grad_x.reshape(x_loc.shape)) + stacked + (d_up[0], d_down[0])
 

time: 1790 us -> 1820 us (1.017)
  other arithmetic: 71.5 us -> 126 us
  waiting for transfers between devices: 672 us -> 643 us
    ppermute x28, waiting for transfers between devices: 76.8 us -> 38.7 us  [swap(): return lax.ppermute(value, 'fsdp', [(0, 1), (1, 0)])]
    reduce_scatter x4, waiting for transfers between devices: 36.1 us -> 54.8 us  [scatter_sum(): return lax.psum_scatter(grad_full, 'sub', scatter_dimension=0, tiled=True)]
  transfers between devices with their start and end apart: 56 -> 56, of which waited for: 26 -> 25; matrix products, arithmetic and copies ran while one was open for 37% -> 38% of each run, Pallas kernels for 21% -> 14%
where the time goes in v2:
time: 1820 us; the launch traced here: 1810 us
  waiting for transfers between devices  643 us (35%)
  matrix products  487 us (27%)
  Pallas kernels  388 us (21%)
  local copies, waits for them, and re-layouts  127 us (7%)
  other arithmetic  126 us (7%)
  starting transfers between devices  23.9 us (1%)
    dot_general x28, matrix products, mixed(): return jnp.einsum(form, left, right, preferred_element_type=jnp.float32)  487 us
    all_gather x10, waiting for transfers between devices, gather(): return lax.all_gather(piece, 'sub', axis=0, tiled=True)  395 us
    pallas_call x2, Pallas kernels, mlp_weight_grads(): pl.pallas_call(functools.partial(mlp_grads_kernel, half), grid_spec=pltpu...  282 us
    ppermute x14, waiting for transfers between devices, exchange(): lax.ppermute(part, AXES, [(d, d ^ i) for d in devices])  155 us
    pallas_call x4, Pallas kernels, by_sequence(): pl.pallas_call(functools.partial(kernel, q_width, head), grid=(rows // se...  90.2 us
    reduce_scatter x4, waiting for transfers between devices, scatter_sum(): return lax.psum_scatter(grad_full, 'sub', scatter_dimension=0, tiled=True)  54.8 us
    unnamed x175, local copies, waits for them, and re-layouts  48.1 us
    ppermute x28, waiting for transfers between devices, swap(): return lax.ppermute(value, 'fsdp', [(0, 1), (1, 0)])  38.7 us
  transfers between devices with their start and end apart: 56, of which 25 were waited for; matrix products, arithmetic and copies ran while one was open for 38% of the time, Pallas kernels for 14%

profile of v2, /device:TPU:0, one launch (start us, length us, event | category | flops | bytes accessed | tf_op | source)
XLA Modules:
  0.0 1811.0 jit_solution(10031936490730244542)
XLA Ops:
  19.0 6.4 fusion.123
  25.4 7.1 reshape_squeeze.28
  35.8 6.0 fusion.125
  41.8 9.3 copy.134
  63.2 7.3 reshape_squeeze.31
  70.5 6.0 fusion.124
  76.5 8.7 copy.142
  113.4 8.1 slice_bitcast_fusion.14
  144.6 11.6 fusion.68.qkv_ref
  156.2 17.0 shard_map.143
  178.5 6.3 fusion.98
  188.7 5.8 fusion.34
  202.5 39.6 %all-gather.15.cloned.1.call-done = bf16[1536,4480]{0,1:T(8,128)(2,1)} async-done(((bf16[384,4480]{0,1:T(8,128)(2,1)}), bf16[1536,4480]{0,1:T(8,128)(2,1)}) %all-gather.15.cloned.1.call-update) | async-done | bytes 13762576 | tf_op jit(solution)/shard_map/all_gather | solution.py:64
  242.2 51.1 %multiply_add_fusion.2 = (f32[2048,4480]{1,0:T(8,128)}, bf16[2048,4480]{1,0:T(8,128)(2,1)}) fusion(bf16[1536,4480]{0,1:T(8,128)(2,1)} %all-gather.15.cloned.1.call-done, bf16[1024,1536]{1,0:T(8,128)(2,1)} %collective-permute-done.3, bf16[1024,1536]{1,0:T(8,128)(2,1)S(1)} %fusion.35), kind=kOutput, calls=%fused_computation.6 | convolution fusion | flops 28326756352 | bytes 75104256 | tf_op jit(solution)/shard_map/td,df->tf/dot_general | solution.py:37
  293.3 77.9 %all-gather.29.cloned.1.call-done = bf16[1,4480,1536]{2,1,0:T(8,128)(2,1)} async-done(((bf16[1,1120,1536]{2,1,0:T(8,128)(2,1)}), bf16[1,4480,1536]{2,1,0:T(8,128)(2,1)}) %all-gather.29.cloned.1.call-update) | async-done | bytes 13762576 | tf_op jit(solution)/shard_map/all_gather | solution.py:64
  371.2 21.4 %fusion.5 = f32[1024,1536]{1,0:T(8,128)} fusion(bf16[1,4480,1536]{2,1,0:T(8,128)(2,1)} %all-gather.29.cloned.1.call-done, bf16[2048,4480]{1,0:T(8,128)(2,1)} %get-tuple-element.34), kind=kOutput, calls=%fused_computation.11 | convolution fusion | flops 14092861440 | bytes 29229056 | tf_op jit(solution)/shard_map/tf,fd->td/dot_general | solution.py:37
  392.9 21.6 %fusion.7 = f32[1024,1536]{1,0:T(8,128)} fusion(bf16[1,4480,1536]{2,1,0:T(8,128)(2,1)} %all-gather.29.cloned.1.call-done, bf16[2048,4480]{1,0:T(8,128)(2,1)} %get-tuple-element.34), kind=kOutput, calls=%fused_computation.13 | convolution fusion | flops 14092861440 | bytes 29229056 | tf_op jit(solution)/shard_map/tf,fd->td/dot_general | solution.py:37
  414.4 5.8 fusion.38
  423.0 8.4 all-gather.17.cloned.1.call-done
  431.3 10.6 fusion.69.qkv_ref
  442.0 17.1 shard_map.144
  464.0 6.6 fusion.93
  474.3 6.0 fusion.31
  484.9 74.6 %all-gather.19.cloned.1.call-done = bf16[1536,4480]{0,1:T(8,128)(2,1)} async-done(((bf16[384,4480]{0,1:T(8,128)(2,1)}), bf16[1536,4480]{0,1:T(8,128)(2,1)}) %all-gather.19.cloned.1.call-update) | async-done | bytes 13762576 | tf_op jit(solution)/shard_map/all_gather | solution.py:64
  559.5 51.1 %multiply_add_fusion = (f32[2048,4480]{1,0:T(8,128)}, bf16[2048,4480]{1,0:T(8,128)(2,1)}) fusion(bf16[1536,4480]{0,1:T(8,128)(2,1)} %all-gather.19.cloned.1.call-done, bf16[1024,1536]{1,0:T(8,128)(2,1)} %collective-permute-done.9, bf16[1024,1536]{1,0:T(8,128)(2,1)} %fusion.32), kind=kOutput, calls=%fused_computation.2 | convolution fusion | flops 28326756352 | bytes 75104256 | tf_op jit(solution)/shard_map/td,df->tf/dot_general | solution.py:37
  610.6 77.2 %all-gather.31.cloned.1.call-done = bf16[1,4480,1536]{2,1,0:T(8,128)(2,1)} async-done(((bf16[1,1120,1536]{2,1,0:T(8,128)(2,1)}), bf16[1,4480,1536]{2,1,0:T(8,128)(2,1)}) %all-gather.31.cloned.1.call-update) | async-done | bytes 13762576 | tf_op jit(solution)/shard_map/all_gather | solution.py:64
  687.8 40.7 %multiply_convert_fusion.1 = bf16[2048,4480]{1,0:T(8,128)(2,1)} fusion(f32[2048,4480]{1,0:T(8,128)} %get-tuple-element.36, bf16[1024,1536]{1,0:T(8,128)(2,1)} %collective-permute-done.12, bf16[1024,1536]{1,0:T(8,128)(2,1)S(1)} %bitcast.151, bf16[1,4480,1536]{2,1,0:T(8,128)(2,1)} %all-gather.31.cloned.1.call-done), kind=kOutput, calls=%fused_computation.1 | convolution fusion | flops 28216655872 | bytes 75104256 | tf_op jit(solution)/shard_map/td,fd->tf/dot_general | solution.py:37
  728.5 21.8 %fusion.13 = f32[1024,1536]{1,0:T(8,128)} fusion(bf16[1536,4480]{0,1:T(8,128)(2,1)} %all-gather.19.cloned.1.call-done, bf16[2048,4480]{1,0:T(8,128)(2,1)} %multiply_convert_fusion.1), kind=kOutput, calls=%fused_computation.37 | convolution fusion | flops 14092861440 | bytes 29229056 | tf_op jit(solution)/shard_map/tf,df->td/dot_general | solution.py:37
  750.4 18.9 %fusion.15 = f32[1024,1536]{1,0:T(8,128)S(1)} fusion(bf16[1536,4480]{0,1:T(8,128)(2,1)} %all-gather.19.cloned.1.call-done, bf16[2048,4480]{1,0:T(8,128)(2,1)} %multiply_convert_fusion.1), kind=kOutput, calls=%fused_computation.39 | convolution fusion | flops 14092861440 | bytes 29229056 | tf_op jit(solution)/shard_map/tf,df->td/dot_general | solution.py:37
  783.3 10.0 fusion.74.d_o_ref
  793.4 27.8 %shard_map.145 = bf16[2048,1024]{1,0:T(8,128)(2,1)} custom-call(bf16[2048,1024]{1,0:T(8,128)(2,1)} %fusion.69.qkv_ref, bf16[2048,768]{1,0:T(8,128)(2,1)} %fusion.74.d_o_ref), custom_call_target="tpu_custom_call" | custom-call | flops 40000000000 | tf_op jit(solution)/shard_map/pallas_call | solution.py:137
  821.2 8.8 fusion.76
  830.4 6.9 fusion.62
  837.5 6.1 fusion.78
  858.9 40.7 %multiply_convert_fusion = bf16[2048,4480]{1,0:T(8,128)(2,1)} fusion(f32[2048,4480]{1,0:T(8,128)} %get-tuple-element.42, bf16[1,4480,1536]{2,1,0:T(8,128)(2,1)} %all-gather.29.cloned.1.call-done, bf16[1024,1536]{1,0:T(8,128)(2,1)S(1)} %collective-permute-done.20, bf16[1024,1536]{1,0:T(8,128)(2,1)} %fusion.26), kind=kOutput, calls=%fused_computation | convolution fusion | flops 28216655872 | bytes 75104256 | tf_op jit(solution)/shard_map/td,fd->tf/dot_general | solution.py:37
  899.6 21.6 %fusion.9 = f32[1024,1536]{1,0:T(8,128)} fusion(bf16[1536,4480]{0,1:T(8,128)(2,1)} %all-gather.15.cloned.1.call-done, bf16[2048,4480]{1,0:T(8,128)(2,1)} %multiply_convert_fusion), kind=kOutput, calls=%fused_computation.33 | convolution fusion | flops 14092861440 | bytes 29229056 | tf_op jit(solution)/shard_map/tf,df->td/dot_general | solution.py:37
  921.3 10.3 fusion.64
  932.1 20.7 %fusion.11 = f32[1024,1536]{1,0:T(8,128)S(1)} fusion(bf16[1536,4480]{0,1:T(8,128)(2,1)} %all-gather.15.cloned.1.call-done, bf16[2048,4480]{1,0:T(8,128)(2,1)} %multiply_convert_fusion), kind=kOutput, calls=%fused_computation.35 | convolution fusion | flops 14092861440 | bytes 29229056 | tf_op jit(solution)/shard_map/tf,df->td/dot_general | solution.py:37
  968.1 9.3 fusion.60
  978.2 7.1 fusion.71.up_ref
  985.4 58.3 %all-gather.21.cloned.1.call-done.n0_ref = bf16[4096,1536]{1,0:T(8,128)(2,1)} async-done(((bf16[1024,1536]{1,0:T(8,128)(2,1)}), bf16[4096,1536]{1,0:T(8,128)(2,1)}) %all-gather.21.cloned.1.call-update) | async-done | bytes 12582928 | tf_op jit(solution)/shard_map/all_gather | solution.py:64
  1043.7 54.8 %reduce-scatter.11.cloned.1.call-done = f32[384,768]{1,0:T(8,128)} async-done(((f32[1536,768]{1,0:T(8,128)}), f32[384,768]{1,0:T(8,128)}) %reduce-scatter.11.cloned.1.call-update) | async-done | bytes 1179664 | tf_op jit(solution)/shard_map/reduce_scatter | solution.py:68
  1100.4 9.3 fusion.75.d_o_ref
  1109.7 28.2 %shard_map.146 = bf16[2048,1024]{1,0:T(8,128)(2,1)} custom-call(bf16[2048,1024]{1,0:T(8,128)(2,1)} %fusion.68.qkv_ref, bf16[2048,768]{1,0:T(8,128)(2,1)} %fusion.75.d_o_ref), custom_call_target="tpu_custom_call" | custom-call | flops 40000000000 | tf_op jit(solution)/shard_map/pallas_call | solution.py:137
  1138.0 8.7 fusion.81
  1147.3 10.6 fusion.66
  1157.9 59.2 %all-gather.23.cloned.1.call-done.g0_ref = bf16[4096,1536]{1,0:T(8,128)(2,1)} async-done(((bf16[1024,1536]{1,0:T(8,128)(2,1)}), bf16[4096,1536]{1,0:T(8,128)(2,1)}) %all-gather.23.cloned.1.call-update) | async-done | bytes 12582928 | tf_op jit(solution)/shard_map/all_gather | solution.py:64
  1217.1 140.9 %mlp_grads.2 = (f32[2,1120,1536]{2,1,0:T(8,128)}, f32[192,1120]{1,0:T(8,128)}, f32[192,1120]{1,0:T(8,128)}, f32[192,1120]{1,0:T(8,128)}, f32[192,1120]{1,0:T(8,1...) custom-call(s32[2]{0:T(128)} %pad_add_fusion.place_ref, ...), custom_call_target="tpu_custom_call" | custom-call | flops 112742891520 | tf_op jit(solution)/shard_map/mlp_grads/pallas_call | solution.py:240
  1364.4 8.3 fusion.73.up_ref
  1375.4 24.7 %collective-permute-done.36.refs_2_ = f32[192,1120]{1,0:T(8,128)S(1)} collective-permute-done((f32[192,1120]{1,0:T(8,128)}, f32[192,1120]{1,0:T(8,128)S(1)}, u32[]{:S(2)}, u32[]{:S(2)}) %collective-permute-start.36) | collective-permute-done | bytes 860192 | tf_op jit(solution)/shard_map/ppermute | solution.py:263
  1401.6 33.3 %collective-permute-done.37.refs_3_ = f32[192,1120]{1,0:T(8,128)S(1)} collective-permute-done((f32[192,1120]{1,0:T(8,128)}, f32[192,1120]{1,0:T(8,128)S(1)}, u32[]{:S(2)}, u32[]{:S(2)}) %collective-permute-start.37) | collective-permute-done | bytes 860192 | tf_op jit(solution)/shard_map/ppermute | solution.py:263
  1442.2 34.1 %collective-permute-done.39.refs_5_ = f32[192,1120]{1,0:T(8,128)} collective-permute-done((f32[192,1120]{1,0:T(8,128)}, f32[192,1120]{1,0:T(8,128)}, u32[]{:S(2)}, u32[]{:S(2)}) %collective-permute-start.39) | collective-permute-done | bytes 860192 | tf_op jit(solution)/shard_map/ppermute | solution.py:263
  1478.6 8.6 fusion.83
  1487.2 11.3 collective-permute-done.41.refs_7_
  1499.5 8.1 assemble.2.refs_8_
  1517.9 8.3 fusion.30
  1534.9 141.0 %mlp_grads.3 = (f32[2,1120,1536]{2,1,0:T(8,128)}, f32[192,1120]{1,0:T(8,128)}, f32[192,1120]{1,0:T(8,128)}, f32[192,1120]{1,0:T(8,128)}, f32[192,1120]{1,0:T(8,1...) custom-call(s32[2]{0:T(128)} %pad_add_fusion.place_ref, ...), custom_call_target="tpu_custom_call", output_to_operand_aliasing={{0}: (7, {})} | custom-call | flops 112742891520 | tf_op jit(solution)/shard_map/mlp_grads/pallas_call | solution.py:240
  1675.9 21.6 %fusion.17 = f32[1024,1536]{1,0:T(8,128)} fusion(bf16[4480,1536]{1,0:T(8,128)(2,1)} %bitcast.168, bf16[2048,4480]{1,0:T(8,128)(2,1)} %get-tuple-element.40), kind=kOutput, calls=%fused_computation.41 | convolution fusion | flops 14092861440 | bytes 29229056 | tf_op jit(solution)/shard_map/tf,fd->td/dot_general | solution.py:37
  1710.5 10.4 collective-permute-done.29.refs_2_
  1722.2 16.6 collective-permute-done.30.refs_3_
  1740.7 21.6 %fusion.19 = f32[1024,1536]{1,0:T(8,128)} fusion(bf16[4480,1536]{1,0:T(8,128)(2,1)} %bitcast.169, bf16[2048,4480]{1,0:T(8,128)(2,1)} %get-tuple-element.40), kind=kOutput, calls=%fused_computation.43 | convolution fusion | flops 14092861440 | bytes 29229056 | tf_op jit(solution)/shard_map/tf,fd->td/dot_general | solution.py:37
  1762.3 23.3 %collective-permute-done.32.refs_5_ = f32[192,1120]{1,0:T(8,128)S(1)} collective-permute-done((f32[192,1120]{1,0:T(8,128)S(1)}, f32[192,1120]{1,0:T(8,128)S(1)}, u32[]{:S(2)}, u32[]{:S(2)}) %collective-permute-start.32) | collective-permute-done | bytes 860192 | tf_op jit(solution)/shard_map/ppermute | solution.py:263
  1787.9 8.1 assemble.3
  1796.1 8.1 add_convert_fusion
  (381 shorter events, 218.7 us)
Async XLA Ops:
  7.2 137.4 %all-gather.13.cloned.1.call-start = ((), (), s32[]{:S(2)}) async-start(), calls=%async_computation.4 | async-start | bytes 6881280 | tf_op jit(solution)/shard_map/all_gather | solution.py:64
  18.2 14.3 collective-permute-start.1
  35.6 206.6 %all-gather.15.cloned.1.call-start = ((), (), s32[]{:S(2)}) async-start(), calls=%async_computation.5 | async-start | bytes 17203200 | tf_op jit(solution)/shard_map/all_gather | solution.py:64
  63.1 34.6 %collective-permute-start.4 = (bf16[192,4480]{1,0:T(8,128)(2,1)}, bf16[192,4480]{1,0:T(8,128)(2,1)}, u32[]{:S(2)}, u32[]{:S(2)}) collective-permute-start(bf16[192,4480]{1,0:T(8,128)(2,1)} %copy.126), channel_id=1, source_target_pairs={{0,1},{1,0},{2,3},{3,2},{4,5},{5,4},{6,7},{7,6}} | collective-permute-start | bytes 5160968 | tf_op jit(solution)/shard_map/ppermute | solution.py:41
  97.3 4.5 collective-permute-start.10
  113.4 257.8 %all-gather.29.cloned.1.call-start = ((), (), s32[]{:S(2)}) async-start(), calls=%async_computation.16 | async-start | bytes 17203200 | tf_op jit(solution)/shard_map/all_gather | solution.py:64
  121.5 309.8 %all-gather.17.cloned.1.call-start = ((), (), s32[]{:S(2)}) async-start(), calls=%async_computation.6 | async-start | bytes 6881280 | tf_op jit(solution)/shard_map/all_gather | solution.py:64
  125.4 2.2 collective-permute-start.7
  129.1 430.4 %all-gather.19.cloned.1.call-start = ((), (), s32[]{:S(2)}) async-start(), calls=%async_computation.7 | async-start | bytes 17203200 | tf_op jit(solution)/shard_map/all_gather | solution.py:64
  135.2 552.6 %all-gather.31.cloned.1.call-start = ((), (), s32[]{:S(2)}) async-start(), calls=%async_computation.17 | async-start | bytes 17203200 | tf_op jit(solution)/shard_map/all_gather | solution.py:64
  138.8 5.8 collective-permute-start
  178.3 10.3 collective-permute-start.2
  196.7 96.5 %copy-start.19 = (bf16[1024,1536]{1,0:T(8,128)(2,1)}, bf16[1024,1536]{1,0:T(8,128)(2,1)S(1)}, u32[]{:S(2)}) copy-start(bf16[1024,1536]{1,0:T(8,128)(2,1)S(1)} %fusion.35) | copy-start | bytes 9437188
  196.7 5.8 collective-permute-start.3
  196.9 765.6 %all-gather.27.cloned.1.call-start = ((), (), s32[]{:S(2)}) async-start(), calls=%async_computation.11 | async-start | bytes 15728640 | tf_op jit(solution)/shard_map/all_gather | solution.py:64
  392.6 21.8 %collective-permute-start.5 = (f32[1024,1536]{1,0:T(8,128)}, f32[1024,1536]{1,0:T(8,128)}, u32[]{:S(2)}, u32[]{:S(2)}) collective-permute-start(f32[1024,1536]{1,0:T(8,128)} %fusion.5), channel_id=1, source_target_pairs={{0,1},{1,0},{2,3},{3,2},{4,5},{5,4},{6,7},{7,6}} | collective-permute-start | bytes 18874376 | tf_op jit(solution)/shard_map/ppermute | solution.py:41
  392.6 21.8 %copy-start.6 = (bf16[1024,1536]{1,0:T(8,128)(2,1)S(1)}, bf16[1024,1536]{1,0:T(8,128)(2,1)}, u32[]{:S(2)}) copy-start(bf16[1024,1536]{1,0:T(8,128)(2,1)} %copy-done.5) | copy-start | bytes 9437188
  392.6 570.1 %all-gather.25.cloned.1.call-start = ((), (), s32[]{:S(2)}) async-start(), calls=%async_computation.10 | async-start | bytes 15728640 | tf_op jit(solution)/shard_map/all_gather | solution.py:64
  422.5 8.9 collective-permute-start.6
  464.0 10.3 collective-permute-start.8
  484.3 75.2 %collective-permute-start.9 = (bf16[1024,1536]{1,0:T(8,128)(2,1)}, bf16[1024,1536]{1,0:T(8,128)(2,1)}, u32[]{:S(2)}, u32[]{:S(2)}) collective-permute-start(bf16[1024,1536]{1,0:T(8,128)(2,1)} %fusion.32), channel_id=1, source_target_pairs={{0,1},{1,0},{2,3},{3,2},{4,5},{5,4},{6,7},{7,6}} | collective-permute-start | bytes 9437192 | tf_op jit(solution)/shard_map/ppermute | solution.py:41
  484.5 126.2 %collective-permute-start.12 = (bf16[1024,1536]{1,0:T(8,128)(2,1)S(1)}, bf16[1024,1536]{1,0:T(8,128)(2,1)}, u32[]{:S(2)}, u32[]{:S(2)}) collective-permute-start(bf16[1024,1536]{1,0:T(8,128)(2,1)S(1)} %bitcast.150), channel_id=1, source_target_pairs={{0,1},{1,0},{2,3},{3,2},{4,5},{5,4},{6,7},{7,6}} | collective-permute-start | bytes 9437192 | tf_op jit(solution)/shard_map/ppermute | solution.py:41
  484.9 558.8 %all-gather.21.cloned.1.call-start = ((), (), s32[]{:S(2)}) async-start(), calls=%async_computation.8 | async-start | bytes 15728640 | tf_op jit(solution)/shard_map/all_gather | solution.py:64
  750.3 19.0 %collective-permute-start.13 = (f32[1024,1536]{1,0:T(8,128)}, f32[1024,1536]{1,0:T(8,128)}, u32[]{:S(2)}, u32[]{:S(2)}) collective-permute-start(f32[1024,1536]{1,0:T(8,128)} %fusion.13), channel_id=1, source_target_pairs={{0,1},{1,0},{2,3},{3,2},{4,5},{5,4},{6,7},{7,6}} | collective-permute-start | bytes 18874376 | tf_op jit(solution)/shard_map/ppermute | solution.py:41
  750.3 348.1 %reduce-scatter.11.cloned.1.call-start = ((), (), s32[]{:S(2)}) async-start(), calls=%async_computation.15 | async-start | bytes 5898240 | tf_op jit(solution)/shard_map/reduce_scatter | solution.py:68
  777.5 5.8 collective-permute-start.14
  830.0 13.7 collective-permute-start.15
  837.3 379.8 %all-gather.23.cloned.1.call-start = ((), (), s32[]{:S(2)}) async-start(), calls=%async_computation.9 | async-start | bytes 15728640 | tf_op jit(solution)/shard_map/all_gather | solution.py:64
  853.0 5.9 collective-permute-start.20
  853.2 505.2 %reduce-scatter.7.cloned.1.call-start = ((), (), s32[]{:S(2)}) async-start(), calls=%async_computation.13 | async-start | bytes 7864320 | tf_op jit(solution)/shard_map/reduce_scatter | solution.py:68
  921.1 31.7 %collective-permute-start.21 = (f32[1024,1536]{1,0:T(8,128)}, f32[1024,1536]{1,0:T(8,128)}, u32[]{:S(2)}, u32[]{:S(2)}) collective-permute-start(f32[1024,1536]{1,0:T(8,128)} %fusion.9), channel_id=1, source_target_pairs={{0,1},{1,0},{2,3},{3,2},{4,5},{5,4},{6,7},{7,6}} | collective-permute-start | bytes 18874376 | tf_op jit(solution)/shard_map/ppermute | solution.py:41
  931.7 581.5 %reduce-scatter.9.cloned.1.call-start = ((), (), s32[]{:S(2)}) async-start(), calls=%async_computation.14 | async-start | bytes 5898240 | tf_op jit(solution)/shard_map/reduce_scatter | solution.py:68
  962.2 5.9 collective-permute-start.22
  962.6 195.3 %collective-permute-start.18 = (bf16[4096,1536]{1,0:T(8,128)(2,1)}, bf16[4096,1536]{1,0:T(8,128)(2,1)}, u32[]{:S(2)}, u32[]{:S(2)}) collective-permute-start(bf16[4096,1536]{1,0:T(8,128)(2,1)} %all-gather.27.cloned.1.call-done.g0_ref), channel_id=1, source_target_pairs={{0,1},{1,0},{2,3},{3,2},{4,5},{5,4},{6,7},{7,6}} | collective-permute-start | bytes 37748744 | tf_op jit(solution)/shard_map/ppermute | solution.py:41
  962.7 254.4 %collective-permute-start.17 = (bf16[4096,1536]{1,0:T(8,128)(2,1)}, bf16[4096,1536]{1,0:T(8,128)(2,1)}, u32[]{:S(2)}, u32[]{:S(2)}) collective-permute-start(bf16[4096,1536]{1,0:T(8,128)(2,1)} %all-gather.25.cloned.1.call-done.n0_ref), channel_id=1, source_target_pairs={{0,1},{1,0},{2,3},{3,2},{4,5},{5,4},{6,7},{7,6}} | collective-permute-start | bytes 37748744 | tf_op jit(solution)/shard_map/ppermute | solution.py:41
  977.4 538.4 %reduce-scatter.5.cloned.1.call-start = ((), (), s32[]{:S(2)}) async-start(), calls=%async_computation.12 | async-start | bytes 7864320 | tf_op jit(solution)/shard_map/reduce_scatter | solution.py:68
  1043.7 491.2 %collective-permute-start.11 = (bf16[4096,1536]{1,0:T(8,128)(2,1)}, bf16[4096,1536]{1,0:T(8,128)(2,1)}, u32[]{:S(2)}, u32[]{:S(2)}) collective-permute-start(bf16[4096,1536]{1,0:T(8,128)(2,1)} %all-gather.21.cloned.1.call-done.n0_ref), channel_id=1, source_target_pairs={{0,1},{1,0},{2,3},{3,2},{4,5},{5,4},{6,7},{7,6}} | collective-permute-start | bytes 37748744 | tf_op jit(solution)/shard_map/ppermute | solution.py:41
  1100.4 259.2 %collective-permute-start.27 = (f32[192,768]{1,0:T(8,128)}, f32[192,768]{1,0:T(8,128)}, u32[]{:S(2)}, u32[]{:S(2)}) collective-permute-start(f32[192,768]{1,0:T(8,128)} %dynamic-slice_bitcast_fusion.2), channel_id=1, source_target_pairs={{0,1},{1,0},{2,3},{3,2},{4,5},{5,4},{6,7},{7,6}} | collective-permute-start | bytes 1769480 | tf_op jit(solution)/shard_map/ppermute | solution.py:41
  1146.7 360.8 %collective-permute-start.23 = (f32[1024,1536]{1,0:T(8,128)}, f32[1024,1536]{1,0:T(8,128)}, u32[]{:S(2)}, u32[]{:S(2)}) collective-permute-start(f32[1024,1536]{1,0:T(8,128)} %fusion.81), channel_id=1, source_target_pairs={{0,1},{1,0},{2,3},{3,2},{4,5},{5,4},{6,7},{7,6}} | collective-permute-start | bytes 18874376 | tf_op jit(solution)/shard_map/ppermute | solution.py:41
  1217.1 317.8 %collective-permute-start.16 = (bf16[4096,1536]{1,0:T(8,128)(2,1)}, bf16[4096,1536]{1,0:T(8,128)(2,1)}, u32[]{:S(2)}, u32[]{:S(2)}) collective-permute-start(bf16[4096,1536]{1,0:T(8,128)(2,1)} %all-gather.23.cloned.1.call-done.g0_ref), channel_id=1, source_target_pairs={{0,1},{1,0},{2,3},{3,2},{4,5},{5,4},{6,7},{7,6}} | collective-permute-start | bytes 37748744 | tf_op jit(solution)/shard_map/ppermute | solution.py:41
  1358.0 6.3 collective-permute-start.35
  1359.6 2.3 collective-permute-start.25
  1362.8 37.3 %collective-permute-start.36 = (f32[192,1120]{1,0:T(8,128)}, f32[192,1120]{1,0:T(8,128)S(1)}, u32[]{:S(2)}, u32[]{:S(2)}) collective-permute-start(f32[192,1120]{1,0:T(8,128)} %get-tuple-element.53), channel_id=1, source_target_pairs={{0,2},{1,3},{2,0},{3,1},{4,6},{5,7},{6,4},{7,5}} | collective-permute-start | bytes 2580488 | tf_op jit(solution)/shard_map/ppermute | solution.py:263
  1364.3 70.6 %collective-permute-start.37 = (f32[192,1120]{1,0:T(8,128)}, f32[192,1120]{1,0:T(8,128)S(1)}, u32[]{:S(2)}, u32[]{:S(2)}) collective-permute-start(f32[192,1120]{1,0:T(8,128)} %get-tuple-element.54), channel_id=1, source_target_pairs={{0,3},{1,2},{2,1},{3,0},{4,7},{5,6},{6,5},{7,4}} | collective-permute-start | bytes 2580488 | tf_op jit(solution)/shard_map/ppermute | solution.py:263
  1400.1 34.8 %copy-start.43 = (f32[192,1120]{1,0:T(8,128)}, f32[192,1120]{1,0:T(8,128)S(1)}, u32[]{:S(2)}) copy-start(f32[192,1120]{1,0:T(8,128)S(1)} %collective-permute-done.36.refs_2_) | copy-start | bytes 2580484
  1400.1 41.5 %collective-permute-start.38 = (f32[192,1120]{1,0:T(8,128)}, f32[192,1120]{1,0:T(8,128)}, u32[]{:S(2)}, u32[]{:S(2)}) collective-permute-start(f32[192,1120]{1,0:T(8,128)} %get-tuple-element.55), channel_id=1, source_target_pairs={{0,4},{1,5},{2,6},{3,7},{4,0},{5,1},{6,2},{7,3}} | collective-permute-start | bytes 2580488 | tf_op jit(solution)/shard_map/ppermute | solution.py:263
  1435.8 40.5 %collective-permute-start.39 = (f32[192,1120]{1,0:T(8,128)}, f32[192,1120]{1,0:T(8,128)}, u32[]{:S(2)}, u32[]{:S(2)}) collective-permute-start(f32[192,1120]{1,0:T(8,128)} %get-tuple-element.56), channel_id=1, source_target_pairs={{0,5},{1,4},{2,7},{3,6},{4,1},{5,0},{6,3},{7,2}} | collective-permute-start | bytes 2580488 | tf_op jit(solution)/shard_map/ppermute | solution.py:263
  1441.7 45.5 %collective-permute-start.40 = (f32[192,1120]{1,0:T(8,128)}, f32[192,1120]{1,0:T(8,128)S(1)}, u32[]{:S(2)}, u32[]{:S(2)}) collective-permute-start(f32[192,1120]{1,0:T(8,128)} %get-tuple-element.57), channel_id=1, source_target_pairs={{0,6},{1,7},{2,4},{3,5},{4,2},{5,3},{6,0},{7,1}} | collective-permute-start | bytes 2580488 | tf_op jit(solution)/shard_map/ppermute | solution.py:263
  1476.3 22.2 %collective-permute-start.41 = (f32[192,1120]{1,0:T(8,128)}, f32[192,1120]{1,0:T(8,128)S(1)}, u32[]{:S(2)}, u32[]{:S(2)}) collective-permute-start(f32[192,1120]{1,0:T(8,128)} %get-tuple-element.58), channel_id=1, source_target_pairs={{0,7},{1,6},{2,5},{3,4},{4,3},{5,2},{6,1},{7,0}} | collective-permute-start | bytes 2580488 | tf_op jit(solution)/shard_map/ppermute | solution.py:263
  1515.1 11.1 collective-permute-start.26
  1517.9 14.6 collective-permute-start.24
  1675.9 22.0 %copy-start.24 = (f32[192,1024]{1,0:T(8,128)S(1)}, f32[192,1024]{1,0:T(8,128)}, u32[]{:S(2)}) copy-start(f32[192,1024]{1,0:T(8,128)} %get-tuple-element.128) | copy-start | bytes 2359300
  1675.9 22.1 %copy-start.23 = (f32[192,1024]{1,0:T(8,128)S(1)}, f32[192,1024]{1,0:T(8,128)}, u32[]{:S(2)}) copy-start(f32[192,1024]{1,0:T(8,128)} %get-tuple-element.129) | copy-start | bytes 2359300
  1675.9 24.3 %copy-start.48 = (f32[1,192,2,128]{3,1,2,0:T(8,128)S(1)}, f32[1,192,2,128]{3,1,2,0:T(8,128)}, u32[]{:S(2)}) copy-start(f32[1,192,2,128]{3,1,2,0:T(8,128)} %maximum_bitcast_fusion.1) | copy-start | bytes 589828
  1697.5 98.5 %collective-permute-start.19 = (f32[1024,1536]{1,0:T(8,128)}, f32[1024,1536]{1,0:T(8,128)}, u32[]{:S(2)}, u32[]{:S(2)}) collective-permute-start(f32[1024,1536]{1,0:T(8,128)} %fusion.17), channel_id=1, source_target_pairs={{0,1},{1,0},{2,3},{3,2},{4,5},{5,4},{6,7},{7,6}} | collective-permute-start | bytes 18874376 | tf_op jit(solution)/shard_map/ppermute | solution.py:41
  1698.0 11.3 collective-permute-start.28
  1698.1 22.8 %collective-permute-start.29 = (f32[192,1120]{1,0:T(8,128)}, f32[192,1120]{1,0:T(8,128)}, u32[]{:S(2)}, u32[]{:S(2)}) collective-permute-start(f32[192,1120]{1,0:T(8,128)} %get-tuple-element.45), channel_id=1, source_target_pairs={{0,2},{1,3},{2,0},{3,1},{4,6},{5,7},{6,4},{7,5}} | collective-permute-start | bytes 2580488 | tf_op jit(solution)/shard_map/ppermute | solution.py:263
  1698.8 39.9 %collective-permute-start.30 = (f32[192,1120]{1,0:T(8,128)}, f32[192,1120]{1,0:T(8,128)}, u32[]{:S(2)}, u32[]{:S(2)}) collective-permute-start(f32[192,1120]{1,0:T(8,128)} %get-tuple-element.46), channel_id=1, source_target_pairs={{0,3},{1,2},{2,1},{3,0},{4,7},{5,6},{6,5},{7,4}} | collective-permute-start | bytes 2580488 | tf_op jit(solution)/shard_map/ppermute | solution.py:263
  1704.1 34.7 %copy-start.74 = (f32[192,1120]{1,0:T(8,128)S(1)}, f32[192,1120]{1,0:T(8,128)}, u32[]{:S(2)}) copy-start(f32[192,1120]{1,0:T(8,128)} %get-tuple-element.50) | copy-start | bytes 2580484
  1707.4 54.9 %collective-permute-start.31 = (f32[192,1120]{1,0:T(8,128)S(1)}, f32[192,1120]{1,0:T(8,128)S(1)}, u32[]{:S(2)}, u32[]{:S(2)}) collective-permute-start(f32[192,1120]{1,0:T(8,128)S(1)} %copy-done.77), channel_id=1, source_target_pairs={{0,4},{1,5},{2,6},{3,7},{4,0},{5,1},{6,2},{7,3}} | collective-permute-start | bytes 2580488 | tf_op jit(solution)/shard_map/ppermute | solution.py:263
  1709.3 76.3 %collective-permute-start.32 = (f32[192,1120]{1,0:T(8,128)S(1)}, f32[192,1120]{1,0:T(8,128)S(1)}, u32[]{:S(2)}, u32[]{:S(2)}) collective-permute-start(f32[192,1120]{1,0:T(8,128)S(1)} %copy-done.76), channel_id=1, source_target_pairs={{0,5},{1,4},{2,7},{3,6},{4,1},{5,0},{6,3},{7,2}} | collective-permute-start | bytes 2580488 | tf_op jit(solution)/shard_map/ppermute | solution.py:263
  1720.9 64.7 %collective-permute-start.33 = (f32[192,1120]{1,0:T(8,128)S(1)}, f32[192,1120]{1,0:T(8,128)S(1)}, u32[]{:S(2)}, u32[]{:S(2)}) collective-permute-start(f32[192,1120]{1,0:T(8,128)S(1)} %copy-done.75), channel_id=1, source_target_pairs={{0,6},{1,7},{2,4},{3,5},{4,2},{5,3},{6,0},{7,1}} | collective-permute-start | bytes 2580488 | tf_op jit(solution)/shard_map/ppermute | solution.py:263
  1738.8 46.8 %collective-permute-start.34 = (f32[192,1120]{1,0:T(8,128)S(1)}, f32[192,1120]{1,0:T(8,128)S(1)}, u32[]{:S(2)}, u32[]{:S(2)}) collective-permute-start(f32[192,1120]{1,0:T(8,128)S(1)} %copy-done.74), channel_id=1, source_target_pairs={{0,7},{1,6},{2,5},{3,4},{4,3},{5,2},{6,1},{7,0}} | collective-permute-start | bytes 2580488 | tf_op jit(solution)/shard_map/ppermute | solution.py:263
  1762.3 23.3 %copy-start.38 = (f32[192,1120]{1,0:T(8,128)}, f32[192,1120]{1,0:T(8,128)S(1)}, u32[]{:S(2)}) copy-start(f32[192,1120]{1,0:T(8,128)S(1)} %collective-permute-done.31.refs_4_) | copy-start | bytes 2580484
  (75 other events, 445.5 us)
Sparse Core Ops, SparseCore 0:
  35.7 60.0 all-gather.12
  113.5 128.6 all-gather.14
  244.5 126.6 all-gather.28
  373.4 57.9 all-gather.16
  432.9 126.5 all-gather.18
  561.1 126.6 all-gather.30
  689.6 116.8 all-gather.26
  808.2 116.8 all-gather.24
  926.8 116.8 all-gather.20
  1047.0 51.3 reduce-scatter.10
  1100.2 116.8 all-gather.22
  1219.9 64.4 reduce-scatter.6
  1287.3 51.3 reduce-scatter.8
  1341.5 96.0 reduce-scatter.4

commit v3 on v2

--- a/solution.py
+++ b/solution.py
@@ -8,7 +8,7 @@
 from jax.sharding import PartitionSpec as P
 
 
-AXES = ("sub", "fsdp")
+CHIP, CORE = AXES = ("sub", "fsdp")
 EPS = 1e-6
 MASK_FILL = -1e30
 GELU_A = (2.0 / 3.141592653589793) ** 0.5
@@ -18,6 +18,7 @@
 QUERY_BLOCK = 256
 TOKEN_TILE = 512
 ROW_TILE = 48
+NEIGHBOURS = (1, 2)
 
 
 def rms_norm(values):
@@ -33,12 +34,28 @@
     return pull_back(grad_norm)[0]
 
 
-def mixed(form, left, right):
-    return jnp.einsum(form, left, right, preferred_element_type=jnp.float32)
+def dot(left, right, contract):
+    return lax.dot_general(left, right, (contract, ((), ())), preferred_element_type=jnp.float32)
+
+
+def times(left, right):
+    return dot(left, right, ((1,), (0,)))
+
+
+def times_flipped(left, right):
+    return dot(left, right, ((1,), (1,)))
+
+
+def over_rows(left, right):
+    return dot(left, right, ((0,), (0,)))
 
 
 def swap(value):
-    return lax.ppermute(value, "fsdp", [(0, 1), (1, 0)])
+    return lax.ppermute(value, CORE, [(0, 1), (1, 0)])
+
+
+def hop(value, step):
+    return lax.ppermute(value, CHIP, [(chip, chip ^ step) for chip in range(CHIPS)])
 
 
 def by_core(core, mine, other):
@@ -60,17 +77,45 @@
     return by_core(core, keep, swap(send))
 
 
-def gather(piece):
-    return lax.all_gather(piece, "sub", axis=0, tiled=True)
+def blank_kernel(_, out_ref):
+    del out_ref
+
+
+def blank(piece):
+    anywhere = pl.BlockSpec(memory_space=pl.ANY)
+    return pl.pallas_call(blank_kernel, in_specs=[anywhere], out_specs=anywhere, name="blank",
+                          out_shape=jax.ShapeDtypeStruct((CHIPS,) + piece.shape, piece.dtype))(piece)
+
+
+def gather_weight(chip, piece):
+    half = piece.shape[0] // 2
+    near = [hop(piece, step) for step in NEIGHBOURS]
+    opposite = [hop(near[0][:half], NEIGHBOURS[1]),
+                hop(near[1][half:], NEIGHBOURS[0])]
+    full = blank(piece)
+    parts = [(piece, 0, 0), (near[0], NEIGHBOURS[0], 0), (near[1], NEIGHBOURS[1], 0),
+             (opposite[0], sum(NEIGHBOURS), 0), (opposite[1], sum(NEIGHBOURS), half)]
+    for part, step, row in parts:
+        full = lax.dynamic_update_slice(full, part[None], (chip ^ step, row, 0))
+    return full.reshape(-1, piece.shape[1])
+
+
+def gather(value):
+    return functools.partial(lax.all_gather, axis=0, tiled=True)(value, CHIP)
+
+
+def gather_rows(value):
+    mine = gather(value)
+    return mine, swap(mine)
 
 
 def scatter_sum(grad_full):
-    return lax.psum_scatter(grad_full, "sub", scatter_dimension=0, tiled=True)
-
-
-def both_halves(left, right, rows, form):
-    other = swap(mixed(form, left[rows:], right))
-    own = lax.optimization_barrier(mixed(form, left[:rows], right))
+    return lax.psum_scatter(grad_full, CHIP, scatter_dimension=0, tiled=True)
+
+
+def both_halves(left, right, rows, product):
+    other = swap(product(left[rows:], right))
+    own = lax.optimization_barrier(product(left[:rows], right))
     return own + other
 
 
@@ -80,10 +125,6 @@
 
 def causal_blocks(seq):
     return [(start, start + QUERY_BLOCK) for start in range(0, seq, QUERY_BLOCK)]
-
-
-def dot(left, right, contract):
-    return lax.dot_general(left, right, (contract, ((), ())), preferred_element_type=jnp.float32)
 
 
 def probabilities(k_blk, q_blk, scale):
@@ -147,26 +188,23 @@
 
 def attn_forward(x_own, weight, q_width, head, seq):
     normed = pair_rows(norm_bf16(x_own))
-    qkv = mixed("td,de->te", normed, weight[:, :q_width + 2 * head]).astype(jnp.bfloat16)
-    o_act = by_sequence(attn_fwd_kernel, seq, q_width, head, (qkv,), q_width, 0, 20_000_000_000)
-    o_weight = weight[:, q_width + 2 * head:]
-    rows = x_own.shape[0]
-    proj = both_halves(o_act, o_weight, rows, "te,de->td")
+    qkv = times(normed, weight[:, :q_width + 2 * head]).astype(jnp.bfloat16)
+    o_act = by_sequence(attn_fwd_kernel, seq, q_width, head, (qkv,), q_width, 0,
+                  20_000_000_000)
+    proj = both_halves(o_act, weight[:, q_width + 2 * head:], x_own.shape[0], times_flipped)
     y_own = (x_own.astype(jnp.float32) + proj).astype(jnp.bfloat16)
     return y_own, (x_own, normed, qkv, o_act)
 
 
 def attn_backward(saved, weight, q_width, head, seq, grad_own):
     x_own, normed, qkv, o_act = saved
-    rows = grad_own.shape[0]
     grad_y = pair_rows(grad_own)
-    d_o = mixed("td,de->te", grad_y, weight[:, q_width + 2 * head:]).astype(jnp.bfloat16)
-    d_qkv = by_sequence(attn_bwd_kernel, seq, q_width, head, (qkv, d_o), qkv.shape[1], 2, 40_000_000_000)
-    w_qkv = weight[:, :q_width + 2 * head]
-    d_norm = both_halves(d_qkv, w_qkv, rows, "te,de->td")
+    d_o = times(grad_y, weight[:, q_width + 2 * head:]).astype(jnp.bfloat16)
+    d_qkv = by_sequence(attn_bwd_kernel, seq, q_width, head, (qkv, d_o), qkv.shape[1], 2,
+                  40_000_000_000)
+    d_norm = both_halves(d_qkv, weight[:, :q_width + 2 * head], grad_own.shape[0], times_flipped)
     grad_x = (grad_own.astype(jnp.float32) + norm_back(x_own, d_norm)).astype(jnp.bfloat16)
-    d_qkv_w = mixed("td,te->de", normed, d_qkv)
-    return grad_x, d_qkv_w, mixed("td,te->de", grad_y, o_act)
+    return grad_x, over_rows(normed, d_qkv), over_rows(grad_y, o_act)
 
 
 def gelu_parts(hidden):
@@ -178,26 +216,19 @@
 
 
 def mlp_hidden(normed, up_weight):
-    return lax.optimization_barrier(gelu_parts(mixed("td,df->tf", normed, up_weight)))
+    return lax.optimization_barrier(gelu_parts(times(normed, up_weight)))
 
 
 def mlp_output(x_own, gelu_act, down_weight):
-    rows = x_own.shape[0]
-    proj = both_halves(gelu_act, down_weight, rows, "tf,fd->td")
+    proj = both_halves(gelu_act, down_weight, x_own.shape[0], times)
     return (x_own.astype(jnp.float32) + proj).astype(jnp.bfloat16)
 
 
 def mlp_backward(x_own, slope, up_weight, down_weight, grad_own):
-    rows = grad_own.shape[0]
-    grad_act = mixed("td,fd->tf", pair_rows(grad_own), down_weight)
+    grad_act = times_flipped(pair_rows(grad_own), down_weight)
     d_hid = (grad_act * slope).astype(jnp.bfloat16)
-    d_norm = both_halves(d_hid, up_weight, rows, "tf,df->td")
+    d_norm = both_halves(d_hid, up_weight, grad_own.shape[0], times_flipped)
     return (grad_own.astype(jnp.float32) + norm_back(x_own, d_norm)).astype(jnp.bfloat16)
-
-
-def all_rows(value):
-    mine = gather(value)
-    return mine, swap(mine)
 
 
 def mlp_grads_kernel(half, place_ref, up_ref, down_ref, n0_ref, n1_ref, g0_ref, g1_ref, *rest):
@@ -294,11 +325,11 @@
 def solution(mesh):
     row_spec = P(AXES)
     weight_spec = P(None, AXES)
-    chips = mesh.shape["sub"]
+    chips = mesh.shape[CHIP]
 
     def body(x_loc, w_q, w_k, w_v, w_o, w_up, w_down, grad_out):
-        core = lax.axis_index("fsdp")
-        chip = lax.axis_index("sub")
+        core = lax.axis_index(CORE)
+        chip = lax.axis_index(CHIP)
         pairs, shard, heads, head = w_q.shape
         seqs, seq, width = x_loc.shape
         q_width = heads // CORES * head
@@ -317,9 +348,9 @@
 
         attn_full, up_full, down_full, up_flip = [], [], [], []
         for layer in range(pairs):
-            attn_full.append(gather(attn_piece(layer)))
-            up_full.append(gather(up_piece(layer)))
-            down_full.append(gather(w_down[layer]))
+            attn_full.append(gather_weight(chip, attn_piece(layer)))
+            up_full.append(gather_weight(chip, up_piece(layer)))
+            down_full.append(gather_weight(chip, w_down[layer]) if layer < pairs - 1 else gather(w_down[layer]))
             cols = [up_full[layer][:, i * block:(i + 1) * block] for i in range(chips)]
             up_flip.append(lax.select_n(chip, *cols).T)
         place = jnp.stack([chip, core]).astype(jnp.int32)
@@ -336,9 +367,9 @@
             attn_saved.append(saved)
             n_own = norm_bf16(x_own)
             gelu_act, slope = mlp_hidden(pair_rows(n_own), up_full[layer])
-            norms = all_rows(n_own)
+            norms = gather_rows(n_own)
             if layer == pairs - 1:
-                parts, d_down = weight_grads(layer, norms, all_rows(grad_x), d_down)
+                parts, d_down = weight_grads(layer, norms, gather_rows(grad_x), d_down)
             mlp_saved.append((x_own, norms, slope))
             if layer < pairs - 1:
                 carry_x = mlp_output(x_own, gelu_act, down_full[layer])
@@ -347,7 +378,7 @@
         for layer in reversed(range(pairs)):
             x_own, norms, slope = mlp_saved[layer]
             if layer < pairs - 1:
-                parts, d_down = weight_grads(layer, norms, all_rows(grad_x), d_down)
+                parts, d_down = weight_grads(layer, norms, gather_rows(grad_x), d_down)
             d_up = [assemble(place, layer, pairs, d_up, parts)]
             grad_x = mlp_backward(x_own, slope, up_full[layer], down_full[layer], grad_x)
             grad_x, d_qkv, d_o = attn_backward(attn_saved[layer], attn_full[layer], q_width, head, seq, grad_x)

time: 1820 us -> 1920 us (1.055)
  local copies, waits for them, and re-layouts: 127 us -> 271 us
  waiting for transfers between devices: 643 us -> 577 us
  starting transfers between devices: 23.9 us -> 43.7 us
    ppermute x28 -> x48, waiting for transfers between devices: 38.7 us -> 453 us  [the longest x20 419 us: hop(): lax.ppermute(value, CHIP, [(chip, chip ^ step) for chip in range(CHIPS)])]
    all_gather x10 -> x5, waiting for transfers between devices: 395 us -> 0.04 us  [gather(): return functools.partial(lax.all_gather, axis=0, tiled=True)(value, CHIP)]
    reduce_scatter x4, waiting for transfers between devices: 54.8 us -> 0.03 us  [scatter_sum(): return lax.psum_scatter(grad_full, CHIP, scatter_dimension=0, tiled=True)]
    dynamic_update_slice x0 -> x20, local copies, waits for them, and re-layouts: none -> 51.5 us  [gather_weight(): full = lax.dynamic_update_slice(full, part[None], (chip ^ step, row, 0))]
    slice x0 -> x12, local copies, waits for them, and re-layouts: none -> 42 us  [the longest x2 22.9 us: body(): cols = [up_full[layer][:, i * block:(i + 1) * block] for i in range(chips)]]
    ppermute x14, waiting for transfers between devices: 155 us -> 124 us  [exchange(): lax.ppermute(part, AXES, [(d, d ^ i) for d in devices])]
    unnamed x175 -> x196, local copies, waits for them, and re-layouts: 48.1 us -> 63.9 us
  transfers between devices with their start and end apart: 56 -> 71, of which waited for: 25 -> 26; matrix products, arithmetic and copies ran while one was open for 38% -> 44% of each run, Pallas kernels for 14% -> 13%
where the time goes in v3:
time: 1920 us; the launch traced here: 1910 us
  waiting for transfers between devices  577 us (30%)
  matrix products  494 us (26%)
  Pallas kernels  389 us (20%)
  local copies, waits for them, and re-layouts  271 us (14%)
  other arithmetic  122 us (6%)
  starting transfers between devices  43.7 us (2%)
    dot_general x28, matrix products, dot(): lax.dot_general(left, right, (contract, ((), ())), preferred_element_type...  494 us
    ppermute x20, waiting for transfers between devices, hop(): lax.ppermute(value, CHIP, [(chip, chip ^ step) for chip in range(CHIPS)])  419 us
    pallas_call x2, Pallas kernels, mlp_weight_grads(): pl.pallas_call(functools.partial(mlp_grads_kernel, half), grid_spec=pltpu...  282 us
    ppermute x14, waiting for transfers between devices, exchange(): lax.ppermute(part, AXES, [(d, d ^ i) for d in devices])  124 us
    pallas_call x4, Pallas kernels, by_sequence(): pl.pallas_call(functools.partial(kernel, q_width, head), grid=(rows // se...  90.7 us
    unnamed x196, local copies, waits for them, and re-layouts  63.9 us
    dynamic_update_slice x20, local copies, waits for them, and re-layouts, gather_weight(): full = lax.dynamic_update_slice(full, part[None], (chip ^ step, row, 0))  51.5 us
  transfers between devices with their start and end apart: 71, of which 26 were waited for; matrix products, arithmetic and copies ran while one was open for 44% of the time, Pallas kernels for 13%

profile of v3, /device:TPU:0, one launch (start us, length us, event | category | flops | bytes accessed | tf_op | source)
XLA Modules:
  0.0 1912.0 jit_solution(8323653093426622629)
XLA Ops:
  43.6 8.4 reshape_squeeze.31
  52.0 9.0 fusion.119
  61.0 8.4 reshape_squeeze.28
  69.4 8.0 fusion.120
  86.8 6.1 slice_bitcast_fusion.15
  130.6 47.2 %collective-permute-done.2 = bf16[384,1792]{1,0:T(8,128)(2,1)} collective-permute-done((bf16[384,1792]{1,0:T(8,128)(2,1)}, bf16[384,1792]{1,0:T(8,128)(2,1)}, u32[]{:S(2)}, u32[]{:S(2)}) %collective-permute-start.2) | collective-permute-done | bytes 1376288 | tf_op jit(solution)/shard_map/ppermute | solution.py:58
  187.1 24.6 %collective-permute-done.4 = bf16[192,1792]{1,0:T(8,128)(2,1)S(1)} collective-permute-done((bf16[192,1792]{1,0:T(8,128)(2,1)S(1)}, bf16[192,1792]{1,0:T(8,128)(2,1)S(1)}, u32[]{:S(2)}, u32[]{:S(2)}) %collective-permute-start.4) | collective-permute-done | bytes 688160 | tf_op jit(solution)/shard_map/ppermute | solution.py:58
  215.6 11.6 fusion.65.qkv_ref
  227.3 17.4 shard_map.143
  252.7 6.2 fusion.91
  274.8 57.3 %collective-permute-done.9 = bf16[384,4480]{1,0:T(8,128)(2,1)} collective-permute-done((bf16[384,4480]{1,0:T(8,128)(2,1)}, bf16[384,4480]{1,0:T(8,128)(2,1)}, u32[]{:S(2)}, u32[]{:S(2)}) %collective-permute-start.9) | collective-permute-done | bytes 3440672 | tf_op jit(solution)/shard_map/ppermute | solution.py:58
  347.4 5.9 fusion.31
  355.6 13.9 collective-permute-done.15
  375.0 30.7 %collective-permute-done.11 = bf16[192,4480]{1,0:T(8,128)(2,1)} collective-permute-done((bf16[192,4480]{1,0:T(8,128)(2,1)}, bf16[192,4480]{1,0:T(8,128)(2,1)}, u32[]{:S(2)}, u32[]{:S(2)}) %collective-permute-start.11) | collective-permute-done | bytes 1720352 | tf_op jit(solution)/shard_map/ppermute | solution.py:58
  413.0 51.4 %multiply_add_fusion.2 = (f32[2048,4480]{1,0:T(8,128)}, bf16[2048,4480]{1,0:T(8,128)(2,1)}) fusion(bf16[1536,4480]{1,0:T(8,128)(2,1)} %bitcast.198, bf16[1024,1536]{1,0:T(8,128)(2,1)} %copy-done.81, bf16[1024,1536]{1,0:T(8,128)(2,1)S(1)} %fusion.32), kind=kOutput, calls=%fused_computation.6 | convolution fusion | flops 28326756352 | bytes 75104256 | tf_op jit(solution)/shard_map/dot_general | solution.py:38
  464.4 21.7 %fusion.16 = f32[1024,1536]{1,0:T(8,128)} fusion(bf16[4480,1536]{1,0:T(8,128)(2,1)} %bitcast.206, bf16[2048,4480]{1,0:T(8,128)(2,1)} %get-tuple-element.34), kind=kOutput, calls=%fused_computation.40 | convolution fusion | flops 14092861440 | bytes 29229056 | tf_op jit(solution)/shard_map/dot_general | solution.py:38
  487.0 10.5 collective-permute-done.19
  501.8 21.8 %fusion.18 = f32[1024,1536]{1,0:T(8,128)} fusion(bf16[4480,1536]{1,0:T(8,128)(2,1)} %bitcast.207, bf16[2048,4480]{1,0:T(8,128)(2,1)} %get-tuple-element.34), kind=kOutput, calls=%fused_computation.42 | convolution fusion | flops 14092861440 | bytes 29229056 | tf_op jit(solution)/shard_map/dot_general | solution.py:38
  523.6 6.0 fusion.35
  536.0 24.5 %collective-permute-done.20 = bf16[384,1792]{1,0:T(8,128)(2,1)} collective-permute-done((bf16[384,1792]{1,0:T(8,128)(2,1)}, bf16[384,1792]{1,0:T(8,128)(2,1)}, u32[]{:S(2)}, u32[]{:S(2)}) %collective-permute-start.20) | collective-permute-done | bytes 1376288 | tf_op jit(solution)/shard_map/ppermute | solution.py:58
  570.3 23.3 %collective-permute-done.22 = bf16[192,1792]{1,0:T(8,128)(2,1)S(1)} collective-permute-done((bf16[192,1792]{1,0:T(8,128)(2,1)S(1)}, bf16[192,1792]{1,0:T(8,128)(2,1)S(1)}, u32[]{:S(2)}, u32[]{:S(2)}) %collective-permute-start.22) | collective-permute-done | bytes 688160 | tf_op jit(solution)/shard_map/ppermute | solution.py:58
  598.0 11.6 fusion.66.qkv_ref
  609.7 17.1 shard_map.144
  631.7 6.4 fusion.86
  642.0 5.8 fusion.28
  666.0 141.8 %collective-permute-done.27 = bf16[384,4480]{1,0:T(8,128)(2,1)} collective-permute-done((bf16[384,4480]{1,0:T(8,128)(2,1)}, bf16[384,4480]{1,0:T(8,128)(2,1)}, u32[]{:S(2)}, u32[]{:S(2)}) %collective-permute-start.27) | collective-permute-done | bytes 3440672 | tf_op jit(solution)/shard_map/ppermute | solution.py:58
  821.1 52.1 %collective-permute-done.29 = bf16[192,4480]{1,0:T(8,128)(2,1)S(1)} collective-permute-done((bf16[192,4480]{1,0:T(8,128)(2,1)S(1)}, bf16[192,4480]{1,0:T(8,128)(2,1)S(1)}, u32[]{:S(2)}, u32[]{:S(2)}) %collective-permute-start.29) | collective-permute-done | bytes 1720352 | tf_op jit(solution)/shard_map/ppermute | solution.py:58
  875.8 53.3 %multiply_add_fusion = (f32[2048,4480]{1,0:T(8,128)}, bf16[2048,4480]{1,0:T(8,128)(2,1)}) fusion(bf16[1536,4480]{1,0:T(8,128)(2,1)} %bitcast.202, bf16[1024,1536]{1,0:T(8,128)(2,1)} %collective-permute-done.25, bf16[1024,1536]{1,0:T(8,128)(2,1)S(1)} %copy-done.21), kind=kOutput, calls=%fused_computation.2 | convolution fusion | flops 28326756352 | bytes 75104256 | tf_op jit(solution)/shard_map/dot_general | solution.py:38
  929.1 41.7 %multiply_convert_fusion.1 = bf16[2048,4480]{1,0:T(8,128)(2,1)} fusion(f32[2048,4480]{1,0:T(8,128)} %get-tuple-element.36, bf16[1024,1536]{1,0:T(8,128)(2,1)} %collective-permute-done.32, bf16[1024,1536]{1,0:T(8,128)(2,1)} %bitcast.55, bf16[1,4480,1536]{2,1,0:T(8,128)(2,1)} %all-gather.15.cloned.1.call-done), kind=kOutput, calls=%fused_computation.1 | convolution fusion | flops 28216655872 | bytes 75104256 | tf_op jit(solution)/shard_map/dot_general | solution.py:38
  970.9 21.6 %fusion.8 = f32[1024,1536]{1,0:T(8,128)} fusion(bf16[1536,4480]{1,0:T(8,128)(2,1)} %bitcast.203, bf16[2048,4480]{1,0:T(8,128)(2,1)} %multiply_convert_fusion.1), kind=kOutput, calls=%fused_computation.32 | convolution fusion | flops 14092861440 | bytes 29229056 | tf_op jit(solution)/shard_map/dot_general | solution.py:38
  992.5 19.4 %fusion.10 = f32[1024,1536]{1,0:T(8,128)S(1)} fusion(bf16[1536,4480]{1,0:T(8,128)(2,1)} %bitcast.204, bf16[2048,4480]{1,0:T(8,128)(2,1)} %multiply_convert_fusion.1), kind=kOutput, calls=%fused_computation.34 | convolution fusion | flops 14092861440 | bytes 29229056 | tf_op jit(solution)/shard_map/dot_general | solution.py:38
  1022.3 6.8 fusion.59
  1029.2 9.3 fusion.67.d_o_ref
  1038.5 27.9 %shard_map.145 = bf16[2048,1024]{1,0:T(8,128)(2,1)} custom-call(bf16[2048,1024]{1,0:T(8,128)(2,1)} %fusion.66.qkv_ref, bf16[2048,768]{1,0:T(8,128)(2,1)} %fusion.67.d_o_ref), custom_call_target="tpu_custom_call" | custom-call | flops 40000000000 | tf_op jit(solution)/shard_map/pallas_call | solution.py:178
  1066.4 11.7 fusion.61
  1078.4 6.2 fusion.69
  1085.2 5.8 fusion.71
  1107.0 42.0 %multiply_convert_fusion = bf16[2048,4480]{1,0:T(8,128)(2,1)} fusion(f32[2048,4480]{1,0:T(8,128)} %get-tuple-element.42, bf16[4480,1536]{1,0:T(8,128)(2,1)} %bitcast.208, bf16[1024,1536]{1,0:T(8,128)(2,1)} %collective-permute-done.40, bf16[1024,1536]{1,0:T(8,128)(2,1)} %copy-done.10), kind=kOutput, calls=%fused_computation | convolution fusion | flops 28216655872 | bytes 75104256 | tf_op jit(solution)/shard_map/dot_general | solution.py:38
  1149.1 22.0 %fusion.4 = f32[1024,1536]{1,0:T(8,128)} fusion(bf16[1536,4480]{1,0:T(8,128)(2,1)} %bitcast.199, bf16[2048,4480]{1,0:T(8,128)(2,1)} %multiply_convert_fusion), kind=kOutput, calls=%fused_computation.28 | convolution fusion | flops 14092861440 | bytes 29229056 | tf_op jit(solution)/shard_map/dot_general | solution.py:38
  1171.1 21.6 %fusion.6 = f32[1024,1536]{1,0:T(8,128)} fusion(bf16[1536,4480]{1,0:T(8,128)(2,1)} %bitcast.200, bf16[2048,4480]{1,0:T(8,128)(2,1)} %multiply_convert_fusion), kind=kOutput, calls=%fused_computation.30 | convolution fusion | flops 14092861440 | bytes 29229056 | tf_op jit(solution)/shard_map/dot_general | solution.py:38
  1197.0 6.8 fusion.25
  1209.9 10.3 fusion.57
  1220.2 11.4 fusion.116
  1262.7 9.3 fusion.68.d_o_ref
  1272.1 28.3 %shard_map.146 = bf16[2048,1024]{1,0:T(8,128)(2,1)} custom-call(bf16[2048,1024]{1,0:T(8,128)(2,1)} %fusion.65.qkv_ref, bf16[2048,768]{1,0:T(8,128)(2,1)} %fusion.68.d_o_ref), custom_call_target="tpu_custom_call" | custom-call | flops 40000000000 | tf_op jit(solution)/shard_map/pallas_call | solution.py:178
  1300.4 11.9 fusion.63
  1312.4 141.4 %mlp_grads.2 = (f32[2,1120,1536]{2,1,0:T(8,128)}, f32[192,1120]{1,0:T(8,128)}, f32[192,1120]{1,0:T(8,128)}, f32[192,1120]{1,0:T(8,128)}, f32[192,1120]{1,0:T(8,1...) custom-call(s32[2]{0:T(128)} %pad_add_fusion.place_ref, ...), custom_call_target="tpu_custom_call" | custom-call | flops 112742891520 | tf_op jit(solution)/shard_map/mlp_grads/pallas_call | solution.py:271
  1454.3 8.6 fusion.74
  1463.0 11.5 fusion.117
  1505.0 12.9 collective-permute-done.56.refs_2_
  1517.9 17.9 collective-permute-done.57.refs_3_
  1543.6 33.4 %collective-permute-done.59.refs_5_ = f32[192,1120]{1,0:T(8,128)} collective-permute-done((f32[192,1120]{1,0:T(8,128)}, f32[192,1120]{1,0:T(8,128)}, u32[]{:S(2)}, u32[]{:S(2)}) %collective-permute-start.59) | collective-permute-done | bytes 860192 | tf_op jit(solution)/shard_map/ppermute | solution.py:294
  1579.4 8.6 fusion.76
  1588.0 11.1 collective-permute-done.61.refs_7_
  1600.0 8.1 assemble.2.refs_8_
  1618.5 8.6 fusion.27
  1635.8 140.9 %mlp_grads.3 = (f32[2,1120,1536]{2,1,0:T(8,128)}, f32[192,1120]{1,0:T(8,128)}, f32[192,1120]{1,0:T(8,128)}, f32[192,1120]{1,0:T(8,128)}, f32[192,1120]{1,0:T(8,1...) custom-call(s32[2]{0:T(128)} %pad_add_fusion.place_ref, ...), custom_call_target="tpu_custom_call", output_to_operand_aliasing={{0}: (7, {})} | custom-call | flops 112742891520 | tf_op jit(solution)/shard_map/mlp_grads/pallas_call | solution.py:271
  1776.7 21.9 %fusion.12 = f32[1024,1536]{1,0:T(8,128)} fusion(bf16[4480,1536]{1,0:T(8,128)(2,1)} %bitcast.237, bf16[2048,4480]{1,0:T(8,128)(2,1)} %get-tuple-element.40), kind=kOutput, calls=%fused_computation.36 | convolution fusion | flops 14092861440 | bytes 29229056 | tf_op jit(solution)/shard_map/dot_general | solution.py:38
  1811.9 10.0 collective-permute-done.49.refs_2_
  1824.3 15.5 collective-permute-done.50.refs_3_
  1842.8 21.6 %fusion.14 = f32[1024,1536]{1,0:T(8,128)} fusion(bf16[4480,1536]{1,0:T(8,128)(2,1)} %bitcast.238, bf16[2048,4480]{1,0:T(8,128)(2,1)} %get-tuple-element.40), kind=kOutput, calls=%fused_computation.38 | convolution fusion | flops 14092861440 | bytes 29229056 | tf_op jit(solution)/shard_map/dot_general | solution.py:38
  1864.4 22.3 %collective-permute-done.52.refs_5_ = f32[192,1120]{1,0:T(8,128)S(1)} collective-permute-done((f32[192,1120]{1,0:T(8,128)S(1)}, f32[192,1120]{1,0:T(8,128)S(1)}, u32[]{:S(2)}, u32[]{:S(2)}) %collective-permute-start.52) | collective-permute-done | bytes 860192 | tf_op jit(solution)/shard_map/ppermute | solution.py:294
  1888.8 8.1 assemble.3
  1896.9 8.3 add_convert_fusion
  (471 shorter events, 370.0 us)
Async XLA Ops:
  7.2 921.9 %all-gather.15.cloned.1.call-start = ((), (), s32[]{:S(2)}) async-start(), calls=%async_computation.12 | async-start | bytes 17203200 | tf_op jit(solution)/shard_map/all_gather | solution.py:104
  11.3 247.6 %collective-permute-start.13 = (bf16[1120,1536]{1,0:T(8,128)(2,1)}, bf16[1120,1536]{1,0:T(8,128)(2,1)}, u32[]{:S(2)}, u32[]{:S(2)}) collective-permute-start(bf16[1120,1536]{1,0:T(8,128)(2,1)} %slice_bitcast_fusion._.down_ref), channel_id=1, source_target_pairs={{0,2},{2,0},{4,6},{6,4},{1,3},{3,1},{5,7},{7,5}} | collective-permute-start | bytes 10321928 | tf_op jit(solution)/shard_map/ppermute | solution.py:58
  14.6 248.8 %collective-permute-start.14 = (bf16[1120,1536]{1,0:T(8,128)(2,1)}, bf16[1120,1536]{1,0:T(8,128)(2,1)}, u32[]{:S(2)}, u32[]{:S(2)}) collective-permute-start(bf16[1120,1536]{1,0:T(8,128)(2,1)} %slice_bitcast_fusion._.down_ref), channel_id=1, source_target_pairs={{0,4},{2,6},{4,0},{6,2},{1,5},{3,7},{5,1},{7,3}} | collective-permute-start | bytes 10321928 | tf_op jit(solution)/shard_map/ppermute | solution.py:58
  36.8 81.1 %collective-permute-start.1 = (bf16[192,1792]{1,0:T(8,128)(2,1)}, bf16[192,1792]{1,0:T(8,128)(2,1)}, u32[]{:S(2)}, u32[]{:S(2)}) collective-permute-start(bf16[192,1792]{1,0:T(8,128)(2,1)} %broadcast_select_fusion.14), channel_id=1, source_target_pairs={{0,1},{1,0},{2,3},{3,2},{4,5},{5,4},{6,7},{7,6}} | collective-permute-start | bytes 2064392 | tf_op jit(solution)/shard_map/ppermute | solution.py:54
  39.8 175.9 %collective-permute-start = (bf16[1024,1536]{1,0:T(8,128)(2,1)}, bf16[1024,1536]{1,0:T(8,128)(2,1)}, u32[]{:S(2)}, u32[]{:S(2)}) collective-permute-start(bf16[1024,1536]{1,0:T(8,128)(2,1)} %fusion.54), channel_id=1, source_target_pairs={{0,1},{1,0},{2,3},{3,2},{4,5},{5,4},{6,7},{7,6}} | collective-permute-start | bytes 9437192 | tf_op jit(solution)/shard_map/ppermute | solution.py:54
  86.8 37.6 %collective-permute-start.8 = (bf16[192,4480]{1,0:T(8,128)(2,1)}, bf16[192,4480]{1,0:T(8,128)(2,1)}, u32[]{:S(2)}, u32[]{:S(2)}) collective-permute-start(bf16[192,4480]{1,0:T(8,128)(2,1)} %select_n.229), channel_id=1, source_target_pairs={{0,1},{1,0},{2,3},{3,2},{4,5},{5,4},{6,7},{7,6}} | collective-permute-start | bytes 5160968 | tf_op jit(solution)/shard_map/ppermute | solution.py:54
  93.0 1112.0 %all-gather.13.cloned.1.call-start = ((), (), s32[]{:S(2)}) async-start(), calls=%async_computation.7 | async-start | bytes 15728640 | tf_op jit(solution)/shard_map/all_gather | solution.py:104
  121.6 56.2 %collective-permute-start.2 = (bf16[384,1792]{1,0:T(8,128)(2,1)}, bf16[384,1792]{1,0:T(8,128)(2,1)}, u32[]{:S(2)}, u32[]{:S(2)}) collective-permute-start(bf16[384,1792]{1,0:T(8,128)(2,1)} %pad_maximum_fusion.24._), channel_id=1, source_target_pairs={{0,2},{2,0},{4,6},{6,4},{1,3},{3,1},{5,7},{7,5}} | collective-permute-start | bytes 4128776 | tf_op jit(solution)/shard_map/ppermute | solution.py:58
  124.4 55.9 %collective-permute-start.3 = (bf16[384,1792]{1,0:T(8,128)(2,1)}, bf16[384,1792]{1,0:T(8,128)(2,1)}, u32[]{:S(2)}, u32[]{:S(2)}) collective-permute-start(bf16[384,1792]{1,0:T(8,128)(2,1)} %pad_maximum_fusion.24._), channel_id=1, source_target_pairs={{0,4},{2,6},{4,0},{6,2},{1,5},{3,7},{5,1},{7,3}} | collective-permute-start | bytes 4128776 | tf_op jit(solution)/shard_map/ppermute | solution.py:58
  178.9 32.7 %collective-permute-start.4 = (bf16[192,1792]{1,0:T(8,128)(2,1)S(1)}, bf16[192,1792]{1,0:T(8,128)(2,1)S(1)}, u32[]{:S(2)}, u32[]{:S(2)}) collective-permute-start(bf16[192,1792]{1,0:T(8,128)(2,1)S(1)} %slice.350), channel_id=1, source_target_pairs={{0,4},{2,6},{4,0},{6,2},{1,5},{3,7},{5,1},{7,3}} | collective-permute-start | bytes 2064392 | tf_op jit(solution)/shard_map/ppermute | solution.py:58
  181.5 32.9 %collective-permute-start.5 = (bf16[192,1792]{1,0:T(8,128)(2,1)S(1)}, bf16[192,1792]{1,0:T(8,128)(2,1)S(1)}, u32[]{:S(2)}, u32[]{:S(2)}) collective-permute-start(bf16[192,1792]{1,0:T(8,128)(2,1)S(1)} %slice.351), channel_id=1, source_target_pairs={{0,2},{2,0},{4,6},{6,4},{1,3},{3,1},{5,7},{7,5}} | collective-permute-start | bytes 2064392 | tf_op jit(solution)/shard_map/ppermute | solution.py:58
  211.6 120.4 %collective-permute-start.9 = (bf16[384,4480]{1,0:T(8,128)(2,1)}, bf16[384,4480]{1,0:T(8,128)(2,1)}, u32[]{:S(2)}, u32[]{:S(2)}) collective-permute-start(bf16[384,4480]{1,0:T(8,128)(2,1)} %pad_maximum_fusion.16._), channel_id=1, source_target_pairs={{0,2},{2,0},{4,6},{6,4},{1,3},{3,1},{5,7},{7,5}} | collective-permute-start | bytes 10321928 | tf_op jit(solution)/shard_map/ppermute | solution.py:58
  214.4 121.8 %collective-permute-start.10 = (bf16[384,4480]{1,0:T(8,128)(2,1)}, bf16[384,4480]{1,0:T(8,128)(2,1)}, u32[]{:S(2)}, u32[]{:S(2)}) collective-permute-start(bf16[384,4480]{1,0:T(8,128)(2,1)} %pad_maximum_fusion.16._), channel_id=1, source_target_pairs={{0,4},{2,6},{4,0},{6,2},{1,5},{3,7},{5,1},{7,3}} | collective-permute-start | bytes 10321928 | tf_op jit(solution)/shard_map/ppermute | solution.py:58
  249.6 97.8 %collective-permute-start.6 = (f32[1024,1536]{1,0:T(8,128)S(1)}, f32[1024,1536]{1,0:T(8,128)}, u32[]{:S(2)}, u32[]{:S(2)}) collective-permute-start(f32[1024,1536]{1,0:T(8,128)S(1)} %fusion.89), channel_id=1, source_target_pairs={{0,1},{1,0},{2,3},{3,2},{4,5},{5,4},{6,7},{7,6}} | collective-permute-start | bytes 18874376 | tf_op jit(solution)/shard_map/ppermute | solution.py:54
  261.7 107.7 %collective-permute-start.15 = (bf16[560,1536]{1,0:T(8,128)(2,1)}, bf16[560,1536]{1,0:T(8,128)(2,1)}, u32[]{:S(2)}, u32[]{:S(2)}) collective-permute-start(bf16[560,1536]{1,0:T(8,128)(2,1)} %slice.360), channel_id=1, source_target_pairs={{0,4},{2,6},{4,0},{6,2},{1,5},{3,7},{5,1},{7,3}} | collective-permute-start | bytes 5160968 | tf_op jit(solution)/shard_map/ppermute | solution.py:58
  266.3 105.9 %collective-permute-start.16 = (bf16[560,1536]{1,0:T(8,128)(2,1)}, bf16[560,1536]{1,0:T(8,128)(2,1)}, u32[]{:S(2)}, u32[]{:S(2)}) collective-permute-start(bf16[560,1536]{1,0:T(8,128)(2,1)} %slice.361), channel_id=1, source_target_pairs={{0,2},{2,0},{4,6},{6,4},{1,3},{3,1},{5,7},{7,5}} | collective-permute-start | bytes 5160968 | tf_op jit(solution)/shard_map/ppermute | solution.py:58
  334.8 70.9 %collective-permute-start.11 = (bf16[192,4480]{1,0:T(8,128)(2,1)}, bf16[192,4480]{1,0:T(8,128)(2,1)}, u32[]{:S(2)}, u32[]{:S(2)}) collective-permute-start(bf16[192,4480]{1,0:T(8,128)(2,1)} %slice.358), channel_id=1, source_target_pairs={{0,4},{2,6},{4,0},{6,2},{1,5},{3,7},{5,1},{7,3}} | collective-permute-start | bytes 5160968 | tf_op jit(solution)/shard_map/ppermute | solution.py:58
  339.0 69.5 %collective-permute-start.12 = (bf16[192,4480]{1,0:T(8,128)(2,1)}, bf16[192,4480]{1,0:T(8,128)(2,1)}, u32[]{:S(2)}, u32[]{:S(2)}) collective-permute-start(bf16[192,4480]{1,0:T(8,128)(2,1)} %slice.359), channel_id=1, source_target_pairs={{0,2},{2,0},{4,6},{6,4},{1,3},{3,1},{5,7},{7,5}} | collective-permute-start | bytes 5160968 | tf_op jit(solution)/shard_map/ppermute | solution.py:58
  355.5 55.8 %collective-permute-start.7 = (bf16[1024,1536]{1,0:T(8,128)(2,1)S(1)}, bf16[1024,1536]{1,0:T(8,128)(2,1)S(1)}, u32[]{:S(2)}, u32[]{:S(2)}) collective-permute-start(bf16[1024,1536]{1,0:T(8,128)(2,1)S(1)} %fusion.32), channel_id=1, source_target_pairs={{0,1},{1,0},{2,3},{3,2},{4,5},{5,4},{6,7},{7,6}} | collective-permute-start | bytes 9437192 | tf_op jit(solution)/shard_map/ppermute | solution.py:54
  486.1 37.5 %collective-permute-start.17 = (f32[1024,1536]{1,0:T(8,128)}, f32[1024,1536]{1,0:T(8,128)}, u32[]{:S(2)}, u32[]{:S(2)}) collective-permute-start(f32[1024,1536]{1,0:T(8,128)} %fusion.16), channel_id=1, source_target_pairs={{0,1},{1,0},{2,3},{3,2},{4,5},{5,4},{6,7},{7,6}} | collective-permute-start | bytes 18874376 | tf_op jit(solution)/shard_map/ppermute | solution.py:54
  486.9 718.1 %all-gather.11.cloned.1.call-start = ((), (), s32[]{:S(2)}) async-start(), calls=%async_computation.6 | async-start | bytes 15728640 | tf_op jit(solution)/shard_map/all_gather | solution.py:104
  499.8 60.7 %collective-permute-start.20 = (bf16[384,1792]{1,0:T(8,128)(2,1)}, bf16[384,1792]{1,0:T(8,128)(2,1)}, u32[]{:S(2)}, u32[]{:S(2)}) collective-permute-start(bf16[384,1792]{1,0:T(8,128)(2,1)} %pad_maximum_fusion.25._), channel_id=1, source_target_pairs={{0,2},{2,0},{4,6},{6,4},{1,3},{3,1},{5,7},{7,5}} | collective-permute-start | bytes 4128776 | tf_op jit(solution)/shard_map/ppermute | solution.py:58
  501.3 61.9 %collective-permute-start.21 = (bf16[384,1792]{1,0:T(8,128)(2,1)}, bf16[384,1792]{1,0:T(8,128)(2,1)}, u32[]{:S(2)}, u32[]{:S(2)}) collective-permute-start(bf16[384,1792]{1,0:T(8,128)(2,1)} %pad_maximum_fusion.25._), channel_id=1, source_target_pairs={{0,4},{2,6},{4,0},{6,2},{1,5},{3,7},{5,1},{7,3}} | collective-permute-start | bytes 4128776 | tf_op jit(solution)/shard_map/ppermute | solution.py:58
  533.5 64.6 %collective-permute-start.18 = (bf16[1024,1536]{1,0:T(8,128)(2,1)}, bf16[1024,1536]{1,0:T(8,128)(2,1)}, u32[]{:S(2)}, u32[]{:S(2)}) collective-permute-start(bf16[1024,1536]{1,0:T(8,128)(2,1)} %fusion.36), channel_id=1, source_target_pairs={{0,1},{1,0},{2,3},{3,2},{4,5},{5,4},{6,7},{7,6}} | collective-permute-start | bytes 9437192 | tf_op jit(solution)/shard_map/ppermute | solution.py:54
  561.7 31.9 %collective-permute-start.22 = (bf16[192,1792]{1,0:T(8,128)(2,1)S(1)}, bf16[192,1792]{1,0:T(8,128)(2,1)S(1)}, u32[]{:S(2)}, u32[]{:S(2)}) collective-permute-start(bf16[192,1792]{1,0:T(8,128)(2,1)S(1)} %slice.370), channel_id=1, source_target_pairs={{0,4},{2,6},{4,0},{6,2},{1,5},{3,7},{5,1},{7,3}} | collective-permute-start | bytes 2064392 | tf_op jit(solution)/shard_map/ppermute | solution.py:58
  564.5 32.6 %collective-permute-start.23 = (bf16[192,1792]{1,0:T(8,128)(2,1)S(1)}, bf16[192,1792]{1,0:T(8,128)(2,1)S(1)}, u32[]{:S(2)}, u32[]{:S(2)}) collective-permute-start(bf16[192,1792]{1,0:T(8,128)(2,1)S(1)} %slice.371), channel_id=1, source_target_pairs={{0,2},{2,0},{4,6},{6,4},{1,3},{3,1},{5,7},{7,5}} | collective-permute-start | bytes 2064392 | tf_op jit(solution)/shard_map/ppermute | solution.py:58
  651.7 606.1 %all-gather.7.cloned.1.call-start = ((), (), s32[]{:S(2)}) async-start(), calls=%async_computation.4 | async-start | bytes 15728640 | tf_op jit(solution)/shard_map/all_gather | solution.py:104
  662.9 144.9 %collective-permute-start.27 = (bf16[384,4480]{1,0:T(8,128)(2,1)}, bf16[384,4480]{1,0:T(8,128)(2,1)}, u32[]{:S(2)}, u32[]{:S(2)}) collective-permute-start(bf16[384,4480]{1,0:T(8,128)(2,1)} %pad_maximum_fusion.17._), channel_id=1, source_target_pairs={{0,2},{2,0},{4,6},{6,4},{1,3},{3,1},{5,7},{7,5}} | collective-permute-start | bytes 10321928 | tf_op jit(solution)/shard_map/ppermute | solution.py:58
  663.7 147.3 %collective-permute-start.28 = (bf16[384,4480]{1,0:T(8,128)(2,1)}, bf16[384,4480]{1,0:T(8,128)(2,1)}, u32[]{:S(2)}, u32[]{:S(2)}) collective-permute-start(bf16[384,4480]{1,0:T(8,128)(2,1)} %pad_maximum_fusion.17._), channel_id=1, source_target_pairs={{0,4},{2,6},{4,0},{6,2},{1,5},{3,7},{5,1},{7,3}} | collective-permute-start | bytes 10321928 | tf_op jit(solution)/shard_map/ppermute | solution.py:58
  664.0 265.1 %collective-permute-start.32 = (bf16[1024,1536]{1,0:T(8,128)(2,1)}, bf16[1024,1536]{1,0:T(8,128)(2,1)}, u32[]{:S(2)}, u32[]{:S(2)}) collective-permute-start(bf16[1024,1536]{1,0:T(8,128)(2,1)} %bitcast.55), channel_id=1, source_target_pairs={{0,1},{1,0},{2,3},{3,2},{4,5},{5,4},{6,7},{7,6}} | collective-permute-start | bytes 9437192 | tf_op jit(solution)/shard_map/ppermute | solution.py:54
  809.4 63.7 %collective-permute-start.29 = (bf16[192,4480]{1,0:T(8,128)(2,1)S(1)}, bf16[192,4480]{1,0:T(8,128)(2,1)S(1)}, u32[]{:S(2)}, u32[]{:S(2)}) collective-permute-start(bf16[192,4480]{1,0:T(8,128)(2,1)S(1)} %slice.378), channel_id=1, source_target_pairs={{0,4},{2,6},{4,0},{6,2},{1,5},{3,7},{5,1},{7,3}} | collective-permute-start | bytes 5160968 | tf_op jit(solution)/shard_map/ppermute | solution.py:58
  812.5 61.9 %collective-permute-start.30 = (bf16[192,4480]{1,0:T(8,128)(2,1)S(1)}, bf16[192,4480]{1,0:T(8,128)(2,1)S(1)}, u32[]{:S(2)}, u32[]{:S(2)}) collective-permute-start(bf16[192,4480]{1,0:T(8,128)(2,1)S(1)} %slice.379), channel_id=1, source_target_pairs={{0,2},{2,0},{4,6},{6,4},{1,3},{3,1},{5,7},{7,5}} | collective-permute-start | bytes 5160968 | tf_op jit(solution)/shard_map/ppermute | solution.py:58
  817.1 58.7 %collective-permute-start.25 = (bf16[1024,1536]{1,0:T(8,128)(2,1)S(1)}, bf16[1024,1536]{1,0:T(8,128)(2,1)}, u32[]{:S(2)}, u32[]{:S(2)}) collective-permute-start(bf16[1024,1536]{1,0:T(8,128)(2,1)S(1)} %copy-done.21), channel_id=1, source_target_pairs={{0,1},{1,0},{2,3},{3,2},{4,5},{5,4},{6,7},{7,6}} | collective-permute-start | bytes 9437192 | tf_op jit(solution)/shard_map/ppermute | solution.py:54
  875.8 382.4 %reduce-scatter.11.cloned.1.call-start = ((), (), s32[]{:S(2)}) async-start(), calls=%async_computation.11 | async-start | bytes 5898240 | tf_op jit(solution)/shard_map/reduce_scatter | solution.py:113
  992.5 19.5 %collective-permute-start.33 = (f32[1024,1536]{1,0:T(8,128)}, f32[1024,1536]{1,0:T(8,128)S(1)}, u32[]{:S(2)}, u32[]{:S(2)}) collective-permute-start(f32[1024,1536]{1,0:T(8,128)} %fusion.8), channel_id=1, source_target_pairs={{0,1},{1,0},{2,3},{3,2},{4,5},{5,4},{6,7},{7,6}} | collective-permute-start | bytes 18874376 | tf_op jit(solution)/shard_map/ppermute | solution.py:54
  1029.2 231.1 %reduce-scatter.7.cloned.1.call-start = ((), (), s32[]{:S(2)}) async-start(), calls=%async_computation.9 | async-start | bytes 7864320 | tf_op jit(solution)/shard_map/reduce_scatter | solution.py:113
  1078.1 234.3 %all-gather.9.cloned.1.call-start = ((), (), s32[]{:S(2)}) async-start(), calls=%async_computation.5 | async-start | bytes 15728640 | tf_op jit(solution)/shard_map/all_gather | solution.py:104
  1102.5 511.2 %reduce-scatter.9.cloned.1.call-start = ((), (), s32[]{:S(2)}) async-start(), calls=%async_computation.10 | async-start | bytes 5898240 | tf_op jit(solution)/shard_map/reduce_scatter | solution.py:113
  1171.1 21.7 %collective-permute-start.41 = (f32[1024,1536]{1,0:T(8,128)}, f32[1024,1536]{1,0:T(8,128)S(1)}, u32[]{:S(2)}, u32[]{:S(2)}) collective-permute-start(f32[1024,1536]{1,0:T(8,128)} %fusion.4), channel_id=1, source_target_pairs={{0,1},{1,0},{2,3},{3,2},{4,5},{5,4},{6,7},{7,6}} | collective-permute-start | bytes 18874376 | tf_op jit(solution)/shard_map/ppermute | solution.py:54
  1205.0 107.4 %collective-permute-start.38 = (bf16[4096,1536]{1,0:T(8,128)(2,1)}, bf16[4096,1536]{1,0:T(8,128)(2,1)}, u32[]{:S(2)}, u32[]{:S(2)}) collective-permute-start(bf16[4096,1536]{1,0:T(8,128)(2,1)} %all-gather.13.cloned.1.call-done.g0_ref), channel_id=1, source_target_pairs={{0,1},{1,0},{2,3},{3,2},{4,5},{5,4},{6,7},{7,6}} | collective-permute-start | bytes 37748744 | tf_op jit(solution)/shard_map/ppermute | solution.py:54
  1205.0 107.5 %collective-permute-start.37 = (bf16[4096,1536]{1,0:T(8,128)(2,1)}, bf16[4096,1536]{1,0:T(8,128)(2,1)}, u32[]{:S(2)}, u32[]{:S(2)}) collective-permute-start(bf16[4096,1536]{1,0:T(8,128)(2,1)} %all-gather.11.cloned.1.call-done.n0_ref), channel_id=1, source_target_pairs={{0,1},{1,0},{2,3},{3,2},{4,5},{5,4},{6,7},{7,6}} | collective-permute-start | bytes 37748744 | tf_op jit(solution)/shard_map/ppermute | solution.py:54
  1220.2 396.3 %reduce-scatter.5.cloned.1.call-start = ((), (), s32[]{:S(2)}) async-start(), calls=%async_computation.8 | async-start | bytes 7864320 | tf_op jit(solution)/shard_map/reduce_scatter | solution.py:113
  1257.8 378.0 %collective-permute-start.31 = (bf16[4096,1536]{1,0:T(8,128)(2,1)}, bf16[4096,1536]{1,0:T(8,128)(2,1)}, u32[]{:S(2)}, u32[]{:S(2)}) collective-permute-start(bf16[4096,1536]{1,0:T(8,128)(2,1)} %all-gather.7.cloned.1.call-done.n0_ref), channel_id=1, source_target_pairs={{0,1},{1,0},{2,3},{3,2},{4,5},{5,4},{6,7},{7,6}} | collective-permute-start | bytes 37748744 | tf_op jit(solution)/shard_map/ppermute | solution.py:54
  1260.1 202.7 %collective-permute-start.47 = (f32[192,768]{1,0:T(8,128)}, f32[192,768]{1,0:T(8,128)}, u32[]{:S(2)}, u32[]{:S(2)}) collective-permute-start(f32[192,768]{1,0:T(8,128)} %dynamic-slice_bitcast_fusion.2), channel_id=1, source_target_pairs={{0,1},{1,0},{2,3},{3,2},{4,5},{5,4},{6,7},{7,6}} | collective-permute-start | bytes 1769480 | tf_op jit(solution)/shard_map/ppermute | solution.py:54
  1262.4 232.8 %collective-permute-start.45 = (f32[192,1024]{1,0:T(8,128)}, f32[192,1024]{1,0:T(8,128)}, u32[]{:S(2)}, u32[]{:S(2)}) collective-permute-start(f32[192,1024]{1,0:T(8,128)} %dynamic-slice_bitcast_fusion), channel_id=1, source_target_pairs={{0,1},{1,0},{2,3},{3,2},{4,5},{5,4},{6,7},{7,6}} | collective-permute-start | bytes 2359304 | tf_op jit(solution)/shard_map/ppermute | solution.py:54
  1312.4 323.4 %collective-permute-start.36 = (bf16[4096,1536]{1,0:T(8,128)(2,1)}, bf16[4096,1536]{1,0:T(8,128)(2,1)}, u32[]{:S(2)}, u32[]{:S(2)}) collective-permute-start(bf16[4096,1536]{1,0:T(8,128)(2,1)} %all-gather.9.cloned.1.call-done.g0_ref), channel_id=1, source_target_pairs={{0,1},{1,0},{2,3},{3,2},{4,5},{5,4},{6,7},{7,6}} | collective-permute-start | bytes 37748744 | tf_op jit(solution)/shard_map/ppermute | solution.py:54
  1453.8 42.4 %collective-permute-start.55 = (f32[192,1120]{1,0:T(8,128)}, f32[192,1120]{1,0:T(8,128)}, u32[]{:S(2)}, u32[]{:S(2)}) collective-permute-start(f32[192,1120]{1,0:T(8,128)} %get-tuple-element.52), channel_id=1, source_target_pairs={{0,1},{1,0},{2,3},{3,2},{4,5},{5,4},{6,7},{7,6}} | collective-permute-start | bytes 2580488 | tf_op jit(solution)/shard_map/ppermute | solution.py:294
  1462.9 145.3 %collective-permute-start.43 = (f32[1024,1536]{1,0:T(8,128)}, f32[1024,1536]{1,0:T(8,128)}, u32[]{:S(2)}, u32[]{:S(2)}) collective-permute-start(f32[1024,1536]{1,0:T(8,128)} %fusion.74), channel_id=1, source_target_pairs={{0,1},{1,0},{2,3},{3,2},{4,5},{5,4},{6,7},{7,6}} | collective-permute-start | bytes 18874376 | tf_op jit(solution)/shard_map/ppermute | solution.py:54
  1495.2 22.7 %collective-permute-start.56 = (f32[192,1120]{1,0:T(8,128)}, f32[192,1120]{1,0:T(8,128)S(1)}, u32[]{:S(2)}, u32[]{:S(2)}) collective-permute-start(f32[192,1120]{1,0:T(8,128)} %get-tuple-element.53), channel_id=1, source_target_pairs={{0,2},{1,3},{2,0},{3,1},{4,6},{5,7},{6,4},{7,5}} | collective-permute-start | bytes 2580488 | tf_op jit(solution)/shard_map/ppermute | solution.py:294
  1496.2 39.6 %collective-permute-start.57 = (f32[192,1120]{1,0:T(8,128)}, f32[192,1120]{1,0:T(8,128)S(1)}, u32[]{:S(2)}, u32[]{:S(2)}) collective-permute-start(f32[192,1120]{1,0:T(8,128)} %get-tuple-element.54), channel_id=1, source_target_pairs={{0,3},{1,2},{2,1},{3,0},{4,7},{5,6},{6,5},{7,4}} | collective-permute-start | bytes 2580488 | tf_op jit(solution)/shard_map/ppermute | solution.py:294
  1517.9 22.8 %collective-permute-start.58 = (f32[192,1120]{1,0:T(8,128)}, f32[192,1120]{1,0:T(8,128)}, u32[]{:S(2)}, u32[]{:S(2)}) collective-permute-start(f32[192,1120]{1,0:T(8,128)} %get-tuple-element.55), channel_id=1, source_target_pairs={{0,4},{1,5},{2,6},{3,7},{4,0},{5,1},{6,2},{7,3}} | collective-permute-start | bytes 2580488 | tf_op jit(solution)/shard_map/ppermute | solution.py:294
  1536.7 40.3 %collective-permute-start.59 = (f32[192,1120]{1,0:T(8,128)}, f32[192,1120]{1,0:T(8,128)}, u32[]{:S(2)}, u32[]{:S(2)}) collective-permute-start(f32[192,1120]{1,0:T(8,128)} %get-tuple-element.56), channel_id=1, source_target_pairs={{0,5},{1,4},{2,7},{3,6},{4,1},{5,0},{6,3},{7,2}} | collective-permute-start | bytes 2580488 | tf_op jit(solution)/shard_map/ppermute | solution.py:294
  1540.8 47.2 %collective-permute-start.60 = (f32[192,1120]{1,0:T(8,128)}, f32[192,1120]{1,0:T(8,128)S(1)}, u32[]{:S(2)}, u32[]{:S(2)}) collective-permute-start(f32[192,1120]{1,0:T(8,128)} %get-tuple-element.57), channel_id=1, source_target_pairs={{0,6},{1,7},{2,4},{3,5},{4,2},{5,3},{6,0},{7,1}} | collective-permute-start | bytes 2580488 | tf_op jit(solution)/shard_map/ppermute | solution.py:294
  1577.0 22.1 %collective-permute-start.61 = (f32[192,1120]{1,0:T(8,128)}, f32[192,1120]{1,0:T(8,128)S(1)}, u32[]{:S(2)}, u32[]{:S(2)}) collective-permute-start(f32[192,1120]{1,0:T(8,128)} %get-tuple-element.58), channel_id=1, source_target_pairs={{0,7},{1,6},{2,5},{3,4},{4,3},{5,2},{6,1},{7,0}} | collective-permute-start | bytes 2580488 | tf_op jit(solution)/shard_map/ppermute | solution.py:294
  1615.7 11.4 collective-permute-start.46
  1618.5 14.8 collective-permute-start.44
  1798.5 98.4 %collective-permute-start.39 = (f32[1024,1536]{1,0:T(8,128)}, f32[1024,1536]{1,0:T(8,128)}, u32[]{:S(2)}, u32[]{:S(2)}) collective-permute-start(f32[1024,1536]{1,0:T(8,128)} %fusion.12), channel_id=1, source_target_pairs={{0,1},{1,0},{2,3},{3,2},{4,5},{5,4},{6,7},{7,6}} | collective-permute-start | bytes 18874376 | tf_op jit(solution)/shard_map/ppermute | solution.py:54
  1799.0 11.3 collective-permute-start.48
  1799.1 22.8 %collective-permute-start.49 = (f32[192,1120]{1,0:T(8,128)}, f32[192,1120]{1,0:T(8,128)}, u32[]{:S(2)}, u32[]{:S(2)}) collective-permute-start(f32[192,1120]{1,0:T(8,128)} %get-tuple-element.45), channel_id=1, source_target_pairs={{0,2},{1,3},{2,0},{3,1},{4,6},{5,7},{6,4},{7,5}} | collective-permute-start | bytes 2580488 | tf_op jit(solution)/shard_map/ppermute | solution.py:294
  1800.2 39.6 %collective-permute-start.50 = (f32[192,1120]{1,0:T(8,128)}, f32[192,1120]{1,0:T(8,128)}, u32[]{:S(2)}, u32[]{:S(2)}) collective-permute-start(f32[192,1120]{1,0:T(8,128)} %get-tuple-element.46), channel_id=1, source_target_pairs={{0,3},{1,2},{2,1},{3,0},{4,7},{5,6},{6,5},{7,4}} | collective-permute-start | bytes 2580488 | tf_op jit(solution)/shard_map/ppermute | solution.py:294
  1808.2 56.3 %collective-permute-start.51 = (f32[192,1120]{1,0:T(8,128)S(1)}, f32[192,1120]{1,0:T(8,128)S(1)}, u32[]{:S(2)}, u32[]{:S(2)}) collective-permute-start(f32[192,1120]{1,0:T(8,128)S(1)} %copy-done.85), channel_id=1, source_target_pairs={{0,4},{1,5},{2,6},{3,7},{4,0},{5,1},{6,2},{7,3}} | collective-permute-start | bytes 2580488 | tf_op jit(solution)/shard_map/ppermute | solution.py:294
  1810.3 76.4 %collective-permute-start.52 = (f32[192,1120]{1,0:T(8,128)S(1)}, f32[192,1120]{1,0:T(8,128)S(1)}, u32[]{:S(2)}, u32[]{:S(2)}) collective-permute-start(f32[192,1120]{1,0:T(8,128)S(1)} %copy-done.84), channel_id=1, source_target_pairs={{0,5},{1,4},{2,7},{3,6},{4,1},{5,0},{6,3},{7,2}} | collective-permute-start | bytes 2580488 | tf_op jit(solution)/shard_map/ppermute | solution.py:294
  1822.0 64.7 %collective-permute-start.53 = (f32[192,1120]{1,0:T(8,128)S(1)}, f32[192,1120]{1,0:T(8,128)S(1)}, u32[]{:S(2)}, u32[]{:S(2)}) collective-permute-start(f32[192,1120]{1,0:T(8,128)S(1)} %copy-done.83), channel_id=1, source_target_pairs={{0,6},{1,7},{2,4},{3,5},{4,2},{5,3},{6,0},{7,1}} | collective-permute-start | bytes 2580488 | tf_op jit(solution)/shard_map/ppermute | solution.py:294
  1839.7 46.9 %collective-permute-start.54 = (f32[192,1120]{1,0:T(8,128)S(1)}, f32[192,1120]{1,0:T(8,128)S(1)}, u32[]{:S(2)}, u32[]{:S(2)}) collective-permute-start(f32[192,1120]{1,0:T(8,128)S(1)} %copy-done.82), channel_id=1, source_target_pairs={{0,7},{1,6},{2,5},{3,4},{4,3},{5,2},{6,1},{7,0}} | collective-permute-start | bytes 2580488 | tf_op jit(solution)/shard_map/ppermute | solution.py:294
  (99 other events, 948.3 us)
Sparse Core Ops, SparseCore 0:
  93.1 208.2 all-gather.14
  487.0 160.3 all-gather.12
  651.8 208.8 all-gather.10
  875.9 116.8 all-gather.6
  1029.3 51.3 reduce-scatter.10
  1083.5 64.4 reduce-scatter.6
  1149.8 116.8 all-gather.8
  1269.6 51.3 reduce-scatter.8
  1323.9 64.4 reduce-scatter.4

commit v4 on v3

--- a/solution.py
+++ b/solution.py
@@ -18,6 +18,7 @@
 QUERY_BLOCK = 256
 TOKEN_TILE = 512
 ROW_TILE = 48
+FLIP_TILE = 256
 NEIGHBOURS = (1, 2)
 
 
@@ -100,12 +101,14 @@
     return full.reshape(-1, piece.shape[1])
 
 
-def gather(value):
-    return functools.partial(lax.all_gather, axis=0, tiled=True)(value, CHIP)
-
-
-def gather_rows(value):
-    mine = gather(value)
+def gather(value, axes):
+    return functools.partial(lax.all_gather, axis=0, tiled=True)(value, axes)
+
+
+def gather_rows(value, swapped):
+    if not swapped:
+        return (gather(value, AXES),)
+    mine = gather(value, CHIP)
     return mine, swap(mine)
 
 
@@ -231,11 +234,14 @@
     return (grad_own.astype(jnp.float32) + norm_back(x_own, d_norm)).astype(jnp.bfloat16)
 
 
-def mlp_grads_kernel(half, place_ref, up_ref, down_ref, n0_ref, n1_ref, g0_ref, g1_ref, *rest):
+def mlp_grads_kernel(steps, arrays, place_ref, up_ref, down_ref, *rest):
+    norms, grads = rest[:arrays], rest[arrays:2 * arrays]
     d_down_ref, parts, d_up_ref, flip_ref = rest[-2 * CHIPS - 3], rest[-2 * CHIPS - 2:-2], rest[-2], rest[-1]
     step = pl.program_id(0)
-    normed = jnp.where(step < half, n0_ref[...], n1_ref[...])
-    grad_y = jnp.where(step < half, g0_ref[...], g1_ref[...])
+    normed, grad_y = norms[0][...], grads[0][...]
+    if arrays > 1:
+        normed = jnp.where(step < steps, normed, norms[1][...])
+        grad_y = jnp.where(step < steps, grad_y, grads[1][...])
 
     @pl.when(step == 0)
     def _():
@@ -260,29 +266,29 @@
 
 def mlp_weight_grads(place, layer, pairs, earlier, up_flip, down_block, norms, grads):
     block, width = down_block.shape
-    half = norms[0].shape[0] // TOKEN_TILE
+    steps = norms[0].shape[0] // TOKEN_TILE
     rows = width // (CHIPS * CORES)
     once = pl.Buffered(1)
     whole = pl.BlockSpec((block, width), lambda i, p: (0, 0), pipeline_mode=once)
-    mine = pl.BlockSpec((TOKEN_TILE, width), lambda i, p: (jnp.minimum(i, half - 1), 0))
-    others = pl.BlockSpec((TOKEN_TILE, width), lambda i, p: (jnp.maximum(i - half, 0), 0))
+    tokens = [pl.BlockSpec((TOKEN_TILE, width), lambda i, p: (jnp.minimum(i, steps - 1), 0)),
+              pl.BlockSpec((TOKEN_TILE, width), lambda i, p: (jnp.maximum(i - steps, 0), 0))][:len(norms)]
     part = pl.BlockSpec((rows, block), lambda i, p: (0, 0), pipeline_mode=once)
-    args = [place, up_flip, down_block, norms[0], norms[1], grads[0], grads[1]] + earlier
+    args = [place, up_flip, down_block, *norms, *grads, *earlier]
     outs = pl.pallas_call(
-        functools.partial(mlp_grads_kernel, half),
+        functools.partial(mlp_grads_kernel, steps, len(norms)),
         grid_spec=pltpu.PrefetchScalarGridSpec(
             num_scalar_prefetch=1,
-            grid=(2 * half,),
-            in_specs=[whole, whole, mine, others, mine, others] + [pl.BlockSpec(memory_space=pl.ANY)] * len(earlier),
+            grid=(steps * len(norms),),
+            in_specs=[whole, whole] + tokens * 2 + [pl.BlockSpec(memory_space=pl.ANY)] * len(earlier),
             out_specs=[pl.BlockSpec((1, block, width), lambda i, p: (layer, 0, 0), pipeline_mode=once)]
             + [part] * (CHIPS * CORES),
             scratch_shapes=[pltpu.VMEM((block, width), jnp.float32), pltpu.VMEM((CORES * rows, block), jnp.float32)],
         ),
         out_shape=[jax.ShapeDtypeStruct((pairs, block, width), jnp.float32)]
         + [jax.ShapeDtypeStruct((rows, block), jnp.float32)] * (CHIPS * CORES),
-        input_output_aliases={7: 0} if earlier else {},
+        input_output_aliases={len(args) - 1: 0} if earlier else {},
         compiler_params=pltpu.CompilerParams(vmem_limit_bytes=60 * 1024 * 1024),
-        cost_estimate=pl.CostEstimate(flops=8 * 2 * norms[0].shape[0] * block * width, bytes_accessed=0,
+        cost_estimate=pl.CostEstimate(flops=8 * len(norms) * norms[0].shape[0] * block * width, bytes_accessed=0,
                                       transcendentals=0),
         name="mlp_grads",
     )(*args)
@@ -322,6 +328,30 @@
     )(place, *parts, *earlier)
 
 
+def flip_kernel(place_ref, up_ref, out_ref):
+    block = out_ref.shape[0]
+    cols = up_ref[:, :block]
+    for i in range(1, CHIPS):
+        cols = jnp.where(place_ref[0] == i, up_ref[:, i * block:(i + 1) * block], cols)
+    out_ref[...] = jnp.transpose(cols.astype(jnp.float32)).astype(jnp.bfloat16)
+
+
+def flip(place, up_weight):
+    width, cols = up_weight.shape
+    return pl.pallas_call(
+        flip_kernel,
+        grid_spec=pltpu.PrefetchScalarGridSpec(
+            num_scalar_prefetch=1,
+            grid=(width // FLIP_TILE,),
+            in_specs=[pl.BlockSpec((FLIP_TILE, cols), lambda i, p: (i, 0))],
+            out_specs=pl.BlockSpec((cols // CHIPS, FLIP_TILE), lambda i, p: (0, i)),
+        ),
+        out_shape=jax.ShapeDtypeStruct((cols // CHIPS, width), jnp.bfloat16),
+        cost_estimate=pl.CostEstimate(flops=5_000_000_000, bytes_accessed=0, transcendentals=0),
+        name="flip",
+    )(place, up_weight)
+
+
 def solution(mesh):
     row_spec = P(AXES)
     weight_spec = P(None, AXES)
@@ -346,14 +376,13 @@
             grid = w_up[layer].reshape(shard, chips, CORES, block)
             return to_columns(core, [grid[:, :, part].reshape(shard, chips * block) for part in range(CORES)])
 
+        place = jnp.stack([chip, core]).astype(jnp.int32)
         attn_full, up_full, down_full, up_flip = [], [], [], []
         for layer in range(pairs):
             attn_full.append(gather_weight(chip, attn_piece(layer)))
             up_full.append(gather_weight(chip, up_piece(layer)))
-            down_full.append(gather_weight(chip, w_down[layer]) if layer < pairs - 1 else gather(w_down[layer]))
-            cols = [up_full[layer][:, i * block:(i + 1) * block] for i in range(chips)]
-            up_flip.append(lax.select_n(chip, *cols).T)
-        place = jnp.stack([chip, core]).astype(jnp.int32)
+            down_full.append(gather_weight(chip, w_down[layer]))
+            up_flip.append(flip(place, up_full[layer]))
         carry_x = x_loc.reshape(seqs * seq, width)
         grad_x = grad_out.reshape(seqs * seq, width)
         attn_saved, mlp_saved, d_up, d_down = [], [], [], []
@@ -367,9 +396,9 @@
             attn_saved.append(saved)
             n_own = norm_bf16(x_own)
             gelu_act, slope = mlp_hidden(pair_rows(n_own), up_full[layer])
-            norms = gather_rows(n_own)
+            norms = gather_rows(n_own, layer == pairs - 1)
             if layer == pairs - 1:
-                parts, d_down = weight_grads(layer, norms, gather_rows(grad_x), d_down)
+                parts, d_down = weight_grads(layer, norms, gather_rows(grad_x, layer == pairs - 1), d_down)
             mlp_saved.append((x_own, norms, slope))
             if layer < pairs - 1:
                 carry_x = mlp_output(x_own, gelu_act, down_full[layer])
@@ -378,7 +407,7 @@
         for layer in reversed(range(pairs)):
             x_own, norms, slope = mlp_saved[layer]
             if layer < pairs - 1:
-                parts, d_down = weight_grads(layer, norms, gather_rows(grad_x), d_down)
+                parts, d_down = weight_grads(layer, norms, gather_rows(grad_x, layer == pairs - 1), d_down)
             d_up = [assemble(place, layer, pairs, d_up, parts)]
             grad_x = mlp_backward(x_own, slope, up_full[layer], down_full[layer], grad_x)
             grad_x, d_qkv, d_o = attn_backward(attn_saved[layer], attn_full[layer], q_width, head, seq, grad_x)

time: 1920 us -> 1870 us (0.974)
  local copies, waits for them, and re-layouts: 271 us -> 233 us
  Pallas kernels: 389 us -> 409 us
    ppermute x20 -> x24, waiting for transfers between devices: 419 us -> 311 us  [hop(): lax.ppermute(value, CHIP, [(chip, chip ^ step) for chip in range(CHIPS)])]
    all_gather x5 -> x4, waiting for transfers between devices: 0.04 us -> 51.5 us  [gather(): return functools.partial(lax.all_gather, axis=0, tiled=True)(value, axes)]
    ppermute x14, waiting for transfers between devices: 124 us -> 174 us  [exchange(): lax.ppermute(part, AXES, [(d, d ^ i) for d in devices])]
    unnamed x196 -> x224, local copies, waits for them, and re-layouts: 63.9 us -> 24.9 us
    dynamic_update_slice x20 -> x26, local copies, waits for them, and re-layouts: 51.5 us -> 78.1 us  [gather_weight(): full = lax.dynamic_update_slice(full, part[None], (chip ^ step, row, 0))]
    slice x2 -> x0, local copies, waits for them, and re-layouts: 22.9 us -> none  [body(): cols = [up_full[layer][:, i * block:(i + 1) * block] for i in range(chips)]]
    pallas_call x2 -> x4, Pallas kernels: 282 us -> 303 us  [the longest x2 280 us: mlp_weight_grads(): pl.pallas_call(functools.partial(mlp_grads_kernel, steps, len(norms)), gr...]
  transfers between devices with their start and end apart: 71 -> 72, of which waited for: 26 -> 29; matrix products, arithmetic and copies ran while one was open for 44% -> 37% of each run, Pallas kernels for 13% -> 15%
where the time goes in v4:
time: 1870 us
  waiting for transfers between devices  570 us (30%)
  matrix products  489 us (26%)
  Pallas kernels  409 us (22%)
  local copies, waits for them, and re-layouts  233 us (12%)
  other arithmetic  104 us (6%)
  starting transfers between devices  43.9 us (2%)
    dot_general x28, matrix products, dot(): lax.dot_general(left, right, (contract, ((), ())), preferred_element_type...  489 us
    ppermute x24, waiting for transfers between devices, hop(): lax.ppermute(value, CHIP, [(chip, chip ^ step) for chip in range(CHIPS)])  311 us
    pallas_call x2, Pallas kernels, mlp_weight_grads(): pl.pallas_call(functools.partial(mlp_grads_kernel, steps, len(norms)), gr...  280 us
    ppermute x14, waiting for transfers between devices, exchange(): lax.ppermute(part, AXES, [(d, d ^ i) for d in devices])  174 us
    pallas_call x4, Pallas kernels, by_sequence(): pl.pallas_call(functools.partial(kernel, q_width, head), grid=(rows // se...  90.6 us
    dynamic_update_slice x26, local copies, waits for them, and re-layouts, gather_weight(): full = lax.dynamic_update_slice(full, part[None], (chip ^ step, row, 0))  78.1 us
    all_gather x4, waiting for transfers between devices, gather(): return functools.partial(lax.all_gather, axis=0, tiled=True)(value, axes)  51.5 us
  transfers between devices with their start and end apart: 72, of which 29 were waited for; matrix products, arithmetic and copies ran while one was open for 37% of the time, Pallas kernels for 15%

profile of v4, /device:TPU:0, one launch (start us, length us, event | category | flops | bytes accessed | tf_op | source)
XLA Modules:
  0.0 1865.3 jit_solution(14382622983896556145)
XLA Ops:
  11.2 6.3 slice_dynamic-update-slice_fusion
  46.3 8.4 reshape_squeeze.31
  54.7 9.2 fusion.116
  63.8 8.4 reshape_squeeze.28
  72.2 8.1 fusion.117
  131.4 23.7 %collective-permute-done.2 = bf16[384,1792]{1,0:T(8,128)(2,1)} collective-permute-done((bf16[384,1792]{1,0:T(8,128)(2,1)}, bf16[384,1792]{1,0:T(8,128)(2,1)}, u32[]{:S(2)}, u32[]{:S(2)}) %collective-permute-start.2) | collective-permute-done | bytes 1376288 | tf_op jit(solution)/shard_map/ppermute | solution.py:59
  165.8 7.5 collective-permute-done.4
  178.5 11.6 fusion.65.qkv_ref
  190.0 17.2 shard_map.143
  215.4 6.2 fusion.91
  238.3 12.6 collective-permute-done.9
  267.0 5.8 fusion.31
  275.2 16.3 collective-permute-done.15
  297.0 27.8 %collective-permute-done.11 = bf16[192,4480]{1,0:T(8,128)(2,1)} collective-permute-done((bf16[192,4480]{1,0:T(8,128)(2,1)}, bf16[192,4480]{1,0:T(8,128)(2,1)}, u32[]{:S(2)}, u32[]{:S(2)}) %collective-permute-start.11) | collective-permute-done | bytes 1720352 | tf_op jit(solution)/shard_map/ppermute | solution.py:59
  332.0 51.8 %multiply_add_fusion.2 = (f32[2048,4480]{1,0:T(8,128)}, bf16[2048,4480]{1,0:T(8,128)(2,1)}) fusion(bf16[1536,4480]{1,0:T(8,128)(2,1)} %bitcast.205, bf16[1024,1536]{1,0:T(8,128)(2,1)} %copy-done.97, bf16[1024,1536]{1,0:T(8,128)(2,1)S(1)} %fusion.32), kind=kOutput, calls=%fused_computation.6 | convolution fusion | flops 28326756352 | bytes 75104256 | tf_op jit(solution)/shard_map/dot_general | solution.py:39
  383.9 21.6 %fusion.16 = f32[1024,1536]{1,0:T(8,128)} fusion(bf16[4480,1536]{1,0:T(8,128)(2,1)} %bitcast.212, bf16[2048,4480]{1,0:T(8,128)(2,1)} %get-tuple-element.34), kind=kOutput, calls=%fused_computation.40 | convolution fusion | flops 14092861440 | bytes 29229056 | tf_op jit(solution)/shard_map/dot_general | solution.py:39
  422.3 21.7 %fusion.18 = f32[1024,1536]{1,0:T(8,128)} fusion(bf16[4480,1536]{1,0:T(8,128)(2,1)} %bitcast.213, bf16[2048,4480]{1,0:T(8,128)(2,1)} %get-tuple-element.34), kind=kOutput, calls=%fused_computation.42 | convolution fusion | flops 14092861440 | bytes 29229056 | tf_op jit(solution)/shard_map/dot_general | solution.py:39
  445.0 6.0 fusion.35
  459.4 140.3 %collective-permute-done.20 = bf16[384,1792]{1,0:T(8,128)(2,1)} collective-permute-done((bf16[384,1792]{1,0:T(8,128)(2,1)}, bf16[384,1792]{1,0:T(8,128)(2,1)}, u32[]{:S(2)}, u32[]{:S(2)}) %collective-permute-start.20) | collective-permute-done | bytes 1376288 | tf_op jit(solution)/shard_map/ppermute | solution.py:59
  609.4 20.6 %collective-permute-done.22 = bf16[192,1792]{1,0:T(8,128)(2,1)S(1)} collective-permute-done((bf16[192,1792]{1,0:T(8,128)(2,1)S(1)}, bf16[192,1792]{1,0:T(8,128)(2,1)S(1)}, u32[]{:S(2)}, u32[]{:S(2)}) %collective-permute-start.22) | collective-permute-done | bytes 688160 | tf_op jit(solution)/shard_map/ppermute | solution.py:59
  633.5 11.6 fusion.66.qkv_ref
  645.1 17.2 shard_map.144
  684.5 21.1 %collective-permute-done.27 = bf16[384,4480]{1,0:T(8,128)(2,1)} collective-permute-done((bf16[384,4480]{1,0:T(8,128)(2,1)}, bf16[384,4480]{1,0:T(8,128)(2,1)}, u32[]{:S(2)}, u32[]{:S(2)}) %collective-permute-start.27) | collective-permute-done | bytes 3440672 | tf_op jit(solution)/shard_map/ppermute | solution.py:59
  721.0 6.1 fusion.86
  730.5 5.8 fusion.28
  738.5 7.6 collective-permute-done.33
  751.6 29.0 %collective-permute-done.29 = bf16[192,4480]{1,0:T(8,128)(2,1)} collective-permute-done((bf16[192,4480]{1,0:T(8,128)(2,1)}, bf16[192,4480]{1,0:T(8,128)(2,1)}, u32[]{:S(2)}, u32[]{:S(2)}) %collective-permute-start.29) | collective-permute-done | bytes 1720352 | tf_op jit(solution)/shard_map/ppermute | solution.py:59
  787.8 51.7 %multiply_add_fusion = (f32[2048,4480]{1,0:T(8,128)}, bf16[2048,4480]{1,0:T(8,128)(2,1)}) fusion(bf16[1536,4480]{1,0:T(8,128)(2,1)} %bitcast.201, bf16[1024,1536]{1,0:T(8,128)(2,1)} %copy-done.98, bf16[1024,1536]{1,0:T(8,128)(2,1)S(1)} %fusion.29), kind=kOutput, calls=%fused_computation.2 | convolution fusion | flops 28326756352 | bytes 75104256 | tf_op jit(solution)/shard_map/dot_general | solution.py:39
  839.5 41.7 %multiply_convert_fusion.1 = bf16[2048,4480]{1,0:T(8,128)(2,1)} fusion(f32[2048,4480]{1,0:T(8,128)} %get-tuple-element.36, bf16[4480,1536]{1,0:T(8,128)(2,1)} %bitcast.209, bf16[1024,1536]{1,0:T(8,128)(2,1)} %collective-permute-done.35, bf16[1024,1536]{1,0:T(8,128)(2,1)} %bitcast.59), kind=kOutput, calls=%fused_computation.1 | convolution fusion | flops 28216655872 | bytes 75104256 | tf_op jit(solution)/shard_map/dot_general | solution.py:39
  881.3 21.6 %fusion.8 = f32[1024,1536]{1,0:T(8,128)} fusion(bf16[1536,4480]{1,0:T(8,128)(2,1)} %bitcast.202, bf16[2048,4480]{1,0:T(8,128)(2,1)} %multiply_convert_fusion.1), kind=kOutput, calls=%fused_computation.32 | convolution fusion | flops 14092861440 | bytes 29229056 | tf_op jit(solution)/shard_map/dot_general | solution.py:39
  902.9 19.2 %fusion.10 = f32[1024,1536]{1,0:T(8,128)S(1)} fusion(bf16[1536,4480]{1,0:T(8,128)(2,1)} %bitcast.203, bf16[2048,4480]{1,0:T(8,128)(2,1)} %multiply_convert_fusion.1), kind=kOutput, calls=%fused_computation.34 | convolution fusion | flops 14092861440 | bytes 29229056 | tf_op jit(solution)/shard_map/dot_general | solution.py:39
  933.6 11.1 fusion.67.d_o_ref
  944.7 28.0 %shard_map.145 = bf16[2048,1024]{1,0:T(8,128)(2,1)} custom-call(bf16[2048,1024]{1,0:T(8,128)(2,1)} %fusion.66.qkv_ref, bf16[2048,768]{1,0:T(8,128)(2,1)} %fusion.67.d_o_ref), custom_call_target="tpu_custom_call" | custom-call | flops 40000000000 | tf_op jit(solution)/shard_map/pallas_call | solution.py:181
  972.7 6.1 fusion.69
  995.3 10.3 fusion.59
  1005.7 40.7 %multiply_convert_fusion = bf16[2048,4480]{1,0:T(8,128)(2,1)} fusion(f32[2048,4480]{1,0:T(8,128)} %get-tuple-element.42, bf16[4480,1536]{1,0:T(8,128)(2,1)} %bitcast.214, bf16[1024,1536]{1,0:T(8,128)(2,1)} %collective-permute-done.42, bf16[1024,1536]{1,0:T(8,128)(2,1)S(1)} %fusion.23), kind=kOutput, calls=%fused_computation | convolution fusion | flops 28216655872 | bytes 75104256 | tf_op jit(solution)/shard_map/dot_general | solution.py:39
  1046.4 21.6 %fusion.4 = f32[1024,1536]{1,0:T(8,128)} fusion(bf16[1536,4480]{1,0:T(8,128)(2,1)} %bitcast.206, bf16[2048,4480]{1,0:T(8,128)(2,1)} %multiply_convert_fusion), kind=kOutput, calls=%fused_computation.28 | convolution fusion | flops 14092861440 | bytes 29229056 | tf_op jit(solution)/shard_map/dot_general | solution.py:39
  1068.5 10.6 fusion.61
  1079.2 19.3 %fusion.6 = f32[1024,1536]{1,0:T(8,128)S(1)} fusion(bf16[1536,4480]{1,0:T(8,128)(2,1)} %bitcast.207, bf16[2048,4480]{1,0:T(8,128)(2,1)} %multiply_convert_fusion), kind=kOutput, calls=%fused_computation.30 | convolution fusion | flops 14092861440 | bytes 29229056 | tf_op jit(solution)/shard_map/dot_general | solution.py:39
  1112.7 6.9 fusion.57
  1119.6 9.3 fusion.68.d_o_ref
  1129.0 28.1 %shard_map.146 = bf16[2048,1024]{1,0:T(8,128)(2,1)} custom-call(bf16[2048,1024]{1,0:T(8,128)(2,1)} %fusion.65.qkv_ref, bf16[2048,768]{1,0:T(8,128)(2,1)} %fusion.68.d_o_ref), custom_call_target="tpu_custom_call" | custom-call | flops 40000000000 | tf_op jit(solution)/shard_map/pallas_call | solution.py:181
  1157.1 11.9 fusion.63
  1173.1 11.2 flip.3.up_ref
  1184.3 11.4 flip.2.up_ref
  1195.8 13.0 collective-permute-done.49
  1211.9 8.7 fusion.74
  1220.8 141.4 %mlp_grads.2 = (f32[2,1120,1536]{2,1,0:T(8,128)}, f32[192,1120]{1,0:T(8,128)}, f32[192,1120]{1,0:T(8,128)}, f32[192,1120]{1,0:T(8,128)}, f32[192,1120]{1,0:T(8,1...) custom-call(s32[2]{0:T(128)} %pad_add_fusion.place_ref, ...), custom_call_target="tpu_custom_call" | custom-call | flops 112742891520 | tf_op jit(solution)/shard_map/mlp_grads/pallas_call | solution.py:277
  1368.8 35.6 %collective-permute-done.58.refs_2_ = f32[192,1120]{1,0:T(8,128)} collective-permute-done((f32[192,1120]{1,0:T(8,128)}, f32[192,1120]{1,0:T(8,128)}, u32[]{:S(2)}, u32[]{:S(2)}) %collective-permute-start.58) | collective-permute-done | bytes 860192 | tf_op jit(solution)/shard_map/ppermute | solution.py:300
  1405.8 35.6 %collective-permute-done.59.refs_3_ = f32[192,1120]{1,0:T(8,128)} collective-permute-done((f32[192,1120]{1,0:T(8,128)}, f32[192,1120]{1,0:T(8,128)}, u32[]{:S(2)}, u32[]{:S(2)}) %collective-permute-start.59) | collective-permute-done | bytes 860192 | tf_op jit(solution)/shard_map/ppermute | solution.py:300
  1444.2 8.9 fusion.76
  1453.1 13.3 collective-permute-done.62.refs_6_
  1466.3 37.1 %collective-permute-done.63.refs_7_ = f32[192,1120]{1,0:T(8,128)S(1)} collective-permute-done((f32[192,1120]{1,0:T(8,128)}, f32[192,1120]{1,0:T(8,128)S(1)}, u32[]{:S(2)}, u32[]{:S(2)}) %collective-permute-start.63) | collective-permute-done | bytes 860192 | tf_op jit(solution)/shard_map/ppermute | solution.py:300
  1504.4 8.1 assemble.2.refs_8_
  1523.1 8.3 fusion.27
  1540.1 51.4 %all-gather.7.cloned.1.call-done.rest_1_ = bf16[8192,1536]{1,0:T(8,128)(2,1)} async-done(((bf16[1024,1536]{1,0:T(8,128)(2,1)}), bf16[8192,1536]{1,0:T(8,128)(2,1)}) %all-gather.7.cloned.1.call-update) | async-done | bytes 25165840 | tf_op jit(solution)/shard_map/all_gather | solution.py:105
  1591.6 138.5 %mlp_grads.3 = (f32[2,1120,1536]{2,1,0:T(8,128)}, f32[192,1120]{1,0:T(8,128)}, f32[192,1120]{1,0:T(8,128)}, f32[192,1120]{1,0:T(8,128)}, f32[192,1120]{1,0:T(8,1...) custom-call(s32[2]{0:T(128)} %pad_add_fusion.place_ref, ...), custom_call_target="tpu_custom_call", output_to_operand_aliasing={{0}: (5, {})} | custom-call | flops 112742891520 | tf_op jit(solution)/shard_map/mlp_grads/pallas_call | solution.py:277
  1730.1 21.6 %fusion.12 = f32[1024,1536]{1,0:T(8,128)} fusion(bf16[4480,1536]{1,0:T(8,128)(2,1)} %bitcast.210, bf16[2048,4480]{1,0:T(8,128)(2,1)} %get-tuple-element.40), kind=kOutput, calls=%fused_computation.36 | convolution fusion | flops 14092861440 | bytes 29229056 | tf_op jit(solution)/shard_map/dot_general | solution.py:39
  1763.7 11.4 collective-permute-done.51.refs_2_
  1776.6 16.5 collective-permute-done.52.refs_3_
  1795.2 21.5 %fusion.14 = f32[1024,1536]{1,0:T(8,128)} fusion(bf16[4480,1536]{1,0:T(8,128)(2,1)} %bitcast.211, bf16[2048,4480]{1,0:T(8,128)(2,1)} %get-tuple-element.40), kind=kOutput, calls=%fused_computation.38 | convolution fusion | flops 14092861440 | bytes 29229056 | tf_op jit(solution)/shard_map/dot_general | solution.py:39
  1816.7 23.2 %collective-permute-done.54.refs_5_ = f32[192,1120]{1,0:T(8,128)S(1)} collective-permute-done((f32[192,1120]{1,0:T(8,128)S(1)}, f32[192,1120]{1,0:T(8,128)S(1)}, u32[]{:S(2)}, u32[]{:S(2)}) %collective-permute-start.54) | collective-permute-done | bytes 860192 | tf_op jit(solution)/shard_map/ppermute | solution.py:300
  1842.1 8.1 assemble.3
  1850.2 8.1 add_convert_fusion
  (506 shorter events, 348.8 us)
Async XLA Ops:
  7.2 1163.3 %all-gather.11.cloned.1.call-start = ((), (), s32[]{:S(2)}) async-start(), calls=%async_computation.7 | async-start | bytes 15728640 | tf_op jit(solution)/shard_map/all_gather | solution.py:105
  17.5 204.1 %collective-permute-start.13 = (bf16[1120,1536]{1,0:T(8,128)(2,1)}, bf16[1120,1536]{1,0:T(8,128)(2,1)}, u32[]{:S(2)}, u32[]{:S(2)}) collective-permute-start(bf16[1120,1536]{1,0:T(8,128)(2,1)} %get-tuple-element.91._.down_ref), channel_id=1, source_target_pairs={{0,2},{2,0},{4,6},{6,4},{1,3},{3,1},{5,7},{7,5}} | collective-permute-start | bytes 10321928 | tf_op jit(solution)/shard_map/ppermute | solution.py:59
  20.8 204.9 %collective-permute-start.14 = (bf16[1120,1536]{1,0:T(8,128)(2,1)}, bf16[1120,1536]{1,0:T(8,128)(2,1)}, u32[]{:S(2)}, u32[]{:S(2)}) collective-permute-start(bf16[1120,1536]{1,0:T(8,128)(2,1)} %get-tuple-element.91._.down_ref), channel_id=1, source_target_pairs={{0,4},{2,6},{4,0},{6,2},{1,5},{3,7},{5,1},{7,3}} | collective-permute-start | bytes 10321928 | tf_op jit(solution)/shard_map/ppermute | solution.py:59
  39.5 78.9 %collective-permute-start.1 = (bf16[192,1792]{1,0:T(8,128)(2,1)}, bf16[192,1792]{1,0:T(8,128)(2,1)}, u32[]{:S(2)}, u32[]{:S(2)}) collective-permute-start(bf16[192,1792]{1,0:T(8,128)(2,1)} %broadcast_select_fusion.14), channel_id=1, source_target_pairs={{0,1},{1,0},{2,3},{3,2},{4,5},{5,4},{6,7},{7,6}} | collective-permute-start | bytes 2064392 | tf_op jit(solution)/shard_map/ppermute | solution.py:55
  42.5 136.0 %collective-permute-start = (bf16[1024,1536]{1,0:T(8,128)(2,1)}, bf16[1024,1536]{1,0:T(8,128)(2,1)}, u32[]{:S(2)}, u32[]{:S(2)}) collective-permute-start(bf16[1024,1536]{1,0:T(8,128)(2,1)} %fusion.54), channel_id=1, source_target_pairs={{0,1},{1,0},{2,3},{3,2},{4,5},{5,4},{6,7},{7,6}} | collective-permute-start | bytes 9437192 | tf_op jit(solution)/shard_map/ppermute | solution.py:55
  89.7 35.7 %collective-permute-start.8 = (bf16[192,4480]{1,0:T(8,128)(2,1)}, bf16[192,4480]{1,0:T(8,128)(2,1)}, u32[]{:S(2)}, u32[]{:S(2)}) collective-permute-start(bf16[192,4480]{1,0:T(8,128)(2,1)} %select_n.192), channel_id=1, source_target_pairs={{0,1},{1,0},{2,3},{3,2},{4,5},{5,4},{6,7},{7,6}} | collective-permute-start | bytes 5160968 | tf_op jit(solution)/shard_map/ppermute | solution.py:55
  122.2 32.9 %collective-permute-start.2 = (bf16[384,1792]{1,0:T(8,128)(2,1)}, bf16[384,1792]{1,0:T(8,128)(2,1)}, u32[]{:S(2)}, u32[]{:S(2)}) collective-permute-start(bf16[384,1792]{1,0:T(8,128)(2,1)} %pad_maximum_fusion.24._), channel_id=1, source_target_pairs={{0,2},{2,0},{4,6},{6,4},{1,3},{3,1},{5,7},{7,5}} | collective-permute-start | bytes 4128776 | tf_op jit(solution)/shard_map/ppermute | solution.py:59
  125.4 32.6 %collective-permute-start.3 = (bf16[384,1792]{1,0:T(8,128)(2,1)}, bf16[384,1792]{1,0:T(8,128)(2,1)}, u32[]{:S(2)}, u32[]{:S(2)}) collective-permute-start(bf16[384,1792]{1,0:T(8,128)(2,1)} %pad_maximum_fusion.24._), channel_id=1, source_target_pairs={{0,4},{2,6},{4,0},{6,2},{1,5},{3,7},{5,1},{7,3}} | collective-permute-start | bytes 4128776 | tf_op jit(solution)/shard_map/ppermute | solution.py:59
  156.3 17.0 collective-permute-start.4
  159.2 17.8 collective-permute-start.5
  173.2 77.6 %collective-permute-start.9 = (bf16[384,4480]{1,0:T(8,128)(2,1)}, bf16[384,4480]{1,0:T(8,128)(2,1)}, u32[]{:S(2)}, u32[]{:S(2)}) collective-permute-start(bf16[384,4480]{1,0:T(8,128)(2,1)} %pad_maximum_fusion.16._), channel_id=1, source_target_pairs={{0,2},{2,0},{4,6},{6,4},{1,3},{3,1},{5,7},{7,5}} | collective-permute-start | bytes 10321928 | tf_op jit(solution)/shard_map/ppermute | solution.py:59
  177.0 77.6 %collective-permute-start.10 = (bf16[384,4480]{1,0:T(8,128)(2,1)}, bf16[384,4480]{1,0:T(8,128)(2,1)}, u32[]{:S(2)}, u32[]{:S(2)}) collective-permute-start(bf16[384,4480]{1,0:T(8,128)(2,1)} %pad_maximum_fusion.16._), channel_id=1, source_target_pairs={{0,4},{2,6},{4,0},{6,2},{1,5},{3,7},{5,1},{7,3}} | collective-permute-start | bytes 10321928 | tf_op jit(solution)/shard_map/ppermute | solution.py:59
  212.2 54.8 %collective-permute-start.6 = (f32[1024,1536]{1,0:T(8,128)S(1)}, f32[1024,1536]{1,0:T(8,128)}, u32[]{:S(2)}, u32[]{:S(2)}) collective-permute-start(f32[1024,1536]{1,0:T(8,128)S(1)} %fusion.89), channel_id=1, source_target_pairs={{0,1},{1,0},{2,3},{3,2},{4,5},{5,4},{6,7},{7,6}} | collective-permute-start | bytes 18874376 | tf_op jit(solution)/shard_map/ppermute | solution.py:55
  224.3 67.2 %collective-permute-start.15 = (bf16[560,1536]{1,0:T(8,128)(2,1)}, bf16[560,1536]{1,0:T(8,128)(2,1)}, u32[]{:S(2)}, u32[]{:S(2)}) collective-permute-start(bf16[560,1536]{1,0:T(8,128)(2,1)} %slice.336), channel_id=1, source_target_pairs={{0,4},{2,6},{4,0},{6,2},{1,5},{3,7},{5,1},{7,3}} | collective-permute-start | bytes 5160968 | tf_op jit(solution)/shard_map/ppermute | solution.py:59
  228.5 65.7 %collective-permute-start.16 = (bf16[560,1536]{1,0:T(8,128)(2,1)}, bf16[560,1536]{1,0:T(8,128)(2,1)}, u32[]{:S(2)}, u32[]{:S(2)}) collective-permute-start(bf16[560,1536]{1,0:T(8,128)(2,1)} %slice.337), channel_id=1, source_target_pairs={{0,2},{2,0},{4,6},{6,4},{1,3},{3,1},{5,7},{7,5}} | collective-permute-start | bytes 5160968 | tf_op jit(solution)/shard_map/ppermute | solution.py:59
  253.6 71.2 %collective-permute-start.11 = (bf16[192,4480]{1,0:T(8,128)(2,1)}, bf16[192,4480]{1,0:T(8,128)(2,1)}, u32[]{:S(2)}, u32[]{:S(2)}) collective-permute-start(bf16[192,4480]{1,0:T(8,128)(2,1)} %slice.334), channel_id=1, source_target_pairs={{0,4},{2,6},{4,0},{6,2},{1,5},{3,7},{5,1},{7,3}} | collective-permute-start | bytes 5160968 | tf_op jit(solution)/shard_map/ppermute | solution.py:59
  257.4 70.2 %collective-permute-start.12 = (bf16[192,4480]{1,0:T(8,128)(2,1)}, bf16[192,4480]{1,0:T(8,128)(2,1)}, u32[]{:S(2)}, u32[]{:S(2)}) collective-permute-start(bf16[192,4480]{1,0:T(8,128)(2,1)} %slice.335), channel_id=1, source_target_pairs={{0,2},{2,0},{4,6},{6,4},{1,3},{3,1},{5,7},{7,5}} | collective-permute-start | bytes 5160968 | tf_op jit(solution)/shard_map/ppermute | solution.py:59
  275.1 55.2 %collective-permute-start.7 = (bf16[1024,1536]{1,0:T(8,128)(2,1)S(1)}, bf16[1024,1536]{1,0:T(8,128)(2,1)S(1)}, u32[]{:S(2)}, u32[]{:S(2)}) collective-permute-start(bf16[1024,1536]{1,0:T(8,128)(2,1)S(1)} %fusion.32), channel_id=1, source_target_pairs={{0,1},{1,0},{2,3},{3,2},{4,5},{5,4},{6,7},{7,6}} | collective-permute-start | bytes 9437192 | tf_op jit(solution)/shard_map/ppermute | solution.py:55
  405.4 38.5 %collective-permute-start.17 = (f32[1024,1536]{1,0:T(8,128)}, f32[1024,1536]{1,0:T(8,128)}, u32[]{:S(2)}, u32[]{:S(2)}) collective-permute-start(f32[1024,1536]{1,0:T(8,128)} %fusion.16), channel_id=1, source_target_pairs={{0,1},{1,0},{2,3},{3,2},{4,5},{5,4},{6,7},{7,6}} | collective-permute-start | bytes 18874376 | tf_op jit(solution)/shard_map/ppermute | solution.py:55
  407.0 262.3 %collective-permute-start.31 = (bf16[1120,1536]{1,0:T(8,128)(2,1)}, bf16[1120,1536]{1,0:T(8,128)(2,1)}, u32[]{:S(2)}, u32[]{:S(2)}) collective-permute-start(bf16[1120,1536]{1,0:T(8,128)(2,1)} %slice_bitcast_fusion._.down_ref), channel_id=1, source_target_pairs={{0,2},{2,0},{4,6},{6,4},{1,3},{3,1},{5,7},{7,5}} | collective-permute-start | bytes 10321928 | tf_op jit(solution)/shard_map/ppermute | solution.py:59
  408.3 264.3 %collective-permute-start.32 = (bf16[1120,1536]{1,0:T(8,128)(2,1)}, bf16[1120,1536]{1,0:T(8,128)(2,1)}, u32[]{:S(2)}, u32[]{:S(2)}) collective-permute-start(bf16[1120,1536]{1,0:T(8,128)(2,1)} %slice_bitcast_fusion._.down_ref), channel_id=1, source_target_pairs={{0,4},{2,6},{4,0},{6,2},{1,5},{3,7},{5,1},{7,3}} | collective-permute-start | bytes 10321928 | tf_op jit(solution)/shard_map/ppermute | solution.py:59
  411.2 42.0 %collective-permute-start.26 = (bf16[192,4480]{1,0:T(8,128)(2,1)}, bf16[192,4480]{1,0:T(8,128)(2,1)}, u32[]{:S(2)}, u32[]{:S(2)}) collective-permute-start(bf16[192,4480]{1,0:T(8,128)(2,1)} %select_n.202), channel_id=1, source_target_pairs={{0,1},{1,0},{2,3},{3,2},{4,5},{5,4},{6,7},{7,6}} | collective-permute-start | bytes 5160968 | tf_op jit(solution)/shard_map/ppermute | solution.py:55
  411.3 759.6 %all-gather.9.cloned.1.call-start = ((), (), s32[]{:S(2)}) async-start(), calls=%async_computation.6 | async-start | bytes 15728640 | tf_op jit(solution)/shard_map/all_gather | solution.py:105
  419.8 179.8 %collective-permute-start.20 = (bf16[384,1792]{1,0:T(8,128)(2,1)}, bf16[384,1792]{1,0:T(8,128)(2,1)}, u32[]{:S(2)}, u32[]{:S(2)}) collective-permute-start(bf16[384,1792]{1,0:T(8,128)(2,1)} %pad_maximum_fusion.25._), channel_id=1, source_target_pairs={{0,2},{2,0},{4,6},{6,4},{1,3},{3,1},{5,7},{7,5}} | collective-permute-start | bytes 4128776 | tf_op jit(solution)/shard_map/ppermute | solution.py:59
  444.0 158.4 %collective-permute-start.21 = (bf16[384,1792]{1,0:T(8,128)(2,1)}, bf16[384,1792]{1,0:T(8,128)(2,1)}, u32[]{:S(2)}, u32[]{:S(2)}) collective-permute-start(bf16[384,1792]{1,0:T(8,128)(2,1)} %pad_maximum_fusion.25._), channel_id=1, source_target_pairs={{0,4},{2,6},{4,0},{6,2},{1,5},{3,7},{5,1},{7,3}} | collective-permute-start | bytes 4128776 | tf_op jit(solution)/shard_map/ppermute | solution.py:59
  453.2 180.2 %collective-permute-start.18 = (bf16[1024,1536]{1,0:T(8,128)(2,1)}, bf16[1024,1536]{1,0:T(8,128)(2,1)}, u32[]{:S(2)}, u32[]{:S(2)}) collective-permute-start(bf16[1024,1536]{1,0:T(8,128)(2,1)} %fusion.36), channel_id=1, source_target_pairs={{0,1},{1,0},{2,3},{3,2},{4,5},{5,4},{6,7},{7,6}} | collective-permute-start | bytes 9437192 | tf_op jit(solution)/shard_map/ppermute | solution.py:55
  600.8 29.1 %collective-permute-start.22 = (bf16[192,1792]{1,0:T(8,128)(2,1)S(1)}, bf16[192,1792]{1,0:T(8,128)(2,1)S(1)}, u32[]{:S(2)}, u32[]{:S(2)}) collective-permute-start(bf16[192,1792]{1,0:T(8,128)(2,1)S(1)} %slice.346), channel_id=1, source_target_pairs={{0,4},{2,6},{4,0},{6,2},{1,5},{3,7},{5,1},{7,3}} | collective-permute-start | bytes 2064392 | tf_op jit(solution)/shard_map/ppermute | solution.py:59
  603.5 28.1 %collective-permute-start.23 = (bf16[192,1792]{1,0:T(8,128)(2,1)S(1)}, bf16[192,1792]{1,0:T(8,128)(2,1)S(1)}, u32[]{:S(2)}, u32[]{:S(2)}) collective-permute-start(bf16[192,1792]{1,0:T(8,128)(2,1)S(1)} %slice.347), channel_id=1, source_target_pairs={{0,2},{2,0},{4,6},{6,4},{1,3},{3,1},{5,7},{7,5}} | collective-permute-start | bytes 2064392 | tf_op jit(solution)/shard_map/ppermute | solution.py:59
  630.0 75.7 %collective-permute-start.27 = (bf16[384,4480]{1,0:T(8,128)(2,1)}, bf16[384,4480]{1,0:T(8,128)(2,1)}, u32[]{:S(2)}, u32[]{:S(2)}) collective-permute-start(bf16[384,4480]{1,0:T(8,128)(2,1)} %pad_maximum_fusion.17._), channel_id=1, source_target_pairs={{0,2},{2,0},{4,6},{6,4},{1,3},{3,1},{5,7},{7,5}} | collective-permute-start | bytes 10321928 | tf_op jit(solution)/shard_map/ppermute | solution.py:59
  631.6 77.6 %collective-permute-start.28 = (bf16[384,4480]{1,0:T(8,128)(2,1)}, bf16[384,4480]{1,0:T(8,128)(2,1)}, u32[]{:S(2)}, u32[]{:S(2)}) collective-permute-start(bf16[384,4480]{1,0:T(8,128)(2,1)} %pad_maximum_fusion.17._), channel_id=1, source_target_pairs={{0,4},{2,6},{4,0},{6,2},{1,5},{3,7},{5,1},{7,3}} | collective-permute-start | bytes 10321928 | tf_op jit(solution)/shard_map/ppermute | solution.py:59
  667.3 59.8 %collective-permute-start.24 = (f32[1024,1536]{1,0:T(8,128)S(1)}, f32[1024,1536]{1,0:T(8,128)S(1)}, u32[]{:S(2)}, u32[]{:S(2)}) collective-permute-start(f32[1024,1536]{1,0:T(8,128)S(1)} %fusion.84), channel_id=1, source_target_pairs={{0,1},{1,0},{2,3},{3,2},{4,5},{5,4},{6,7},{7,6}} | collective-permute-start | bytes 18874376 | tf_op jit(solution)/shard_map/ppermute | solution.py:55
  669.3 170.2 %collective-permute-start.35 = (bf16[1024,1536]{1,0:T(8,128)(2,1)}, bf16[1024,1536]{1,0:T(8,128)(2,1)}, u32[]{:S(2)}, u32[]{:S(2)}) collective-permute-start(bf16[1024,1536]{1,0:T(8,128)(2,1)} %bitcast.59), channel_id=1, source_target_pairs={{0,1},{1,0},{2,3},{3,2},{4,5},{5,4},{6,7},{7,6}} | collective-permute-start | bytes 9437192 | tf_op jit(solution)/shard_map/ppermute | solution.py:55
  672.6 73.5 %collective-permute-start.33 = (bf16[560,1536]{1,0:T(8,128)(2,1)}, bf16[560,1536]{1,0:T(8,128)(2,1)}, u32[]{:S(2)}, u32[]{:S(2)}) collective-permute-start(bf16[560,1536]{1,0:T(8,128)(2,1)} %slice.356), channel_id=1, source_target_pairs={{0,4},{2,6},{4,0},{6,2},{1,5},{3,7},{5,1},{7,3}} | collective-permute-start | bytes 5160968 | tf_op jit(solution)/shard_map/ppermute | solution.py:59
  705.6 43.2 %collective-permute-start.34 = (bf16[560,1536]{1,0:T(8,128)(2,1)}, bf16[560,1536]{1,0:T(8,128)(2,1)}, u32[]{:S(2)}, u32[]{:S(2)}) collective-permute-start(bf16[560,1536]{1,0:T(8,128)(2,1)} %slice.357), channel_id=1, source_target_pairs={{0,2},{2,0},{4,6},{6,4},{1,3},{3,1},{5,7},{7,5}} | collective-permute-start | bytes 5160968 | tf_op jit(solution)/shard_map/ppermute | solution.py:59
  709.2 71.4 %collective-permute-start.29 = (bf16[192,4480]{1,0:T(8,128)(2,1)}, bf16[192,4480]{1,0:T(8,128)(2,1)}, u32[]{:S(2)}, u32[]{:S(2)}) collective-permute-start(bf16[192,4480]{1,0:T(8,128)(2,1)} %slice.354), channel_id=1, source_target_pairs={{0,4},{2,6},{4,0},{6,2},{1,5},{3,7},{5,1},{7,3}} | collective-permute-start | bytes 5160968 | tf_op jit(solution)/shard_map/ppermute | solution.py:59
  729.7 53.6 %collective-permute-start.30 = (bf16[192,4480]{1,0:T(8,128)(2,1)}, bf16[192,4480]{1,0:T(8,128)(2,1)}, u32[]{:S(2)}, u32[]{:S(2)}) collective-permute-start(bf16[192,4480]{1,0:T(8,128)(2,1)} %slice.355), channel_id=1, source_target_pairs={{0,2},{2,0},{4,6},{6,4},{1,3},{3,1},{5,7},{7,5}} | collective-permute-start | bytes 5160968 | tf_op jit(solution)/shard_map/ppermute | solution.py:59
  746.1 40.1 %collective-permute-start.25 = (bf16[1024,1536]{1,0:T(8,128)(2,1)S(1)}, bf16[1024,1536]{1,0:T(8,128)(2,1)S(1)}, u32[]{:S(2)}, u32[]{:S(2)}) collective-permute-start(bf16[1024,1536]{1,0:T(8,128)(2,1)S(1)} %fusion.29), channel_id=1, source_target_pairs={{0,1},{1,0},{2,3},{3,2},{4,5},{5,4},{6,7},{7,6}} | collective-permute-start | bytes 9437192 | tf_op jit(solution)/shard_map/ppermute | solution.py:55
  902.9 19.3 %collective-permute-start.36 = (f32[1024,1536]{1,0:T(8,128)}, f32[1024,1536]{1,0:T(8,128)S(1)}, u32[]{:S(2)}, u32[]{:S(2)}) collective-permute-start(f32[1024,1536]{1,0:T(8,128)} %fusion.8), channel_id=1, source_target_pairs={{0,1},{1,0},{2,3},{3,2},{4,5},{5,4},{6,7},{7,6}} | collective-permute-start | bytes 18874376 | tf_op jit(solution)/shard_map/ppermute | solution.py:55
  928.1 243.5 %reduce-scatter.11.cloned.1.call-start = ((), (), s32[]{:S(2)}) async-start(), calls=%async_computation.11 | async-start | bytes 5898240 | tf_op jit(solution)/shard_map/reduce_scatter | solution.py:116
  1005.6 204.7 %reduce-scatter.7.cloned.1.call-start = ((), (), s32[]{:S(2)}) async-start(), calls=%async_computation.9 | async-start | bytes 7864320 | tf_op jit(solution)/shard_map/reduce_scatter | solution.py:116
  1068.1 30.5 %collective-permute-start.43 = (f32[1024,1536]{1,0:T(8,128)}, f32[1024,1536]{1,0:T(8,128)}, u32[]{:S(2)}, u32[]{:S(2)}) collective-permute-start(f32[1024,1536]{1,0:T(8,128)} %fusion.4), channel_id=1, source_target_pairs={{0,1},{1,0},{2,3},{3,2},{4,5},{5,4},{6,7},{7,6}} | collective-permute-start | bytes 18874376 | tf_op jit(solution)/shard_map/ppermute | solution.py:55
  1079.1 439.0 %reduce-scatter.9.cloned.1.call-start = ((), (), s32[]{:S(2)}) async-start(), calls=%async_computation.10 | async-start | bytes 5898240 | tf_op jit(solution)/shard_map/reduce_scatter | solution.py:116
  1119.6 401.1 %reduce-scatter.5.cloned.1.call-start = ((), (), s32[]{:S(2)}) async-start(), calls=%async_computation.8 | async-start | bytes 7864320 | tf_op jit(solution)/shard_map/reduce_scatter | solution.py:116
  1169.0 371.2 %all-gather.5.cloned.1.call-start = ((), (), s32[]{:S(2)}) async-start(), calls=%async_computation.4 | async-start | bytes 28311552 | tf_op jit(solution)/shard_map/all_gather | solution.py:105
  1169.7 421.9 %all-gather.7.cloned.1.call-start = ((), (), s32[]{:S(2)}) async-start(), calls=%async_computation.5 | async-start | bytes 28311552 | tf_op jit(solution)/shard_map/all_gather | solution.py:105
  1170.5 50.3 %collective-permute-start.40 = (bf16[4096,1536]{1,0:T(8,128)(2,1)}, bf16[4096,1536]{1,0:T(8,128)(2,1)}, u32[]{:S(2)}, u32[]{:S(2)}) collective-permute-start(bf16[4096,1536]{1,0:T(8,128)(2,1)} %all-gather.11.cloned.1.call-done.rest_2_), channel_id=1, source_target_pairs={{0,1},{1,0},{2,3},{3,2},{4,5},{5,4},{6,7},{7,6}} | collective-permute-start | bytes 37748744 | tf_op jit(solution)/shard_map/ppermute | solution.py:55
  1170.9 49.9 %collective-permute-start.39 = (bf16[4096,1536]{1,0:T(8,128)(2,1)}, bf16[4096,1536]{1,0:T(8,128)(2,1)}, u32[]{:S(2)}, u32[]{:S(2)}) collective-permute-start(bf16[4096,1536]{1,0:T(8,128)(2,1)} %all-gather.9.cloned.1.call-done.rest_0_), channel_id=1, source_target_pairs={{0,1},{1,0},{2,3},{3,2},{4,5},{5,4},{6,7},{7,6}} | collective-permute-start | bytes 37748744 | tf_op jit(solution)/shard_map/ppermute | solution.py:55
  1172.7 36.0 %collective-permute-start.49 = (f32[192,768]{1,0:T(8,128)S(1)}, f32[192,768]{1,0:T(8,128)S(1)}, u32[]{:S(2)}, u32[]{:S(2)}) collective-permute-start(f32[192,768]{1,0:T(8,128)S(1)} %dynamic-slice_bitcast_fusion.2), channel_id=1, source_target_pairs={{0,1},{1,0},{2,3},{3,2},{4,5},{5,4},{6,7},{7,6}} | collective-permute-start | bytes 1769480 | tf_op jit(solution)/shard_map/ppermute | solution.py:55
  1211.5 152.6 %collective-permute-start.47 = (f32[192,1024]{1,0:T(8,128)S(1)}, f32[192,1024]{1,0:T(8,128)S(1)}, u32[]{:S(2)}, u32[]{:S(2)}) collective-permute-start(f32[192,1024]{1,0:T(8,128)S(1)} %dynamic-slice_bitcast_fusion), channel_id=1, source_target_pairs={{0,1},{1,0},{2,3},{3,2},{4,5},{5,4},{6,7},{7,6}} | collective-permute-start | bytes 2359304 | tf_op jit(solution)/shard_map/ppermute | solution.py:55
  1220.6 291.9 %collective-permute-start.45 = (f32[1024,1536]{1,0:T(8,128)}, f32[1024,1536]{1,0:T(8,128)}, u32[]{:S(2)}, u32[]{:S(2)}) collective-permute-start(f32[1024,1536]{1,0:T(8,128)} %fusion.74), channel_id=1, source_target_pairs={{0,1},{1,0},{2,3},{3,2},{4,5},{5,4},{6,7},{7,6}} | collective-permute-start | bytes 18874376 | tf_op jit(solution)/shard_map/ppermute | solution.py:55
  1362.6 41.8 %collective-permute-start.58 = (f32[192,1120]{1,0:T(8,128)}, f32[192,1120]{1,0:T(8,128)}, u32[]{:S(2)}, u32[]{:S(2)}) collective-permute-start(f32[192,1120]{1,0:T(8,128)} %get-tuple-element.53), channel_id=1, source_target_pairs={{0,2},{1,3},{2,0},{3,1},{4,6},{5,7},{6,4},{7,5}} | collective-permute-start | bytes 2580488 | tf_op jit(solution)/shard_map/ppermute | solution.py:300
  1364.0 77.4 %collective-permute-start.59 = (f32[192,1120]{1,0:T(8,128)}, f32[192,1120]{1,0:T(8,128)}, u32[]{:S(2)}, u32[]{:S(2)}) collective-permute-start(f32[192,1120]{1,0:T(8,128)} %get-tuple-element.54), channel_id=1, source_target_pairs={{0,3},{1,2},{2,1},{3,0},{4,7},{5,6},{6,5},{7,4}} | collective-permute-start | bytes 2580488 | tf_op jit(solution)/shard_map/ppermute | solution.py:300
  1366.8 86.2 %collective-permute-start.60 = (f32[192,1120]{1,0:T(8,128)}, f32[192,1120]{1,0:T(8,128)S(1)}, u32[]{:S(2)}, u32[]{:S(2)}) collective-permute-start(f32[192,1120]{1,0:T(8,128)} %get-tuple-element.55), channel_id=1, source_target_pairs={{0,4},{1,5},{2,6},{3,7},{4,0},{5,1},{6,2},{7,3}} | collective-permute-start | bytes 2580488 | tf_op jit(solution)/shard_map/ppermute | solution.py:300
  1368.0 85.0 %collective-permute-start.61 = (f32[192,1120]{1,0:T(8,128)}, f32[192,1120]{1,0:T(8,128)S(1)}, u32[]{:S(2)}, u32[]{:S(2)}) collective-permute-start(f32[192,1120]{1,0:T(8,128)} %get-tuple-element.56), channel_id=1, source_target_pairs={{0,5},{1,4},{2,7},{3,6},{4,1},{5,0},{6,3},{7,2}} | collective-permute-start | bytes 2580488 | tf_op jit(solution)/shard_map/ppermute | solution.py:300
  1404.4 62.0 %collective-permute-start.62 = (f32[192,1120]{1,0:T(8,128)}, f32[192,1120]{1,0:T(8,128)S(1)}, u32[]{:S(2)}, u32[]{:S(2)}) collective-permute-start(f32[192,1120]{1,0:T(8,128)} %get-tuple-element.57), channel_id=1, source_target_pairs={{0,6},{1,7},{2,4},{3,5},{4,2},{5,3},{6,0},{7,1}} | collective-permute-start | bytes 2580488 | tf_op jit(solution)/shard_map/ppermute | solution.py:300
  1441.4 62.0 %collective-permute-start.63 = (f32[192,1120]{1,0:T(8,128)}, f32[192,1120]{1,0:T(8,128)S(1)}, u32[]{:S(2)}, u32[]{:S(2)}) collective-permute-start(f32[192,1120]{1,0:T(8,128)} %get-tuple-element.58), channel_id=1, source_target_pairs={{0,7},{1,6},{2,5},{3,4},{4,3},{5,2},{6,1},{7,0}} | collective-permute-start | bytes 2580488 | tf_op jit(solution)/shard_map/ppermute | solution.py:300
  1523.1 14.6 collective-permute-start.46
  1751.7 98.5 %collective-permute-start.41 = (f32[1024,1536]{1,0:T(8,128)}, f32[1024,1536]{1,0:T(8,128)}, u32[]{:S(2)}, u32[]{:S(2)}) collective-permute-start(f32[1024,1536]{1,0:T(8,128)} %fusion.12), channel_id=1, source_target_pairs={{0,1},{1,0},{2,3},{3,2},{4,5},{5,4},{6,7},{7,6}} | collective-permute-start | bytes 18874376 | tf_op jit(solution)/shard_map/ppermute | solution.py:55
  1752.3 22.8 %collective-permute-start.51 = (f32[192,1120]{1,0:T(8,128)}, f32[192,1120]{1,0:T(8,128)}, u32[]{:S(2)}, u32[]{:S(2)}) collective-permute-start(f32[192,1120]{1,0:T(8,128)} %get-tuple-element.45), channel_id=1, source_target_pairs={{0,2},{1,3},{2,0},{3,1},{4,6},{5,7},{6,4},{7,5}} | collective-permute-start | bytes 2580488 | tf_op jit(solution)/shard_map/ppermute | solution.py:300
  1753.7 39.3 %collective-permute-start.52 = (f32[192,1120]{1,0:T(8,128)}, f32[192,1120]{1,0:T(8,128)}, u32[]{:S(2)}, u32[]{:S(2)}) collective-permute-start(f32[192,1120]{1,0:T(8,128)} %get-tuple-element.46), channel_id=1, source_target_pairs={{0,3},{1,2},{2,1},{3,0},{4,7},{5,6},{6,5},{7,4}} | collective-permute-start | bytes 2580488 | tf_op jit(solution)/shard_map/ppermute | solution.py:300
  1761.3 55.4 %collective-permute-start.53 = (f32[192,1120]{1,0:T(8,128)S(1)}, f32[192,1120]{1,0:T(8,128)S(1)}, u32[]{:S(2)}, u32[]{:S(2)}) collective-permute-start(f32[192,1120]{1,0:T(8,128)S(1)} %copy-done.102), channel_id=1, source_target_pairs={{0,4},{1,5},{2,6},{3,7},{4,0},{5,1},{6,2},{7,3}} | collective-permute-start | bytes 2580488 | tf_op jit(solution)/shard_map/ppermute | solution.py:300
  1763.5 76.4 %collective-permute-start.54 = (f32[192,1120]{1,0:T(8,128)S(1)}, f32[192,1120]{1,0:T(8,128)S(1)}, u32[]{:S(2)}, u32[]{:S(2)}) collective-permute-start(f32[192,1120]{1,0:T(8,128)S(1)} %copy-done.101), channel_id=1, source_target_pairs={{0,5},{1,4},{2,7},{3,6},{4,1},{5,0},{6,3},{7,2}} | collective-permute-start | bytes 2580488 | tf_op jit(solution)/shard_map/ppermute | solution.py:300
  1775.1 64.8 %collective-permute-start.55 = (f32[192,1120]{1,0:T(8,128)S(1)}, f32[192,1120]{1,0:T(8,128)S(1)}, u32[]{:S(2)}, u32[]{:S(2)}) collective-permute-start(f32[192,1120]{1,0:T(8,128)S(1)} %copy-done.100), channel_id=1, source_target_pairs={{0,6},{1,7},{2,4},{3,5},{4,2},{5,3},{6,0},{7,1}} | collective-permute-start | bytes 2580488 | tf_op jit(solution)/shard_map/ppermute | solution.py:300
  1793.1 46.8 %collective-permute-start.56 = (f32[192,1120]{1,0:T(8,128)S(1)}, f32[192,1120]{1,0:T(8,128)S(1)}, u32[]{:S(2)}, u32[]{:S(2)}) collective-permute-start(f32[192,1120]{1,0:T(8,128)S(1)} %copy-done.99), channel_id=1, source_target_pairs={{0,7},{1,6},{2,5},{3,4},{4,3},{5,2},{6,1},{7,0}} | collective-permute-start | bytes 2580488 | tf_op jit(solution)/shard_map/ppermute | solution.py:300
  (118 other events, 1577.7 us)
Sparse Core Ops, SparseCore 0:
  411.4 217.1 all-gather.10
  928.3 116.7 all-gather.8
  1048.0 51.4 reduce-scatter.10
  1102.2 64.4 reduce-scatter.6
  1169.5 51.3 reduce-scatter.8
  1223.7 64.4 reduce-scatter.4
  1290.0 159.4 all-gather.4
  1451.3 140.2 all-gather.6

commit v5 on v4

--- a/solution.py
+++ b/solution.py
@@ -63,9 +63,7 @@
     return jnp.where(core == 0, mine, other), jnp.where(core == 0, other, mine)
 
 
-def to_columns(core, halves):
-    keep = jnp.where(core == 0, halves[0], halves[1])
-    send = jnp.where(core == 0, halves[1], halves[0])
+def to_columns(core, keep, send):
     first, second = by_core(core, keep, swap(send))
     return jnp.concatenate([first, second], axis=0)
 
@@ -101,15 +99,8 @@
     return full.reshape(-1, piece.shape[1])
 
 
-def gather(value, axes):
-    return functools.partial(lax.all_gather, axis=0, tiled=True)(value, axes)
-
-
-def gather_rows(value, swapped):
-    if not swapped:
-        return (gather(value, AXES),)
-    mine = gather(value, CHIP)
-    return mine, swap(mine)
+def gather_rows(value):
+    return functools.partial(lax.all_gather, axis=0, tiled=True)(value, AXES)
 
 
 def scatter_sum(grad_full):
@@ -234,14 +225,10 @@
     return (grad_own.astype(jnp.float32) + norm_back(x_own, d_norm)).astype(jnp.bfloat16)
 
 
-def mlp_grads_kernel(steps, arrays, place_ref, up_ref, down_ref, *rest):
-    norms, grads = rest[:arrays], rest[arrays:2 * arrays]
+def mlp_grads_kernel(place_ref, up_ref, down_ref, norm_ref, grad_ref, *rest):
     d_down_ref, parts, d_up_ref, flip_ref = rest[-2 * CHIPS - 3], rest[-2 * CHIPS - 2:-2], rest[-2], rest[-1]
     step = pl.program_id(0)
-    normed, grad_y = norms[0][...], grads[0][...]
-    if arrays > 1:
-        normed = jnp.where(step < steps, normed, norms[1][...])
-        grad_y = jnp.where(step < steps, grad_y, grads[1][...])
+    normed, grad_y = norm_ref[...], grad_ref[...]
 
     @pl.when(step == 0)
     def _():
@@ -266,20 +253,18 @@
 
 def mlp_weight_grads(place, layer, pairs, earlier, up_flip, down_block, norms, grads):
     block, width = down_block.shape
-    steps = norms[0].shape[0] // TOKEN_TILE
     rows = width // (CHIPS * CORES)
     once = pl.Buffered(1)
     whole = pl.BlockSpec((block, width), lambda i, p: (0, 0), pipeline_mode=once)
-    tokens = [pl.BlockSpec((TOKEN_TILE, width), lambda i, p: (jnp.minimum(i, steps - 1), 0)),
-              pl.BlockSpec((TOKEN_TILE, width), lambda i, p: (jnp.maximum(i - steps, 0), 0))][:len(norms)]
+    tokens = pl.BlockSpec((TOKEN_TILE, width), lambda i, p: (i, 0))
     part = pl.BlockSpec((rows, block), lambda i, p: (0, 0), pipeline_mode=once)
-    args = [place, up_flip, down_block, *norms, *grads, *earlier]
+    args = [place, up_flip, down_block, norms, grads, *earlier]
     outs = pl.pallas_call(
-        functools.partial(mlp_grads_kernel, steps, len(norms)),
+        mlp_grads_kernel,
         grid_spec=pltpu.PrefetchScalarGridSpec(
             num_scalar_prefetch=1,
-            grid=(steps * len(norms),),
-            in_specs=[whole, whole] + tokens * 2 + [pl.BlockSpec(memory_space=pl.ANY)] * len(earlier),
+            grid=(norms.shape[0] // TOKEN_TILE,),
+            in_specs=[whole, whole, tokens, tokens] + [pl.BlockSpec(memory_space=pl.ANY)] * len(earlier),
             out_specs=[pl.BlockSpec((1, block, width), lambda i, p: (layer, 0, 0), pipeline_mode=once)]
             + [part] * (CHIPS * CORES),
             scratch_shapes=[pltpu.VMEM((block, width), jnp.float32), pltpu.VMEM((CORES * rows, block), jnp.float32)],
@@ -288,7 +273,7 @@
         + [jax.ShapeDtypeStruct((rows, block), jnp.float32)] * (CHIPS * CORES),
         input_output_aliases={len(args) - 1: 0} if earlier else {},
         compiler_params=pltpu.CompilerParams(vmem_limit_bytes=60 * 1024 * 1024),
-        cost_estimate=pl.CostEstimate(flops=8 * len(norms) * norms[0].shape[0] * block * width, bytes_accessed=0,
+        cost_estimate=pl.CostEstimate(flops=8 * norms.shape[0] * block * width, bytes_accessed=0,
                                       transcendentals=0),
         name="mlp_grads",
     )(*args)
@@ -328,6 +313,32 @@
     )(place, *parts, *earlier)
 
 
+def split_kernel(place_ref, rows_ref, keep_ref, send_ref):
+    block = rows_ref.shape[2] // (CHIPS * CORES)
+    for i in range(CHIPS):
+        pair = [rows_ref[0, :, (CORES * i + j) * block:(CORES * i + j + 1) * block] for j in range(CORES)]
+        cols = slice(i * block, (i + 1) * block)
+        keep_ref[:, cols] = jnp.where(place_ref[1] == 0, pair[0], pair[1])
+        send_ref[:, cols] = jnp.where(place_ref[1] == 0, pair[1], pair[0])
+
+
+def split_columns(place, layer, weight):
+    rows, cols = weight.shape[1:]
+    half = jax.ShapeDtypeStruct((rows, cols // CORES), weight.dtype)
+    return pl.pallas_call(
+        split_kernel,
+        grid_spec=pltpu.PrefetchScalarGridSpec(
+            num_scalar_prefetch=1,
+            grid=(rows // ROW_TILE,),
+            in_specs=[pl.BlockSpec((1, ROW_TILE, cols), lambda i, p: (layer, i, 0))],
+            out_specs=[pl.BlockSpec((ROW_TILE, cols // CORES), lambda i, p: (i, 0))] * CORES,
+        ),
+        out_shape=[half] * CORES,
+        cost_estimate=pl.CostEstimate(flops=5_000_000_000, bytes_accessed=0, transcendentals=0),
+        name="split",
+    )(place, weight)
+
+
 def flip_kernel(place_ref, up_ref, out_ref):
     block = out_ref.shape[0]
     cols = up_ref[:, :block]
@@ -355,7 +366,6 @@
 def solution(mesh):
     row_spec = P(AXES)
     weight_spec = P(None, AXES)
-    chips = mesh.shape[CHIP]
 
     def body(x_loc, w_q, w_k, w_v, w_o, w_up, w_down, grad_out):
         core = lax.axis_index(CORE)
@@ -363,26 +373,28 @@
         pairs, shard, heads, head = w_q.shape
         seqs, seq, width = x_loc.shape
         q_width = heads // CORES * head
-        block = w_down.shape[1]
-
-        def attn_piece(layer):
+
+        place = jnp.stack([chip, core]).astype(jnp.int32)
+
+        def attn_piece(layer, core):
             halves = []
             for part in range(CORES):
                 cols = [w[layer].reshape(shard, CORES, -1)[:, part] for w in (w_q, w_k, w_v, w_o)]
                 halves.append(jnp.concatenate(cols, axis=1))
-            return to_columns(core, halves)
-
-        def up_piece(layer):
-            grid = w_up[layer].reshape(shard, chips, CORES, block)
-            return to_columns(core, [grid[:, :, part].reshape(shard, chips * block) for part in range(CORES)])
-
-        place = jnp.stack([chip, core]).astype(jnp.int32)
+            return to_columns(core, *by_core(core, *halves))
+
+        def up_piece(layer, core, place):
+            return to_columns(core, *split_columns(place, layer, w_up))
+
         attn_full, up_full, down_full, up_flip = [], [], [], []
-        for layer in range(pairs):
-            attn_full.append(gather_weight(chip, attn_piece(layer)))
-            up_full.append(gather_weight(chip, up_piece(layer)))
+
+        def gather_weights(layer, core, place):
+            attn_full.append(gather_weight(chip, attn_piece(layer, core)))
+            up_full.append(gather_weight(chip, up_piece(layer, core, place)))
             down_full.append(gather_weight(chip, w_down[layer]))
             up_flip.append(flip(place, up_full[layer]))
+
+        gather_weights(0, core, place)
         carry_x = x_loc.reshape(seqs * seq, width)
         grad_x = grad_out.reshape(seqs * seq, width)
         attn_saved, mlp_saved, d_up, d_down = [], [], [], []
@@ -394,11 +406,14 @@
         for layer in range(pairs):
             x_own, saved = attn_forward(carry_x, attn_full[layer], q_width, head, seq)
             attn_saved.append(saved)
+            if layer < pairs - 1:
+                x_own, *later = lax.optimization_barrier((x_own, core, place))
+                gather_weights(layer + 1, *later)
             n_own = norm_bf16(x_own)
             gelu_act, slope = mlp_hidden(pair_rows(n_own), up_full[layer])
-            norms = gather_rows(n_own, layer == pairs - 1)
+            norms = gather_rows(n_own)
             if layer == pairs - 1:
-                parts, d_down = weight_grads(layer, norms, gather_rows(grad_x, layer == pairs - 1), d_down)
+                parts, d_down = weight_grads(layer, norms, gather_rows(grad_x), d_down)
             mlp_saved.append((x_own, norms, slope))
             if layer < pairs - 1:
                 carry_x = mlp_output(x_own, gelu_act, down_full[layer])
@@ -407,7 +422,7 @@
         for layer in reversed(range(pairs)):
             x_own, norms, slope = mlp_saved[layer]
             if layer < pairs - 1:
-                parts, d_down = weight_grads(layer, norms, gather_rows(grad_x, layer == pairs - 1), d_down)
+                parts, d_down = weight_grads(layer, norms, gather_rows(grad_x), d_down)
             d_up = [assemble(place, layer, pairs, d_up, parts)]
             grad_x = mlp_backward(x_own, slope, up_full[layer], down_full[layer], grad_x)
             grad_x, d_qkv, d_o = attn_backward(attn_saved[layer], attn_full[layer], q_width, head, seq, grad_x)

time: 1870 us -> 1940 us (1.037)
  waiting for transfers between devices: 570 us -> 704 us
  local copies, waits for them, and re-layouts: 233 us -> 171 us
    reduce_scatter x4, waiting for transfers between devices: 0.03 us -> 209 us  [scatter_sum(): return lax.psum_scatter(grad_full, CHIP, scatter_dimension=0, tiled=True)]
    ppermute x14, waiting for transfers between devices: 174 us -> 64.8 us  [exchange(): lax.ppermute(part, AXES, [(d, d ^ i) for d in devices])]
    all_gather x4, waiting for transfers between devices: 51.5 us -> 114 us  [gather_rows(): return functools.partial(lax.all_gather, axis=0, tiled=True)(value, AXES)]
    slice x3 -> x0, local copies, waits for them, and re-layouts: 20.6 us -> none  [the longest x2 17.3 us: up_piece(): grid[:, :, part].reshape(shard, chips * block)]
    pallas_call x2 -> x4, Pallas kernels: 280 us -> 290 us  [the longest x2 277 us: mlp_weight_grads(): pl.pallas_call(mlp_grads_kernel, grid_spec=pltpu.PrefetchScalarGridSpec(n...]
  transfers between devices with their start and end apart: 72 -> 70, of which waited for: 29 -> 24; matrix products, arithmetic and copies ran while one was open for 37% -> 32% of each run, Pallas kernels for 15% -> 20%
where the time goes in v5:
time: 1940 us; the launch traced here: 1930 us
  waiting for transfers between devices  704 us (36%)
  matrix products  485 us (25%)
  Pallas kernels  419 us (22%)
  local copies, waits for them, and re-layouts  171 us (9%)
  other arithmetic  97.7 us (5%)
  starting transfers between devices  39.5 us (2%)
    dot_general x28, matrix products, dot(): lax.dot_general(left, right, (contract, ((), ())), preferred_element_type...  485 us
    ppermute x24, waiting for transfers between devices, hop(): lax.ppermute(value, CHIP, [(chip, chip ^ step) for chip in range(CHIPS)])  298 us
    pallas_call x2, Pallas kernels, mlp_weight_grads(): pl.pallas_call(mlp_grads_kernel, grid_spec=pltpu.PrefetchScalarGridSpec(n...  277 us
    reduce_scatter x4, waiting for transfers between devices, scatter_sum(): return lax.psum_scatter(grad_full, CHIP, scatter_dimension=0, tiled=True)  209 us
    all_gather x4, waiting for transfers between devices, gather_rows(): return functools.partial(lax.all_gather, axis=0, tiled=True)(value, AXES)  114 us
    pallas_call x4, Pallas kernels, by_sequence(): pl.pallas_call(functools.partial(kernel, q_width, head), grid=(rows // se...  90.4 us
    dynamic_update_slice x26, local copies, waits for them, and re-layouts, gather_weight(): full = lax.dynamic_update_slice(full, part[None], (chip ^ step, row, 0))  69.7 us
    ppermute x14, waiting for transfers between devices, exchange(): lax.ppermute(part, AXES, [(d, d ^ i) for d in devices])  64.8 us
  transfers between devices with their start and end apart: 70, of which 24 were waited for; matrix products, arithmetic and copies ran while one was open for 32% of the time, Pallas kernels for 20%

profile of v5, /device:TPU:0, one launch (start us, length us, event | category | flops | bytes accessed | tf_op | source)
XLA Modules:
  0.0 1933.5 jit_solution(3046924689188209898)
XLA Ops:
  12.0 6.4 slice_dynamic-update-slice_fusion
  45.5 6.5 split.2
  89.5 36.5 %collective-permute-done.2 = bf16[384,1792]{1,0:T(8,128)(2,1)} collective-permute-done((bf16[384,1792]{1,0:T(8,128)(2,1)}, bf16[384,1792]{1,0:T(8,128)(2,1)}, u32[]{:S(2)}, u32[]{:S(2)}) %collective-permute-start.2) | collective-permute-done | bytes 1376288 | tf_op jit(solution)/shard_map/ppermute | solution.py:59
  136.5 7.2 collective-permute-done.4
  149.7 11.8 fusion.65.qkv_ref
  161.5 17.0 shard_map.143
  186.6 6.2 fusion.91
  208.3 85.4 %collective-permute-done.9 = bf16[384,4480]{1,0:T(8,128)(2,1)} collective-permute-done((bf16[384,4480]{1,0:T(8,128)(2,1)}, bf16[384,4480]{1,0:T(8,128)(2,1)}, u32[]{:S(2)}, u32[]{:S(2)}) %collective-permute-start.9) | collective-permute-done | bytes 3440672 | tf_op jit(solution)/shard_map/ppermute | solution.py:59
  301.0 43.1 %collective-permute-done.10 = bf16[384,4480]{1,0:T(8,128)(2,1)S(1)} collective-permute-done((bf16[384,4480]{1,0:T(8,128)(2,1)}, bf16[384,4480]{1,0:T(8,128)(2,1)S(1)}, u32[]{:S(2)}, u32[]{:S(2)}) %collective-permute-start.10) | collective-permute-done | bytes 3440672 | tf_op jit(solution)/shard_map/ppermute | solution.py:59
  354.4 26.7 %collective-permute-done.15 = bf16[560,1536]{1,0:T(8,128)(2,1)} collective-permute-done((bf16[560,1536]{1,0:T(8,128)(2,1)}, bf16[560,1536]{1,0:T(8,128)(2,1)}, u32[]{:S(2)}, u32[]{:S(2)}) %collective-permute-start.15) | collective-permute-done | bytes 1720352 | tf_op jit(solution)/shard_map/ppermute | solution.py:59
  388.5 27.8 %collective-permute-done.11 = bf16[192,4480]{1,0:T(8,128)(2,1)} collective-permute-done((bf16[192,4480]{1,0:T(8,128)(2,1)}, bf16[192,4480]{1,0:T(8,128)(2,1)}, u32[]{:S(2)}, u32[]{:S(2)}) %collective-permute-start.11) | collective-permute-done | bytes 1720352 | tf_op jit(solution)/shard_map/ppermute | solution.py:59
  419.1 6.3 collective-permute-done.12
  426.7 51.7 %multiply_add_fusion.2 = (f32[2048,4480]{1,0:T(8,128)}, bf16[2048,4480]{1,0:T(8,128)(2,1)}) fusion(bf16[1536,4480]{1,0:T(8,128)(2,1)} %bitcast.192, bf16[1024,1536]{1,0:T(8,128)(2,1)} %collective-permute-done.7, bf16[1024,1536]{1,0:T(8,128)(2,1)S(1)} %fusion.32), kind=kOutput, calls=%fused_computation.6 | convolution fusion | flops 28326756352 | bytes 75104256 | tf_op jit(solution)/shard_map/dot_general | solution.py:39
  478.4 21.5 %fusion.16 = f32[1024,1536]{1,0:T(8,128)} fusion(bf16[4480,1536]{1,0:T(8,128)(2,1)} %bitcast.203, bf16[2048,4480]{1,0:T(8,128)(2,1)} %get-tuple-element.44), kind=kOutput, calls=%fused_computation.40 | convolution fusion | flops 14092861440 | bytes 29229056 | tf_op jit(solution)/shard_map/dot_general | solution.py:39
  507.0 6.7 split.3
  517.7 21.5 %fusion.18 = f32[1024,1536]{1,0:T(8,128)} fusion(bf16[4480,1536]{1,0:T(8,128)(2,1)} %bitcast.204, bf16[2048,4480]{1,0:T(8,128)(2,1)} %get-tuple-element.44), kind=kOutput, calls=%fused_computation.42 | convolution fusion | flops 14092861440 | bytes 29229056 | tf_op jit(solution)/shard_map/dot_general | solution.py:39
  541.3 6.0 fusion.35
  554.1 21.4 %collective-permute-done.20 = bf16[384,1792]{1,0:T(8,128)(2,1)S(1)} collective-permute-done((bf16[384,1792]{1,0:T(8,128)(2,1)}, bf16[384,1792]{1,0:T(8,128)(2,1)S(1)}, u32[]{:S(2)}, u32[]{:S(2)}) %collective-permute-start.20) | collective-permute-done | bytes 1376288 | tf_op jit(solution)/shard_map/ppermute | solution.py:59
  578.1 13.9 collective-permute-done.22
  597.6 9.7 fusion.66.qkv_ref
  607.2 17.3 shard_map.144
  624.5 7.4 fusion.84
  649.9 17.3 collective-permute-done.27
  678.1 6.2 fusion.86
  684.3 5.8 fusion.28
  697.4 9.8 collective-permute-done.29
  714.9 52.0 %multiply_add_fusion = (f32[2048,4480]{1,0:T(8,128)}, bf16[2048,4480]{1,0:T(8,128)(2,1)}) fusion(bf16[1536,4480]{1,0:T(8,128)(2,1)} %bitcast.199, bf16[1024,1536]{1,0:T(8,128)(2,1)} %copy-done.94, bf16[1024,1536]{1,0:T(8,128)(2,1)} %copy-done.24), kind=kOutput, calls=%fused_computation.2 | convolution fusion | flops 28326756352 | bytes 75104256 | tf_op jit(solution)/shard_map/dot_general | solution.py:39
  766.9 40.8 %multiply_convert_fusion.1 = bf16[2048,4480]{1,0:T(8,128)(2,1)} fusion(f32[2048,4480]{1,0:T(8,128)} %get-tuple-element.50, bf16[4480,1536]{1,0:T(8,128)(2,1)} %bitcast.196, bf16[1024,1536]{1,0:T(8,128)(2,1)} %collective-permute-done.35, bf16[1024,1536]{1,0:T(8,128)(2,1)S(1)} %bitcast.208), kind=kOutput, calls=%fused_computation.1 | convolution fusion | flops 28216655872 | bytes 75104256 | tf_op jit(solution)/shard_map/dot_general | solution.py:39
  807.7 21.6 %fusion.8 = f32[1024,1536]{1,0:T(8,128)} fusion(bf16[1536,4480]{1,0:T(8,128)(2,1)} %bitcast.200, bf16[2048,4480]{1,0:T(8,128)(2,1)} %multiply_convert_fusion.1), kind=kOutput, calls=%fused_computation.32 | convolution fusion | flops 14092861440 | bytes 29229056 | tf_op jit(solution)/shard_map/dot_general | solution.py:39
  829.2 19.2 fusion.10
  853.4 5.3 collective-permute-done.37
  860.3 10.0 fusion.67.d_o_ref
  870.3 28.0 %shard_map.145 = bf16[2048,1024]{1,0:T(8,128)(2,1)} custom-call(bf16[2048,1024]{1,0:T(8,128)(2,1)} %fusion.66.qkv_ref, bf16[2048,768]{1,0:T(8,128)(2,1)} %fusion.67.d_o_ref), custom_call_target="tpu_custom_call" | custom-call | flops 40000000000 | tf_op jit(solution)/shard_map/pallas_call | solution.py:172
  898.4 6.1 fusion.69
  904.9 5.5 fusion.71
  920.9 10.4 fusion.59
  931.4 41.6 %multiply_convert_fusion = bf16[2048,4480]{1,0:T(8,128)(2,1)} fusion(f32[2048,4480]{1,0:T(8,128)} %get-tuple-element.56, bf16[4480,1536]{1,0:T(8,128)(2,1)} %bitcast.205, bf16[1024,1536]{1,0:T(8,128)(2,1)} %collective-permute-done.40, bf16[1024,1536]{1,0:T(8,128)(2,1)S(1)} %fusion.23), kind=kOutput, calls=%fused_computation | convolution fusion | flops 28216655872 | bytes 75104256 | tf_op jit(solution)/shard_map/dot_general | solution.py:39
  973.0 21.8 %fusion.4 = f32[1024,1536]{1,0:T(8,128)} fusion(bf16[1536,4480]{1,0:T(8,128)(2,1)} %bitcast.193, bf16[2048,4480]{1,0:T(8,128)(2,1)} %multiply_convert_fusion), kind=kOutput, calls=%fused_computation.28 | convolution fusion | flops 14092861440 | bytes 29229056 | tf_op jit(solution)/shard_map/dot_general | solution.py:39
  995.2 8.9 fusion.61
  1004.2 19.4 %fusion.6 = f32[1024,1536]{1,0:T(8,128)S(1)} fusion(bf16[1536,4480]{1,0:T(8,128)(2,1)} %bitcast.194, bf16[2048,4480]{1,0:T(8,128)(2,1)} %multiply_convert_fusion), kind=kOutput, calls=%fused_computation.30 | convolution fusion | flops 14092861440 | bytes 29229056 | tf_op jit(solution)/shard_map/dot_general | solution.py:39
  1032.6 5.6 collective-permute-done.42
  1038.3 6.9 fusion.57
  1045.2 9.4 fusion.68.d_o_ref
  1054.6 28.1 %shard_map.146 = bf16[2048,1024]{1,0:T(8,128)(2,1)} custom-call(bf16[2048,1024]{1,0:T(8,128)(2,1)} %fusion.65.qkv_ref, bf16[2048,768]{1,0:T(8,128)(2,1)} %fusion.68.d_o_ref), custom_call_target="tpu_custom_call" | custom-call | flops 40000000000 | tf_op jit(solution)/shard_map/pallas_call | solution.py:172
  1082.7 11.9 fusion.63
  1097.2 9.5 fusion.74
  1106.6 11.2 flip.2.up_ref
  1120.7 11.0 flip.3.up_ref
  1138.9 6.1 fusion.76
  1145.1 7.1 fusion.56
  1156.7 8.5 fusion.27
  1170.2 205.6 %reduce-scatter.5.cloned.1.call-done = f32[384,1024]{1,0:T(8,128)} async-done(((f32[1536,1024]{1,0:T(8,128)}), f32[384,1024]{1,0:T(8,128)}) %reduce-scatter.5.cloned.1.call-update) | async-done | bytes 1572880 | tf_op jit(solution)/shard_map/reduce_scatter | solution.py:107
  1377.1 138.4 %mlp_grads.2 = (f32[2,1120,1536]{2,1,0:T(8,128)}, f32[192,1120]{1,0:T(8,128)}, f32[192,1120]{1,0:T(8,128)}, f32[192,1120]{1,0:T(8,128)}, f32[192,1120]{1,0:T(8,1...) custom-call(s32[2]{0:T(128)} %pad_add_fusion.place_ref, ...), custom_call_target="tpu_custom_call" | custom-call | flops 112742891520 | tf_op jit(solution)/shard_map/mlp_grads/pallas_call | solution.py:262
  1522.8 114.3 %all-gather.7.cloned.1.call-done.grad_ref = bf16[8192,1536]{1,0:T(8,128)(2,1)} async-done(((bf16[1024,1536]{1,0:T(8,128)(2,1)}), bf16[8192,1536]{1,0:T(8,128)(2,1)}) %all-gather.7.cloned.1.call-update) | async-done | bytes 25165840 | tf_op jit(solution)/shard_map/all_gather | solution.py:103
  1637.1 138.4 %mlp_grads.3 = (f32[2,1120,1536]{2,1,0:T(8,128)}, f32[192,1120]{1,0:T(8,128)}, f32[192,1120]{1,0:T(8,128)}, f32[192,1120]{1,0:T(8,128)}, f32[192,1120]{1,0:T(8,1...) custom-call(s32[2]{0:T(128)} %pad_add_fusion.place_ref, ...), custom_call_target="tpu_custom_call", output_to_operand_aliasing={{0}: (5, {})} | custom-call | flops 112742891520 | tf_op jit(solution)/shard_map/mlp_grads/pallas_call | solution.py:262
  1777.1 21.5 %fusion.12 = f32[1024,1536]{1,0:T(8,128)} fusion(bf16[4480,1536]{1,0:T(8,128)(2,1)} %bitcast.197, bf16[2048,4480]{1,0:T(8,128)(2,1)} %get-tuple-element.54), kind=kOutput, calls=%fused_computation.36 | convolution fusion | flops 14092861440 | bytes 29229056 | tf_op jit(solution)/shard_map/dot_general | solution.py:39
  1810.1 11.6 collective-permute-done.61.refs_7_
  1821.7 8.2 assemble.2.refs_8_
  1831.4 9.5 collective-permute-done.49.refs_2_
  1841.7 17.9 collective-permute-done.50.refs_3_
  1860.3 21.6 %fusion.14 = f32[1024,1536]{1,0:T(8,128)} fusion(bf16[4480,1536]{1,0:T(8,128)(2,1)} %bitcast.198, bf16[2048,4480]{1,0:T(8,128)(2,1)} %get-tuple-element.54), kind=kOutput, calls=%fused_computation.38 | convolution fusion | flops 14092861440 | bytes 29229056 | tf_op jit(solution)/shard_map/dot_general | solution.py:39
  1881.9 25.8 %collective-permute-done.52.refs_5_ = f32[192,1120]{1,0:T(8,128)S(1)} collective-permute-done((f32[192,1120]{1,0:T(8,128)S(1)}, f32[192,1120]{1,0:T(8,128)S(1)}, u32[]{:S(2)}, u32[]{:S(2)}) %collective-permute-start.52) | collective-permute-done | bytes 860192 | tf_op jit(solution)/shard_map/ppermute | solution.py:285
  1909.8 8.1 assemble.3
  1917.9 8.1 add_convert_fusion
  (487 shorter events, 284.4 us)
Async XLA Ops:
  8.0 1109.9 %reduce-scatter.11.cloned.1.call-start = ((), (), s32[]{:S(2)}) async-start(), calls=%async_computation.11 | async-start | bytes 5898240 | tf_op jit(solution)/shard_map/reduce_scatter | solution.py:107
  18.4 174.4 %collective-permute-start.13 = (bf16[1120,1536]{1,0:T(8,128)(2,1)}, bf16[1120,1536]{1,0:T(8,128)(2,1)}, u32[]{:S(2)}, u32[]{:S(2)}) collective-permute-start(bf16[1120,1536]{1,0:T(8,128)(2,1)} %get-tuple-element.99._.down_ref), channel_id=1, source_target_pairs={{0,2},{2,0},{4,6},{6,4},{1,3},{3,1},{5,7},{7,5}} | collective-permute-start | bytes 10321928 | tf_op jit(solution)/shard_map/ppermute | solution.py:59
  21.8 173.8 %collective-permute-start.14 = (bf16[1120,1536]{1,0:T(8,128)(2,1)}, bf16[1120,1536]{1,0:T(8,128)(2,1)}, u32[]{:S(2)}, u32[]{:S(2)}) collective-permute-start(bf16[1120,1536]{1,0:T(8,128)(2,1)} %get-tuple-element.99._.down_ref), channel_id=1, source_target_pairs={{0,4},{2,6},{4,0},{6,2},{1,5},{3,7},{5,1},{7,3}} | collective-permute-start | bytes 10321928 | tf_op jit(solution)/shard_map/ppermute | solution.py:59
  40.2 36.3 %collective-permute-start.1 = (bf16[192,1792]{1,0:T(8,128)(2,1)}, bf16[192,1792]{1,0:T(8,128)(2,1)}, u32[]{:S(2)}, u32[]{:S(2)}) collective-permute-start(bf16[192,1792]{1,0:T(8,128)(2,1)} %broadcast_select_fusion.10), channel_id=1, source_target_pairs={{0,1},{1,0},{2,3},{3,2},{4,5},{5,4},{6,7},{7,6}} | collective-permute-start | bytes 2064392 | tf_op jit(solution)/shard_map/ppermute | solution.py:55
  44.4 105.3 %collective-permute-start = (bf16[1024,1536]{1,0:T(8,128)(2,1)}, bf16[1024,1536]{1,0:T(8,128)(2,1)}, u32[]{:S(2)}, u32[]{:S(2)}) collective-permute-start(bf16[1024,1536]{1,0:T(8,128)(2,1)} %fusion.54), channel_id=1, source_target_pairs={{0,1},{1,0},{2,3},{3,2},{4,5},{5,4},{6,7},{7,6}} | collective-permute-start | bytes 9437192 | tf_op jit(solution)/shard_map/ppermute | solution.py:55
  52.1 31.3 %collective-permute-start.8 = (bf16[192,4480]{1,0:T(8,128)(2,1)}, bf16[192,4480]{1,0:T(8,128)(2,1)}, u32[]{:S(2)}, u32[]{:S(2)}) collective-permute-start(bf16[192,4480]{1,0:T(8,128)(2,1)} %get-tuple-element.43), channel_id=1, source_target_pairs={{0,1},{1,0},{2,3},{3,2},{4,5},{5,4},{6,7},{7,6}} | collective-permute-start | bytes 5160968 | tf_op jit(solution)/shard_map/ppermute | solution.py:55
  80.2 45.8 %collective-permute-start.2 = (bf16[384,1792]{1,0:T(8,128)(2,1)}, bf16[384,1792]{1,0:T(8,128)(2,1)}, u32[]{:S(2)}, u32[]{:S(2)}) collective-permute-start(bf16[384,1792]{1,0:T(8,128)(2,1)} %pad_maximum_fusion.24._), channel_id=1, source_target_pairs={{0,2},{2,0},{4,6},{6,4},{1,3},{3,1},{5,7},{7,5}} | collective-permute-start | bytes 4128776 | tf_op jit(solution)/shard_map/ppermute | solution.py:59
  83.4 45.5 %collective-permute-start.3 = (bf16[384,1792]{1,0:T(8,128)(2,1)}, bf16[384,1792]{1,0:T(8,128)(2,1)}, u32[]{:S(2)}, u32[]{:S(2)}) collective-permute-start(bf16[384,1792]{1,0:T(8,128)(2,1)} %pad_maximum_fusion.24._), channel_id=1, source_target_pairs={{0,4},{2,6},{4,0},{6,2},{1,5},{3,7},{5,1},{7,3}} | collective-permute-start | bytes 4128776 | tf_op jit(solution)/shard_map/ppermute | solution.py:59
  127.1 16.6 collective-permute-start.4
  130.0 17.2 collective-permute-start.5
  143.8 357.0 %collective-permute-start.31 = (bf16[1120,1536]{1,0:T(8,128)(2,1)}, bf16[1120,1536]{1,0:T(8,128)(2,1)}, u32[]{:S(2)}, u32[]{:S(2)}) collective-permute-start(bf16[1120,1536]{1,0:T(8,128)(2,1)} %slice_bitcast_fusion._.down_ref), channel_id=1, source_target_pairs={{0,2},{2,0},{4,6},{6,4},{1,3},{3,1},{5,7},{7,5}} | collective-permute-start | bytes 10321928 | tf_op jit(solution)/shard_map/ppermute | solution.py:59
  147.2 146.4 %collective-permute-start.9 = (bf16[384,4480]{1,0:T(8,128)(2,1)}, bf16[384,4480]{1,0:T(8,128)(2,1)}, u32[]{:S(2)}, u32[]{:S(2)}) collective-permute-start(bf16[384,4480]{1,0:T(8,128)(2,1)} %pad_maximum_fusion.16._), channel_id=1, source_target_pairs={{0,2},{2,0},{4,6},{6,4},{1,3},{3,1},{5,7},{7,5}} | collective-permute-start | bytes 10321928 | tf_op jit(solution)/shard_map/ppermute | solution.py:59
  183.5 163.4 %collective-permute-start.6 = (f32[1024,1536]{1,0:T(8,128)S(1)}, f32[1024,1536]{1,0:T(8,128)S(1)}, u32[]{:S(2)}, u32[]{:S(2)}) collective-permute-start(f32[1024,1536]{1,0:T(8,128)S(1)} %fusion.89), channel_id=1, source_target_pairs={{0,1},{1,0},{2,3},{3,2},{4,5},{5,4},{6,7},{7,6}} | collective-permute-start | bytes 18874376 | tf_op jit(solution)/shard_map/ppermute | solution.py:55
  192.8 310.7 %collective-permute-start.32 = (bf16[1120,1536]{1,0:T(8,128)(2,1)}, bf16[1120,1536]{1,0:T(8,128)(2,1)}, u32[]{:S(2)}, u32[]{:S(2)}) collective-permute-start(bf16[1120,1536]{1,0:T(8,128)(2,1)} %slice_bitcast_fusion._.down_ref), channel_id=1, source_target_pairs={{0,4},{2,6},{4,0},{6,2},{1,5},{3,7},{5,1},{7,3}} | collective-permute-start | bytes 10321928 | tf_op jit(solution)/shard_map/ppermute | solution.py:59
  195.6 148.5 %collective-permute-start.10 = (bf16[384,4480]{1,0:T(8,128)(2,1)}, bf16[384,4480]{1,0:T(8,128)(2,1)S(1)}, u32[]{:S(2)}, u32[]{:S(2)}) collective-permute-start(bf16[384,4480]{1,0:T(8,128)(2,1)} %pad_maximum_fusion.16._), channel_id=1, source_target_pairs={{0,4},{2,6},{4,0},{6,2},{1,5},{3,7},{5,1},{7,3}} | collective-permute-start | bytes 10321928 | tf_op jit(solution)/shard_map/ppermute | solution.py:59
  293.7 87.4 %collective-permute-start.15 = (bf16[560,1536]{1,0:T(8,128)(2,1)}, bf16[560,1536]{1,0:T(8,128)(2,1)}, u32[]{:S(2)}, u32[]{:S(2)}) collective-permute-start(bf16[560,1536]{1,0:T(8,128)(2,1)} %slice.310), channel_id=1, source_target_pairs={{0,4},{2,6},{4,0},{6,2},{1,5},{3,7},{5,1},{7,3}} | collective-permute-start | bytes 5160968 | tf_op jit(solution)/shard_map/ppermute | solution.py:59
  344.0 41.3 %collective-permute-start.16 = (bf16[560,1536]{1,0:T(8,128)(2,1)}, bf16[560,1536]{1,0:T(8,128)(2,1)}, u32[]{:S(2)}, u32[]{:S(2)}) collective-permute-start(bf16[560,1536]{1,0:T(8,128)(2,1)} %slice.311), channel_id=1, source_target_pairs={{0,2},{2,0},{4,6},{6,4},{1,3},{3,1},{5,7},{7,5}} | collective-permute-start | bytes 5160968 | tf_op jit(solution)/shard_map/ppermute | solution.py:59
  346.9 69.4 %collective-permute-start.11 = (bf16[192,4480]{1,0:T(8,128)(2,1)}, bf16[192,4480]{1,0:T(8,128)(2,1)}, u32[]{:S(2)}, u32[]{:S(2)}) collective-permute-start(bf16[192,4480]{1,0:T(8,128)(2,1)} %slice.308), channel_id=1, source_target_pairs={{0,4},{2,6},{4,0},{6,2},{1,5},{3,7},{5,1},{7,3}} | collective-permute-start | bytes 5160968 | tf_op jit(solution)/shard_map/ppermute | solution.py:59
  381.0 45.7 %collective-permute-start.7 = (bf16[1024,1536]{1,0:T(8,128)(2,1)S(1)}, bf16[1024,1536]{1,0:T(8,128)(2,1)}, u32[]{:S(2)}, u32[]{:S(2)}) collective-permute-start(bf16[1024,1536]{1,0:T(8,128)(2,1)S(1)} %fusion.32), channel_id=1, source_target_pairs={{0,1},{1,0},{2,3},{3,2},{4,5},{5,4},{6,7},{7,6}} | collective-permute-start | bytes 9437192 | tf_op jit(solution)/shard_map/ppermute | solution.py:55
  385.4 40.0 %collective-permute-start.12 = (bf16[192,4480]{1,0:T(8,128)(2,1)S(1)}, bf16[192,4480]{1,0:T(8,128)(2,1)S(1)}, u32[]{:S(2)}, u32[]{:S(2)}) collective-permute-start(bf16[192,4480]{1,0:T(8,128)(2,1)S(1)} %slice.309), channel_id=1, source_target_pairs={{0,2},{2,0},{4,6},{6,4},{1,3},{3,1},{5,7},{7,5}} | collective-permute-start | bytes 5160968 | tf_op jit(solution)/shard_map/ppermute | solution.py:59
  500.0 39.3 %collective-permute-start.17 = (f32[1024,1536]{1,0:T(8,128)}, f32[1024,1536]{1,0:T(8,128)}, u32[]{:S(2)}, u32[]{:S(2)}) collective-permute-start(f32[1024,1536]{1,0:T(8,128)} %fusion.16), channel_id=1, source_target_pairs={{0,1},{1,0},{2,3},{3,2},{4,5},{5,4},{6,7},{7,6}} | collective-permute-start | bytes 18874376 | tf_op jit(solution)/shard_map/ppermute | solution.py:55
  500.2 13.5 collective-permute-start.19
  503.5 136.3 %collective-permute-start.33 = (bf16[560,1536]{1,0:T(8,128)(2,1)}, bf16[560,1536]{1,0:T(8,128)(2,1)}, u32[]{:S(2)}, u32[]{:S(2)}) collective-permute-start(bf16[560,1536]{1,0:T(8,128)(2,1)} %slice.328), channel_id=1, source_target_pairs={{0,4},{2,6},{4,0},{6,2},{1,5},{3,7},{5,1},{7,3}} | collective-permute-start | bytes 5160968 | tf_op jit(solution)/shard_map/ppermute | solution.py:59
  506.3 136.9 %collective-permute-start.34 = (bf16[560,1536]{1,0:T(8,128)(2,1)}, bf16[560,1536]{1,0:T(8,128)(2,1)}, u32[]{:S(2)}, u32[]{:S(2)}) collective-permute-start(bf16[560,1536]{1,0:T(8,128)(2,1)} %slice.329), channel_id=1, source_target_pairs={{0,2},{2,0},{4,6},{6,4},{1,3},{3,1},{5,7},{7,5}} | collective-permute-start | bytes 5160968 | tf_op jit(solution)/shard_map/ppermute | solution.py:59
  513.7 34.2 %collective-permute-start.26 = (bf16[192,4480]{1,0:T(8,128)(2,1)}, bf16[192,4480]{1,0:T(8,128)(2,1)}, u32[]{:S(2)}, u32[]{:S(2)}) collective-permute-start(bf16[192,4480]{1,0:T(8,128)(2,1)} %get-tuple-element.48), channel_id=1, source_target_pairs={{0,1},{1,0},{2,3},{3,2},{4,5},{5,4},{6,7},{7,6}} | collective-permute-start | bytes 5160968 | tf_op jit(solution)/shard_map/ppermute | solution.py:55
  515.3 60.1 %collective-permute-start.20 = (bf16[384,1792]{1,0:T(8,128)(2,1)}, bf16[384,1792]{1,0:T(8,128)(2,1)S(1)}, u32[]{:S(2)}, u32[]{:S(2)}) collective-permute-start(bf16[384,1792]{1,0:T(8,128)(2,1)} %pad_maximum_fusion.25._), channel_id=1, source_target_pairs={{0,2},{2,0},{4,6},{6,4},{1,3},{3,1},{5,7},{7,5}} | collective-permute-start | bytes 4128776 | tf_op jit(solution)/shard_map/ppermute | solution.py:59
  539.3 38.0 %collective-permute-start.21 = (bf16[384,1792]{1,0:T(8,128)(2,1)}, bf16[384,1792]{1,0:T(8,128)(2,1)S(1)}, u32[]{:S(2)}, u32[]{:S(2)}) collective-permute-start(bf16[384,1792]{1,0:T(8,128)(2,1)} %pad_maximum_fusion.25._), channel_id=1, source_target_pairs={{0,4},{2,6},{4,0},{6,2},{1,5},{3,7},{5,1},{7,3}} | collective-permute-start | bytes 4128776 | tf_op jit(solution)/shard_map/ppermute | solution.py:59
  547.9 46.1 %collective-permute-start.18 = (bf16[1024,1536]{1,0:T(8,128)(2,1)S(1)}, bf16[1024,1536]{1,0:T(8,128)(2,1)S(1)}, u32[]{:S(2)}, u32[]{:S(2)}) collective-permute-start(bf16[1024,1536]{1,0:T(8,128)(2,1)S(1)} %fusion.36), channel_id=1, source_target_pairs={{0,1},{1,0},{2,3},{3,2},{4,5},{5,4},{6,7},{7,6}} | collective-permute-start | bytes 9437192 | tf_op jit(solution)/shard_map/ppermute | solution.py:55
  575.5 16.5 collective-permute-start.22
  577.3 16.1 collective-permute-start.23
  592.0 75.1 %collective-permute-start.27 = (bf16[384,4480]{1,0:T(8,128)(2,1)}, bf16[384,4480]{1,0:T(8,128)(2,1)}, u32[]{:S(2)}, u32[]{:S(2)}) collective-permute-start(bf16[384,4480]{1,0:T(8,128)(2,1)} %pad_maximum_fusion.17._), channel_id=1, source_target_pairs={{0,2},{2,0},{4,6},{6,4},{1,3},{3,1},{5,7},{7,5}} | collective-permute-start | bytes 10321928 | tf_op jit(solution)/shard_map/ppermute | solution.py:59
  593.4 77.5 %collective-permute-start.28 = (bf16[384,4480]{1,0:T(8,128)(2,1)}, bf16[384,4480]{1,0:T(8,128)(2,1)}, u32[]{:S(2)}, u32[]{:S(2)}) collective-permute-start(bf16[384,4480]{1,0:T(8,128)(2,1)} %pad_maximum_fusion.17._), channel_id=1, source_target_pairs={{0,4},{2,6},{4,0},{6,2},{1,5},{3,7},{5,1},{7,3}} | collective-permute-start | bytes 10321928 | tf_op jit(solution)/shard_map/ppermute | solution.py:59
  631.9 52.4 %collective-permute-start.24 = (f32[1024,1536]{1,0:T(8,128)}, f32[1024,1536]{1,0:T(8,128)}, u32[]{:S(2)}, u32[]{:S(2)}) collective-permute-start(f32[1024,1536]{1,0:T(8,128)} %fusion.84), channel_id=1, source_target_pairs={{0,1},{1,0},{2,3},{3,2},{4,5},{5,4},{6,7},{7,6}} | collective-permute-start | bytes 18874376 | tf_op jit(solution)/shard_map/ppermute | solution.py:55
  639.8 127.1 %collective-permute-start.35 = (bf16[1024,1536]{1,0:T(8,128)(2,1)}, bf16[1024,1536]{1,0:T(8,128)(2,1)}, u32[]{:S(2)}, u32[]{:S(2)}) collective-permute-start(bf16[1024,1536]{1,0:T(8,128)(2,1)} %bitcast.206), channel_id=1, source_target_pairs={{0,1},{1,0},{2,3},{3,2},{4,5},{5,4},{6,7},{7,6}} | collective-permute-start | bytes 9437192 | tf_op jit(solution)/shard_map/ppermute | solution.py:55
  669.9 37.4 %collective-permute-start.29 = (bf16[192,4480]{1,0:T(8,128)(2,1)}, bf16[192,4480]{1,0:T(8,128)(2,1)}, u32[]{:S(2)}, u32[]{:S(2)}) collective-permute-start(bf16[192,4480]{1,0:T(8,128)(2,1)} %slice.326), channel_id=1, source_target_pairs={{0,4},{2,6},{4,0},{6,2},{1,5},{3,7},{5,1},{7,3}} | collective-permute-start | bytes 5160968 | tf_op jit(solution)/shard_map/ppermute | solution.py:59
  673.7 36.8 %collective-permute-start.30 = (bf16[192,4480]{1,0:T(8,128)(2,1)}, bf16[192,4480]{1,0:T(8,128)(2,1)}, u32[]{:S(2)}, u32[]{:S(2)}) collective-permute-start(bf16[192,4480]{1,0:T(8,128)(2,1)} %slice.327), channel_id=1, source_target_pairs={{0,2},{2,0},{4,6},{6,4},{1,3},{3,1},{5,7},{7,5}} | collective-permute-start | bytes 5160968 | tf_op jit(solution)/shard_map/ppermute | solution.py:59
  692.3 21.0 %collective-permute-start.25 = (bf16[1024,1536]{1,0:T(8,128)(2,1)S(1)}, bf16[1024,1536]{1,0:T(8,128)(2,1)S(1)}, u32[]{:S(2)}, u32[]{:S(2)}) collective-permute-start(bf16[1024,1536]{1,0:T(8,128)(2,1)S(1)} %fusion.29), channel_id=1, source_target_pairs={{0,1},{1,0},{2,3},{3,2},{4,5},{5,4},{6,7},{7,6}} | collective-permute-start | bytes 9437192 | tf_op jit(solution)/shard_map/ppermute | solution.py:55
  829.2 19.3 collective-permute-start.36
  931.3 188.0 %reduce-scatter.7.cloned.1.call-start = ((), (), s32[]{:S(2)}) async-start(), calls=%async_computation.9 | async-start | bytes 7864320 | tf_op jit(solution)/shard_map/reduce_scatter | solution.py:107
  994.8 28.8 %collective-permute-start.41 = (f32[1024,1536]{1,0:T(8,128)}, f32[1024,1536]{1,0:T(8,128)}, u32[]{:S(2)}, u32[]{:S(2)}) collective-permute-start(f32[1024,1536]{1,0:T(8,128)} %fusion.4), channel_id=1, source_target_pairs={{0,1},{1,0},{2,3},{3,2},{4,5},{5,4},{6,7},{7,6}} | collective-permute-start | bytes 18874376 | tf_op jit(solution)/shard_map/ppermute | solution.py:55
  1004.1 151.4 %reduce-scatter.9.cloned.1.call-start = ((), (), s32[]{:S(2)}) async-start(), calls=%async_computation.10 | async-start | bytes 5898240 | tf_op jit(solution)/shard_map/reduce_scatter | solution.py:107
  1045.2 330.6 %reduce-scatter.5.cloned.1.call-start = ((), (), s32[]{:S(2)}) async-start(), calls=%async_computation.8 | async-start | bytes 7864320 | tf_op jit(solution)/shard_map/reduce_scatter | solution.py:107
  1094.7 282.4 %all-gather.11.cloned.1.call-start = ((), (), s32[]{:S(2)}) async-start(), calls=%async_computation.7 | async-start | bytes 28311552 | tf_op jit(solution)/shard_map/all_gather | solution.py:103
  1095.3 281.8 %all-gather.9.cloned.1.call-start = ((), (), s32[]{:S(2)}) async-start(), calls=%async_computation.6 | async-start | bytes 28311552 | tf_op jit(solution)/shard_map/all_gather | solution.py:103
  1095.8 427.0 %all-gather.5.cloned.1.call-start = ((), (), s32[]{:S(2)}) async-start(), calls=%async_computation.4 | async-start | bytes 28311552 | tf_op jit(solution)/shard_map/all_gather | solution.py:103
  1096.4 540.7 %all-gather.7.cloned.1.call-start = ((), (), s32[]{:S(2)}) async-start(), calls=%async_computation.5 | async-start | bytes 28311552 | tf_op jit(solution)/shard_map/all_gather | solution.py:103
  1106.6 38.4 %collective-permute-start.43 = (f32[1024,1536]{1,0:T(8,128)}, f32[1024,1536]{1,0:T(8,128)}, u32[]{:S(2)}, u32[]{:S(2)}) collective-permute-start(f32[1024,1536]{1,0:T(8,128)} %fusion.74), channel_id=1, source_target_pairs={{0,1},{1,0},{2,3},{3,2},{4,5},{5,4},{6,7},{7,6}} | collective-permute-start | bytes 18874376 | tf_op jit(solution)/shard_map/ppermute | solution.py:55
  1120.5 13.9 collective-permute-start.45
  1377.0 141.8 %collective-permute-start.44 = (f32[192,1024]{1,0:T(8,128)S(1)}, f32[192,1024]{1,0:T(8,128)}, u32[]{:S(2)}, u32[]{:S(2)}) collective-permute-start(f32[192,1024]{1,0:T(8,128)S(1)} %dynamic-slice_bitcast_fusion.1), channel_id=1, source_target_pairs={{0,1},{1,0},{2,3},{3,2},{4,5},{5,4},{6,7},{7,6}} | collective-permute-start | bytes 2359304 | tf_op jit(solution)/shard_map/ppermute | solution.py:55
  1515.4 260.1 %collective-permute-start.55 = (f32[192,1120]{1,0:T(8,128)}, f32[192,1120]{1,0:T(8,128)S(1)}, u32[]{:S(2)}, u32[]{:S(2)}) collective-permute-start(f32[192,1120]{1,0:T(8,128)} %get-tuple-element.66), channel_id=1, source_target_pairs={{0,1},{1,0},{2,3},{3,2},{4,5},{5,4},{6,7},{7,6}} | collective-permute-start | bytes 2580488 | tf_op jit(solution)/shard_map/ppermute | solution.py:285
  1515.7 282.9 %collective-permute-start.56 = (f32[192,1120]{1,0:T(8,128)}, f32[192,1120]{1,0:T(8,128)}, u32[]{:S(2)}, u32[]{:S(2)}) collective-permute-start(f32[192,1120]{1,0:T(8,128)} %get-tuple-element.67), channel_id=1, source_target_pairs={{0,2},{1,3},{2,0},{3,1},{4,6},{5,7},{6,4},{7,5}} | collective-permute-start | bytes 2580488 | tf_op jit(solution)/shard_map/ppermute | solution.py:285
  1517.2 282.5 %collective-permute-start.57 = (f32[192,1120]{1,0:T(8,128)}, f32[192,1120]{1,0:T(8,128)}, u32[]{:S(2)}, u32[]{:S(2)}) collective-permute-start(f32[192,1120]{1,0:T(8,128)} %get-tuple-element.68), channel_id=1, source_target_pairs={{0,3},{1,2},{2,1},{3,0},{4,7},{5,6},{6,5},{7,4}} | collective-permute-start | bytes 2580488 | tf_op jit(solution)/shard_map/ppermute | solution.py:285
  1517.3 284.4 %collective-permute-start.58 = (f32[192,1120]{1,0:T(8,128)}, f32[192,1120]{1,0:T(8,128)}, u32[]{:S(2)}, u32[]{:S(2)}) collective-permute-start(f32[192,1120]{1,0:T(8,128)} %get-tuple-element.69), channel_id=1, source_target_pairs={{0,4},{1,5},{2,6},{3,7},{4,0},{5,1},{6,2},{7,3}} | collective-permute-start | bytes 2580488 | tf_op jit(solution)/shard_map/ppermute | solution.py:285
  1518.8 283.0 %collective-permute-start.59 = (f32[192,1120]{1,0:T(8,128)}, f32[192,1120]{1,0:T(8,128)}, u32[]{:S(2)}, u32[]{:S(2)}) collective-permute-start(f32[192,1120]{1,0:T(8,128)} %get-tuple-element.70), channel_id=1, source_target_pairs={{0,5},{1,4},{2,7},{3,6},{4,1},{5,0},{6,3},{7,2}} | collective-permute-start | bytes 2580488 | tf_op jit(solution)/shard_map/ppermute | solution.py:285
  1775.6 27.6 %collective-permute-start.60 = (f32[192,1120]{1,0:T(8,128)}, f32[192,1120]{1,0:T(8,128)S(1)}, u32[]{:S(2)}, u32[]{:S(2)}) collective-permute-start(f32[192,1120]{1,0:T(8,128)} %get-tuple-element.71), channel_id=1, source_target_pairs={{0,6},{1,7},{2,4},{3,5},{4,2},{5,3},{6,0},{7,1}} | collective-permute-start | bytes 2580488 | tf_op jit(solution)/shard_map/ppermute | solution.py:285
  1798.6 23.0 %collective-permute-start.61 = (f32[192,1120]{1,0:T(8,128)}, f32[192,1120]{1,0:T(8,128)}, u32[]{:S(2)}, u32[]{:S(2)}) collective-permute-start(f32[192,1120]{1,0:T(8,128)} %get-tuple-element.72), channel_id=1, source_target_pairs={{0,7},{1,6},{2,5},{3,4},{4,3},{5,2},{6,1},{7,0}} | collective-permute-start | bytes 2580488 | tf_op jit(solution)/shard_map/ppermute | solution.py:285
  1799.7 118.2 %collective-permute-start.39 = (f32[1024,1536]{1,0:T(8,128)}, f32[1024,1536]{1,0:T(8,128)}, u32[]{:S(2)}, u32[]{:S(2)}) collective-permute-start(f32[1024,1536]{1,0:T(8,128)} %fusion.12), channel_id=1, source_target_pairs={{0,1},{1,0},{2,3},{3,2},{4,5},{5,4},{6,7},{7,6}} | collective-permute-start | bytes 18874376 | tf_op jit(solution)/shard_map/ppermute | solution.py:55
  1801.7 29.7 %collective-permute-start.48 = (f32[192,1120]{1,0:T(8,128)}, f32[192,1120]{1,0:T(8,128)}, u32[]{:S(2)}, u32[]{:S(2)}) collective-permute-start(f32[192,1120]{1,0:T(8,128)} %get-tuple-element.58), channel_id=1, source_target_pairs={{0,1},{1,0},{2,3},{3,2},{4,5},{5,4},{6,7},{7,6}} | collective-permute-start | bytes 2580488 | tf_op jit(solution)/shard_map/ppermute | solution.py:285
  1801.8 39.2 %collective-permute-start.49 = (f32[192,1120]{1,0:T(8,128)}, f32[192,1120]{1,0:T(8,128)}, u32[]{:S(2)}, u32[]{:S(2)}) collective-permute-start(f32[192,1120]{1,0:T(8,128)} %get-tuple-element.59), channel_id=1, source_target_pairs={{0,2},{1,3},{2,0},{3,1},{4,6},{5,7},{6,4},{7,5}} | collective-permute-start | bytes 2580488 | tf_op jit(solution)/shard_map/ppermute | solution.py:285
  1803.2 56.4 %collective-permute-start.50 = (f32[192,1120]{1,0:T(8,128)}, f32[192,1120]{1,0:T(8,128)}, u32[]{:S(2)}, u32[]{:S(2)}) collective-permute-start(f32[192,1120]{1,0:T(8,128)} %get-tuple-element.60), channel_id=1, source_target_pairs={{0,3},{1,2},{2,1},{3,0},{4,7},{5,6},{6,5},{7,4}} | collective-permute-start | bytes 2580488 | tf_op jit(solution)/shard_map/ppermute | solution.py:285
  1829.9 52.0 %collective-permute-start.51 = (f32[192,1120]{1,0:T(8,128)S(1)}, f32[192,1120]{1,0:T(8,128)S(1)}, u32[]{:S(2)}, u32[]{:S(2)}) collective-permute-start(f32[192,1120]{1,0:T(8,128)S(1)} %copy-done.98), channel_id=1, source_target_pairs={{0,4},{1,5},{2,6},{3,7},{4,0},{5,1},{6,2},{7,3}} | collective-permute-start | bytes 2580488 | tf_op jit(solution)/shard_map/ppermute | solution.py:285
  1831.4 76.2 %collective-permute-start.52 = (f32[192,1120]{1,0:T(8,128)S(1)}, f32[192,1120]{1,0:T(8,128)S(1)}, u32[]{:S(2)}, u32[]{:S(2)}) collective-permute-start(f32[192,1120]{1,0:T(8,128)S(1)} %copy-done.97), channel_id=1, source_target_pairs={{0,5},{1,4},{2,7},{3,6},{4,1},{5,0},{6,3},{7,2}} | collective-permute-start | bytes 2580488 | tf_op jit(solution)/shard_map/ppermute | solution.py:285
  1840.9 66.7 %collective-permute-start.53 = (f32[192,1120]{1,0:T(8,128)S(1)}, f32[192,1120]{1,0:T(8,128)S(1)}, u32[]{:S(2)}, u32[]{:S(2)}) collective-permute-start(f32[192,1120]{1,0:T(8,128)S(1)} %copy-done.96), channel_id=1, source_target_pairs={{0,6},{1,7},{2,4},{3,5},{4,2},{5,3},{6,0},{7,1}} | collective-permute-start | bytes 2580488 | tf_op jit(solution)/shard_map/ppermute | solution.py:285
  1859.6 48.0 %collective-permute-start.54 = (f32[192,1120]{1,0:T(8,128)S(1)}, f32[192,1120]{1,0:T(8,128)S(1)}, u32[]{:S(2)}, u32[]{:S(2)}) collective-permute-start(f32[192,1120]{1,0:T(8,128)S(1)} %copy-done.95), channel_id=1, source_target_pairs={{0,7},{1,6},{2,5},{3,4},{4,3},{5,2},{6,1},{7,0}} | collective-permute-start | bytes 2580488 | tf_op jit(solution)/shard_map/ppermute | solution.py:285
  (112 other events, 1515.9 us)
Sparse Core Ops, SparseCore 0:
  931.4 51.3 reduce-scatter.10
  1004.3 64.2 reduce-scatter.6
  1071.5 83.9 reduce-scatter.8
  1158.3 217.4 reduce-scatter.4
Sparse Core Ops, SparseCore 1:
  1097.0 127.3 all-gather.10
  1226.1 134.1 all-gather.8
  1361.9 120.7 all-gather.4
  1484.5 152.6 all-gather.6

commit v6 on v5

--- a/solution.py
+++ b/solution.py
@@ -341,10 +341,10 @@
 
 def flip_kernel(place_ref, up_ref, out_ref):
     block = out_ref.shape[0]
-    cols = up_ref[:, :block]
-    for i in range(1, CHIPS):
-        cols = jnp.where(place_ref[0] == i, up_ref[:, i * block:(i + 1) * block], cols)
-    out_ref[...] = jnp.transpose(cols.astype(jnp.float32)).astype(jnp.bfloat16)
+    for i in range(CHIPS):
+        @pl.when(place_ref[0] == i)
+        def _():
+            out_ref[...] = jnp.transpose(up_ref[:, i * block:(i + 1) * block])
 
 
 def flip(place, up_weight):

time: 1940 us -> 1940 us (level)
  no operation moved by 1% of the time
where the time goes in v6:
time: 1940 us; the launch traced here: 1930 us
  waiting for transfers between devices  708 us (36%)
  matrix products  485 us (25%)
  Pallas kernels  415 us (21%)
  local copies, waits for them, and re-layouts  171 us (9%)
  other arithmetic  97.9 us (5%)
  starting transfers between devices  39.5 us (2%)
    dot_general x28, matrix products, dot(): lax.dot_general(left, right, (contract, ((), ())), preferred_element_type...  485 us
    ppermute x24, waiting for transfers between devices, hop(): lax.ppermute(value, CHIP, [(chip, chip ^ step) for chip in range(CHIPS)])  298 us
    pallas_call x2, Pallas kernels, mlp_weight_grads(): pl.pallas_call(mlp_grads_kernel, grid_spec=pltpu.PrefetchScalarGridSpec(n...  277 us
    reduce_scatter x4, waiting for transfers between devices, scatter_sum(): return lax.psum_scatter(grad_full, CHIP, scatter_dimension=0, tiled=True)  213 us
    all_gather x4, waiting for transfers between devices, gather_rows(): return functools.partial(lax.all_gather, axis=0, tiled=True)(value, AXES)  114 us
    pallas_call x4, Pallas kernels, by_sequence(): pl.pallas_call(functools.partial(kernel, q_width, head), grid=(rows // se...  90.4 us
    dynamic_update_slice x26, local copies, waits for them, and re-layouts, gather_weight(): full = lax.dynamic_update_slice(full, part[None], (chip ^ step, row, 0))  69.7 us
    ppermute x14, waiting for transfers between devices, exchange(): lax.ppermute(part, AXES, [(d, d ^ i) for d in devices])  64.8 us
  transfers between devices with their start and end apart: 70, of which 24 were waited for; matrix products, arithmetic and copies ran while one was open for 32% of the time, Pallas kernels for 20%

profile of v6, /device:TPU:0, one launch (start us, length us, event | category | flops | bytes accessed | tf_op | source)
XLA Modules:
  0.0 1933.5 jit_solution(2775194806895970431)
XLA Ops:
  12.0 6.4 slice_dynamic-update-slice_fusion
  45.5 6.5 split.2
  89.5 36.5 %collective-permute-done.2 = bf16[384,1792]{1,0:T(8,128)(2,1)} collective-permute-done((bf16[384,1792]{1,0:T(8,128)(2,1)}, bf16[384,1792]{1,0:T(8,128)(2,1)}, u32[]{:S(2)}, u32[]{:S(2)}) %collective-permute-start.2) | collective-permute-done | bytes 1376288 | tf_op jit(solution)/shard_map/ppermute | solution.py:59
  136.5 7.2 collective-permute-done.4
  149.7 11.8 fusion.65.qkv_ref
  161.5 17.0 shard_map.143
  186.6 6.2 fusion.91
  208.3 85.4 %collective-permute-done.9 = bf16[384,4480]{1,0:T(8,128)(2,1)} collective-permute-done((bf16[384,4480]{1,0:T(8,128)(2,1)}, bf16[384,4480]{1,0:T(8,128)(2,1)}, u32[]{:S(2)}, u32[]{:S(2)}) %collective-permute-start.9) | collective-permute-done | bytes 3440672 | tf_op jit(solution)/shard_map/ppermute | solution.py:59
  301.0 43.1 %collective-permute-done.10 = bf16[384,4480]{1,0:T(8,128)(2,1)S(1)} collective-permute-done((bf16[384,4480]{1,0:T(8,128)(2,1)}, bf16[384,4480]{1,0:T(8,128)(2,1)S(1)}, u32[]{:S(2)}, u32[]{:S(2)}) %collective-permute-start.10) | collective-permute-done | bytes 3440672 | tf_op jit(solution)/shard_map/ppermute | solution.py:59
  354.4 26.7 %collective-permute-done.15 = bf16[560,1536]{1,0:T(8,128)(2,1)} collective-permute-done((bf16[560,1536]{1,0:T(8,128)(2,1)}, bf16[560,1536]{1,0:T(8,128)(2,1)}, u32[]{:S(2)}, u32[]{:S(2)}) %collective-permute-start.15) | collective-permute-done | bytes 1720352 | tf_op jit(solution)/shard_map/ppermute | solution.py:59
  388.5 27.8 %collective-permute-done.11 = bf16[192,4480]{1,0:T(8,128)(2,1)} collective-permute-done((bf16[192,4480]{1,0:T(8,128)(2,1)}, bf16[192,4480]{1,0:T(8,128)(2,1)}, u32[]{:S(2)}, u32[]{:S(2)}) %collective-permute-start.11) | collective-permute-done | bytes 1720352 | tf_op jit(solution)/shard_map/ppermute | solution.py:59
  419.1 6.3 collective-permute-done.12
  426.7 51.7 %multiply_add_fusion.2 = (f32[2048,4480]{1,0:T(8,128)}, bf16[2048,4480]{1,0:T(8,128)(2,1)}) fusion(bf16[1536,4480]{1,0:T(8,128)(2,1)} %bitcast.192, bf16[1024,1536]{1,0:T(8,128)(2,1)} %collective-permute-done.7, bf16[1024,1536]{1,0:T(8,128)(2,1)S(1)} %fusion.32), kind=kOutput, calls=%fused_computation.6 | convolution fusion | flops 28326756352 | bytes 75104256 | tf_op jit(solution)/shard_map/dot_general | solution.py:39
  478.4 21.5 %fusion.16 = f32[1024,1536]{1,0:T(8,128)} fusion(bf16[4480,1536]{1,0:T(8,128)(2,1)} %bitcast.203, bf16[2048,4480]{1,0:T(8,128)(2,1)} %get-tuple-element.44), kind=kOutput, calls=%fused_computation.40 | convolution fusion | flops 14092861440 | bytes 29229056 | tf_op jit(solution)/shard_map/dot_general | solution.py:39
  507.0 6.7 split.3
  517.7 21.5 %fusion.18 = f32[1024,1536]{1,0:T(8,128)} fusion(bf16[4480,1536]{1,0:T(8,128)(2,1)} %bitcast.204, bf16[2048,4480]{1,0:T(8,128)(2,1)} %get-tuple-element.44), kind=kOutput, calls=%fused_computation.42 | convolution fusion | flops 14092861440 | bytes 29229056 | tf_op jit(solution)/shard_map/dot_general | solution.py:39
  541.3 6.0 fusion.35
  554.1 21.4 %collective-permute-done.20 = bf16[384,1792]{1,0:T(8,128)(2,1)S(1)} collective-permute-done((bf16[384,1792]{1,0:T(8,128)(2,1)}, bf16[384,1792]{1,0:T(8,128)(2,1)S(1)}, u32[]{:S(2)}, u32[]{:S(2)}) %collective-permute-start.20) | collective-permute-done | bytes 1376288 | tf_op jit(solution)/shard_map/ppermute | solution.py:59
  578.1 13.9 collective-permute-done.22
  597.6 9.7 fusion.66.qkv_ref
  607.2 17.3 shard_map.144
  624.5 7.4 fusion.84
  649.9 17.3 collective-permute-done.27
  678.1 6.2 fusion.86
  684.3 5.8 fusion.28
  697.4 9.8 collective-permute-done.29
  714.9 52.0 %multiply_add_fusion = (f32[2048,4480]{1,0:T(8,128)}, bf16[2048,4480]{1,0:T(8,128)(2,1)}) fusion(bf16[1536,4480]{1,0:T(8,128)(2,1)} %bitcast.199, bf16[1024,1536]{1,0:T(8,128)(2,1)} %copy-done.94, bf16[1024,1536]{1,0:T(8,128)(2,1)} %copy-done.24), kind=kOutput, calls=%fused_computation.2 | convolution fusion | flops 28326756352 | bytes 75104256 | tf_op jit(solution)/shard_map/dot_general | solution.py:39
  766.9 40.8 %multiply_convert_fusion.1 = bf16[2048,4480]{1,0:T(8,128)(2,1)} fusion(f32[2048,4480]{1,0:T(8,128)} %get-tuple-element.50, bf16[4480,1536]{1,0:T(8,128)(2,1)} %bitcast.196, bf16[1024,1536]{1,0:T(8,128)(2,1)} %collective-permute-done.35, bf16[1024,1536]{1,0:T(8,128)(2,1)S(1)} %bitcast.208), kind=kOutput, calls=%fused_computation.1 | convolution fusion | flops 28216655872 | bytes 75104256 | tf_op jit(solution)/shard_map/dot_general | solution.py:39
  807.7 21.6 %fusion.8 = f32[1024,1536]{1,0:T(8,128)} fusion(bf16[1536,4480]{1,0:T(8,128)(2,1)} %bitcast.200, bf16[2048,4480]{1,0:T(8,128)(2,1)} %multiply_convert_fusion.1), kind=kOutput, calls=%fused_computation.32 | convolution fusion | flops 14092861440 | bytes 29229056 | tf_op jit(solution)/shard_map/dot_general | solution.py:39
  829.2 19.2 fusion.10
  860.3 10.0 fusion.67.d_o_ref
  870.3 28.0 %shard_map.145 = bf16[2048,1024]{1,0:T(8,128)(2,1)} custom-call(bf16[2048,1024]{1,0:T(8,128)(2,1)} %fusion.66.qkv_ref, bf16[2048,768]{1,0:T(8,128)(2,1)} %fusion.67.d_o_ref), custom_call_target="tpu_custom_call" | custom-call | flops 40000000000 | tf_op jit(solution)/shard_map/pallas_call | solution.py:172
  898.4 6.1 fusion.69
  904.9 5.5 fusion.71
  920.9 10.4 fusion.59
  931.4 41.6 %multiply_convert_fusion = bf16[2048,4480]{1,0:T(8,128)(2,1)} fusion(f32[2048,4480]{1,0:T(8,128)} %get-tuple-element.56, bf16[4480,1536]{1,0:T(8,128)(2,1)} %bitcast.205, bf16[1024,1536]{1,0:T(8,128)(2,1)} %collective-permute-done.40, bf16[1024,1536]{1,0:T(8,128)(2,1)S(1)} %fusion.23), kind=kOutput, calls=%fused_computation | convolution fusion | flops 28216655872 | bytes 75104256 | tf_op jit(solution)/shard_map/dot_general | solution.py:39
  973.0 21.8 %fusion.4 = f32[1024,1536]{1,0:T(8,128)} fusion(bf16[1536,4480]{1,0:T(8,128)(2,1)} %bitcast.193, bf16[2048,4480]{1,0:T(8,128)(2,1)} %multiply_convert_fusion), kind=kOutput, calls=%fused_computation.28 | convolution fusion | flops 14092861440 | bytes 29229056 | tf_op jit(solution)/shard_map/dot_general | solution.py:39
  995.2 8.9 fusion.61
  1004.2 19.4 %fusion.6 = f32[1024,1536]{1,0:T(8,128)S(1)} fusion(bf16[1536,4480]{1,0:T(8,128)(2,1)} %bitcast.194, bf16[2048,4480]{1,0:T(8,128)(2,1)} %multiply_convert_fusion), kind=kOutput, calls=%fused_computation.30 | convolution fusion | flops 14092861440 | bytes 29229056 | tf_op jit(solution)/shard_map/dot_general | solution.py:39
  1032.6 5.6 collective-permute-done.42
  1038.3 6.9 fusion.57
  1045.2 9.4 fusion.68.d_o_ref
  1054.6 28.1 %shard_map.146 = bf16[2048,1024]{1,0:T(8,128)(2,1)} custom-call(bf16[2048,1024]{1,0:T(8,128)(2,1)} %fusion.65.qkv_ref, bf16[2048,768]{1,0:T(8,128)(2,1)} %fusion.68.d_o_ref), custom_call_target="tpu_custom_call" | custom-call | flops 40000000000 | tf_op jit(solution)/shard_map/pallas_call | solution.py:172
  1082.7 11.9 fusion.63
  1097.2 9.5 fusion.74
  1106.6 9.2 flip.2.up_ref
  1118.7 9.0 flip.3.up_ref
  1134.8 6.1 fusion.76
  1141.0 7.2 fusion.56
  1148.3 7.2 reduce-scatter.9.cloned.1.call-done
  1156.7 8.5 fusion.27
  1170.2 205.6 %reduce-scatter.5.cloned.1.call-done = f32[384,1024]{1,0:T(8,128)} async-done(((f32[1536,1024]{1,0:T(8,128)}), f32[384,1024]{1,0:T(8,128)}) %reduce-scatter.5.cloned.1.call-update) | async-done | bytes 1572880 | tf_op jit(solution)/shard_map/reduce_scatter | solution.py:107
  1377.1 138.4 %mlp_grads.2 = (f32[2,1120,1536]{2,1,0:T(8,128)}, f32[192,1120]{1,0:T(8,128)}, f32[192,1120]{1,0:T(8,128)}, f32[192,1120]{1,0:T(8,128)}, f32[192,1120]{1,0:T(8,1...) custom-call(s32[2]{0:T(128)} %pad_add_fusion.place_ref, ...), custom_call_target="tpu_custom_call" | custom-call | flops 112742891520 | tf_op jit(solution)/shard_map/mlp_grads/pallas_call | solution.py:262
  1522.8 114.3 %all-gather.7.cloned.1.call-done.grad_ref = bf16[8192,1536]{1,0:T(8,128)(2,1)} async-done(((bf16[1024,1536]{1,0:T(8,128)(2,1)}), bf16[8192,1536]{1,0:T(8,128)(2,1)}) %all-gather.7.cloned.1.call-update) | async-done | bytes 25165840 | tf_op jit(solution)/shard_map/all_gather | solution.py:103
  1637.1 138.4 %mlp_grads.3 = (f32[2,1120,1536]{2,1,0:T(8,128)}, f32[192,1120]{1,0:T(8,128)}, f32[192,1120]{1,0:T(8,128)}, f32[192,1120]{1,0:T(8,128)}, f32[192,1120]{1,0:T(8,1...) custom-call(s32[2]{0:T(128)} %pad_add_fusion.place_ref, ...), custom_call_target="tpu_custom_call", output_to_operand_aliasing={{0}: (5, {})} | custom-call | flops 112742891520 | tf_op jit(solution)/shard_map/mlp_grads/pallas_call | solution.py:262
  1777.1 21.5 %fusion.12 = f32[1024,1536]{1,0:T(8,128)} fusion(bf16[4480,1536]{1,0:T(8,128)(2,1)} %bitcast.197, bf16[2048,4480]{1,0:T(8,128)(2,1)} %get-tuple-element.54), kind=kOutput, calls=%fused_computation.36 | convolution fusion | flops 14092861440 | bytes 29229056 | tf_op jit(solution)/shard_map/dot_general | solution.py:39
  1810.1 11.6 collective-permute-done.61.refs_7_
  1821.7 8.2 assemble.2.refs_8_
  1831.4 9.5 collective-permute-done.49.refs_2_
  1841.7 17.9 collective-permute-done.50.refs_3_
  1860.3 21.6 %fusion.14 = f32[1024,1536]{1,0:T(8,128)} fusion(bf16[4480,1536]{1,0:T(8,128)(2,1)} %bitcast.198, bf16[2048,4480]{1,0:T(8,128)(2,1)} %get-tuple-element.54), kind=kOutput, calls=%fused_computation.38 | convolution fusion | flops 14092861440 | bytes 29229056 | tf_op jit(solution)/shard_map/dot_general | solution.py:39
  1881.9 25.8 %collective-permute-done.52.refs_5_ = f32[192,1120]{1,0:T(8,128)S(1)} collective-permute-done((f32[192,1120]{1,0:T(8,128)S(1)}, f32[192,1120]{1,0:T(8,128)S(1)}, u32[]{:S(2)}, u32[]{:S(2)}) %collective-permute-start.52) | collective-permute-done | bytes 860192 | tf_op jit(solution)/shard_map/ppermute | solution.py:285
  1909.8 8.1 assemble.3
  1917.9 8.1 add_convert_fusion
  (487 shorter events, 286.4 us)
Async XLA Ops:
  8.0 1107.8 %reduce-scatter.11.cloned.1.call-start = ((), (), s32[]{:S(2)}) async-start(), calls=%async_computation.11 | async-start | bytes 5898240 | tf_op jit(solution)/shard_map/reduce_scatter | solution.py:107
  18.4 174.4 %collective-permute-start.13 = (bf16[1120,1536]{1,0:T(8,128)(2,1)}, bf16[1120,1536]{1,0:T(8,128)(2,1)}, u32[]{:S(2)}, u32[]{:S(2)}) collective-permute-start(bf16[1120,1536]{1,0:T(8,128)(2,1)} %get-tuple-element.99._.down_ref), channel_id=1, source_target_pairs={{0,2},{2,0},{4,6},{6,4},{1,3},{3,1},{5,7},{7,5}} | collective-permute-start | bytes 10321928 | tf_op jit(solution)/shard_map/ppermute | solution.py:59
  21.8 173.8 %collective-permute-start.14 = (bf16[1120,1536]{1,0:T(8,128)(2,1)}, bf16[1120,1536]{1,0:T(8,128)(2,1)}, u32[]{:S(2)}, u32[]{:S(2)}) collective-permute-start(bf16[1120,1536]{1,0:T(8,128)(2,1)} %get-tuple-element.99._.down_ref), channel_id=1, source_target_pairs={{0,4},{2,6},{4,0},{6,2},{1,5},{3,7},{5,1},{7,3}} | collective-permute-start | bytes 10321928 | tf_op jit(solution)/shard_map/ppermute | solution.py:59
  40.2 36.3 %collective-permute-start.1 = (bf16[192,1792]{1,0:T(8,128)(2,1)}, bf16[192,1792]{1,0:T(8,128)(2,1)}, u32[]{:S(2)}, u32[]{:S(2)}) collective-permute-start(bf16[192,1792]{1,0:T(8,128)(2,1)} %broadcast_select_fusion.10), channel_id=1, source_target_pairs={{0,1},{1,0},{2,3},{3,2},{4,5},{5,4},{6,7},{7,6}} | collective-permute-start | bytes 2064392 | tf_op jit(solution)/shard_map/ppermute | solution.py:55
  44.4 105.3 %collective-permute-start = (bf16[1024,1536]{1,0:T(8,128)(2,1)}, bf16[1024,1536]{1,0:T(8,128)(2,1)}, u32[]{:S(2)}, u32[]{:S(2)}) collective-permute-start(bf16[1024,1536]{1,0:T(8,128)(2,1)} %fusion.54), channel_id=1, source_target_pairs={{0,1},{1,0},{2,3},{3,2},{4,5},{5,4},{6,7},{7,6}} | collective-permute-start | bytes 9437192 | tf_op jit(solution)/shard_map/ppermute | solution.py:55
  52.1 31.3 %collective-permute-start.8 = (bf16[192,4480]{1,0:T(8,128)(2,1)}, bf16[192,4480]{1,0:T(8,128)(2,1)}, u32[]{:S(2)}, u32[]{:S(2)}) collective-permute-start(bf16[192,4480]{1,0:T(8,128)(2,1)} %get-tuple-element.43), channel_id=1, source_target_pairs={{0,1},{1,0},{2,3},{3,2},{4,5},{5,4},{6,7},{7,6}} | collective-permute-start | bytes 5160968 | tf_op jit(solution)/shard_map/ppermute | solution.py:55
  80.2 45.8 %collective-permute-start.2 = (bf16[384,1792]{1,0:T(8,128)(2,1)}, bf16[384,1792]{1,0:T(8,128)(2,1)}, u32[]{:S(2)}, u32[]{:S(2)}) collective-permute-start(bf16[384,1792]{1,0:T(8,128)(2,1)} %pad_maximum_fusion.24._), channel_id=1, source_target_pairs={{0,2},{2,0},{4,6},{6,4},{1,3},{3,1},{5,7},{7,5}} | collective-permute-start | bytes 4128776 | tf_op jit(solution)/shard_map/ppermute | solution.py:59
  83.4 45.5 %collective-permute-start.3 = (bf16[384,1792]{1,0:T(8,128)(2,1)}, bf16[384,1792]{1,0:T(8,128)(2,1)}, u32[]{:S(2)}, u32[]{:S(2)}) collective-permute-start(bf16[384,1792]{1,0:T(8,128)(2,1)} %pad_maximum_fusion.24._), channel_id=1, source_target_pairs={{0,4},{2,6},{4,0},{6,2},{1,5},{3,7},{5,1},{7,3}} | collective-permute-start | bytes 4128776 | tf_op jit(solution)/shard_map/ppermute | solution.py:59
  127.1 16.6 collective-permute-start.4
  130.0 17.2 collective-permute-start.5
  143.8 357.0 %collective-permute-start.31 = (bf16[1120,1536]{1,0:T(8,128)(2,1)}, bf16[1120,1536]{1,0:T(8,128)(2,1)}, u32[]{:S(2)}, u32[]{:S(2)}) collective-permute-start(bf16[1120,1536]{1,0:T(8,128)(2,1)} %slice_bitcast_fusion._.down_ref), channel_id=1, source_target_pairs={{0,2},{2,0},{4,6},{6,4},{1,3},{3,1},{5,7},{7,5}} | collective-permute-start | bytes 10321928 | tf_op jit(solution)/shard_map/ppermute | solution.py:59
  147.2 146.4 %collective-permute-start.9 = (bf16[384,4480]{1,0:T(8,128)(2,1)}, bf16[384,4480]{1,0:T(8,128)(2,1)}, u32[]{:S(2)}, u32[]{:S(2)}) collective-permute-start(bf16[384,4480]{1,0:T(8,128)(2,1)} %pad_maximum_fusion.16._), channel_id=1, source_target_pairs={{0,2},{2,0},{4,6},{6,4},{1,3},{3,1},{5,7},{7,5}} | collective-permute-start | bytes 10321928 | tf_op jit(solution)/shard_map/ppermute | solution.py:59
  183.5 163.4 %collective-permute-start.6 = (f32[1024,1536]{1,0:T(8,128)S(1)}, f32[1024,1536]{1,0:T(8,128)S(1)}, u32[]{:S(2)}, u32[]{:S(2)}) collective-permute-start(f32[1024,1536]{1,0:T(8,128)S(1)} %fusion.89), channel_id=1, source_target_pairs={{0,1},{1,0},{2,3},{3,2},{4,5},{5,4},{6,7},{7,6}} | collective-permute-start | bytes 18874376 | tf_op jit(solution)/shard_map/ppermute | solution.py:55
  192.8 310.7 %collective-permute-start.32 = (bf16[1120,1536]{1,0:T(8,128)(2,1)}, bf16[1120,1536]{1,0:T(8,128)(2,1)}, u32[]{:S(2)}, u32[]{:S(2)}) collective-permute-start(bf16[1120,1536]{1,0:T(8,128)(2,1)} %slice_bitcast_fusion._.down_ref), channel_id=1, source_target_pairs={{0,4},{2,6},{4,0},{6,2},{1,5},{3,7},{5,1},{7,3}} | collective-permute-start | bytes 10321928 | tf_op jit(solution)/shard_map/ppermute | solution.py:59
  195.6 148.5 %collective-permute-start.10 = (bf16[384,4480]{1,0:T(8,128)(2,1)}, bf16[384,4480]{1,0:T(8,128)(2,1)S(1)}, u32[]{:S(2)}, u32[]{:S(2)}) collective-permute-start(bf16[384,4480]{1,0:T(8,128)(2,1)} %pad_maximum_fusion.16._), channel_id=1, source_target_pairs={{0,4},{2,6},{4,0},{6,2},{1,5},{3,7},{5,1},{7,3}} | collective-permute-start | bytes 10321928 | tf_op jit(solution)/shard_map/ppermute | solution.py:59
  293.7 87.4 %collective-permute-start.15 = (bf16[560,1536]{1,0:T(8,128)(2,1)}, bf16[560,1536]{1,0:T(8,128)(2,1)}, u32[]{:S(2)}, u32[]{:S(2)}) collective-permute-start(bf16[560,1536]{1,0:T(8,128)(2,1)} %slice.310), channel_id=1, source_target_pairs={{0,4},{2,6},{4,0},{6,2},{1,5},{3,7},{5,1},{7,3}} | collective-permute-start | bytes 5160968 | tf_op jit(solution)/shard_map/ppermute | solution.py:59
  344.0 41.3 %collective-permute-start.16 = (bf16[560,1536]{1,0:T(8,128)(2,1)}, bf16[560,1536]{1,0:T(8,128)(2,1)}, u32[]{:S(2)}, u32[]{:S(2)}) collective-permute-start(bf16[560,1536]{1,0:T(8,128)(2,1)} %slice.311), channel_id=1, source_target_pairs={{0,2},{2,0},{4,6},{6,4},{1,3},{3,1},{5,7},{7,5}} | collective-permute-start | bytes 5160968 | tf_op jit(solution)/shard_map/ppermute | solution.py:59
  346.9 69.4 %collective-permute-start.11 = (bf16[192,4480]{1,0:T(8,128)(2,1)}, bf16[192,4480]{1,0:T(8,128)(2,1)}, u32[]{:S(2)}, u32[]{:S(2)}) collective-permute-start(bf16[192,4480]{1,0:T(8,128)(2,1)} %slice.308), channel_id=1, source_target_pairs={{0,4},{2,6},{4,0},{6,2},{1,5},{3,7},{5,1},{7,3}} | collective-permute-start | bytes 5160968 | tf_op jit(solution)/shard_map/ppermute | solution.py:59
  381.0 45.7 %collective-permute-start.7 = (bf16[1024,1536]{1,0:T(8,128)(2,1)S(1)}, bf16[1024,1536]{1,0:T(8,128)(2,1)}, u32[]{:S(2)}, u32[]{:S(2)}) collective-permute-start(bf16[1024,1536]{1,0:T(8,128)(2,1)S(1)} %fusion.32), channel_id=1, source_target_pairs={{0,1},{1,0},{2,3},{3,2},{4,5},{5,4},{6,7},{7,6}} | collective-permute-start | bytes 9437192 | tf_op jit(solution)/shard_map/ppermute | solution.py:55
  385.4 40.0 %collective-permute-start.12 = (bf16[192,4480]{1,0:T(8,128)(2,1)S(1)}, bf16[192,4480]{1,0:T(8,128)(2,1)S(1)}, u32[]{:S(2)}, u32[]{:S(2)}) collective-permute-start(bf16[192,4480]{1,0:T(8,128)(2,1)S(1)} %slice.309), channel_id=1, source_target_pairs={{0,2},{2,0},{4,6},{6,4},{1,3},{3,1},{5,7},{7,5}} | collective-permute-start | bytes 5160968 | tf_op jit(solution)/shard_map/ppermute | solution.py:59
  500.0 39.3 %collective-permute-start.17 = (f32[1024,1536]{1,0:T(8,128)}, f32[1024,1536]{1,0:T(8,128)}, u32[]{:S(2)}, u32[]{:S(2)}) collective-permute-start(f32[1024,1536]{1,0:T(8,128)} %fusion.16), channel_id=1, source_target_pairs={{0,1},{1,0},{2,3},{3,2},{4,5},{5,4},{6,7},{7,6}} | collective-permute-start | bytes 18874376 | tf_op jit(solution)/shard_map/ppermute | solution.py:55
  500.2 13.5 collective-permute-start.19
  503.5 136.3 %collective-permute-start.33 = (bf16[560,1536]{1,0:T(8,128)(2,1)}, bf16[560,1536]{1,0:T(8,128)(2,1)}, u32[]{:S(2)}, u32[]{:S(2)}) collective-permute-start(bf16[560,1536]{1,0:T(8,128)(2,1)} %slice.328), channel_id=1, source_target_pairs={{0,4},{2,6},{4,0},{6,2},{1,5},{3,7},{5,1},{7,3}} | collective-permute-start | bytes 5160968 | tf_op jit(solution)/shard_map/ppermute | solution.py:59
  506.3 136.9 %collective-permute-start.34 = (bf16[560,1536]{1,0:T(8,128)(2,1)}, bf16[560,1536]{1,0:T(8,128)(2,1)}, u32[]{:S(2)}, u32[]{:S(2)}) collective-permute-start(bf16[560,1536]{1,0:T(8,128)(2,1)} %slice.329), channel_id=1, source_target_pairs={{0,2},{2,0},{4,6},{6,4},{1,3},{3,1},{5,7},{7,5}} | collective-permute-start | bytes 5160968 | tf_op jit(solution)/shard_map/ppermute | solution.py:59
  513.7 34.2 %collective-permute-start.26 = (bf16[192,4480]{1,0:T(8,128)(2,1)}, bf16[192,4480]{1,0:T(8,128)(2,1)}, u32[]{:S(2)}, u32[]{:S(2)}) collective-permute-start(bf16[192,4480]{1,0:T(8,128)(2,1)} %get-tuple-element.48), channel_id=1, source_target_pairs={{0,1},{1,0},{2,3},{3,2},{4,5},{5,4},{6,7},{7,6}} | collective-permute-start | bytes 5160968 | tf_op jit(solution)/shard_map/ppermute | solution.py:55
  515.3 60.1 %collective-permute-start.20 = (bf16[384,1792]{1,0:T(8,128)(2,1)}, bf16[384,1792]{1,0:T(8,128)(2,1)S(1)}, u32[]{:S(2)}, u32[]{:S(2)}) collective-permute-start(bf16[384,1792]{1,0:T(8,128)(2,1)} %pad_maximum_fusion.25._), channel_id=1, source_target_pairs={{0,2},{2,0},{4,6},{6,4},{1,3},{3,1},{5,7},{7,5}} | collective-permute-start | bytes 4128776 | tf_op jit(solution)/shard_map/ppermute | solution.py:59
  539.3 38.0 %collective-permute-start.21 = (bf16[384,1792]{1,0:T(8,128)(2,1)}, bf16[384,1792]{1,0:T(8,128)(2,1)S(1)}, u32[]{:S(2)}, u32[]{:S(2)}) collective-permute-start(bf16[384,1792]{1,0:T(8,128)(2,1)} %pad_maximum_fusion.25._), channel_id=1, source_target_pairs={{0,4},{2,6},{4,0},{6,2},{1,5},{3,7},{5,1},{7,3}} | collective-permute-start | bytes 4128776 | tf_op jit(solution)/shard_map/ppermute | solution.py:59
  547.9 46.1 %collective-permute-start.18 = (bf16[1024,1536]{1,0:T(8,128)(2,1)S(1)}, bf16[1024,1536]{1,0:T(8,128)(2,1)S(1)}, u32[]{:S(2)}, u32[]{:S(2)}) collective-permute-start(bf16[1024,1536]{1,0:T(8,128)(2,1)S(1)} %fusion.36), channel_id=1, source_target_pairs={{0,1},{1,0},{2,3},{3,2},{4,5},{5,4},{6,7},{7,6}} | collective-permute-start | bytes 9437192 | tf_op jit(solution)/shard_map/ppermute | solution.py:55
  575.5 16.5 collective-permute-start.22
  577.3 16.1 collective-permute-start.23
  592.0 75.1 %collective-permute-start.27 = (bf16[384,4480]{1,0:T(8,128)(2,1)}, bf16[384,4480]{1,0:T(8,128)(2,1)}, u32[]{:S(2)}, u32[]{:S(2)}) collective-permute-start(bf16[384,4480]{1,0:T(8,128)(2,1)} %pad_maximum_fusion.17._), channel_id=1, source_target_pairs={{0,2},{2,0},{4,6},{6,4},{1,3},{3,1},{5,7},{7,5}} | collective-permute-start | bytes 10321928 | tf_op jit(solution)/shard_map/ppermute | solution.py:59
  593.4 77.5 %collective-permute-start.28 = (bf16[384,4480]{1,0:T(8,128)(2,1)}, bf16[384,4480]{1,0:T(8,128)(2,1)}, u32[]{:S(2)}, u32[]{:S(2)}) collective-permute-start(bf16[384,4480]{1,0:T(8,128)(2,1)} %pad_maximum_fusion.17._), channel_id=1, source_target_pairs={{0,4},{2,6},{4,0},{6,2},{1,5},{3,7},{5,1},{7,3}} | collective-permute-start | bytes 10321928 | tf_op jit(solution)/shard_map/ppermute | solution.py:59
  631.9 52.4 %collective-permute-start.24 = (f32[1024,1536]{1,0:T(8,128)}, f32[1024,1536]{1,0:T(8,128)}, u32[]{:S(2)}, u32[]{:S(2)}) collective-permute-start(f32[1024,1536]{1,0:T(8,128)} %fusion.84), channel_id=1, source_target_pairs={{0,1},{1,0},{2,3},{3,2},{4,5},{5,4},{6,7},{7,6}} | collective-permute-start | bytes 18874376 | tf_op jit(solution)/shard_map/ppermute | solution.py:55
  639.8 127.1 %collective-permute-start.35 = (bf16[1024,1536]{1,0:T(8,128)(2,1)}, bf16[1024,1536]{1,0:T(8,128)(2,1)}, u32[]{:S(2)}, u32[]{:S(2)}) collective-permute-start(bf16[1024,1536]{1,0:T(8,128)(2,1)} %bitcast.206), channel_id=1, source_target_pairs={{0,1},{1,0},{2,3},{3,2},{4,5},{5,4},{6,7},{7,6}} | collective-permute-start | bytes 9437192 | tf_op jit(solution)/shard_map/ppermute | solution.py:55
  669.9 37.4 %collective-permute-start.29 = (bf16[192,4480]{1,0:T(8,128)(2,1)}, bf16[192,4480]{1,0:T(8,128)(2,1)}, u32[]{:S(2)}, u32[]{:S(2)}) collective-permute-start(bf16[192,4480]{1,0:T(8,128)(2,1)} %slice.326), channel_id=1, source_target_pairs={{0,4},{2,6},{4,0},{6,2},{1,5},{3,7},{5,1},{7,3}} | collective-permute-start | bytes 5160968 | tf_op jit(solution)/shard_map/ppermute | solution.py:59
  673.7 36.8 %collective-permute-start.30 = (bf16[192,4480]{1,0:T(8,128)(2,1)}, bf16[192,4480]{1,0:T(8,128)(2,1)}, u32[]{:S(2)}, u32[]{:S(2)}) collective-permute-start(bf16[192,4480]{1,0:T(8,128)(2,1)} %slice.327), channel_id=1, source_target_pairs={{0,2},{2,0},{4,6},{6,4},{1,3},{3,1},{5,7},{7,5}} | collective-permute-start | bytes 5160968 | tf_op jit(solution)/shard_map/ppermute | solution.py:59
  692.3 21.0 %collective-permute-start.25 = (bf16[1024,1536]{1,0:T(8,128)(2,1)S(1)}, bf16[1024,1536]{1,0:T(8,128)(2,1)S(1)}, u32[]{:S(2)}, u32[]{:S(2)}) collective-permute-start(bf16[1024,1536]{1,0:T(8,128)(2,1)S(1)} %fusion.29), channel_id=1, source_target_pairs={{0,1},{1,0},{2,3},{3,2},{4,5},{5,4},{6,7},{7,6}} | collective-permute-start | bytes 9437192 | tf_op jit(solution)/shard_map/ppermute | solution.py:55
  829.2 19.3 collective-permute-start.36
  931.3 186.0 %reduce-scatter.7.cloned.1.call-start = ((), (), s32[]{:S(2)}) async-start(), calls=%async_computation.9 | async-start | bytes 7864320 | tf_op jit(solution)/shard_map/reduce_scatter | solution.py:107
  994.8 28.8 %collective-permute-start.41 = (f32[1024,1536]{1,0:T(8,128)}, f32[1024,1536]{1,0:T(8,128)}, u32[]{:S(2)}, u32[]{:S(2)}) collective-permute-start(f32[1024,1536]{1,0:T(8,128)} %fusion.4), channel_id=1, source_target_pairs={{0,1},{1,0},{2,3},{3,2},{4,5},{5,4},{6,7},{7,6}} | collective-permute-start | bytes 18874376 | tf_op jit(solution)/shard_map/ppermute | solution.py:55
  1004.1 151.4 %reduce-scatter.9.cloned.1.call-start = ((), (), s32[]{:S(2)}) async-start(), calls=%async_computation.10 | async-start | bytes 5898240 | tf_op jit(solution)/shard_map/reduce_scatter | solution.py:107
  1045.2 330.6 %reduce-scatter.5.cloned.1.call-start = ((), (), s32[]{:S(2)}) async-start(), calls=%async_computation.8 | async-start | bytes 7864320 | tf_op jit(solution)/shard_map/reduce_scatter | solution.py:107
  1094.7 282.4 %all-gather.11.cloned.1.call-start = ((), (), s32[]{:S(2)}) async-start(), calls=%async_computation.7 | async-start | bytes 28311552 | tf_op jit(solution)/shard_map/all_gather | solution.py:103
  1095.3 281.8 %all-gather.9.cloned.1.call-start = ((), (), s32[]{:S(2)}) async-start(), calls=%async_computation.6 | async-start | bytes 28311552 | tf_op jit(solution)/shard_map/all_gather | solution.py:103
  1095.8 427.0 %all-gather.5.cloned.1.call-start = ((), (), s32[]{:S(2)}) async-start(), calls=%async_computation.4 | async-start | bytes 28311552 | tf_op jit(solution)/shard_map/all_gather | solution.py:103
  1096.4 540.7 %all-gather.7.cloned.1.call-start = ((), (), s32[]{:S(2)}) async-start(), calls=%async_computation.5 | async-start | bytes 28311552 | tf_op jit(solution)/shard_map/all_gather | solution.py:103
  1106.6 34.4 %collective-permute-start.43 = (f32[1024,1536]{1,0:T(8,128)}, f32[1024,1536]{1,0:T(8,128)}, u32[]{:S(2)}, u32[]{:S(2)}) collective-permute-start(f32[1024,1536]{1,0:T(8,128)} %fusion.74), channel_id=1, source_target_pairs={{0,1},{1,0},{2,3},{3,2},{4,5},{5,4},{6,7},{7,6}} | collective-permute-start | bytes 18874376 | tf_op jit(solution)/shard_map/ppermute | solution.py:55
  1118.5 11.9 collective-permute-start.45
  1377.0 141.8 %collective-permute-start.44 = (f32[192,1024]{1,0:T(8,128)S(1)}, f32[192,1024]{1,0:T(8,128)}, u32[]{:S(2)}, u32[]{:S(2)}) collective-permute-start(f32[192,1024]{1,0:T(8,128)S(1)} %dynamic-slice_bitcast_fusion.1), channel_id=1, source_target_pairs={{0,1},{1,0},{2,3},{3,2},{4,5},{5,4},{6,7},{7,6}} | collective-permute-start | bytes 2359304 | tf_op jit(solution)/shard_map/ppermute | solution.py:55
  1515.4 260.1 %collective-permute-start.55 = (f32[192,1120]{1,0:T(8,128)}, f32[192,1120]{1,0:T(8,128)S(1)}, u32[]{:S(2)}, u32[]{:S(2)}) collective-permute-start(f32[192,1120]{1,0:T(8,128)} %get-tuple-element.66), channel_id=1, source_target_pairs={{0,1},{1,0},{2,3},{3,2},{4,5},{5,4},{6,7},{7,6}} | collective-permute-start | bytes 2580488 | tf_op jit(solution)/shard_map/ppermute | solution.py:285
  1515.7 282.9 %collective-permute-start.56 = (f32[192,1120]{1,0:T(8,128)}, f32[192,1120]{1,0:T(8,128)}, u32[]{:S(2)}, u32[]{:S(2)}) collective-permute-start(f32[192,1120]{1,0:T(8,128)} %get-tuple-element.67), channel_id=1, source_target_pairs={{0,2},{1,3},{2,0},{3,1},{4,6},{5,7},{6,4},{7,5}} | collective-permute-start | bytes 2580488 | tf_op jit(solution)/shard_map/ppermute | solution.py:285
  1517.2 282.5 %collective-permute-start.57 = (f32[192,1120]{1,0:T(8,128)}, f32[192,1120]{1,0:T(8,128)}, u32[]{:S(2)}, u32[]{:S(2)}) collective-permute-start(f32[192,1120]{1,0:T(8,128)} %get-tuple-element.68), channel_id=1, source_target_pairs={{0,3},{1,2},{2,1},{3,0},{4,7},{5,6},{6,5},{7,4}} | collective-permute-start | bytes 2580488 | tf_op jit(solution)/shard_map/ppermute | solution.py:285
  1517.3 284.4 %collective-permute-start.58 = (f32[192,1120]{1,0:T(8,128)}, f32[192,1120]{1,0:T(8,128)}, u32[]{:S(2)}, u32[]{:S(2)}) collective-permute-start(f32[192,1120]{1,0:T(8,128)} %get-tuple-element.69), channel_id=1, source_target_pairs={{0,4},{1,5},{2,6},{3,7},{4,0},{5,1},{6,2},{7,3}} | collective-permute-start | bytes 2580488 | tf_op jit(solution)/shard_map/ppermute | solution.py:285
  1518.8 283.0 %collective-permute-start.59 = (f32[192,1120]{1,0:T(8,128)}, f32[192,1120]{1,0:T(8,128)}, u32[]{:S(2)}, u32[]{:S(2)}) collective-permute-start(f32[192,1120]{1,0:T(8,128)} %get-tuple-element.70), channel_id=1, source_target_pairs={{0,5},{1,4},{2,7},{3,6},{4,1},{5,0},{6,3},{7,2}} | collective-permute-start | bytes 2580488 | tf_op jit(solution)/shard_map/ppermute | solution.py:285
  1775.6 27.6 %collective-permute-start.60 = (f32[192,1120]{1,0:T(8,128)}, f32[192,1120]{1,0:T(8,128)S(1)}, u32[]{:S(2)}, u32[]{:S(2)}) collective-permute-start(f32[192,1120]{1,0:T(8,128)} %get-tuple-element.71), channel_id=1, source_target_pairs={{0,6},{1,7},{2,4},{3,5},{4,2},{5,3},{6,0},{7,1}} | collective-permute-start | bytes 2580488 | tf_op jit(solution)/shard_map/ppermute | solution.py:285
  1798.6 23.0 %collective-permute-start.61 = (f32[192,1120]{1,0:T(8,128)}, f32[192,1120]{1,0:T(8,128)}, u32[]{:S(2)}, u32[]{:S(2)}) collective-permute-start(f32[192,1120]{1,0:T(8,128)} %get-tuple-element.72), channel_id=1, source_target_pairs={{0,7},{1,6},{2,5},{3,4},{4,3},{5,2},{6,1},{7,0}} | collective-permute-start | bytes 2580488 | tf_op jit(solution)/shard_map/ppermute | solution.py:285
  1799.7 118.2 %collective-permute-start.39 = (f32[1024,1536]{1,0:T(8,128)}, f32[1024,1536]{1,0:T(8,128)}, u32[]{:S(2)}, u32[]{:S(2)}) collective-permute-start(f32[1024,1536]{1,0:T(8,128)} %fusion.12), channel_id=1, source_target_pairs={{0,1},{1,0},{2,3},{3,2},{4,5},{5,4},{6,7},{7,6}} | collective-permute-start | bytes 18874376 | tf_op jit(solution)/shard_map/ppermute | solution.py:55
  1801.7 29.7 %collective-permute-start.48 = (f32[192,1120]{1,0:T(8,128)}, f32[192,1120]{1,0:T(8,128)}, u32[]{:S(2)}, u32[]{:S(2)}) collective-permute-start(f32[192,1120]{1,0:T(8,128)} %get-tuple-element.58), channel_id=1, source_target_pairs={{0,1},{1,0},{2,3},{3,2},{4,5},{5,4},{6,7},{7,6}} | collective-permute-start | bytes 2580488 | tf_op jit(solution)/shard_map/ppermute | solution.py:285
  1801.8 39.2 %collective-permute-start.49 = (f32[192,1120]{1,0:T(8,128)}, f32[192,1120]{1,0:T(8,128)}, u32[]{:S(2)}, u32[]{:S(2)}) collective-permute-start(f32[192,1120]{1,0:T(8,128)} %get-tuple-element.59), channel_id=1, source_target_pairs={{0,2},{1,3},{2,0},{3,1},{4,6},{5,7},{6,4},{7,5}} | collective-permute-start | bytes 2580488 | tf_op jit(solution)/shard_map/ppermute | solution.py:285
  1803.2 56.4 %collective-permute-start.50 = (f32[192,1120]{1,0:T(8,128)}, f32[192,1120]{1,0:T(8,128)}, u32[]{:S(2)}, u32[]{:S(2)}) collective-permute-start(f32[192,1120]{1,0:T(8,128)} %get-tuple-element.60), channel_id=1, source_target_pairs={{0,3},{1,2},{2,1},{3,0},{4,7},{5,6},{6,5},{7,4}} | collective-permute-start | bytes 2580488 | tf_op jit(solution)/shard_map/ppermute | solution.py:285
  1829.9 52.0 %collective-permute-start.51 = (f32[192,1120]{1,0:T(8,128)S(1)}, f32[192,1120]{1,0:T(8,128)S(1)}, u32[]{:S(2)}, u32[]{:S(2)}) collective-permute-start(f32[192,1120]{1,0:T(8,128)S(1)} %copy-done.98), channel_id=1, source_target_pairs={{0,4},{1,5},{2,6},{3,7},{4,0},{5,1},{6,2},{7,3}} | collective-permute-start | bytes 2580488 | tf_op jit(solution)/shard_map/ppermute | solution.py:285
  1831.4 76.2 %collective-permute-start.52 = (f32[192,1120]{1,0:T(8,128)S(1)}, f32[192,1120]{1,0:T(8,128)S(1)}, u32[]{:S(2)}, u32[]{:S(2)}) collective-permute-start(f32[192,1120]{1,0:T(8,128)S(1)} %copy-done.97), channel_id=1, source_target_pairs={{0,5},{1,4},{2,7},{3,6},{4,1},{5,0},{6,3},{7,2}} | collective-permute-start | bytes 2580488 | tf_op jit(solution)/shard_map/ppermute | solution.py:285
  1840.9 66.7 %collective-permute-start.53 = (f32[192,1120]{1,0:T(8,128)S(1)}, f32[192,1120]{1,0:T(8,128)S(1)}, u32[]{:S(2)}, u32[]{:S(2)}) collective-permute-start(f32[192,1120]{1,0:T(8,128)S(1)} %copy-done.96), channel_id=1, source_target_pairs={{0,6},{1,7},{2,4},{3,5},{4,2},{5,3},{6,0},{7,1}} | collective-permute-start | bytes 2580488 | tf_op jit(solution)/shard_map/ppermute | solution.py:285
  1859.6 48.0 %collective-permute-start.54 = (f32[192,1120]{1,0:T(8,128)S(1)}, f32[192,1120]{1,0:T(8,128)S(1)}, u32[]{:S(2)}, u32[]{:S(2)}) collective-permute-start(f32[192,1120]{1,0:T(8,128)S(1)} %copy-done.95), channel_id=1, source_target_pairs={{0,7},{1,6},{2,5},{3,4},{4,3},{5,2},{6,1},{7,0}} | collective-permute-start | bytes 2580488 | tf_op jit(solution)/shard_map/ppermute | solution.py:285
  (112 other events, 1516.2 us)
Sparse Core Ops, SparseCore 0:
  931.4 51.3 reduce-scatter.10
  1004.3 64.2 reduce-scatter.6
  1071.5 83.9 reduce-scatter.8
  1158.3 217.4 reduce-scatter.4
Sparse Core Ops, SparseCore 1:
  1097.0 127.3 all-gather.10
  1226.1 134.1 all-gather.8
  1361.9 120.7 all-gather.4
  1484.5 152.6 all-gather.6

commit v7 on v6

--- a/solution.py
+++ b/solution.py
@@ -19,6 +19,8 @@
 TOKEN_TILE = 512
 ROW_TILE = 48
 FLIP_TILE = 256
+WIDTH_TILE = 512
+COLUMN_TILE = 896
 NEIGHBOURS = (1, 2)
 
 
@@ -45,10 +47,6 @@
 
 def times_flipped(left, right):
     return dot(left, right, ((1,), (1,)))
-
-
-def over_rows(left, right):
-    return dot(left, right, ((0,), (0,)))
 
 
 def swap(value):
@@ -190,6 +188,28 @@
     return y_own, (x_own, normed, qkv, o_act)
 
 
+def attn_grads_kernel(norm_ref, d_qkv_ref, grad_ref, o_ref, out_ref):
+    width = d_qkv_ref.shape[1]
+    out_ref[:, :width] = dot(norm_ref[...], d_qkv_ref[...], ((0,), (0,)))
+    out_ref[:, width:] = dot(grad_ref[...], o_ref[...], ((0,), (0,)))
+
+
+def attn_grads(normed, d_qkv, grad_y, o_act):
+    rows, width = normed.shape
+    cols = d_qkv.shape[1] + o_act.shape[1]
+    piece = pl.BlockSpec((rows, WIDTH_TILE), lambda i: (0, i))
+    whole = [pl.BlockSpec(arg.shape, lambda i: (0, 0), pipeline_mode=pl.Buffered(1)) for arg in (d_qkv, o_act)]
+    return pl.pallas_call(
+        attn_grads_kernel,
+        grid=(width // WIDTH_TILE,),
+        in_specs=[piece, whole[0], piece, whole[1]],
+        out_specs=pl.BlockSpec((WIDTH_TILE, cols), lambda i: (i, 0)),
+        out_shape=jax.ShapeDtypeStruct((width, cols), jnp.float32),
+        cost_estimate=pl.CostEstimate(flops=2 * rows * width * cols, bytes_accessed=0, transcendentals=0),
+        name="attn_grads",
+    )(normed, d_qkv, grad_y, o_act)
+
+
 def attn_backward(saved, weight, q_width, head, seq, grad_own):
     x_own, normed, qkv, o_act = saved
     grad_y = pair_rows(grad_own)
@@ -198,7 +218,7 @@
                   40_000_000_000)
     d_norm = both_halves(d_qkv, weight[:, :q_width + 2 * head], grad_own.shape[0], times_flipped)
     grad_x = (grad_own.astype(jnp.float32) + norm_back(x_own, d_norm)).astype(jnp.bfloat16)
-    return grad_x, over_rows(normed, d_qkv), over_rows(grad_y, o_act)
+    return grad_x, attn_grads(normed, d_qkv, grad_y, o_act)
 
 
 def gelu_parts(hidden):
@@ -218,10 +238,37 @@
     return (x_own.astype(jnp.float32) + proj).astype(jnp.bfloat16)
 
 
+def mlp_back_kernel(grad_ref, slope_ref, down_ref, up_ref, out_ref):
+    @pl.when(pl.program_id(0) == 0)
+    def _():
+        out_ref[...] = jnp.zeros_like(out_ref)
+
+    d_hid = (dot(grad_ref[...], down_ref[...], ((1,), (1,))) * slope_ref[...]).astype(jnp.bfloat16)
+    out_ref[...] += dot(d_hid, up_ref[...], ((1,), (1,)))
+
+
+def mlp_back(half, grad_y, slope, down_weight, up_weight):
+    rows, (width, cols) = grad_y.shape[0] // CORES, up_weight.shape
+    once = pl.Buffered(1)
+    return pl.pallas_call(
+        mlp_back_kernel,
+        grid=(cols // COLUMN_TILE,),
+        in_specs=[pl.BlockSpec((rows, width), lambda i: (half, 0), pipeline_mode=once),
+                  pl.BlockSpec((rows, COLUMN_TILE), lambda i: (half, i)),
+                  pl.BlockSpec((COLUMN_TILE, width), lambda i: (i, 0)),
+                  pl.BlockSpec((width, COLUMN_TILE), lambda i: (0, i))],
+        out_specs=pl.BlockSpec((rows, width), lambda i: (0, 0), pipeline_mode=once),
+        out_shape=jax.ShapeDtypeStruct((rows, width), jnp.float32),
+        compiler_params=pltpu.CompilerParams(vmem_limit_bytes=50 * 1024 * 1024),
+        cost_estimate=pl.CostEstimate(flops=4 * rows * width * cols, bytes_accessed=0, transcendentals=0),
+        name="mlp_back",
+    )(grad_y, slope, down_weight, up_weight)
+
+
 def mlp_backward(x_own, slope, up_weight, down_weight, grad_own):
-    grad_act = times_flipped(pair_rows(grad_own), down_weight)
-    d_hid = (grad_act * slope).astype(jnp.bfloat16)
-    d_norm = both_halves(d_hid, up_weight, grad_own.shape[0], times_flipped)
+    args = (pair_rows(grad_own), slope, down_weight, up_weight)
+    other = swap(mlp_back(1, *args))
+    d_norm = mlp_back(0, *args) + other
     return (grad_own.astype(jnp.float32) + norm_back(x_own, d_norm)).astype(jnp.bfloat16)
 
 
@@ -425,14 +472,13 @@
                 parts, d_down = weight_grads(layer, norms, gather_rows(grad_x), d_down)
             d_up = [assemble(place, layer, pairs, d_up, parts)]
             grad_x = mlp_backward(x_own, slope, up_full[layer], down_full[layer], grad_x)
-            grad_x, d_qkv, d_o = attn_backward(attn_saved[layer], attn_full[layer], q_width, head, seq, grad_x)
-            parts = to_rows(core, scatter_sum(d_o))
-            grad_lists[3].append(jnp.concatenate(parts, axis=1).reshape(shard, heads, head))
-            parts = to_rows(core, scatter_sum(d_qkv))
-            grad_lists[0].append(jnp.concatenate([part[:, :q_width] for part in parts], axis=1)
-                                 .reshape(shard, heads, head))
-            grad_lists[1].append(jnp.stack([part[:, q_width:q_width + head] for part in parts], axis=1))
-            grad_lists[2].append(jnp.stack([part[:, q_width + head:] for part in parts], axis=1))
+            grad_x, d_attn = attn_backward(attn_saved[layer], attn_full[layer], q_width, head, seq, grad_x)
+            parts = to_rows(core, scatter_sum(d_attn))
+            k_end, v_end = q_width + head, q_width + 2 * head
+            for cols, start, end in zip(grad_lists[::3], (0, v_end), (q_width, v_end + q_width)):
+                cols.append(jnp.concatenate([part[:, start:end] for part in parts], axis=1).reshape(shard, heads, head))
+            grad_lists[1].append(jnp.stack([part[:, q_width:k_end] for part in parts], axis=1))
+            grad_lists[2].append(jnp.stack([part[:, k_end:v_end] for part in parts], axis=1))
         last, d_down = lax.optimization_barrier((last, d_down))
         y_loc = mlp_output(*last).reshape(x_loc.shape)
         stacked = tuple(jnp.stack(grad_list[::-1]) for grad_list in grad_lists)

time: 1940 us -> 1870 us (0.964)
  Pallas kernels: 415 us -> 623 us
  matrix products: 485 us -> 285 us
  waiting for transfers between devices: 708 us -> 569 us
  other arithmetic: 97.9 us -> 140 us
    pallas_call x0 -> x6, Pallas kernels: none -> 206 us  [the longest x4 169 us: mlp_back(): pl.pallas_call(mlp_back_kernel, grid=(cols // COLUMN_TILE,), in_specs=[pl...]
    dot_general x28 -> x18, matrix products: 485 us -> 285 us  [dot(): lax.dot_general(left, right, (contract, ((), ())), preferred_element_type...]
    all_gather x4, waiting for transfers between devices: 114 us -> 0.01 us  [gather_rows(): return functools.partial(lax.all_gather, axis=0, tiled=True)(value, AXES)]
    ppermute x24, waiting for transfers between devices: 298 us -> 242 us  [hop(): lax.ppermute(value, CHIP, [(chip, chip ^ step) for chip in range(CHIPS)])]
    concatenate x4 -> x10, other arithmetic: 2.57 us -> 34.4 us  [the longest x6 29.8 us: pair_rows(): return jnp.concatenate([value, swap(value)], axis=0)]
    reduce_scatter x4 -> x2, waiting for transfers between devices: 213 us -> 238 us  [scatter_sum(): return lax.psum_scatter(grad_full, CHIP, scatter_dimension=0, tiled=True)]
  transfers between devices with their start and end apart: 70 -> 66, of which waited for: 24 -> 21; matrix products, arithmetic and copies ran while one was open for 32% -> 25% of each run, Pallas kernels for 20% -> 21%
where the time goes in v7:
time: 1870 us; the launch traced here: 1850 us
  Pallas kernels  623 us (33%)
  waiting for transfers between devices  569 us (30%)
  matrix products  285 us (15%)
  local copies, waits for them, and re-layouts  173 us (9%)
  other arithmetic  140 us (7%)
  starting transfers between devices  47.4 us (3%)
    dot_general x18, matrix products, dot(): lax.dot_general(left, right, (contract, ((), ())), preferred_element_type...  285 us
    pallas_call x2, Pallas kernels, mlp_weight_grads(): pl.pallas_call(mlp_grads_kernel, grid_spec=pltpu.PrefetchScalarGridSpec(n...  276 us
    ppermute x24, waiting for transfers between devices, hop(): lax.ppermute(value, CHIP, [(chip, chip ^ step) for chip in range(CHIPS)])  242 us
    reduce_scatter x2, waiting for transfers between devices, scatter_sum(): return lax.psum_scatter(grad_full, CHIP, scatter_dimension=0, tiled=True)  238 us
    pallas_call x4, Pallas kernels, mlp_back(): pl.pallas_call(mlp_back_kernel, grid=(cols // COLUMN_TILE,), in_specs=[pl...  169 us
    pallas_call x4, Pallas kernels, by_sequence(): pl.pallas_call(functools.partial(kernel, q_width, head), grid=(rows // se...  90.7 us
    ppermute x14, waiting for transfers between devices, exchange(): lax.ppermute(part, AXES, [(d, d ^ i) for d in devices])  80.2 us
    dynamic_update_slice x26, local copies, waits for them, and re-layouts, gather_weight(): full = lax.dynamic_update_slice(full, part[None], (chip ^ step, row, 0))  71.1 us
  transfers between devices with their start and end apart: 66, of which 21 were waited for; matrix products, arithmetic and copies ran while one was open for 25% of the time, Pallas kernels for 21%

profile of v7, /device:TPU:0, one launch (start us, length us, event | category | flops | bytes accessed | tf_op | source)
XLA Modules:
  0.0 1855.0 jit_solution(13899825220128045029)
XLA Ops:
  12.0 6.3 slice_dynamic-update-slice_fusion
  43.4 6.5 split.2
  90.2 35.6 %collective-permute-done.2 = bf16[384,1792]{1,0:T(8,128)(2,1)} collective-permute-done((bf16[384,1792]{1,0:T(8,128)(2,1)}, bf16[384,1792]{1,0:T(8,128)(2,1)}, u32[]{:S(2)}, u32[]{:S(2)}) %collective-permute-start.2) | collective-permute-done | bytes 1376288 | tf_op jit(solution)/shard_map/ppermute | solution.py:57
  136.4 7.2 collective-permute-done.4
  148.3 11.7 convolution_convert_fusion.1.qkv_ref
  160.0 17.1 shard_map.143.o_ref
  182.0 6.2 fusion.65
  204.0 17.2 collective-permute-done.9
  229.7 31.8 %collective-permute-done.15 = bf16[560,1536]{1,0:T(8,128)(2,1)S(1)} collective-permute-done((bf16[560,1536]{1,0:T(8,128)(2,1)S(1)}, bf16[560,1536]{1,0:T(8,128)(2,1)S(1)}, u32[]{:S(2)}, u32[]{:S(2)}) %collective-permute-start.15) | collective-permute-done | bytes 1720352 | tf_op jit(solution)/shard_map/ppermute | solution.py:57
  280.0 51.9 %collective-permute-done.16 = bf16[560,1536]{1,0:T(8,128)(2,1)} collective-permute-done((bf16[560,1536]{1,0:T(8,128)(2,1)}, bf16[560,1536]{1,0:T(8,128)(2,1)}, u32[]{:S(2)}, u32[]{:S(2)}) %collective-permute-start.16) | collective-permute-done | bytes 1720352 | tf_op jit(solution)/shard_map/ppermute | solution.py:57
  334.6 33.4 %collective-permute-done.11 = bf16[192,4480]{1,0:T(8,128)(2,1)} collective-permute-done((bf16[192,4480]{1,0:T(8,128)(2,1)}, bf16[192,4480]{1,0:T(8,128)(2,1)}, u32[]{:S(2)}, u32[]{:S(2)}) %collective-permute-start.11) | collective-permute-done | bytes 1720352 | tf_op jit(solution)/shard_map/ppermute | solution.py:57
  376.3 51.5 %multiply_add_fusion.2 = (f32[2048,4480]{1,0:T(8,128)}, bf16[2048,4480]{1,0:T(8,128)(2,1)}) fusion(bf16[1536,4480]{1,0:T(8,128)(2,1)} %bitcast.178, bf16[1024,1536]{1,0:T(8,128)(2,1)} %collective-permute-done.7, bf16[1024,1536]{1,0:T(8,128)(2,1)S(1)} %fusion.24), kind=kOutput, calls=%fused_computation.4 | convolution fusion | flops 28326756352 | bytes 75104256 | tf_op jit(solution)/shard_map/dot_general | solution.py:41
  427.8 21.5 %fusion.8 = f32[1024,1536]{1,0:T(8,128)} fusion(bf16[4480,1536]{1,0:T(8,128)(2,1)} %bitcast.182, bf16[2048,4480]{1,0:T(8,128)(2,1)} %get-tuple-element.44), kind=kOutput, calls=%fused_computation.30 | convolution fusion | flops 14092861440 | bytes 29229056 | tf_op jit(solution)/shard_map/dot_general | solution.py:41
  449.3 6.0 pad_maximum_fusion.2.grad_ref
  462.9 6.8 split.3
  475.1 21.5 %fusion.10 = f32[1024,1536]{1,0:T(8,128)} fusion(bf16[4480,1536]{1,0:T(8,128)(2,1)} %bitcast.183, bf16[2048,4480]{1,0:T(8,128)(2,1)} %get-tuple-element.44), kind=kOutput, calls=%fused_computation.32 | convolution fusion | flops 14092861440 | bytes 29229056 | tf_op jit(solution)/shard_map/dot_general | solution.py:41
  497.2 6.0 fusion.27
  510.0 21.7 %collective-permute-done.20 = bf16[384,1792]{1,0:T(8,128)(2,1)S(1)} collective-permute-done((bf16[384,1792]{1,0:T(8,128)(2,1)}, bf16[384,1792]{1,0:T(8,128)(2,1)S(1)}, u32[]{:S(2)}, u32[]{:S(2)}) %collective-permute-start.20) | collective-permute-done | bytes 1376288 | tf_op jit(solution)/shard_map/ppermute | solution.py:57
  534.2 14.3 collective-permute-done.22
  553.9 9.6 convolution_convert_fusion.qkv_ref
  563.5 17.5 shard_map.144.o_ref
  581.0 7.4 fusion.58
  605.9 17.7 collective-permute-done.27
  635.1 6.1 fusion.60
  641.2 5.8 fusion.20
  654.4 9.4 collective-permute-done.29
  671.5 51.5 %multiply_add_fusion = (f32[2048,4480]{1,0:T(8,128)}, bf16[2048,4480]{1,0:T(8,128)(2,1)}) fusion(bf16[1536,4480]{1,0:T(8,128)(2,1)} %bitcast.174, bf16[1024,1536]{1,0:T(8,128)(2,1)} %copy-done.83, bf16[1024,1536]{1,0:T(8,128)(2,1)S(1)} %fusion.21), kind=kOutput, calls=%fused_computation | convolution fusion | flops 28326756352 | bytes 75104256 | tf_op jit(solution)/shard_map/dot_general | solution.py:41
  723.0 42.1 %mlp_back.5 = f32[1024,1536]{1,0:T(8,128)} custom-call(bf16[2048,1536]{1,0:T(8,128)(2,1)} %pad_maximum_fusion.2.grad_ref, f32[2048,4480]{1,0:T(8,128)} %get-tuple-element.50.slope_ref, bf16[4480,1536]{1,0:T(8,128)(2,1)} %bitcast.170, bf16[1536,4480]{1,0:T(8,128)(2,1)} %bitcast.175), custom_call_target="tpu_custom_call" | custom-call | flops 28185722880 | tf_op jit(solution)/shard_map/mlp_back/pallas_call | solution.py:253
  765.1 42.1 %mlp_back.4 = f32[1024,1536]{1,0:T(8,128)} custom-call(bf16[2048,1536]{1,0:T(8,128)(2,1)} %pad_maximum_fusion.2.grad_ref, f32[2048,4480]{1,0:T(8,128)} %get-tuple-element.50.slope_ref, bf16[4480,1536]{1,0:T(8,128)(2,1)} %bitcast.171, bf16[1536,4480]{1,0:T(8,128)(2,1)} %bitcast.176), custom_call_target="tpu_custom_call" | custom-call | flops 28185722880 | tf_op jit(solution)/shard_map/mlp_back/pallas_call | solution.py:253
  816.1 6.6 pad_maximum_fusion.1.norm_ref
  824.4 10.3 convolution_convert_fusion.3.d_o_ref
  834.7 27.7 %shard_map.145.d_qkv_ref = bf16[2048,1024]{1,0:T(8,128)(2,1)} custom-call(bf16[2048,1024]{1,0:T(8,128)(2,1)} %convolution_convert_fusion.qkv_ref, bf16[2048,768]{1,0:T(8,128)(2,1)} %convolution_convert_fusion.3.d_o_ref), custom_call_target="tpu_custom_call" | custom-call | flops 40000000000 | tf_op jit(solution)/shard_map/pallas_call | solution.py:170
  867.2 18.8 %attn_grads.3 = f32[1536,1792]{1,0:T(8,128)} custom-call(bf16[2048,1536]{1,0:T(8,128)(2,1)} %pad_maximum_fusion.1.norm_ref, bf16[2048,1024]{1,0:T(8,128)(2,1)} %shard_map.145.d_qkv_ref, bf16[2048,1536]{1,0:T(8,128)(2,1)} %pad_maximum_fusion.3.grad_ref, bf16[2048,768]{1,0:T(8,128)(2,1)} %shard_map.144.o_ref), custom_call_target="tpu_custom_call" | custom-call | flops 11274289152 | tf_op jit(solution)/shard_map/attn_grads/pallas_call | solution.py:202
  887.3 6.3 fusion.43
  894.0 8.6 fusion.45
  912.6 5.6 collective-permute-done.40
  921.3 42.0 %mlp_back.7 = f32[1024,1536]{1,0:T(8,128)} custom-call(bf16[2048,1536]{1,0:T(8,128)(2,1)} %pad_maximum_fusion.4.grad_ref, f32[2048,4480]{1,0:T(8,128)} %get-tuple-element.56.slope_ref, bf16[4480,1536]{1,0:T(8,128)(2,1)} %bitcast.184, bf16[1536,4480]{1,0:T(8,128)(2,1)} %bitcast.179), custom_call_target="tpu_custom_call" | custom-call | flops 28185722880 | tf_op jit(solution)/shard_map/mlp_back/pallas_call | solution.py:253
  963.4 42.4 %mlp_back.6 = f32[1024,1536]{1,0:T(8,128)} custom-call(bf16[2048,1536]{1,0:T(8,128)(2,1)} %pad_maximum_fusion.4.grad_ref, f32[2048,4480]{1,0:T(8,128)} %get-tuple-element.56.slope_ref, bf16[4480,1536]{1,0:T(8,128)(2,1)} %bitcast.185, bf16[1536,4480]{1,0:T(8,128)(2,1)} %bitcast.180), custom_call_target="tpu_custom_call" | custom-call | flops 28185722880 | tf_op jit(solution)/shard_map/mlp_back/pallas_call | solution.py:253
  1005.8 5.9 fusion.26
  1011.8 5.6 fusion.17
  1018.4 6.2 pad_maximum_fusion.norm_ref
  1027.7 10.0 convolution_convert_fusion.2.d_o_ref
  1037.7 28.5 %shard_map.146.d_qkv_ref = bf16[2048,1024]{1,0:T(8,128)(2,1)} custom-call(bf16[2048,1024]{1,0:T(8,128)(2,1)} %convolution_convert_fusion.1.qkv_ref, bf16[2048,768]{1,0:T(8,128)(2,1)} %convolution_convert_fusion.2.d_o_ref), custom_call_target="tpu_custom_call" | custom-call | flops 40000000000 | tf_op jit(solution)/shard_map/pallas_call | solution.py:170
  1066.2 18.4 attn_grads.2
  1085.9 11.6 flip.2.up_ref
  1097.5 9.3 flip.3.up_ref
  1106.8 77.5 %reduce-scatter.5.cloned.1.call-done = f32[384,1792]{1,0:T(8,128)} async-done(((f32[1536,1792]{1,0:T(8,128)}), f32[384,1792]{1,0:T(8,128)}) %reduce-scatter.5.cloned.1.call-update) | async-done | bytes 2752528 | tf_op jit(solution)/shard_map/reduce_scatter | solution.py:105
  1186.0 8.8 fusion.48
  1195.7 5.3 fusion.50
  1212.0 138.3 %mlp_grads.2 = (f32[2,1120,1536]{2,1,0:T(8,128)}, f32[192,1120]{1,0:T(8,128)}, f32[192,1120]{1,0:T(8,128)}, f32[192,1120]{1,0:T(8,128)}, f32[192,1120]{1,0:T(8,1...) custom-call(s32[2]{0:T(128)} %pad_add_fusion.place_ref, ...), custom_call_target="tpu_custom_call" | custom-call | flops 112742891520 | tf_op jit(solution)/shard_map/mlp_grads/pallas_call | solution.py:309
  1352.1 5.5 fusion.42
  1359.3 160.4 %reduce-scatter.3.cloned.1.call-done = f32[384,1792]{1,0:T(8,128)} async-done(((f32[1536,1792]{1,0:T(8,128)}), f32[384,1792]{1,0:T(8,128)}) %reduce-scatter.3.cloned.1.call-update) | async-done | bytes 2752528 | tf_op jit(solution)/shard_map/reduce_scatter | solution.py:105
  1525.3 8.2 fusion.19
  1533.5 12.4 collective-permute-done.58.refs_6_
  1546.0 16.3 collective-permute-done.59.refs_7_
  1562.3 8.1 assemble.2.refs_8_
  1576.7 138.0 %mlp_grads.3 = (f32[2,1120,1536]{2,1,0:T(8,128)}, f32[192,1120]{1,0:T(8,128)}, f32[192,1120]{1,0:T(8,128)}, f32[192,1120]{1,0:T(8,128)}, f32[192,1120]{1,0:T(8,1...) custom-call(s32[2]{0:T(128)} %pad_add_fusion.place_ref, ...), custom_call_target="tpu_custom_call", output_to_operand_aliasing={{0}: (5, {})} | custom-call | flops 112742891520 | tf_op jit(solution)/shard_map/mlp_grads/pallas_call | solution.py:309
  1714.7 21.9 %fusion.4 = f32[1024,1536]{1,0:T(8,128)} fusion(bf16[4480,1536]{1,0:T(8,128)(2,1)} %bitcast.172, bf16[2048,4480]{1,0:T(8,128)(2,1)} %get-tuple-element.54), kind=kOutput, calls=%fused_computation.26 | convolution fusion | flops 14092861440 | bytes 29229056 | tf_op jit(solution)/shard_map/dot_general | solution.py:41
  1752.1 10.0 collective-permute-done.47.refs_2_
  1763.5 16.5 collective-permute-done.48.refs_3_
  1782.1 21.5 %fusion.6 = f32[1024,1536]{1,0:T(8,128)} fusion(bf16[4480,1536]{1,0:T(8,128)(2,1)} %bitcast.173, bf16[2048,4480]{1,0:T(8,128)(2,1)} %get-tuple-element.54), kind=kOutput, calls=%fused_computation.28 | convolution fusion | flops 14092861440 | bytes 29229056 | tf_op jit(solution)/shard_map/dot_general | solution.py:41
  1803.6 24.9 %collective-permute-done.50.refs_5_ = f32[192,1120]{1,0:T(8,128)S(1)} collective-permute-done((f32[192,1120]{1,0:T(8,128)S(1)}, f32[192,1120]{1,0:T(8,128)S(1)}, u32[]{:S(2)}, u32[]{:S(2)}) %collective-permute-start.50) | collective-permute-done | bytes 860192 | tf_op jit(solution)/shard_map/ppermute | solution.py:332
  1830.6 8.1 assemble.3
  1838.8 8.2 add_convert_fusion
  (456 shorter events, 300.2 us)
Async XLA Ops:
  8.0 1176.3 %reduce-scatter.5.cloned.1.call-start = ((), (), s32[]{:S(2)}) async-start(), calls=%async_computation.7 | async-start | bytes 13762560 | tf_op jit(solution)/shard_map/reduce_scatter | solution.py:105
  18.3 169.9 %collective-permute-start.13 = (bf16[1120,1536]{1,0:T(8,128)(2,1)}, bf16[1120,1536]{1,0:T(8,128)(2,1)}, u32[]{:S(2)}, u32[]{:S(2)}) collective-permute-start(bf16[1120,1536]{1,0:T(8,128)(2,1)} %get-tuple-element.99._.down_ref), channel_id=1, source_target_pairs={{0,2},{2,0},{4,6},{6,4},{1,3},{3,1},{5,7},{7,5}} | collective-permute-start | bytes 10321928 | tf_op jit(solution)/shard_map/ppermute | solution.py:57
  21.6 173.9 %collective-permute-start.14 = (bf16[1120,1536]{1,0:T(8,128)(2,1)}, bf16[1120,1536]{1,0:T(8,128)(2,1)}, u32[]{:S(2)}, u32[]{:S(2)}) collective-permute-start(bf16[1120,1536]{1,0:T(8,128)(2,1)} %get-tuple-element.99._.down_ref), channel_id=1, source_target_pairs={{0,4},{2,6},{4,0},{6,2},{1,5},{3,7},{5,1},{7,3}} | collective-permute-start | bytes 10321928 | tf_op jit(solution)/shard_map/ppermute | solution.py:57
  38.0 35.0 %collective-permute-start.1 = (bf16[192,1792]{1,0:T(8,128)(2,1)}, bf16[192,1792]{1,0:T(8,128)(2,1)}, u32[]{:S(2)}, u32[]{:S(2)}) collective-permute-start(bf16[192,1792]{1,0:T(8,128)(2,1)} %broadcast_select_fusion.10), channel_id=1, source_target_pairs={{0,1},{1,0},{2,3},{3,2},{4,5},{5,4},{6,7},{7,6}} | collective-permute-start | bytes 2064392 | tf_op jit(solution)/shard_map/ppermute | solution.py:53
  42.2 106.1 %collective-permute-start = (bf16[1024,1536]{1,0:T(8,128)(2,1)}, bf16[1024,1536]{1,0:T(8,128)(2,1)}, u32[]{:S(2)}, u32[]{:S(2)}) collective-permute-start(bf16[1024,1536]{1,0:T(8,128)(2,1)} %fusion.40), channel_id=1, source_target_pairs={{0,1},{1,0},{2,3},{3,2},{4,5},{5,4},{6,7},{7,6}} | collective-permute-start | bytes 9437192 | tf_op jit(solution)/shard_map/ppermute | solution.py:53
  49.9 30.3 %collective-permute-start.8 = (bf16[192,4480]{1,0:T(8,128)(2,1)}, bf16[192,4480]{1,0:T(8,128)(2,1)}, u32[]{:S(2)}, u32[]{:S(2)}) collective-permute-start(bf16[192,4480]{1,0:T(8,128)(2,1)} %get-tuple-element.43), channel_id=1, source_target_pairs={{0,1},{1,0},{2,3},{3,2},{4,5},{5,4},{6,7},{7,6}} | collective-permute-start | bytes 5160968 | tf_op jit(solution)/shard_map/ppermute | solution.py:53
  77.2 48.7 %collective-permute-start.2 = (bf16[384,1792]{1,0:T(8,128)(2,1)}, bf16[384,1792]{1,0:T(8,128)(2,1)}, u32[]{:S(2)}, u32[]{:S(2)}) collective-permute-start(bf16[384,1792]{1,0:T(8,128)(2,1)} %pad_maximum_fusion.10._), channel_id=1, source_target_pairs={{0,2},{2,0},{4,6},{6,4},{1,3},{3,1},{5,7},{7,5}} | collective-permute-start | bytes 4128776 | tf_op jit(solution)/shard_map/ppermute | solution.py:57
  80.2 48.6 %collective-permute-start.3 = (bf16[384,1792]{1,0:T(8,128)(2,1)}, bf16[384,1792]{1,0:T(8,128)(2,1)}, u32[]{:S(2)}, u32[]{:S(2)}) collective-permute-start(bf16[384,1792]{1,0:T(8,128)(2,1)} %pad_maximum_fusion.10._), channel_id=1, source_target_pairs={{0,4},{2,6},{4,0},{6,2},{1,5},{3,7},{5,1},{7,3}} | collective-permute-start | bytes 4128776 | tf_op jit(solution)/shard_map/ppermute | solution.py:57
  127.0 16.6 collective-permute-start.4
  129.9 17.2 collective-permute-start.5
  143.6 77.6 %collective-permute-start.9 = (bf16[384,4480]{1,0:T(8,128)(2,1)}, bf16[384,4480]{1,0:T(8,128)(2,1)}, u32[]{:S(2)}, u32[]{:S(2)}) collective-permute-start(bf16[384,4480]{1,0:T(8,128)(2,1)} %pad_maximum_fusion.6._), channel_id=1, source_target_pairs={{0,2},{2,0},{4,6},{6,4},{1,3},{3,1},{5,7},{7,5}} | collective-permute-start | bytes 10321928 | tf_op jit(solution)/shard_map/ppermute | solution.py:57
  147.2 78.3 %collective-permute-start.10 = (bf16[384,4480]{1,0:T(8,128)(2,1)}, bf16[384,4480]{1,0:T(8,128)(2,1)}, u32[]{:S(2)}, u32[]{:S(2)}) collective-permute-start(bf16[384,4480]{1,0:T(8,128)(2,1)} %pad_maximum_fusion.6._), channel_id=1, source_target_pairs={{0,4},{2,6},{4,0},{6,2},{1,5},{3,7},{5,1},{7,3}} | collective-permute-start | bytes 10321928 | tf_op jit(solution)/shard_map/ppermute | solution.py:57
  182.0 89.1 %collective-permute-start.6 = (f32[1024,1536]{1,0:T(8,128)S(1)}, f32[1024,1536]{1,0:T(8,128)S(1)}, u32[]{:S(2)}, u32[]{:S(2)}) collective-permute-start(f32[1024,1536]{1,0:T(8,128)S(1)} %fusion.63), channel_id=1, source_target_pairs={{0,1},{1,0},{2,3},{3,2},{4,5},{5,4},{6,7},{7,6}} | collective-permute-start | bytes 18874376 | tf_op jit(solution)/shard_map/ppermute | solution.py:53
  189.8 71.7 %collective-permute-start.15 = (bf16[560,1536]{1,0:T(8,128)(2,1)S(1)}, bf16[560,1536]{1,0:T(8,128)(2,1)S(1)}, u32[]{:S(2)}, u32[]{:S(2)}) collective-permute-start(bf16[560,1536]{1,0:T(8,128)(2,1)S(1)} %slice.310), channel_id=1, source_target_pairs={{0,4},{2,6},{4,0},{6,2},{1,5},{3,7},{5,1},{7,3}} | collective-permute-start | bytes 5160968 | tf_op jit(solution)/shard_map/ppermute | solution.py:57
  195.5 259.8 %collective-permute-start.31 = (bf16[1120,1536]{1,0:T(8,128)(2,1)}, bf16[1120,1536]{1,0:T(8,128)(2,1)}, u32[]{:S(2)}, u32[]{:S(2)}) collective-permute-start(bf16[1120,1536]{1,0:T(8,128)(2,1)} %slice_bitcast_fusion._.down_ref), channel_id=1, source_target_pairs={{0,2},{2,0},{4,6},{6,4},{1,3},{3,1},{5,7},{7,5}} | collective-permute-start | bytes 10321928 | tf_op jit(solution)/shard_map/ppermute | solution.py:57
  221.2 238.3 %collective-permute-start.32 = (bf16[1120,1536]{1,0:T(8,128)(2,1)}, bf16[1120,1536]{1,0:T(8,128)(2,1)}, u32[]{:S(2)}, u32[]{:S(2)}) collective-permute-start(bf16[1120,1536]{1,0:T(8,128)(2,1)} %slice_bitcast_fusion._.down_ref), channel_id=1, source_target_pairs={{0,4},{2,6},{4,0},{6,2},{1,5},{3,7},{5,1},{7,3}} | collective-permute-start | bytes 10321928 | tf_op jit(solution)/shard_map/ppermute | solution.py:57
  225.5 106.3 %collective-permute-start.16 = (bf16[560,1536]{1,0:T(8,128)(2,1)}, bf16[560,1536]{1,0:T(8,128)(2,1)}, u32[]{:S(2)}, u32[]{:S(2)}) collective-permute-start(bf16[560,1536]{1,0:T(8,128)(2,1)} %slice.311), channel_id=1, source_target_pairs={{0,2},{2,0},{4,6},{6,4},{1,3},{3,1},{5,7},{7,5}} | collective-permute-start | bytes 5160968 | tf_op jit(solution)/shard_map/ppermute | solution.py:57
  261.5 106.4 %collective-permute-start.11 = (bf16[192,4480]{1,0:T(8,128)(2,1)}, bf16[192,4480]{1,0:T(8,128)(2,1)}, u32[]{:S(2)}, u32[]{:S(2)}) collective-permute-start(bf16[192,4480]{1,0:T(8,128)(2,1)} %slice.308), channel_id=1, source_target_pairs={{0,4},{2,6},{4,0},{6,2},{1,5},{3,7},{5,1},{7,3}} | collective-permute-start | bytes 5160968 | tf_op jit(solution)/shard_map/ppermute | solution.py:57
  271.1 99.8 %collective-permute-start.12 = (bf16[192,4480]{1,0:T(8,128)(2,1)}, bf16[192,4480]{1,0:T(8,128)(2,1)}, u32[]{:S(2)}, u32[]{:S(2)}) collective-permute-start(bf16[192,4480]{1,0:T(8,128)(2,1)} %slice.309), channel_id=1, source_target_pairs={{0,2},{2,0},{4,6},{6,4},{1,3},{3,1},{5,7},{7,5}} | collective-permute-start | bytes 5160968 | tf_op jit(solution)/shard_map/ppermute | solution.py:57
  331.8 44.5 %collective-permute-start.7 = (bf16[1024,1536]{1,0:T(8,128)(2,1)S(1)}, bf16[1024,1536]{1,0:T(8,128)(2,1)}, u32[]{:S(2)}, u32[]{:S(2)}) collective-permute-start(bf16[1024,1536]{1,0:T(8,128)(2,1)S(1)} %fusion.24), channel_id=1, source_target_pairs={{0,1},{1,0},{2,3},{3,2},{4,5},{5,4},{6,7},{7,6}} | collective-permute-start | bytes 9437192 | tf_op jit(solution)/shard_map/ppermute | solution.py:53
  368.0 81.3 %collective-permute-start.35 = (bf16[1024,1536]{1,0:T(8,128)(2,1)}, bf16[1024,1536]{1,0:T(8,128)(2,1)}, u32[]{:S(2)}, u32[]{:S(2)}) collective-permute-start(bf16[1024,1536]{1,0:T(8,128)(2,1)} %bitcast.59), channel_id=1, source_target_pairs={{0,1},{1,0},{2,3},{3,2},{4,5},{5,4},{6,7},{7,6}} | collective-permute-start | bytes 9437192 | tf_op jit(solution)/shard_map/ppermute | solution.py:53
  375.8 93.9 %collective-permute-start.19 = (bf16[192,1792]{1,0:T(8,128)(2,1)}, bf16[192,1792]{1,0:T(8,128)(2,1)}, u32[]{:S(2)}, u32[]{:S(2)}) collective-permute-start(bf16[192,1792]{1,0:T(8,128)(2,1)} %broadcast_select_fusion.6), channel_id=1, source_target_pairs={{0,1},{1,0},{2,3},{3,2},{4,5},{5,4},{6,7},{7,6}} | collective-permute-start | bytes 2064392 | tf_op jit(solution)/shard_map/ppermute | solution.py:53
  449.3 47.3 %collective-permute-start.17 = (f32[1024,1536]{1,0:T(8,128)}, f32[1024,1536]{1,0:T(8,128)}, u32[]{:S(2)}, u32[]{:S(2)}) collective-permute-start(f32[1024,1536]{1,0:T(8,128)} %fusion.8), channel_id=1, source_target_pairs={{0,1},{1,0},{2,3},{3,2},{4,5},{5,4},{6,7},{7,6}} | collective-permute-start | bytes 18874376 | tf_op jit(solution)/shard_map/ppermute | solution.py:53
  458.1 138.3 %collective-permute-start.33 = (bf16[560,1536]{1,0:T(8,128)(2,1)}, bf16[560,1536]{1,0:T(8,128)(2,1)}, u32[]{:S(2)}, u32[]{:S(2)}) collective-permute-start(bf16[560,1536]{1,0:T(8,128)(2,1)} %slice.328), channel_id=1, source_target_pairs={{0,4},{2,6},{4,0},{6,2},{1,5},{3,7},{5,1},{7,3}} | collective-permute-start | bytes 5160968 | tf_op jit(solution)/shard_map/ppermute | solution.py:57
  462.3 136.8 %collective-permute-start.34 = (bf16[560,1536]{1,0:T(8,128)(2,1)}, bf16[560,1536]{1,0:T(8,128)(2,1)}, u32[]{:S(2)}, u32[]{:S(2)}) collective-permute-start(bf16[560,1536]{1,0:T(8,128)(2,1)} %slice.329), channel_id=1, source_target_pairs={{0,2},{2,0},{4,6},{6,4},{1,3},{3,1},{5,7},{7,5}} | collective-permute-start | bytes 5160968 | tf_op jit(solution)/shard_map/ppermute | solution.py:57
  469.6 34.2 %collective-permute-start.26 = (bf16[192,4480]{1,0:T(8,128)(2,1)}, bf16[192,4480]{1,0:T(8,128)(2,1)}, u32[]{:S(2)}, u32[]{:S(2)}) collective-permute-start(bf16[192,4480]{1,0:T(8,128)(2,1)} %get-tuple-element.48), channel_id=1, source_target_pairs={{0,1},{1,0},{2,3},{3,2},{4,5},{5,4},{6,7},{7,6}} | collective-permute-start | bytes 5160968 | tf_op jit(solution)/shard_map/ppermute | solution.py:53
  472.4 59.3 %collective-permute-start.20 = (bf16[384,1792]{1,0:T(8,128)(2,1)}, bf16[384,1792]{1,0:T(8,128)(2,1)S(1)}, u32[]{:S(2)}, u32[]{:S(2)}) collective-permute-start(bf16[384,1792]{1,0:T(8,128)(2,1)} %pad_maximum_fusion.11._), channel_id=1, source_target_pairs={{0,2},{2,0},{4,6},{6,4},{1,3},{3,1},{5,7},{7,5}} | collective-permute-start | bytes 4128776 | tf_op jit(solution)/shard_map/ppermute | solution.py:57
  496.6 35.8 %collective-permute-start.21 = (bf16[384,1792]{1,0:T(8,128)(2,1)}, bf16[384,1792]{1,0:T(8,128)(2,1)S(1)}, u32[]{:S(2)}, u32[]{:S(2)}) collective-permute-start(bf16[384,1792]{1,0:T(8,128)(2,1)} %pad_maximum_fusion.11._), channel_id=1, source_target_pairs={{0,4},{2,6},{4,0},{6,2},{1,5},{3,7},{5,1},{7,3}} | collective-permute-start | bytes 4128776 | tf_op jit(solution)/shard_map/ppermute | solution.py:57
  503.8 46.8 %collective-permute-start.18 = (bf16[1024,1536]{1,0:T(8,128)(2,1)S(1)}, bf16[1024,1536]{1,0:T(8,128)(2,1)S(1)}, u32[]{:S(2)}, u32[]{:S(2)}) collective-permute-start(bf16[1024,1536]{1,0:T(8,128)(2,1)S(1)} %fusion.28), channel_id=1, source_target_pairs={{0,1},{1,0},{2,3},{3,2},{4,5},{5,4},{6,7},{7,6}} | collective-permute-start | bytes 9437192 | tf_op jit(solution)/shard_map/ppermute | solution.py:53
  531.8 16.7 collective-permute-start.22
  532.4 16.6 collective-permute-start.23
  548.5 75.1 %collective-permute-start.27 = (bf16[384,4480]{1,0:T(8,128)(2,1)}, bf16[384,4480]{1,0:T(8,128)(2,1)}, u32[]{:S(2)}, u32[]{:S(2)}) collective-permute-start(bf16[384,4480]{1,0:T(8,128)(2,1)} %pad_maximum_fusion.7._), channel_id=1, source_target_pairs={{0,2},{2,0},{4,6},{6,4},{1,3},{3,1},{5,7},{7,5}} | collective-permute-start | bytes 10321928 | tf_op jit(solution)/shard_map/ppermute | solution.py:57
  549.1 77.9 %collective-permute-start.28 = (bf16[384,4480]{1,0:T(8,128)(2,1)}, bf16[384,4480]{1,0:T(8,128)(2,1)}, u32[]{:S(2)}, u32[]{:S(2)}) collective-permute-start(bf16[384,4480]{1,0:T(8,128)(2,1)} %pad_maximum_fusion.7._), channel_id=1, source_target_pairs={{0,4},{2,6},{4,0},{6,2},{1,5},{3,7},{5,1},{7,3}} | collective-permute-start | bytes 10321928 | tf_op jit(solution)/shard_map/ppermute | solution.py:57
  588.4 52.9 %collective-permute-start.24 = (f32[1024,1536]{1,0:T(8,128)}, f32[1024,1536]{1,0:T(8,128)}, u32[]{:S(2)}, u32[]{:S(2)}) collective-permute-start(f32[1024,1536]{1,0:T(8,128)} %fusion.58), channel_id=1, source_target_pairs={{0,1},{1,0},{2,3},{3,2},{4,5},{5,4},{6,7},{7,6}} | collective-permute-start | bytes 18874376 | tf_op jit(solution)/shard_map/ppermute | solution.py:53
  626.4 37.4 %collective-permute-start.29 = (bf16[192,4480]{1,0:T(8,128)(2,1)}, bf16[192,4480]{1,0:T(8,128)(2,1)}, u32[]{:S(2)}, u32[]{:S(2)}) collective-permute-start(bf16[192,4480]{1,0:T(8,128)(2,1)} %slice.326), channel_id=1, source_target_pairs={{0,4},{2,6},{4,0},{6,2},{1,5},{3,7},{5,1},{7,3}} | collective-permute-start | bytes 5160968 | tf_op jit(solution)/shard_map/ppermute | solution.py:57
  630.1 37.0 %collective-permute-start.30 = (bf16[192,4480]{1,0:T(8,128)(2,1)}, bf16[192,4480]{1,0:T(8,128)(2,1)}, u32[]{:S(2)}, u32[]{:S(2)}) collective-permute-start(bf16[192,4480]{1,0:T(8,128)(2,1)} %slice.327), channel_id=1, source_target_pairs={{0,2},{2,0},{4,6},{6,4},{1,3},{3,1},{5,7},{7,5}} | collective-permute-start | bytes 5160968 | tf_op jit(solution)/shard_map/ppermute | solution.py:57
  649.3 20.6 %collective-permute-start.25 = (bf16[1024,1536]{1,0:T(8,128)(2,1)S(1)}, bf16[1024,1536]{1,0:T(8,128)(2,1)S(1)}, u32[]{:S(2)}, u32[]{:S(2)}) collective-permute-start(bf16[1024,1536]{1,0:T(8,128)(2,1)S(1)} %fusion.21), channel_id=1, source_target_pairs={{0,1},{1,0},{2,3},{3,2},{4,5},{5,4},{6,7},{7,6}} | collective-permute-start | bytes 9437192 | tf_op jit(solution)/shard_map/ppermute | solution.py:53
  765.1 42.2 %collective-permute-start.36 = (f32[1024,1536]{1,0:T(8,128)}, f32[1024,1536]{1,0:T(8,128)S(1)}, u32[]{:S(2)}, u32[]{:S(2)}) collective-permute-start(f32[1024,1536]{1,0:T(8,128)} %mlp_back.5), channel_id=1, source_target_pairs={{0,1},{1,0},{2,3},{3,2},{4,5},{5,4},{6,7},{7,6}} | collective-permute-start | bytes 18874376 | tf_op jit(solution)/shard_map/ppermute | solution.py:53
  886.1 325.9 %all-gather.11.cloned.1.call-start = ((), (), s32[]{:S(2)}) async-start(), calls=%async_computation.5 | async-start | bytes 28311552 | tf_op jit(solution)/shard_map/all_gather | solution.py:101
  886.7 325.3 %all-gather.9.cloned.1.call-start = ((), (), s32[]{:S(2)}) async-start(), calls=%async_computation.4 | async-start | bytes 28311552 | tf_op jit(solution)/shard_map/all_gather | solution.py:101
  887.3 632.5 %reduce-scatter.3.cloned.1.call-start = ((), (), s32[]{:S(2)}) async-start(), calls=%async_computation.6 | async-start | bytes 13762560 | tf_op jit(solution)/shard_map/reduce_scatter | solution.py:105
  893.6 10.2 collective-permute-start.38
  963.3 42.5 %collective-permute-start.41 = (f32[1024,1536]{1,0:T(8,128)}, f32[1024,1536]{1,0:T(8,128)S(1)}, u32[]{:S(2)}, u32[]{:S(2)}) collective-permute-start(f32[1024,1536]{1,0:T(8,128)} %mlp_back.7), channel_id=1, source_target_pairs={{0,1},{1,0},{2,3},{3,2},{4,5},{5,4},{6,7},{7,6}} | collective-permute-start | bytes 18874376 | tf_op jit(solution)/shard_map/ppermute | solution.py:53
  1017.5 7.1 collective-permute-start.42
  1084.6 492.1 %all-gather.5.cloned.1.call-start = ((), (), s32[]{:S(2)}) async-start(), calls=%async_computation.2 | async-start | bytes 28311552 | tf_op jit(solution)/shard_map/all_gather | solution.py:101
  1085.2 491.5 %all-gather.7.cloned.1.call-start = ((), (), s32[]{:S(2)}) async-start(), calls=%async_computation.3 | async-start | bytes 28311552 | tf_op jit(solution)/shard_map/all_gather | solution.py:101
  1185.9 15.1 collective-permute-start.45
  1194.8 157.3 %collective-permute-start.43 = (f32[1024,1536]{1,0:T(8,128)}, f32[1024,1536]{1,0:T(8,128)}, u32[]{:S(2)}, u32[]{:S(2)}) collective-permute-start(f32[1024,1536]{1,0:T(8,128)} %fusion.48), channel_id=1, source_target_pairs={{0,1},{1,0},{2,3},{3,2},{4,5},{5,4},{6,7},{7,6}} | collective-permute-start | bytes 18874376 | tf_op jit(solution)/shard_map/ppermute | solution.py:53
  1350.2 172.0 %collective-permute-start.53 = (f32[192,1120]{1,0:T(8,128)}, f32[192,1120]{1,0:T(8,128)}, u32[]{:S(2)}, u32[]{:S(2)}) collective-permute-start(f32[192,1120]{1,0:T(8,128)} %get-tuple-element.66), channel_id=1, source_target_pairs={{0,1},{1,0},{2,3},{3,2},{4,5},{5,4},{6,7},{7,6}} | collective-permute-start | bytes 2580488 | tf_op jit(solution)/shard_map/ppermute | solution.py:332
  1350.3 173.4 %collective-permute-start.54 = (f32[192,1120]{1,0:T(8,128)}, f32[192,1120]{1,0:T(8,128)}, u32[]{:S(2)}, u32[]{:S(2)}) collective-permute-start(f32[192,1120]{1,0:T(8,128)} %get-tuple-element.67), channel_id=1, source_target_pairs={{0,2},{1,3},{2,0},{3,1},{4,6},{5,7},{6,4},{7,5}} | collective-permute-start | bytes 2580488 | tf_op jit(solution)/shard_map/ppermute | solution.py:332
  1351.7 172.4 %collective-permute-start.55 = (f32[192,1120]{1,0:T(8,128)}, f32[192,1120]{1,0:T(8,128)}, u32[]{:S(2)}, u32[]{:S(2)}) collective-permute-start(f32[192,1120]{1,0:T(8,128)} %get-tuple-element.68), channel_id=1, source_target_pairs={{0,3},{1,2},{2,1},{3,0},{4,7},{5,6},{6,5},{7,4}} | collective-permute-start | bytes 2580488 | tf_op jit(solution)/shard_map/ppermute | solution.py:332
  1357.6 175.9 %collective-permute-start.56 = (f32[192,1120]{1,0:T(8,128)}, f32[192,1120]{1,0:T(8,128)}, u32[]{:S(2)}, u32[]{:S(2)}) collective-permute-start(f32[192,1120]{1,0:T(8,128)} %get-tuple-element.69), channel_id=1, source_target_pairs={{0,4},{1,5},{2,6},{3,7},{4,0},{5,1},{6,2},{7,3}} | collective-permute-start | bytes 2580488 | tf_op jit(solution)/shard_map/ppermute | solution.py:332
  1359.1 174.4 %collective-permute-start.57 = (f32[192,1120]{1,0:T(8,128)}, f32[192,1120]{1,0:T(8,128)}, u32[]{:S(2)}, u32[]{:S(2)}) collective-permute-start(f32[192,1120]{1,0:T(8,128)} %get-tuple-element.70), channel_id=1, source_target_pairs={{0,5},{1,4},{2,7},{3,6},{4,1},{5,0},{6,3},{7,2}} | collective-permute-start | bytes 2580488 | tf_op jit(solution)/shard_map/ppermute | solution.py:332
  1522.2 23.7 %collective-permute-start.58 = (f32[192,1120]{1,0:T(8,128)}, f32[192,1120]{1,0:T(8,128)}, u32[]{:S(2)}, u32[]{:S(2)}) collective-permute-start(f32[192,1120]{1,0:T(8,128)} %get-tuple-element.71), channel_id=1, source_target_pairs={{0,6},{1,7},{2,4},{3,5},{4,2},{5,3},{6,0},{7,1}} | collective-permute-start | bytes 2580488 | tf_op jit(solution)/shard_map/ppermute | solution.py:332
  1523.7 38.6 %collective-permute-start.59 = (f32[192,1120]{1,0:T(8,128)}, f32[192,1120]{1,0:T(8,128)}, u32[]{:S(2)}, u32[]{:S(2)}) collective-permute-start(f32[192,1120]{1,0:T(8,128)} %get-tuple-element.72), channel_id=1, source_target_pairs={{0,7},{1,6},{2,5},{3,4},{4,3},{5,2},{6,1},{7,0}} | collective-permute-start | bytes 2580488 | tf_op jit(solution)/shard_map/ppermute | solution.py:332
  1524.1 46.2 %collective-permute-start.44 = (f32[192,1792]{1,0:T(8,128)}, f32[192,1792]{1,0:T(8,128)}, u32[]{:S(2)}, u32[]{:S(2)}) collective-permute-start(f32[192,1792]{1,0:T(8,128)} %dynamic-slice_bitcast_fusion.1), channel_id=1, source_target_pairs={{0,1},{1,0},{2,3},{3,2},{4,5},{5,4},{6,7},{7,6}} | collective-permute-start | bytes 4128776 | tf_op jit(solution)/shard_map/ppermute | solution.py:53
  1736.7 102.1 %collective-permute-start.39 = (f32[1024,1536]{1,0:T(8,128)}, f32[1024,1536]{1,0:T(8,128)}, u32[]{:S(2)}, u32[]{:S(2)}) collective-permute-start(f32[1024,1536]{1,0:T(8,128)} %fusion.4), channel_id=1, source_target_pairs={{0,1},{1,0},{2,3},{3,2},{4,5},{5,4},{6,7},{7,6}} | collective-permute-start | bytes 18874376 | tf_op jit(solution)/shard_map/ppermute | solution.py:53
  1739.2 12.7 collective-permute-start.46
  1739.2 22.8 %collective-permute-start.47 = (f32[192,1120]{1,0:T(8,128)}, f32[192,1120]{1,0:T(8,128)}, u32[]{:S(2)}, u32[]{:S(2)}) collective-permute-start(f32[192,1120]{1,0:T(8,128)} %get-tuple-element.59), channel_id=1, source_target_pairs={{0,2},{1,3},{2,0},{3,1},{4,6},{5,7},{6,4},{7,5}} | collective-permute-start | bytes 2580488 | tf_op jit(solution)/shard_map/ppermute | solution.py:332
  1740.7 39.3 %collective-permute-start.48 = (f32[192,1120]{1,0:T(8,128)}, f32[192,1120]{1,0:T(8,128)}, u32[]{:S(2)}, u32[]{:S(2)}) collective-permute-start(f32[192,1120]{1,0:T(8,128)} %get-tuple-element.60), channel_id=1, source_target_pairs={{0,3},{1,2},{2,1},{3,0},{4,7},{5,6},{6,5},{7,4}} | collective-permute-start | bytes 2580488 | tf_op jit(solution)/shard_map/ppermute | solution.py:332
  1750.4 53.2 %collective-permute-start.49 = (f32[192,1120]{1,0:T(8,128)S(1)}, f32[192,1120]{1,0:T(8,128)S(1)}, u32[]{:S(2)}, u32[]{:S(2)}) collective-permute-start(f32[192,1120]{1,0:T(8,128)S(1)} %copy-done.87), channel_id=1, source_target_pairs={{0,4},{1,5},{2,6},{3,7},{4,0},{5,1},{6,2},{7,3}} | collective-permute-start | bytes 2580488 | tf_op jit(solution)/shard_map/ppermute | solution.py:332
  1751.9 76.6 %collective-permute-start.50 = (f32[192,1120]{1,0:T(8,128)S(1)}, f32[192,1120]{1,0:T(8,128)S(1)}, u32[]{:S(2)}, u32[]{:S(2)}) collective-permute-start(f32[192,1120]{1,0:T(8,128)S(1)} %copy-done.86), channel_id=1, source_target_pairs={{0,5},{1,4},{2,7},{3,6},{4,1},{5,0},{6,3},{7,2}} | collective-permute-start | bytes 2580488 | tf_op jit(solution)/shard_map/ppermute | solution.py:332
  1762.1 66.4 %collective-permute-start.51 = (f32[192,1120]{1,0:T(8,128)S(1)}, f32[192,1120]{1,0:T(8,128)S(1)}, u32[]{:S(2)}, u32[]{:S(2)}) collective-permute-start(f32[192,1120]{1,0:T(8,128)S(1)} %copy-done.85), channel_id=1, source_target_pairs={{0,6},{1,7},{2,4},{3,5},{4,2},{5,3},{6,0},{7,1}} | collective-permute-start | bytes 2580488 | tf_op jit(solution)/shard_map/ppermute | solution.py:332
  1780.0 48.4 %collective-permute-start.52 = (f32[192,1120]{1,0:T(8,128)S(1)}, f32[192,1120]{1,0:T(8,128)S(1)}, u32[]{:S(2)}, u32[]{:S(2)}) collective-permute-start(f32[192,1120]{1,0:T(8,128)S(1)} %copy-done.84), channel_id=1, source_target_pairs={{0,7},{1,6},{2,5},{3,4},{4,3},{5,2},{6,1},{7,0}} | collective-permute-start | bytes 2580488 | tf_op jit(solution)/shard_map/ppermute | solution.py:332
  (98 other events, 2377.5 us)
Sparse Core Ops, SparseCore 0:
  886.2 298.0 reduce-scatter.4
  1187.4 332.2 reduce-scatter.2
Sparse Core Ops, SparseCore 1:
  888.4 141.2 all-gather.10
  1031.3 139.9 all-gather.8
  1173.0 129.8 all-gather.4
  1304.7 180.3 all-gather.6

commit v8 on v6

--- a/solution.py
+++ b/solution.py
@@ -19,6 +19,7 @@
 TOKEN_TILE = 512
 ROW_TILE = 48
 FLIP_TILE = 256
+WIDTH_TILE = 512
 NEIGHBOURS = (1, 2)
 
 
@@ -45,10 +46,6 @@
 
 def times_flipped(left, right):
     return dot(left, right, ((1,), (1,)))
-
-
-def over_rows(left, right):
-    return dot(left, right, ((0,), (0,)))
 
 
 def swap(value):
@@ -72,8 +69,39 @@
     rows = grad.shape[0] // CORES
     grad = grad.reshape((CORES, rows) + grad.shape[1:])
     keep = lax.dynamic_index_in_dim(grad, core, 0, keepdims=False)
-    send = lax.dynamic_index_in_dim(grad, 1 - core, 0, keepdims=False)
-    return by_core(core, keep, swap(send))
+    return keep, swap(lax.dynamic_index_in_dim(grad, 1 - core, 0, keepdims=False))
+
+
+def heads_kernel(place_ref, mine_ref, other_ref, *refs):
+    outs = refs[-4:]
+    head = outs[0].shape[3]
+    for part in range(CORES):
+        mine, other = mine_ref[...], other_ref[...]
+        cols = jnp.where(place_ref[1] == part, mine, other)
+        start = 0
+        for out in outs:
+            count = out.shape[2] // CORES
+            for i in range(count):
+                out[0, :, part * count + i, :] = cols[:, start:start + head]
+                start += head
+
+
+def place_heads(place, layer, shapes, earlier, mine, other):
+    rows, cols = mine.shape
+    anywhere = [pl.BlockSpec(memory_space=pl.ANY)] * len(earlier)
+    return pl.pallas_call(
+        heads_kernel,
+        grid_spec=pltpu.PrefetchScalarGridSpec(
+            num_scalar_prefetch=1,
+            grid=(rows // ROW_TILE,),
+            in_specs=[pl.BlockSpec((ROW_TILE, cols), lambda i, p: (i, 0))] * CORES + anywhere,
+            out_specs=[pl.BlockSpec((1, ROW_TILE) + shape[2:], lambda i, p: (layer, i, 0, 0)) for shape in shapes],
+        ),
+        out_shape=[jax.ShapeDtypeStruct(shape, jnp.float32) for shape in shapes],
+        input_output_aliases={3 + i: i for i in range(len(earlier))},
+        cost_estimate=pl.CostEstimate(flops=2_000_000_000, bytes_accessed=0, transcendentals=0),
+        name="place_heads",
+    )(place, mine, other, *earlier)
 
 
 def blank_kernel(_, out_ref):
@@ -190,6 +218,28 @@
     return y_own, (x_own, normed, qkv, o_act)
 
 
+def attn_grads_kernel(norm_ref, d_qkv_ref, grad_ref, o_ref, out_ref):
+    width = d_qkv_ref.shape[1]
+    out_ref[:, :width] = dot(norm_ref[...], d_qkv_ref[...], ((0,), (0,)))
+    out_ref[:, width:] = dot(grad_ref[...], o_ref[...], ((0,), (0,)))
+
+
+def attn_grads(normed, d_qkv, grad_y, o_act):
+    rows, width = normed.shape
+    cols = d_qkv.shape[1] + o_act.shape[1]
+    piece = pl.BlockSpec((rows, WIDTH_TILE), lambda i: (0, i))
+    whole = [pl.BlockSpec(arg.shape, lambda i: (0, 0), pipeline_mode=pl.Buffered(1)) for arg in (d_qkv, o_act)]
+    return pl.pallas_call(
+        attn_grads_kernel,
+        grid=(width // WIDTH_TILE,),
+        in_specs=[piece, whole[0], piece, whole[1]],
+        out_specs=pl.BlockSpec((WIDTH_TILE, cols), lambda i: (i, 0)),
+        out_shape=jax.ShapeDtypeStruct((width, cols), jnp.float32),
+        cost_estimate=pl.CostEstimate(flops=2 * rows * width * cols, bytes_accessed=0, transcendentals=0),
+        name="attn_grads",
+    )(normed, d_qkv, grad_y, o_act)
+
+
 def attn_backward(saved, weight, q_width, head, seq, grad_own):
     x_own, normed, qkv, o_act = saved
     grad_y = pair_rows(grad_own)
@@ -198,7 +248,7 @@
                   40_000_000_000)
     d_norm = both_halves(d_qkv, weight[:, :q_width + 2 * head], grad_own.shape[0], times_flipped)
     grad_x = (grad_own.astype(jnp.float32) + norm_back(x_own, d_norm)).astype(jnp.bfloat16)
-    return grad_x, over_rows(normed, d_qkv), over_rows(grad_y, o_act)
+    return grad_x, attn_grads(normed, d_qkv, grad_y, o_act)
 
 
 def gelu_parts(hidden):
@@ -418,25 +468,19 @@
             if layer < pairs - 1:
                 carry_x = mlp_output(x_own, gelu_act, down_full[layer])
         last = (x_own, gelu_act, down_full[-1])
-        grad_lists = ([], [], [], [])
+        d_heads, head_shapes = [], [weight.shape for weight in (w_q, w_k, w_v, w_o)]
         for layer in reversed(range(pairs)):
             x_own, norms, slope = mlp_saved[layer]
             if layer < pairs - 1:
                 parts, d_down = weight_grads(layer, norms, gather_rows(grad_x), d_down)
             d_up = [assemble(place, layer, pairs, d_up, parts)]
             grad_x = mlp_backward(x_own, slope, up_full[layer], down_full[layer], grad_x)
-            grad_x, d_qkv, d_o = attn_backward(attn_saved[layer], attn_full[layer], q_width, head, seq, grad_x)
-            parts = to_rows(core, scatter_sum(d_o))
-            grad_lists[3].append(jnp.concatenate(parts, axis=1).reshape(shard, heads, head))
-            parts = to_rows(core, scatter_sum(d_qkv))
-            grad_lists[0].append(jnp.concatenate([part[:, :q_width] for part in parts], axis=1)
-                                 .reshape(shard, heads, head))
-            grad_lists[1].append(jnp.stack([part[:, q_width:q_width + head] for part in parts], axis=1))
-            grad_lists[2].append(jnp.stack([part[:, q_width + head:] for part in parts], axis=1))
+            grad_x, d_attn = attn_backward(attn_saved[layer], attn_full[layer], q_width, head, seq, grad_x)
+            parts = to_rows(core, scatter_sum(d_attn))
+            d_heads = place_heads(place, layer, head_shapes, d_heads, *parts)
         last, d_down = lax.optimization_barrier((last, d_down))
         y_loc = mlp_output(*last).reshape(x_loc.shape)
-        stacked = tuple(jnp.stack(grad_list[::-1]) for grad_list in grad_lists)
-        return (y_loc, grad_x.reshape(x_loc.shape)) + stacked + (d_up[0], d_down[0])
+        return (y_loc, grad_x.reshape(x_loc.shape)) + (*d_heads, d_up[0], d_down[0])
 
     return jax.shard_map(body, mesh=mesh, in_specs=(row_spec,) + (weight_spec,) * 6 + (row_spec,),
                          out_specs=(row_spec, row_spec) + (weight_spec,) * 6, check_vma=False)

time: 1940 us -> 1890 us (0.974)
  waiting for transfers between devices: 708 us -> 604 us
  Pallas kernels: 415 us -> 467 us
    all_gather x4, waiting for transfers between devices: 114 us -> 0.01 us  [gather_rows(): return functools.partial(lax.all_gather, axis=0, tiled=True)(value, AXES)]
    pallas_call x0 -> x4, Pallas kernels: none -> 48.6 us  [the longest x2 37.5 us: attn_grads(): pl.pallas_call(attn_grads_kernel, grid=(width // WIDTH_TILE,), in_specs=[...]
    reduce_scatter x4 -> x2, waiting for transfers between devices: 213 us -> 232 us  [scatter_sum(): return lax.psum_scatter(grad_full, CHIP, scatter_dimension=0, tiled=True)]
    dot_general x28 -> x24, matrix products: 485 us -> 467 us  [dot(): lax.dot_general(left, right, (contract, ((), ())), preferred_element_type...]
  transfers between devices with their start and end apart: 70 -> 66, of which waited for: 24 -> 22; matrix products, arithmetic and copies ran while one was open for 32% -> 33% of each run, Pallas kernels for 20% -> 22%
where the time goes in v8:
time: 1890 us; the launch traced here: 1880 us
  waiting for transfers between devices  604 us (32%)
  Pallas kernels  467 us (25%)
  matrix products  467 us (25%)
  local copies, waits for them, and re-layouts  169 us (9%)
  other arithmetic  114 us (6%)
  starting transfers between devices  45.3 us (2%)
    dot_general x24, matrix products, dot(): lax.dot_general(left, right, (contract, ((), ())), preferred_element_type...  467 us
    ppermute x24, waiting for transfers between devices, hop(): lax.ppermute(value, CHIP, [(chip, chip ^ step) for chip in range(CHIPS)])  299 us
    pallas_call x2, Pallas kernels, mlp_weight_grads(): pl.pallas_call(mlp_grads_kernel, grid_spec=pltpu.PrefetchScalarGridSpec(n...  281 us
    reduce_scatter x2, waiting for transfers between devices, scatter_sum(): return lax.psum_scatter(grad_full, CHIP, scatter_dimension=0, tiled=True)  232 us
    pallas_call x4, Pallas kernels, by_sequence(): pl.pallas_call(functools.partial(kernel, q_width, head), grid=(rows // se...  89.9 us
    dynamic_update_slice x26, local copies, waits for them, and re-layouts, gather_weight(): full = lax.dynamic_update_slice(full, part[None], (chip ^ step, row, 0))  69.6 us
    ppermute x14, waiting for transfers between devices, exchange(): lax.ppermute(part, AXES, [(d, d ^ i) for d in devices])  62.9 us
  transfers between devices with their start and end apart: 66, of which 22 were waited for; matrix products, arithmetic and copies ran while one was open for 33% of the time, Pallas kernels for 22%

profile of v8, /device:TPU:0, one launch (start us, length us, event | category | flops | bytes accessed | tf_op | source)
XLA Modules:
  0.0 1882.9 jit_solution(6383277125659953698)
XLA Ops:
  12.0 6.4 slice_dynamic-update-slice_fusion
  45.1 6.5 split.2
  89.0 36.9 %collective-permute-done.2 = bf16[384,1792]{1,0:T(8,128)(2,1)} collective-permute-done((bf16[384,1792]{1,0:T(8,128)(2,1)}, bf16[384,1792]{1,0:T(8,128)(2,1)}, u32[]{:S(2)}, u32[]{:S(2)}) %collective-permute-start.2) | collective-permute-done | bytes 1376288 | tf_op jit(solution)/shard_map/ppermute | solution.py:56
  136.7 7.0 collective-permute-done.4
  150.1 21.3 %convolution_convert_fusion.1.qkv_ref = bf16[2048,1024]{1,0:T(8,128)(2,1)} fusion(bf16[1536,1792]{1,0:T(8,128)(2,1)} %bitcast.169, bf16[1024,1536]{1,0:T(8,128)(2,1)} %collective-permute-done, bf16[1024,1536]{1,0:T(8,128)(2,1)} %fusion.54), kind=kOutput, calls=%fused_computation.92 | convolution fusion | flops 6457131008 | bytes 13631488 | tf_op jit(solution)/shard_map/dot_general | solution.py:40
  171.4 17.1 shard_map.143.o_ref
  196.6 6.2 fusion.79
  218.2 75.5 %collective-permute-done.9 = bf16[384,4480]{1,0:T(8,128)(2,1)} collective-permute-done((bf16[384,4480]{1,0:T(8,128)(2,1)}, bf16[384,4480]{1,0:T(8,128)(2,1)}, u32[]{:S(2)}, u32[]{:S(2)}) %collective-permute-start.9) | collective-permute-done | bytes 3440672 | tf_op jit(solution)/shard_map/ppermute | solution.py:56
  300.9 53.0 %collective-permute-done.10 = bf16[384,4480]{1,0:T(8,128)(2,1)S(1)} collective-permute-done((bf16[384,4480]{1,0:T(8,128)(2,1)}, bf16[384,4480]{1,0:T(8,128)(2,1)S(1)}, u32[]{:S(2)}, u32[]{:S(2)}) %collective-permute-start.10) | collective-permute-done | bytes 3440672 | tf_op jit(solution)/shard_map/ppermute | solution.py:56
  364.4 26.5 %collective-permute-done.15 = bf16[560,1536]{1,0:T(8,128)(2,1)} collective-permute-done((bf16[560,1536]{1,0:T(8,128)(2,1)}, bf16[560,1536]{1,0:T(8,128)(2,1)}, u32[]{:S(2)}, u32[]{:S(2)}) %collective-permute-start.15) | collective-permute-done | bytes 1720352 | tf_op jit(solution)/shard_map/ppermute | solution.py:56
  398.3 27.9 %collective-permute-done.11 = bf16[192,4480]{1,0:T(8,128)(2,1)} collective-permute-done((bf16[192,4480]{1,0:T(8,128)(2,1)}, bf16[192,4480]{1,0:T(8,128)(2,1)}, u32[]{:S(2)}, u32[]{:S(2)}) %collective-permute-start.11) | collective-permute-done | bytes 1720352 | tf_op jit(solution)/shard_map/ppermute | solution.py:56
  429.0 6.3 collective-permute-done.12
  436.6 51.7 %multiply_add_fusion.2 = (f32[2048,4480]{1,0:T(8,128)}, bf16[2048,4480]{1,0:T(8,128)(2,1)}) fusion(bf16[1536,4480]{1,0:T(8,128)(2,1)} %bitcast.152, bf16[1024,1536]{1,0:T(8,128)(2,1)} %collective-permute-done.7, bf16[1024,1536]{1,0:T(8,128)(2,1)S(1)} %fusion.32), kind=kOutput, calls=%fused_computation.6 | convolution fusion | flops 28326756352 | bytes 75104256 | tf_op jit(solution)/shard_map/dot_general | solution.py:40
  488.4 21.5 %fusion.16 = f32[1024,1536]{1,0:T(8,128)} fusion(bf16[4480,1536]{1,0:T(8,128)(2,1)} %bitcast.163, bf16[2048,4480]{1,0:T(8,128)(2,1)} %get-tuple-element.52), kind=kOutput, calls=%fused_computation.40 | convolution fusion | flops 14092861440 | bytes 29229056 | tf_op jit(solution)/shard_map/dot_general | solution.py:40
  516.7 6.7 split.3
  527.7 21.5 %fusion.18 = f32[1024,1536]{1,0:T(8,128)} fusion(bf16[4480,1536]{1,0:T(8,128)(2,1)} %bitcast.164, bf16[2048,4480]{1,0:T(8,128)(2,1)} %get-tuple-element.52), kind=kOutput, calls=%fused_computation.42 | convolution fusion | flops 14092861440 | bytes 29229056 | tf_op jit(solution)/shard_map/dot_general | solution.py:40
  551.3 6.0 fusion.35
  564.0 21.4 %collective-permute-done.20 = bf16[384,1792]{1,0:T(8,128)(2,1)S(1)} collective-permute-done((bf16[384,1792]{1,0:T(8,128)(2,1)}, bf16[384,1792]{1,0:T(8,128)(2,1)S(1)}, u32[]{:S(2)}, u32[]{:S(2)}) %collective-permute-start.20) | collective-permute-done | bytes 1376288 | tf_op jit(solution)/shard_map/ppermute | solution.py:56
  588.0 14.0 collective-permute-done.22
  607.3 9.7 convolution_convert_fusion.qkv_ref
  617.0 17.3 shard_map.144.o_ref
  634.3 7.4 fusion.72
  659.7 17.4 collective-permute-done.27
  688.0 6.1 fusion.74
  694.1 5.8 fusion.28
  707.3 9.9 collective-permute-done.29
  724.7 52.0 %multiply_add_fusion = (f32[2048,4480]{1,0:T(8,128)}, bf16[2048,4480]{1,0:T(8,128)(2,1)}) fusion(bf16[1536,4480]{1,0:T(8,128)(2,1)} %bitcast.159, bf16[1024,1536]{1,0:T(8,128)(2,1)} %copy-done.83, bf16[1024,1536]{1,0:T(8,128)(2,1)} %copy-done.26), kind=kOutput, calls=%fused_computation.2 | convolution fusion | flops 28326756352 | bytes 75104256 | tf_op jit(solution)/shard_map/dot_general | solution.py:40
  776.8 40.8 %multiply_convert_fusion.1 = bf16[2048,4480]{1,0:T(8,128)(2,1)} fusion(f32[2048,4480]{1,0:T(8,128)} %get-tuple-element.58, bf16[4480,1536]{1,0:T(8,128)(2,1)} %bitcast.156, bf16[1024,1536]{1,0:T(8,128)(2,1)} %collective-permute-done.35, bf16[1024,1536]{1,0:T(8,128)(2,1)S(1)} %bitcast.168), kind=kOutput, calls=%fused_computation.1 | convolution fusion | flops 28216655872 | bytes 75104256 | tf_op jit(solution)/shard_map/dot_general | solution.py:40
  817.6 21.6 %fusion.8 = f32[1024,1536]{1,0:T(8,128)} fusion(bf16[1536,4480]{1,0:T(8,128)(2,1)} %bitcast.160, bf16[2048,4480]{1,0:T(8,128)(2,1)} %multiply_convert_fusion.1), kind=kOutput, calls=%fused_computation.32 | convolution fusion | flops 14092861440 | bytes 29229056 | tf_op jit(solution)/shard_map/dot_general | solution.py:40
  839.2 19.2 %fusion.10 = f32[1024,1536]{1,0:T(8,128)S(1)} fusion(bf16[1536,4480]{1,0:T(8,128)(2,1)} %bitcast.161, bf16[2048,4480]{1,0:T(8,128)(2,1)} %multiply_convert_fusion.1), kind=kOutput, calls=%fused_computation.34 | convolution fusion | flops 14092861440 | bytes 29229056 | tf_op jit(solution)/shard_map/dot_general | solution.py:40
  866.5 5.6 pad_maximum_fusion.1.norm_ref
  873.9 10.0 convolution_convert_fusion.3.d_o_ref
  883.9 27.6 %shard_map.145.d_qkv_ref = bf16[2048,1024]{1,0:T(8,128)(2,1)} custom-call(bf16[2048,1024]{1,0:T(8,128)(2,1)} %convolution_convert_fusion.qkv_ref, bf16[2048,768]{1,0:T(8,128)(2,1)} %convolution_convert_fusion.3.d_o_ref), custom_call_target="tpu_custom_call" | custom-call | flops 40000000000 | tf_op jit(solution)/shard_map/pallas_call | solution.py:200
  916.5 18.8 attn_grads.3
  935.9 9.4 fusion.57
  946.2 7.2 fusion.59
  960.5 5.5 fusion.23
  966.3 5.6 collective-permute-done.40
  971.9 41.5 %multiply_convert_fusion = bf16[2048,4480]{1,0:T(8,128)(2,1)} fusion(f32[2048,4480]{1,0:T(8,128)} %get-tuple-element.64, bf16[4480,1536]{1,0:T(8,128)(2,1)} %bitcast.165, bf16[1024,1536]{1,0:T(8,128)(2,1)S(1)} %collective-permute-done.40, bf16[1024,1536]{1,0:T(8,128)(2,1)} %fusion.23), kind=kOutput, calls=%fused_computation | convolution fusion | flops 28216655872 | bytes 75104256 | tf_op jit(solution)/shard_map/dot_general | solution.py:40
  1013.4 21.6 %fusion.4 = f32[1024,1536]{1,0:T(8,128)} fusion(bf16[1536,4480]{1,0:T(8,128)(2,1)} %bitcast.153, bf16[2048,4480]{1,0:T(8,128)(2,1)} %multiply_convert_fusion), kind=kOutput, calls=%fused_computation.28 | convolution fusion | flops 14092861440 | bytes 29229056 | tf_op jit(solution)/shard_map/dot_general | solution.py:40
  1035.8 21.8 %fusion.6 = f32[1024,1536]{1,0:T(8,128)} fusion(bf16[1536,4480]{1,0:T(8,128)(2,1)} %bitcast.154, bf16[2048,4480]{1,0:T(8,128)(2,1)} %multiply_convert_fusion), kind=kOutput, calls=%fused_computation.30 | convolution fusion | flops 14092861440 | bytes 29229056 | tf_op jit(solution)/shard_map/dot_general | solution.py:40
  1066.6 7.1 pad_maximum_fusion.norm_ref
  1076.7 10.1 convolution_convert_fusion.2.d_o_ref
  1086.8 28.0 %shard_map.146.d_qkv_ref = bf16[2048,1024]{1,0:T(8,128)(2,1)} custom-call(bf16[2048,1024]{1,0:T(8,128)(2,1)} %convolution_convert_fusion.1.qkv_ref, bf16[2048,768]{1,0:T(8,128)(2,1)} %convolution_convert_fusion.2.d_o_ref), custom_call_target="tpu_custom_call" | custom-call | flops 40000000000 | tf_op jit(solution)/shard_map/pallas_call | solution.py:200
  1114.8 18.7 attn_grads.2
  1134.8 9.2 fusion.62
  1144.6 89.0 %reduce-scatter.5.cloned.1.call-done = f32[384,1792]{1,0:T(8,128)} async-done(((f32[1536,1792]{1,0:T(8,128)}), f32[384,1792]{1,0:T(8,128)}) %reduce-scatter.5.cloned.1.call-update) | async-done | bytes 2752528 | tf_op jit(solution)/shard_map/reduce_scatter | solution.py:135
  1237.1 9.4 flip.2.up_ref
  1246.5 8.9 flip.3.up_ref
  1255.4 8.7 fusion.64
  1264.1 5.7 place_heads.2
  1269.8 9.3 fusion.56
  1279.7 142.5 %mlp_grads.2 = (f32[2,1120,1536]{2,1,0:T(8,128)}, f32[192,1120]{1,0:T(8,128)}, f32[192,1120]{1,0:T(8,128)}, f32[192,1120]{1,0:T(8,128)}, f32[192,1120]{1,0:T(8,1...) custom-call(s32[2]{0:T(128)} %pad_add_fusion.place_ref, ...), custom_call_target="tpu_custom_call" | custom-call | flops 112742891520 | tf_op jit(solution)/shard_map/mlp_grads/pallas_call | solution.py:312
  1425.7 142.5 %reduce-scatter.3.cloned.1.call-done = f32[384,1792]{1,0:T(8,128)} async-done(((f32[1536,1792]{1,0:T(8,128)}), f32[384,1792]{1,0:T(8,128)}) %reduce-scatter.3.cloned.1.call-update) | async-done | bytes 2752528 | tf_op jit(solution)/shard_map/reduce_scatter | solution.py:135
  1571.7 138.2 %mlp_grads.3 = (f32[2,1120,1536]{2,1,0:T(8,128)}, f32[192,1120]{1,0:T(8,128)}, f32[192,1120]{1,0:T(8,128)}, f32[192,1120]{1,0:T(8,128)}, f32[192,1120]{1,0:T(8,1...) custom-call(s32[2]{0:T(128)} %pad_add_fusion.place_ref, ...), custom_call_target="tpu_custom_call", output_to_operand_aliasing={{0}: (5, {})} | custom-call | flops 112742891520 | tf_op jit(solution)/shard_map/mlp_grads/pallas_call | solution.py:312
  1712.9 21.7 %fusion.12 = f32[1024,1536]{1,0:T(8,128)} fusion(bf16[4480,1536]{1,0:T(8,128)(2,1)} %bitcast.157, bf16[2048,4480]{1,0:T(8,128)(2,1)} %get-tuple-element.62), kind=kOutput, calls=%fused_computation.36 | convolution fusion | flops 14092861440 | bytes 29229056 | tf_op jit(solution)/shard_map/dot_general | solution.py:40
  1738.2 12.5 collective-permute-done.59.refs_7_
  1757.7 8.1 assemble.2.refs_8_
  1781.7 7.0 collective-permute-done.48.refs_3_
  1791.7 21.5 %fusion.14 = f32[1024,1536]{1,0:T(8,128)} fusion(bf16[4480,1536]{1,0:T(8,128)(2,1)} %bitcast.158, bf16[2048,4480]{1,0:T(8,128)(2,1)} %get-tuple-element.62), kind=kOutput, calls=%fused_computation.38 | convolution fusion | flops 14092861440 | bytes 29229056 | tf_op jit(solution)/shard_map/dot_general | solution.py:40
  1813.2 25.9 %collective-permute-done.49.refs_4_ = f32[192,1120]{1,0:T(8,128)S(1)} collective-permute-done((f32[192,1120]{1,0:T(8,128)S(1)}, f32[192,1120]{1,0:T(8,128)S(1)}, u32[]{:S(2)}, u32[]{:S(2)}) %collective-permute-start.49) | collective-permute-done | bytes 860192 | tf_op jit(solution)/shard_map/ppermute | solution.py:335
  1839.0 17.6 collective-permute-done.50.refs_5_
  1858.8 8.1 assemble.3
  1866.9 8.1 add_convert_fusion
  (426 shorter events, 292.5 us)
Async XLA Ops:
  8.0 1225.6 %reduce-scatter.5.cloned.1.call-start = ((), (), s32[]{:S(2)}) async-start(), calls=%async_computation.7 | async-start | bytes 13762560 | tf_op jit(solution)/shard_map/reduce_scatter | solution.py:135
  18.3 184.4 %collective-permute-start.13 = (bf16[1120,1536]{1,0:T(8,128)(2,1)}, bf16[1120,1536]{1,0:T(8,128)(2,1)}, u32[]{:S(2)}, u32[]{:S(2)}) collective-permute-start(bf16[1120,1536]{1,0:T(8,128)(2,1)} %get-tuple-element.115._.down_ref), channel_id=1, source_target_pairs={{0,2},{2,0},{4,6},{6,4},{1,3},{3,1},{5,7},{7,5}} | collective-permute-start | bytes 10321928 | tf_op jit(solution)/shard_map/ppermute | solution.py:56
  21.7 183.8 %collective-permute-start.14 = (bf16[1120,1536]{1,0:T(8,128)(2,1)}, bf16[1120,1536]{1,0:T(8,128)(2,1)}, u32[]{:S(2)}, u32[]{:S(2)}) collective-permute-start(bf16[1120,1536]{1,0:T(8,128)(2,1)} %get-tuple-element.115._.down_ref), channel_id=1, source_target_pairs={{0,4},{2,6},{4,0},{6,2},{1,5},{3,7},{5,1},{7,3}} | collective-permute-start | bytes 10321928 | tf_op jit(solution)/shard_map/ppermute | solution.py:56
  39.9 36.2 %collective-permute-start.1 = (bf16[192,1792]{1,0:T(8,128)(2,1)}, bf16[192,1792]{1,0:T(8,128)(2,1)}, u32[]{:S(2)}, u32[]{:S(2)}) collective-permute-start(bf16[192,1792]{1,0:T(8,128)(2,1)} %broadcast_select_fusion.10), channel_id=1, source_target_pairs={{0,1},{1,0},{2,3},{3,2},{4,5},{5,4},{6,7},{7,6}} | collective-permute-start | bytes 2064392 | tf_op jit(solution)/shard_map/ppermute | solution.py:52
  44.0 106.1 %collective-permute-start = (bf16[1024,1536]{1,0:T(8,128)(2,1)}, bf16[1024,1536]{1,0:T(8,128)(2,1)}, u32[]{:S(2)}, u32[]{:S(2)}) collective-permute-start(bf16[1024,1536]{1,0:T(8,128)(2,1)} %fusion.54), channel_id=1, source_target_pairs={{0,1},{1,0},{2,3},{3,2},{4,5},{5,4},{6,7},{7,6}} | collective-permute-start | bytes 9437192 | tf_op jit(solution)/shard_map/ppermute | solution.py:52
  51.7 31.1 %collective-permute-start.8 = (bf16[192,4480]{1,0:T(8,128)(2,1)}, bf16[192,4480]{1,0:T(8,128)(2,1)}, u32[]{:S(2)}, u32[]{:S(2)}) collective-permute-start(bf16[192,4480]{1,0:T(8,128)(2,1)} %get-tuple-element.51), channel_id=1, source_target_pairs={{0,1},{1,0},{2,3},{3,2},{4,5},{5,4},{6,7},{7,6}} | collective-permute-start | bytes 5160968 | tf_op jit(solution)/shard_map/ppermute | solution.py:52
  79.8 46.1 %collective-permute-start.2 = (bf16[384,1792]{1,0:T(8,128)(2,1)}, bf16[384,1792]{1,0:T(8,128)(2,1)}, u32[]{:S(2)}, u32[]{:S(2)}) collective-permute-start(bf16[384,1792]{1,0:T(8,128)(2,1)} %pad_maximum_fusion.6._), channel_id=1, source_target_pairs={{0,2},{2,0},{4,6},{6,4},{1,3},{3,1},{5,7},{7,5}} | collective-permute-start | bytes 4128776 | tf_op jit(solution)/shard_map/ppermute | solution.py:56
  82.8 46.1 %collective-permute-start.3 = (bf16[384,1792]{1,0:T(8,128)(2,1)}, bf16[384,1792]{1,0:T(8,128)(2,1)}, u32[]{:S(2)}, u32[]{:S(2)}) collective-permute-start(bf16[384,1792]{1,0:T(8,128)(2,1)} %pad_maximum_fusion.6._), channel_id=1, source_target_pairs={{0,4},{2,6},{4,0},{6,2},{1,5},{3,7},{5,1},{7,3}} | collective-permute-start | bytes 4128776 | tf_op jit(solution)/shard_map/ppermute | solution.py:56
  127.0 16.6 collective-permute-start.4
  130.1 17.3 collective-permute-start.5
  143.7 367.0 %collective-permute-start.31 = (bf16[1120,1536]{1,0:T(8,128)(2,1)}, bf16[1120,1536]{1,0:T(8,128)(2,1)}, u32[]{:S(2)}, u32[]{:S(2)}) collective-permute-start(bf16[1120,1536]{1,0:T(8,128)(2,1)} %slice_bitcast_fusion._.down_ref), channel_id=1, source_target_pairs={{0,2},{2,0},{4,6},{6,4},{1,3},{3,1},{5,7},{7,5}} | collective-permute-start | bytes 10321928 | tf_op jit(solution)/shard_map/ppermute | solution.py:56
  147.4 146.3 %collective-permute-start.9 = (bf16[384,4480]{1,0:T(8,128)(2,1)}, bf16[384,4480]{1,0:T(8,128)(2,1)}, u32[]{:S(2)}, u32[]{:S(2)}) collective-permute-start(bf16[384,4480]{1,0:T(8,128)(2,1)} %pad_maximum_fusion.4._), channel_id=1, source_target_pairs={{0,2},{2,0},{4,6},{6,4},{1,3},{3,1},{5,7},{7,5}} | collective-permute-start | bytes 10321928 | tf_op jit(solution)/shard_map/ppermute | solution.py:56
  193.4 163.1 %collective-permute-start.6 = (f32[1024,1536]{1,0:T(8,128)S(1)}, f32[1024,1536]{1,0:T(8,128)S(1)}, u32[]{:S(2)}, u32[]{:S(2)}) collective-permute-start(f32[1024,1536]{1,0:T(8,128)S(1)} %fusion.77), channel_id=1, source_target_pairs={{0,1},{1,0},{2,3},{3,2},{4,5},{5,4},{6,7},{7,6}} | collective-permute-start | bytes 18874376 | tf_op jit(solution)/shard_map/ppermute | solution.py:52
  202.7 310.7 %collective-permute-start.32 = (bf16[1120,1536]{1,0:T(8,128)(2,1)}, bf16[1120,1536]{1,0:T(8,128)(2,1)}, u32[]{:S(2)}, u32[]{:S(2)}) collective-permute-start(bf16[1120,1536]{1,0:T(8,128)(2,1)} %slice_bitcast_fusion._.down_ref), channel_id=1, source_target_pairs={{0,4},{2,6},{4,0},{6,2},{1,5},{3,7},{5,1},{7,3}} | collective-permute-start | bytes 10321928 | tf_op jit(solution)/shard_map/ppermute | solution.py:56
  205.5 148.5 %collective-permute-start.10 = (bf16[384,4480]{1,0:T(8,128)(2,1)}, bf16[384,4480]{1,0:T(8,128)(2,1)S(1)}, u32[]{:S(2)}, u32[]{:S(2)}) collective-permute-start(bf16[384,4480]{1,0:T(8,128)(2,1)} %pad_maximum_fusion.4._), channel_id=1, source_target_pairs={{0,4},{2,6},{4,0},{6,2},{1,5},{3,7},{5,1},{7,3}} | collective-permute-start | bytes 10321928 | tf_op jit(solution)/shard_map/ppermute | solution.py:56
  293.7 97.2 %collective-permute-start.15 = (bf16[560,1536]{1,0:T(8,128)(2,1)}, bf16[560,1536]{1,0:T(8,128)(2,1)}, u32[]{:S(2)}, u32[]{:S(2)}) collective-permute-start(bf16[560,1536]{1,0:T(8,128)(2,1)} %slice.262), channel_id=1, source_target_pairs={{0,4},{2,6},{4,0},{6,2},{1,5},{3,7},{5,1},{7,3}} | collective-permute-start | bytes 5160968 | tf_op jit(solution)/shard_map/ppermute | solution.py:56
  354.0 41.3 %collective-permute-start.16 = (bf16[560,1536]{1,0:T(8,128)(2,1)}, bf16[560,1536]{1,0:T(8,128)(2,1)}, u32[]{:S(2)}, u32[]{:S(2)}) collective-permute-start(bf16[560,1536]{1,0:T(8,128)(2,1)} %slice.263), channel_id=1, source_target_pairs={{0,2},{2,0},{4,6},{6,4},{1,3},{3,1},{5,7},{7,5}} | collective-permute-start | bytes 5160968 | tf_op jit(solution)/shard_map/ppermute | solution.py:56
  356.8 69.5 %collective-permute-start.11 = (bf16[192,4480]{1,0:T(8,128)(2,1)}, bf16[192,4480]{1,0:T(8,128)(2,1)}, u32[]{:S(2)}, u32[]{:S(2)}) collective-permute-start(bf16[192,4480]{1,0:T(8,128)(2,1)} %slice.260), channel_id=1, source_target_pairs={{0,4},{2,6},{4,0},{6,2},{1,5},{3,7},{5,1},{7,3}} | collective-permute-start | bytes 5160968 | tf_op jit(solution)/shard_map/ppermute | solution.py:56
  390.9 45.7 %collective-permute-start.7 = (bf16[1024,1536]{1,0:T(8,128)(2,1)S(1)}, bf16[1024,1536]{1,0:T(8,128)(2,1)}, u32[]{:S(2)}, u32[]{:S(2)}) collective-permute-start(bf16[1024,1536]{1,0:T(8,128)(2,1)S(1)} %fusion.32), channel_id=1, source_target_pairs={{0,1},{1,0},{2,3},{3,2},{4,5},{5,4},{6,7},{7,6}} | collective-permute-start | bytes 9437192 | tf_op jit(solution)/shard_map/ppermute | solution.py:52
  395.3 40.0 %collective-permute-start.12 = (bf16[192,4480]{1,0:T(8,128)(2,1)S(1)}, bf16[192,4480]{1,0:T(8,128)(2,1)S(1)}, u32[]{:S(2)}, u32[]{:S(2)}) collective-permute-start(bf16[192,4480]{1,0:T(8,128)(2,1)S(1)} %slice.261), channel_id=1, source_target_pairs={{0,2},{2,0},{4,6},{6,4},{1,3},{3,1},{5,7},{7,5}} | collective-permute-start | bytes 5160968 | tf_op jit(solution)/shard_map/ppermute | solution.py:56
  509.9 39.3 %collective-permute-start.17 = (f32[1024,1536]{1,0:T(8,128)}, f32[1024,1536]{1,0:T(8,128)}, u32[]{:S(2)}, u32[]{:S(2)}) collective-permute-start(f32[1024,1536]{1,0:T(8,128)} %fusion.16), channel_id=1, source_target_pairs={{0,1},{1,0},{2,3},{3,2},{4,5},{5,4},{6,7},{7,6}} | collective-permute-start | bytes 18874376 | tf_op jit(solution)/shard_map/ppermute | solution.py:52
  510.2 13.3 collective-permute-start.19
  513.5 136.1 %collective-permute-start.33 = (bf16[560,1536]{1,0:T(8,128)(2,1)}, bf16[560,1536]{1,0:T(8,128)(2,1)}, u32[]{:S(2)}, u32[]{:S(2)}) collective-permute-start(bf16[560,1536]{1,0:T(8,128)(2,1)} %slice.280), channel_id=1, source_target_pairs={{0,4},{2,6},{4,0},{6,2},{1,5},{3,7},{5,1},{7,3}} | collective-permute-start | bytes 5160968 | tf_op jit(solution)/shard_map/ppermute | solution.py:56
  516.2 136.6 %collective-permute-start.34 = (bf16[560,1536]{1,0:T(8,128)(2,1)}, bf16[560,1536]{1,0:T(8,128)(2,1)}, u32[]{:S(2)}, u32[]{:S(2)}) collective-permute-start(bf16[560,1536]{1,0:T(8,128)(2,1)} %slice.281), channel_id=1, source_target_pairs={{0,2},{2,0},{4,6},{6,4},{1,3},{3,1},{5,7},{7,5}} | collective-permute-start | bytes 5160968 | tf_op jit(solution)/shard_map/ppermute | solution.py:56
  523.5 34.5 %collective-permute-start.26 = (bf16[192,4480]{1,0:T(8,128)(2,1)}, bf16[192,4480]{1,0:T(8,128)(2,1)}, u32[]{:S(2)}, u32[]{:S(2)}) collective-permute-start(bf16[192,4480]{1,0:T(8,128)(2,1)} %get-tuple-element.56), channel_id=1, source_target_pairs={{0,1},{1,0},{2,3},{3,2},{4,5},{5,4},{6,7},{7,6}} | collective-permute-start | bytes 5160968 | tf_op jit(solution)/shard_map/ppermute | solution.py:52
  525.0 60.4 %collective-permute-start.20 = (bf16[384,1792]{1,0:T(8,128)(2,1)}, bf16[384,1792]{1,0:T(8,128)(2,1)S(1)}, u32[]{:S(2)}, u32[]{:S(2)}) collective-permute-start(bf16[384,1792]{1,0:T(8,128)(2,1)} %pad_maximum_fusion.7._), channel_id=1, source_target_pairs={{0,2},{2,0},{4,6},{6,4},{1,3},{3,1},{5,7},{7,5}} | collective-permute-start | bytes 4128776 | tf_op jit(solution)/shard_map/ppermute | solution.py:56
  549.3 38.0 %collective-permute-start.21 = (bf16[384,1792]{1,0:T(8,128)(2,1)}, bf16[384,1792]{1,0:T(8,128)(2,1)S(1)}, u32[]{:S(2)}, u32[]{:S(2)}) collective-permute-start(bf16[384,1792]{1,0:T(8,128)(2,1)} %pad_maximum_fusion.7._), channel_id=1, source_target_pairs={{0,4},{2,6},{4,0},{6,2},{1,5},{3,7},{5,1},{7,3}} | collective-permute-start | bytes 4128776 | tf_op jit(solution)/shard_map/ppermute | solution.py:56
  558.0 46.0 %collective-permute-start.18 = (bf16[1024,1536]{1,0:T(8,128)(2,1)S(1)}, bf16[1024,1536]{1,0:T(8,128)(2,1)S(1)}, u32[]{:S(2)}, u32[]{:S(2)}) collective-permute-start(bf16[1024,1536]{1,0:T(8,128)(2,1)S(1)} %fusion.36), channel_id=1, source_target_pairs={{0,1},{1,0},{2,3},{3,2},{4,5},{5,4},{6,7},{7,6}} | collective-permute-start | bytes 9437192 | tf_op jit(solution)/shard_map/ppermute | solution.py:52
  585.5 16.5 collective-permute-start.22
  587.3 16.1 collective-permute-start.23
  602.0 75.1 %collective-permute-start.27 = (bf16[384,4480]{1,0:T(8,128)(2,1)}, bf16[384,4480]{1,0:T(8,128)(2,1)}, u32[]{:S(2)}, u32[]{:S(2)}) collective-permute-start(bf16[384,4480]{1,0:T(8,128)(2,1)} %pad_maximum_fusion.5._), channel_id=1, source_target_pairs={{0,2},{2,0},{4,6},{6,4},{1,3},{3,1},{5,7},{7,5}} | collective-permute-start | bytes 10321928 | tf_op jit(solution)/shard_map/ppermute | solution.py:56
  603.4 77.5 %collective-permute-start.28 = (bf16[384,4480]{1,0:T(8,128)(2,1)}, bf16[384,4480]{1,0:T(8,128)(2,1)}, u32[]{:S(2)}, u32[]{:S(2)}) collective-permute-start(bf16[384,4480]{1,0:T(8,128)(2,1)} %pad_maximum_fusion.5._), channel_id=1, source_target_pairs={{0,4},{2,6},{4,0},{6,2},{1,5},{3,7},{5,1},{7,3}} | collective-permute-start | bytes 10321928 | tf_op jit(solution)/shard_map/ppermute | solution.py:56
  641.6 52.5 %collective-permute-start.24 = (f32[1024,1536]{1,0:T(8,128)}, f32[1024,1536]{1,0:T(8,128)}, u32[]{:S(2)}, u32[]{:S(2)}) collective-permute-start(f32[1024,1536]{1,0:T(8,128)} %fusion.72), channel_id=1, source_target_pairs={{0,1},{1,0},{2,3},{3,2},{4,5},{5,4},{6,7},{7,6}} | collective-permute-start | bytes 18874376 | tf_op jit(solution)/shard_map/ppermute | solution.py:52
  649.6 127.2 %collective-permute-start.35 = (bf16[1024,1536]{1,0:T(8,128)(2,1)}, bf16[1024,1536]{1,0:T(8,128)(2,1)}, u32[]{:S(2)}, u32[]{:S(2)}) collective-permute-start(bf16[1024,1536]{1,0:T(8,128)(2,1)} %bitcast.166), channel_id=1, source_target_pairs={{0,1},{1,0},{2,3},{3,2},{4,5},{5,4},{6,7},{7,6}} | collective-permute-start | bytes 9437192 | tf_op jit(solution)/shard_map/ppermute | solution.py:52
  679.9 37.4 %collective-permute-start.29 = (bf16[192,4480]{1,0:T(8,128)(2,1)}, bf16[192,4480]{1,0:T(8,128)(2,1)}, u32[]{:S(2)}, u32[]{:S(2)}) collective-permute-start(bf16[192,4480]{1,0:T(8,128)(2,1)} %slice.278), channel_id=1, source_target_pairs={{0,4},{2,6},{4,0},{6,2},{1,5},{3,7},{5,1},{7,3}} | collective-permute-start | bytes 5160968 | tf_op jit(solution)/shard_map/ppermute | solution.py:56
  683.7 36.7 %collective-permute-start.30 = (bf16[192,4480]{1,0:T(8,128)(2,1)}, bf16[192,4480]{1,0:T(8,128)(2,1)}, u32[]{:S(2)}, u32[]{:S(2)}) collective-permute-start(bf16[192,4480]{1,0:T(8,128)(2,1)} %slice.279), channel_id=1, source_target_pairs={{0,2},{2,0},{4,6},{6,4},{1,3},{3,1},{5,7},{7,5}} | collective-permute-start | bytes 5160968 | tf_op jit(solution)/shard_map/ppermute | solution.py:56
  702.2 20.9 %collective-permute-start.25 = (bf16[1024,1536]{1,0:T(8,128)(2,1)S(1)}, bf16[1024,1536]{1,0:T(8,128)(2,1)S(1)}, u32[]{:S(2)}, u32[]{:S(2)}) collective-permute-start(bf16[1024,1536]{1,0:T(8,128)(2,1)S(1)} %fusion.29), channel_id=1, source_target_pairs={{0,1},{1,0},{2,3},{3,2},{4,5},{5,4},{6,7},{7,6}} | collective-permute-start | bytes 9437192 | tf_op jit(solution)/shard_map/ppermute | solution.py:52
  839.2 19.3 %collective-permute-start.36 = (f32[1024,1536]{1,0:T(8,128)}, f32[1024,1536]{1,0:T(8,128)S(1)}, u32[]{:S(2)}, u32[]{:S(2)}) collective-permute-start(f32[1024,1536]{1,0:T(8,128)} %fusion.8), channel_id=1, source_target_pairs={{0,1},{1,0},{2,3},{3,2},{4,5},{5,4},{6,7},{7,6}} | collective-permute-start | bytes 18874376 | tf_op jit(solution)/shard_map/ppermute | solution.py:52
  935.3 344.4 %all-gather.11.cloned.1.call-start = ((), (), s32[]{:S(2)}) async-start(), calls=%async_computation.5 | async-start | bytes 28311552 | tf_op jit(solution)/shard_map/all_gather | solution.py:131
  935.9 343.8 %all-gather.9.cloned.1.call-start = ((), (), s32[]{:S(2)}) async-start(), calls=%async_computation.4 | async-start | bytes 28311552 | tf_op jit(solution)/shard_map/all_gather | solution.py:131
  945.3 10.9 collective-permute-start.38
  946.2 622.1 %reduce-scatter.3.cloned.1.call-start = ((), (), s32[]{:S(2)}) async-start(), calls=%async_computation.6 | async-start | bytes 13762560 | tf_op jit(solution)/shard_map/reduce_scatter | solution.py:135
  1035.0 22.7 %collective-permute-start.41 = (f32[1024,1536]{1,0:T(8,128)}, f32[1024,1536]{1,0:T(8,128)S(1)}, u32[]{:S(2)}, u32[]{:S(2)}) collective-permute-start(f32[1024,1536]{1,0:T(8,128)} %fusion.4), channel_id=1, source_target_pairs={{0,1},{1,0},{2,3},{3,2},{4,5},{5,4},{6,7},{7,6}} | collective-permute-start | bytes 18874376 | tf_op jit(solution)/shard_map/ppermute | solution.py:52
  1066.5 7.2 collective-permute-start.42
  1133.5 438.2 %all-gather.5.cloned.1.call-start = ((), (), s32[]{:S(2)}) async-start(), calls=%async_computation.2 | async-start | bytes 28311552 | tf_op jit(solution)/shard_map/all_gather | solution.py:131
  1134.1 437.6 %all-gather.7.cloned.1.call-start = ((), (), s32[]{:S(2)}) async-start(), calls=%async_computation.3 | async-start | bytes 28311552 | tf_op jit(solution)/shard_map/all_gather | solution.py:131
  1144.1 125.7 %collective-permute-start.43 = (f32[1024,1536]{1,0:T(8,128)}, f32[1024,1536]{1,0:T(8,128)}, u32[]{:S(2)}, u32[]{:S(2)}) collective-permute-start(f32[1024,1536]{1,0:T(8,128)} %fusion.62), channel_id=1, source_target_pairs={{0,1},{1,0},{2,3},{3,2},{4,5},{5,4},{6,7},{7,6}} | collective-permute-start | bytes 18874376 | tf_op jit(solution)/shard_map/ppermute | solution.py:52
  1237.1 27.0 %collective-permute-start.45 = (f32[192,1792]{1,0:T(8,128)}, f32[192,1792]{1,0:T(8,128)}, u32[]{:S(2)}, u32[]{:S(2)}) collective-permute-start(f32[192,1792]{1,0:T(8,128)} %get-tuple-element.120), channel_id=1, source_target_pairs={{0,1},{1,0},{2,3},{3,2},{4,5},{5,4},{6,7},{7,6}} | collective-permute-start | bytes 4128776 | tf_op jit(solution)/shard_map/ppermute | solution.py:52
  1422.2 287.8 %collective-permute-start.53 = (f32[192,1120]{1,0:T(8,128)}, f32[192,1120]{1,0:T(8,128)S(1)}, u32[]{:S(2)}, u32[]{:S(2)}) collective-permute-start(f32[192,1120]{1,0:T(8,128)} %get-tuple-element.82), channel_id=1, source_target_pairs={{0,1},{1,0},{2,3},{3,2},{4,5},{5,4},{6,7},{7,6}} | collective-permute-start | bytes 2580488 | tf_op jit(solution)/shard_map/ppermute | solution.py:335
  1422.3 289.2 %collective-permute-start.54 = (f32[192,1120]{1,0:T(8,128)}, f32[192,1120]{1,0:T(8,128)S(1)}, u32[]{:S(2)}, u32[]{:S(2)}) collective-permute-start(f32[192,1120]{1,0:T(8,128)} %get-tuple-element.83), channel_id=1, source_target_pairs={{0,2},{1,3},{2,0},{3,1},{4,6},{5,7},{6,4},{7,5}} | collective-permute-start | bytes 2580488 | tf_op jit(solution)/shard_map/ppermute | solution.py:335
  1424.0 310.6 %collective-permute-start.55 = (f32[192,1120]{1,0:T(8,128)}, f32[192,1120]{1,0:T(8,128)}, u32[]{:S(2)}, u32[]{:S(2)}) collective-permute-start(f32[192,1120]{1,0:T(8,128)} %get-tuple-element.84), channel_id=1, source_target_pairs={{0,3},{1,2},{2,1},{3,0},{4,7},{5,6},{6,5},{7,4}} | collective-permute-start | bytes 2580488 | tf_op jit(solution)/shard_map/ppermute | solution.py:335
  1424.1 312.2 %collective-permute-start.56 = (f32[192,1120]{1,0:T(8,128)}, f32[192,1120]{1,0:T(8,128)}, u32[]{:S(2)}, u32[]{:S(2)}) collective-permute-start(f32[192,1120]{1,0:T(8,128)} %get-tuple-element.85), channel_id=1, source_target_pairs={{0,4},{1,5},{2,6},{3,7},{4,0},{5,1},{6,2},{7,3}} | collective-permute-start | bytes 2580488 | tf_op jit(solution)/shard_map/ppermute | solution.py:335
  1425.7 310.7 %collective-permute-start.57 = (f32[192,1120]{1,0:T(8,128)}, f32[192,1120]{1,0:T(8,128)}, u32[]{:S(2)}, u32[]{:S(2)}) collective-permute-start(f32[192,1120]{1,0:T(8,128)} %get-tuple-element.86), channel_id=1, source_target_pairs={{0,5},{1,4},{2,7},{3,6},{4,1},{5,0},{6,3},{7,2}} | collective-permute-start | bytes 2580488 | tf_op jit(solution)/shard_map/ppermute | solution.py:335
  1710.0 27.9 %collective-permute-start.58 = (f32[192,1120]{1,0:T(8,128)}, f32[192,1120]{1,0:T(8,128)S(1)}, u32[]{:S(2)}, u32[]{:S(2)}) collective-permute-start(f32[192,1120]{1,0:T(8,128)} %get-tuple-element.87), channel_id=1, source_target_pairs={{0,6},{1,7},{2,4},{3,5},{4,2},{5,3},{6,0},{7,1}} | collective-permute-start | bytes 2580488 | tf_op jit(solution)/shard_map/ppermute | solution.py:335
  1712.4 38.3 %collective-permute-start.59 = (f32[192,1120]{1,0:T(8,128)}, f32[192,1120]{1,0:T(8,128)S(1)}, u32[]{:S(2)}, u32[]{:S(2)}) collective-permute-start(f32[192,1120]{1,0:T(8,128)} %get-tuple-element.88), channel_id=1, source_target_pairs={{0,7},{1,6},{2,5},{3,4},{4,3},{5,2},{6,1},{7,0}} | collective-permute-start | bytes 2580488 | tf_op jit(solution)/shard_map/ppermute | solution.py:335
  1734.6 31.2 %collective-permute-start.44 = (f32[192,1792]{1,0:T(8,128)S(1)}, f32[192,1792]{1,0:T(8,128)S(1)}, u32[]{:S(2)}, u32[]{:S(2)}) collective-permute-start(f32[192,1792]{1,0:T(8,128)S(1)} %copy-done.48), channel_id=1, source_target_pairs={{0,1},{1,0},{2,3},{3,2},{4,5},{5,4},{6,7},{7,6}} | collective-permute-start | bytes 4128776 | tf_op jit(solution)/shard_map/ppermute | solution.py:52
  1736.3 43.7 %collective-permute-start.46 = (f32[192,1120]{1,0:T(8,128)}, f32[192,1120]{1,0:T(8,128)}, u32[]{:S(2)}, u32[]{:S(2)}) collective-permute-start(f32[192,1120]{1,0:T(8,128)} %get-tuple-element.74), channel_id=1, source_target_pairs={{0,1},{1,0},{2,3},{3,2},{4,5},{5,4},{6,7},{7,6}} | collective-permute-start | bytes 2580488 | tf_op jit(solution)/shard_map/ppermute | solution.py:335
  1736.4 43.9 %collective-permute-start.47 = (f32[192,1120]{1,0:T(8,128)}, f32[192,1120]{1,0:T(8,128)}, u32[]{:S(2)}, u32[]{:S(2)}) collective-permute-start(f32[192,1120]{1,0:T(8,128)} %get-tuple-element.75), channel_id=1, source_target_pairs={{0,2},{1,3},{2,0},{3,1},{4,6},{5,7},{6,4},{7,5}} | collective-permute-start | bytes 2580488 | tf_op jit(solution)/shard_map/ppermute | solution.py:335
  1737.8 50.8 %collective-permute-start.48 = (f32[192,1120]{1,0:T(8,128)}, f32[192,1120]{1,0:T(8,128)}, u32[]{:S(2)}, u32[]{:S(2)}) collective-permute-start(f32[192,1120]{1,0:T(8,128)} %get-tuple-element.76), channel_id=1, source_target_pairs={{0,3},{1,2},{2,1},{3,0},{4,7},{5,6},{6,5},{7,4}} | collective-permute-start | bytes 2580488 | tf_op jit(solution)/shard_map/ppermute | solution.py:335
  1750.7 116.2 %collective-permute-start.39 = (f32[1024,1536]{1,0:T(8,128)}, f32[1024,1536]{1,0:T(8,128)}, u32[]{:S(2)}, u32[]{:S(2)}) collective-permute-start(f32[1024,1536]{1,0:T(8,128)} %fusion.12), channel_id=1, source_target_pairs={{0,1},{1,0},{2,3},{3,2},{4,5},{5,4},{6,7},{7,6}} | collective-permute-start | bytes 18874376 | tf_op jit(solution)/shard_map/ppermute | solution.py:52
  1778.6 60.4 %collective-permute-start.49 = (f32[192,1120]{1,0:T(8,128)S(1)}, f32[192,1120]{1,0:T(8,128)S(1)}, u32[]{:S(2)}, u32[]{:S(2)}) collective-permute-start(f32[192,1120]{1,0:T(8,128)S(1)} %copy-done.87), channel_id=1, source_target_pairs={{0,4},{1,5},{2,6},{3,7},{4,0},{5,1},{6,2},{7,3}} | collective-permute-start | bytes 2580488 | tf_op jit(solution)/shard_map/ppermute | solution.py:335
  1780.1 76.6 %collective-permute-start.50 = (f32[192,1120]{1,0:T(8,128)S(1)}, f32[192,1120]{1,0:T(8,128)S(1)}, u32[]{:S(2)}, u32[]{:S(2)}) collective-permute-start(f32[192,1120]{1,0:T(8,128)S(1)} %copy-done.86), channel_id=1, source_target_pairs={{0,5},{1,4},{2,7},{3,6},{4,1},{5,0},{6,3},{7,2}} | collective-permute-start | bytes 2580488 | tf_op jit(solution)/shard_map/ppermute | solution.py:335
  1780.2 76.4 %collective-permute-start.51 = (f32[192,1120]{1,0:T(8,128)S(1)}, f32[192,1120]{1,0:T(8,128)S(1)}, u32[]{:S(2)}, u32[]{:S(2)}) collective-permute-start(f32[192,1120]{1,0:T(8,128)S(1)} %copy-done.85), channel_id=1, source_target_pairs={{0,6},{1,7},{2,4},{3,5},{4,2},{5,3},{6,0},{7,1}} | collective-permute-start | bytes 2580488 | tf_op jit(solution)/shard_map/ppermute | solution.py:335
  1788.7 68.0 %collective-permute-start.52 = (f32[192,1120]{1,0:T(8,128)S(1)}, f32[192,1120]{1,0:T(8,128)S(1)}, u32[]{:S(2)}, u32[]{:S(2)}) collective-permute-start(f32[192,1120]{1,0:T(8,128)S(1)} %copy-done.84), channel_id=1, source_target_pairs={{0,7},{1,6},{2,5},{3,4},{4,3},{5,2},{6,1},{7,0}} | collective-permute-start | bytes 2580488 | tf_op jit(solution)/shard_map/ppermute | solution.py:335
  (96 other events, 1354.5 us)
Sparse Core Ops, SparseCore 0:
  935.4 298.1 reduce-scatter.4
  1236.7 331.5 reduce-scatter.2
Sparse Core Ops, SparseCore 1:
  937.6 141.2 all-gather.10
  1080.6 139.9 all-gather.8
  1222.2 129.8 all-gather.4
  1354.0 181.0 all-gather.6

commit v9 on v8

--- a/solution.py
+++ b/solution.py
@@ -21,6 +21,7 @@
 FLIP_TILE = 256
 WIDTH_TILE = 512
 NEIGHBOURS = (1, 2)
+BY_HEAD = (True, False, False, True)
 
 
 def rms_norm(values):
@@ -76,14 +77,26 @@
     outs = refs[-4:]
     head = outs[0].shape[3]
     for part in range(CORES):
-        mine, other = mine_ref[...], other_ref[...]
-        cols = jnp.where(place_ref[1] == part, mine, other)
+        cols = jnp.where(place_ref[1] == part, mine_ref[...], other_ref[...])
         start = 0
-        for out in outs:
-            count = out.shape[2] // CORES
-            for i in range(count):
-                out[0, :, part * count + i, :] = cols[:, start:start + head]
+        for out, by_head in zip(outs, BY_HEAD):
+            count = out.shape[1 if by_head else 2] // CORES
+            for i in range(part * count, (part + 1) * count):
+                if by_head:
+                    out[0, i] = cols[:, start:start + head]
+                else:
+                    out[0, :, i, :] = cols[:, start:start + head]
                 start += head
+
+
+def flip_heads(weight):
+    return weight.transpose(0, 2, 1, 3)
+
+
+def heads_specs(shapes, layer):
+    return [pl.BlockSpec((1, shape[1], ROW_TILE, shape[3]), lambda i, p: (layer, 0, i, 0)) if by_head
+            else pl.BlockSpec((1, ROW_TILE) + shape[2:], lambda i, p: (layer, i, 0, 0))
+            for shape, by_head in zip(shapes, BY_HEAD)]
 
 
 def place_heads(place, layer, shapes, earlier, mine, other):
@@ -95,13 +108,44 @@
             num_scalar_prefetch=1,
             grid=(rows // ROW_TILE,),
             in_specs=[pl.BlockSpec((ROW_TILE, cols), lambda i, p: (i, 0))] * CORES + anywhere,
-            out_specs=[pl.BlockSpec((1, ROW_TILE) + shape[2:], lambda i, p: (layer, i, 0, 0)) for shape in shapes],
+            out_specs=heads_specs(shapes, layer),
         ),
         out_shape=[jax.ShapeDtypeStruct(shape, jnp.float32) for shape in shapes],
         input_output_aliases={3 + i: i for i in range(len(earlier))},
         cost_estimate=pl.CostEstimate(flops=2_000_000_000, bytes_accessed=0, transcendentals=0),
         name="place_heads",
     )(place, mine, other, *earlier)
+
+
+def pack_kernel(place_ref, *refs):
+    weights, outs = refs[:4], refs[4:]
+    head = weights[0].shape[3]
+    start = 0
+    for weight, by_head in zip(weights, BY_HEAD):
+        count = weight.shape[1 if by_head else 2] // CORES
+        for i in range(count):
+            pair = [weight[0, i + part * count] if by_head else weight[0, :, i + part * count, :] for part in range(CORES)]
+            for j, out in enumerate(outs):
+                out[:, start:start + head] = jnp.where(place_ref[1] == j, pair[0], pair[1])
+            start += head
+
+
+def pack_heads(place, layer, weights):
+    rows, head = weights[1].shape[1], weights[1].shape[3]
+    cols = sum(weight.shape[1 if by_head else 2] for weight, by_head in zip(weights, BY_HEAD)) // CORES * head
+    half = jax.ShapeDtypeStruct((rows, cols), weights[0].dtype)
+    return pl.pallas_call(
+        pack_kernel,
+        grid_spec=pltpu.PrefetchScalarGridSpec(
+            num_scalar_prefetch=1,
+            grid=(rows // ROW_TILE,),
+            in_specs=heads_specs([weight.shape for weight in weights], layer),
+            out_specs=[pl.BlockSpec((ROW_TILE, cols), lambda i, p: (i, 0))] * CORES,
+        ),
+        out_shape=[half] * CORES,
+        cost_estimate=pl.CostEstimate(flops=2_000_000_000, bytes_accessed=0, transcendentals=0),
+        name="pack",
+    )(place, *weights)
 
 
 def blank_kernel(_, out_ref):
@@ -301,20 +345,22 @@
                 parts[CORES * i + j][...] = flip_ref[pl.ds(start, rows), :]
 
 
-def mlp_weight_grads(place, layer, pairs, earlier, up_flip, down_block, norms, grads):
+def mlp_weight_grads(place, layer, pairs, earlier, up_flip, down_block, tokens):
     block, width = down_block.shape
     rows = width // (CHIPS * CORES)
     once = pl.Buffered(1)
     whole = pl.BlockSpec((block, width), lambda i, p: (0, 0), pipeline_mode=once)
-    tokens = pl.BlockSpec((TOKEN_TILE, width), lambda i, p: (i, 0))
+    tiles = tokens.shape[0] // (2 * CHIPS * CORES * TOKEN_TILE)
+    norms, grads = [pl.BlockSpec((TOKEN_TILE, width), lambda i, p, k=k: (2 * tiles * (i // tiles) + k * tiles + i % tiles, 0))
+                    for k in range(2)]
     part = pl.BlockSpec((rows, block), lambda i, p: (0, 0), pipeline_mode=once)
-    args = [place, up_flip, down_block, norms, grads, *earlier]
+    args = [place, up_flip, down_block, tokens, tokens, *earlier]
     outs = pl.pallas_call(
         mlp_grads_kernel,
         grid_spec=pltpu.PrefetchScalarGridSpec(
             num_scalar_prefetch=1,
-            grid=(norms.shape[0] // TOKEN_TILE,),
-            in_specs=[whole, whole, tokens, tokens] + [pl.BlockSpec(memory_space=pl.ANY)] * len(earlier),
+            grid=(tiles * CHIPS * CORES,),
+            in_specs=[whole, whole, norms, grads] + [pl.BlockSpec(memory_space=pl.ANY)] * len(earlier),
             out_specs=[pl.BlockSpec((1, block, width), lambda i, p: (layer, 0, 0), pipeline_mode=once)]
             + [part] * (CHIPS * CORES),
             scratch_shapes=[pltpu.VMEM((block, width), jnp.float32), pltpu.VMEM((CORES * rows, block), jnp.float32)],
@@ -323,7 +369,7 @@
         + [jax.ShapeDtypeStruct((rows, block), jnp.float32)] * (CHIPS * CORES),
         input_output_aliases={len(args) - 1: 0} if earlier else {},
         compiler_params=pltpu.CompilerParams(vmem_limit_bytes=60 * 1024 * 1024),
-        cost_estimate=pl.CostEstimate(flops=8 * norms.shape[0] * block * width, bytes_accessed=0,
+        cost_estimate=pl.CostEstimate(flops=4 * tokens.shape[0] * block * width, bytes_accessed=0,
                                       transcendentals=0),
         name="mlp_grads",
     )(*args)
@@ -420,18 +466,16 @@
     def body(x_loc, w_q, w_k, w_v, w_o, w_up, w_down, grad_out):
         core = lax.axis_index(CORE)
         chip = lax.axis_index(CHIP)
-        pairs, shard, heads, head = w_q.shape
+        pairs, _, heads, head = w_q.shape
         seqs, seq, width = x_loc.shape
         q_width = heads // CORES * head
 
         place = jnp.stack([chip, core]).astype(jnp.int32)
 
-        def attn_piece(layer, core):
-            halves = []
-            for part in range(CORES):
-                cols = [w[layer].reshape(shard, CORES, -1)[:, part] for w in (w_q, w_k, w_v, w_o)]
-                halves.append(jnp.concatenate(cols, axis=1))
-            return to_columns(core, *by_core(core, *halves))
+        heads_in = [flip_heads(w) if by_head else w for w, by_head in zip((w_q, w_k, w_v, w_o), BY_HEAD)]
+
+        def attn_piece(layer, core, place):
+            return to_columns(core, *pack_heads(place, layer, heads_in))
 
         def up_piece(layer, core, place):
             return to_columns(core, *split_columns(place, layer, w_up))
@@ -439,9 +483,9 @@
         attn_full, up_full, down_full, up_flip = [], [], [], []
 
         def gather_weights(layer, core, place):
-            attn_full.append(gather_weight(chip, attn_piece(layer, core)))
+            attn_full.append(gather_weight(chip, attn_piece(layer, core, place)))
             up_full.append(gather_weight(chip, up_piece(layer, core, place)))
-            down_full.append(gather_weight(chip, w_down[layer]))
+            down_full.append(gather_weight(chip, lax.optimization_barrier(w_down[layer])))
             up_flip.append(flip(place, up_full[layer]))
 
         gather_weights(0, core, place)
@@ -449,8 +493,9 @@
         grad_x = grad_out.reshape(seqs * seq, width)
         attn_saved, mlp_saved, d_up, d_down = [], [], [], []
 
-        def weight_grads(layer, norms, grads, d_down):
-            down, parts = mlp_weight_grads(place, layer, pairs, d_down, up_flip[layer], w_down[layer], norms, grads)
+        def weight_grads(layer, n_own, grad_own, d_down):
+            tokens = gather_rows(jnp.concatenate([n_own, grad_own], axis=0))
+            down, parts = mlp_weight_grads(place, layer, pairs, d_down, up_flip[layer], w_down[layer], tokens)
             return exchange(parts), [down]
 
         for layer in range(pairs):
@@ -461,26 +506,26 @@
                 gather_weights(layer + 1, *later)
             n_own = norm_bf16(x_own)
             gelu_act, slope = mlp_hidden(pair_rows(n_own), up_full[layer])
-            norms = gather_rows(n_own)
             if layer == pairs - 1:
-                parts, d_down = weight_grads(layer, norms, gather_rows(grad_x), d_down)
-            mlp_saved.append((x_own, norms, slope))
+                parts, d_down = weight_grads(layer, n_own, grad_x, d_down)
+            mlp_saved.append((x_own, n_own, slope))
             if layer < pairs - 1:
                 carry_x = mlp_output(x_own, gelu_act, down_full[layer])
         last = (x_own, gelu_act, down_full[-1])
-        d_heads, head_shapes = [], [weight.shape for weight in (w_q, w_k, w_v, w_o)]
+        d_heads, head_shapes = [], [weight.shape for weight in heads_in]
         for layer in reversed(range(pairs)):
-            x_own, norms, slope = mlp_saved[layer]
+            x_own, n_own, slope = mlp_saved[layer]
             if layer < pairs - 1:
-                parts, d_down = weight_grads(layer, norms, gather_rows(grad_x), d_down)
+                parts, d_down = weight_grads(layer, n_own, grad_x, d_down)
             d_up = [assemble(place, layer, pairs, d_up, parts)]
             grad_x = mlp_backward(x_own, slope, up_full[layer], down_full[layer], grad_x)
             grad_x, d_attn = attn_backward(attn_saved[layer], attn_full[layer], q_width, head, seq, grad_x)
             parts = to_rows(core, scatter_sum(d_attn))
             d_heads = place_heads(place, layer, head_shapes, d_heads, *parts)
+        heads_out = tuple(flip_heads(w) if by_head else w for w, by_head in zip(d_heads, BY_HEAD))
         last, d_down = lax.optimization_barrier((last, d_down))
         y_loc = mlp_output(*last).reshape(x_loc.shape)
-        return (y_loc, grad_x.reshape(x_loc.shape)) + (*d_heads, d_up[0], d_down[0])
+        return (y_loc, grad_x.reshape(x_loc.shape)) + heads_out + (d_up[0], d_down[0])
 
     return jax.shard_map(body, mesh=mesh, in_specs=(row_spec,) + (weight_spec,) * 6 + (row_spec,),
                          out_specs=(row_spec, row_spec) + (weight_spec,) * 6, check_vma=False)

time: 1890 us -> 2050 us (1.085)
  waiting for transfers between devices: 604 us -> 802 us
  local copies, waits for them, and re-layouts: 169 us -> 121 us
    reduce_scatter x2, waiting for transfers between devices: 232 us -> 437 us  [scatter_sum(): return lax.psum_scatter(grad_full, CHIP, scatter_dimension=0, tiled=True)]
    ppermute x24, waiting for transfers between devices: 299 us -> 272 us  [hop(): lax.ppermute(value, CHIP, [(chip, chip ^ step) for chip in range(CHIPS)])]
    ppermute x14, waiting for transfers between devices: 62.9 us -> 84.3 us  [exchange(): lax.ppermute(part, AXES, [(d, d ^ i) for d in devices])]
  transfers between devices with their start and end apart: 66 -> 64, of which waited for: 22 -> 19; matrix products, arithmetic and copies ran while one was open for 33% -> 28% of each run, Pallas kernels for 22% -> 22%
where the time goes in v9:
time: 2050 us; the launch traced here: 2030 us
  waiting for transfers between devices  802 us (39%)
  Pallas kernels  471 us (23%)
  matrix products  459 us (22%)
  local copies, waits for them, and re-layouts  121 us (6%)
  other arithmetic  118 us (6%)
  starting transfers between devices  47.9 us (2%)
    dot_general x24, matrix products, dot(): lax.dot_general(left, right, (contract, ((), ())), preferred_element_type...  459 us
    reduce_scatter x2, waiting for transfers between devices, scatter_sum(): return lax.psum_scatter(grad_full, CHIP, scatter_dimension=0, tiled=True)  437 us
    pallas_call x2, Pallas kernels, mlp_weight_grads(): pl.pallas_call(mlp_grads_kernel, grid_spec=pltpu.PrefetchScalarGridSpec(n...  277 us
    ppermute x24, waiting for transfers between devices, hop(): lax.ppermute(value, CHIP, [(chip, chip ^ step) for chip in range(CHIPS)])  272 us
    pallas_call x4, Pallas kernels, by_sequence(): pl.pallas_call(functools.partial(kernel, q_width, head), grid=(rows // se...  90 us
    ppermute x14, waiting for transfers between devices, exchange(): lax.ppermute(part, AXES, [(d, d ^ i) for d in devices])  84.3 us
    dynamic_update_slice x26, local copies, waits for them, and re-layouts, gather_weight(): full = lax.dynamic_update_slice(full, part[None], (chip ^ step, row, 0))  67.9 us
  transfers between devices with their start and end apart: 64, of which 19 were waited for; matrix products, arithmetic and copies ran while one was open for 28% of the time, Pallas kernels for 22%

profile of v9, /device:TPU:0, one launch (start us, length us, event | category | flops | bytes accessed | tf_op | source)
XLA Modules:
  0.0 2035.0 jit_solution(15976684660388937131)
XLA Ops:
  8.0 6.3 slice_bitcast_fusion
  29.2 6.5 split.2
  56.5 65.4 %collective-permute-done.2 = bf16[384,1792]{1,0:T(8,128)(2,1)} collective-permute-done((bf16[384,1792]{1,0:T(8,128)(2,1)}, bf16[384,1792]{1,0:T(8,128)(2,1)}, u32[]{:S(2)}, u32[]{:S(2)}) %collective-permute-start.2) | collective-permute-done | bytes 1376288 | tf_op jit(solution)/shard_map/ppermute | solution.py:57
  132.7 7.0 collective-permute-done.4
  144.4 11.6 convolution_convert_fusion.1.qkv_ref
  156.0 17.1 shard_map.143.o_ref
  178.0 6.4 fusion.75
  200.2 17.0 collective-permute-done.9
  225.8 31.8 %collective-permute-done.15 = bf16[560,1536]{1,0:T(8,128)(2,1)S(1)} collective-permute-done((bf16[560,1536]{1,0:T(8,128)(2,1)S(1)}, bf16[560,1536]{1,0:T(8,128)(2,1)S(1)}, u32[]{:S(2)}, u32[]{:S(2)}) %collective-permute-start.15) | collective-permute-done | bytes 1720352 | tf_op jit(solution)/shard_map/ppermute | solution.py:57
  275.5 52.4 %collective-permute-done.16 = bf16[560,1536]{1,0:T(8,128)(2,1)} collective-permute-done((bf16[560,1536]{1,0:T(8,128)(2,1)}, bf16[560,1536]{1,0:T(8,128)(2,1)}, u32[]{:S(2)}, u32[]{:S(2)}) %collective-permute-start.16) | collective-permute-done | bytes 1720352 | tf_op jit(solution)/shard_map/ppermute | solution.py:57
  330.6 33.4 %collective-permute-done.11 = bf16[192,4480]{1,0:T(8,128)(2,1)} collective-permute-done((bf16[192,4480]{1,0:T(8,128)(2,1)}, bf16[192,4480]{1,0:T(8,128)(2,1)}, u32[]{:S(2)}, u32[]{:S(2)}) %collective-permute-start.11) | collective-permute-done | bytes 1720352 | tf_op jit(solution)/shard_map/ppermute | solution.py:57
  374.3 51.7 %multiply_add_fusion.2 = (f32[2048,4480]{1,0:T(8,128)}, bf16[2048,4480]{1,0:T(8,128)(2,1)}) fusion(bf16[1536,4480]{1,0:T(8,128)(2,1)} %bitcast.127, bf16[1024,1536]{1,0:T(8,128)(2,1)S(1)} %fusion.34, bf16[1024,1536]{1,0:T(8,128)(2,1)} %collective-permute-done.7), kind=kOutput, calls=%fused_computation.6 | convolution fusion | flops 28326756352 | bytes 75104256 | tf_op jit(solution)/shard_map/dot_general | solution.py:41
  426.0 21.5 %fusion.16 = f32[1024,1536]{1,0:T(8,128)} fusion(bf16[4480,1536]{1,0:T(8,128)(2,1)} %bitcast.120, bf16[2048,4480]{1,0:T(8,128)(2,1)} %get-tuple-element.58), kind=kOutput, calls=%fused_computation.40 | convolution fusion | flops 14092861440 | bytes 29229056 | tf_op jit(solution)/shard_map/dot_general | solution.py:41
  459.5 6.6 split.3
  471.1 21.7 %fusion.18 = f32[1024,1536]{1,0:T(8,128)} fusion(bf16[4480,1536]{1,0:T(8,128)(2,1)} %bitcast.121, bf16[2048,4480]{1,0:T(8,128)(2,1)} %get-tuple-element.58), kind=kOutput, calls=%fused_computation.42 | convolution fusion | flops 14092861440 | bytes 29229056 | tf_op jit(solution)/shard_map/dot_general | solution.py:41
  493.5 6.0 fusion.37
  506.2 21.6 %collective-permute-done.20 = bf16[384,1792]{1,0:T(8,128)(2,1)S(1)} collective-permute-done((bf16[384,1792]{1,0:T(8,128)(2,1)}, bf16[384,1792]{1,0:T(8,128)(2,1)S(1)}, u32[]{:S(2)}, u32[]{:S(2)}) %collective-permute-start.20) | collective-permute-done | bytes 1376288 | tf_op jit(solution)/shard_map/ppermute | solution.py:57
  530.4 13.7 collective-permute-done.22
  549.7 9.7 convolution_convert_fusion.qkv_ref
  559.4 17.2 shard_map.144.o_ref
  576.6 7.4 fusion.68
  602.0 16.7 collective-permute-done.27
  629.2 6.2 fusion.70
  635.5 5.8 fusion.30
  641.9 5.5 bitcast_dynamic-update-slice_fusion.3
  647.5 9.5 collective-permute-done.29
  665.6 51.7 %multiply_add_fusion = (f32[2048,4480]{1,0:T(8,128)}, bf16[2048,4480]{1,0:T(8,128)(2,1)}) fusion(bf16[1536,4480]{1,0:T(8,128)(2,1)} %bitcast.123, bf16[1024,1536]{1,0:T(8,128)(2,1)S(1)} %fusion.31, bf16[1024,1536]{1,0:T(8,128)(2,1)} %copy-done.59), kind=kOutput, calls=%fused_computation.2 | convolution fusion | flops 28326756352 | bytes 75104256 | tf_op jit(solution)/shard_map/dot_general | solution.py:41
  717.3 41.7 %multiply_convert_fusion.1 = bf16[2048,4480]{1,0:T(8,128)(2,1)} fusion(f32[2048,4480]{1,0:T(8,128)} %get-tuple-element.66, bf16[4480,1536]{1,0:T(8,128)(2,1)} %bitcast.42, bf16[1024,1536]{1,0:T(8,128)(2,1)} %collective-permute-done.35, bf16[1024,1536]{1,0:T(8,128)(2,1)} %bitcast.43), kind=kOutput, calls=%fused_computation.1 | convolution fusion | flops 28216655872 | bytes 75104256 | tf_op jit(solution)/shard_map/dot_general | solution.py:41
  759.0 21.6 %fusion.8 = f32[1024,1536]{1,0:T(8,128)} fusion(bf16[1536,4480]{1,0:T(8,128)(2,1)} %bitcast.124, bf16[2048,4480]{1,0:T(8,128)(2,1)} %multiply_convert_fusion.1), kind=kOutput, calls=%fused_computation.32 | convolution fusion | flops 14092861440 | bytes 29229056 | tf_op jit(solution)/shard_map/dot_general | solution.py:41
  780.6 19.2 fusion.10
  804.7 5.3 collective-permute-done.37
  811.7 10.0 convolution_convert_fusion.3.d_o_ref
  821.7 28.1 %shard_map.145.d_qkv_ref = bf16[2048,1024]{1,0:T(8,128)(2,1)} custom-call(bf16[2048,1024]{1,0:T(8,128)(2,1)} %convolution_convert_fusion.qkv_ref, bf16[2048,768]{1,0:T(8,128)(2,1)} %convolution_convert_fusion.3.d_o_ref), custom_call_target="tpu_custom_call" | custom-call | flops 40000000000 | tf_op jit(solution)/shard_map/pallas_call | solution.py:244
  849.8 6.1 fusion.53
  856.3 7.5 fusion.55
  874.4 6.1 pad_maximum_fusion.7.norm_ref
  883.4 18.4 attn_grads.3
  901.9 41.6 %multiply_convert_fusion = bf16[2048,4480]{1,0:T(8,128)(2,1)} fusion(f32[2048,4480]{1,0:T(8,128)} %get-tuple-element.72, bf16[4480,1536]{1,0:T(8,128)(2,1)} %bitcast.122, bf16[1024,1536]{1,0:T(8,128)(2,1)} %collective-permute-done.40, bf16[1024,1536]{1,0:T(8,128)(2,1)S(1)} %fusion.25), kind=kOutput, calls=%fused_computation | convolution fusion | flops 28216655872 | bytes 75104256 | tf_op jit(solution)/shard_map/dot_general | solution.py:41
  943.6 21.9 %fusion.4 = f32[1024,1536]{1,0:T(8,128)} fusion(bf16[1536,4480]{1,0:T(8,128)(2,1)} %bitcast.128, bf16[2048,4480]{1,0:T(8,128)(2,1)} %multiply_convert_fusion), kind=kOutput, calls=%fused_computation.28 | convolution fusion | flops 14092861440 | bytes 29229056 | tf_op jit(solution)/shard_map/dot_general | solution.py:41
  965.5 21.8 %fusion.6 = f32[1024,1536]{1,0:T(8,128)} fusion(bf16[1536,4480]{1,0:T(8,128)(2,1)} %bitcast.129, bf16[2048,4480]{1,0:T(8,128)(2,1)} %multiply_convert_fusion), kind=kOutput, calls=%fused_computation.30 | convolution fusion | flops 14092861440 | bytes 29229056 | tf_op jit(solution)/shard_map/dot_general | solution.py:41
  996.8 6.1 pad_maximum_fusion.6.norm_ref
  1005.9 10.0 convolution_convert_fusion.2.d_o_ref
  1016.0 27.7 %shard_map.146.d_qkv_ref = bf16[2048,1024]{1,0:T(8,128)(2,1)} custom-call(bf16[2048,1024]{1,0:T(8,128)(2,1)} %convolution_convert_fusion.1.qkv_ref, bf16[2048,768]{1,0:T(8,128)(2,1)} %convolution_convert_fusion.2.d_o_ref), custom_call_target="tpu_custom_call" | custom-call | flops 40000000000 | tf_op jit(solution)/shard_map/pallas_call | solution.py:244
  1043.7 18.7 attn_grads.2
  1062.5 6.0 pad_maximum_fusion.2
  1068.6 6.2 pad_maximum_fusion
  1074.8 11.8 fusion.58
  1091.1 9.2 flip.2.up_ref
  1100.3 8.9 flip.3.up_ref
  1109.1 8.7 fusion.60
  1117.8 5.1 place_heads.2
  1122.9 5.5 fusion.52
  1129.0 437.1 %reduce-scatter.3.cloned.1.call-done = f32[384,1792]{1,0:T(8,128)} async-done(((f32[1536,1792]{1,0:T(8,128)}), f32[384,1792]{1,0:T(8,128)}) %reduce-scatter.3.cloned.1.call-update) | async-done | bytes 2752528 | tf_op jit(solution)/shard_map/reduce_scatter | solution.py:179
  1569.5 138.5 %mlp_grads.2 = (f32[2,1120,1536]{2,1,0:T(8,128)}, f32[192,1120]{1,0:T(8,128)}, f32[192,1120]{1,0:T(8,128)}, f32[192,1120]{1,0:T(8,128)}, f32[192,1120]{1,0:T(8,1...) custom-call(s32[2]{0:T(128)} %pad_add_fusion.place_ref, ...), custom_call_target="tpu_custom_call" | custom-call | flops 112742891520 | tf_op jit(solution)/shard_map/mlp_grads/pallas_call | solution.py:358
  1710.6 138.5 %mlp_grads.3 = (f32[2,1120,1536]{2,1,0:T(8,128)}, f32[192,1120]{1,0:T(8,128)}, f32[192,1120]{1,0:T(8,128)}, f32[192,1120]{1,0:T(8,128)}, f32[192,1120]{1,0:T(8,1...) custom-call(s32[2]{0:T(128)} %pad_add_fusion.place_ref, ...), custom_call_target="tpu_custom_call", output_to_operand_aliasing={{0}: (5, {})} | custom-call | flops 112742891520 | tf_op jit(solution)/shard_map/mlp_grads/pallas_call | solution.py:358
  1852.1 22.3 %fusion.12 = f32[1024,1536]{1,0:T(8,128)} fusion(bf16[4480,1536]{1,0:T(8,128)(2,1)} %bitcast.42, bf16[2048,4480]{1,0:T(8,128)(2,1)} %get-tuple-element.70), kind=kOutput, calls=%fused_computation.36 | convolution fusion | flops 14092861440 | bytes 29229056 | tf_op jit(solution)/shard_map/dot_general | solution.py:41
  1877.4 31.1 %collective-permute-done.57.refs_5_ = f32[192,1120]{1,0:T(8,128)S(1)} collective-permute-done((f32[192,1120]{1,0:T(8,128)}, f32[192,1120]{1,0:T(8,128)S(1)}, u32[]{:S(2)}, u32[]{:S(2)}) %collective-permute-start.57) | collective-permute-done | bytes 860192 | tf_op jit(solution)/shard_map/ppermute | solution.py:381
  1911.2 5.5 fusion.29
  1922.5 8.1 assemble.2.refs_8_
  1935.7 21.5 %fusion.14 = f32[1024,1536]{1,0:T(8,128)} fusion(bf16[4480,1536]{1,0:T(8,128)(2,1)} %bitcast.42, bf16[2048,4480]{1,0:T(8,128)(2,1)} %get-tuple-element.70), kind=kOutput, calls=%fused_computation.38 | convolution fusion | flops 14092861440 | bytes 29229056 | tf_op jit(solution)/shard_map/dot_general | solution.py:41
  1957.1 34.1 %collective-permute-done.49.refs_4_ = f32[192,1120]{1,0:T(8,128)S(1)} collective-permute-done((f32[192,1120]{1,0:T(8,128)}, f32[192,1120]{1,0:T(8,128)S(1)}, u32[]{:S(2)}, u32[]{:S(2)}) %collective-permute-start.49) | collective-permute-done | bytes 860192 | tf_op jit(solution)/shard_map/ppermute | solution.py:381
  1991.2 17.5 collective-permute-done.50.refs_5_
  2010.9 8.1 assemble.3
  2019.1 8.1 add_convert_fusion
  (340 shorter events, 247.4 us)
Async XLA Ops:
  8.0 1079.3 %reduce-scatter.5.cloned.1.call-start = ((), (), s32[]{:S(2)}) async-start(), calls=%async_computation.5 | async-start | bytes 13762560 | tf_op jit(solution)/shard_map/reduce_scatter | solution.py:179
  14.3 170.1 %collective-permute-start.13 = (bf16[1120,1536]{1,0:T(8,128)(2,1)}, bf16[1120,1536]{1,0:T(8,128)(2,1)}, u32[]{:S(2)}, u32[]{:S(2)}) collective-permute-start(bf16[1120,1536]{1,0:T(8,128)(2,1)} %get-tuple-element.107._.down_ref), channel_id=1, source_target_pairs={{0,2},{2,0},{4,6},{6,4},{1,3},{3,1},{5,7},{7,5}} | collective-permute-start | bytes 10321928 | tf_op jit(solution)/shard_map/ppermute | solution.py:57
  17.6 174.1 %collective-permute-start.14 = (bf16[1120,1536]{1,0:T(8,128)(2,1)}, bf16[1120,1536]{1,0:T(8,128)(2,1)}, u32[]{:S(2)}, u32[]{:S(2)}) collective-permute-start(bf16[1120,1536]{1,0:T(8,128)(2,1)} %get-tuple-element.107._.down_ref), channel_id=1, source_target_pairs={{0,4},{2,6},{4,0},{6,2},{1,5},{3,7},{5,1},{7,3}} | collective-permute-start | bytes 10321928 | tf_op jit(solution)/shard_map/ppermute | solution.py:57
  24.5 15.3 collective-permute-start.1
  28.7 115.7 %collective-permute-start = (bf16[1024,1536]{1,0:T(8,128)(2,1)}, bf16[1024,1536]{1,0:T(8,128)(2,1)}, u32[]{:S(2)}, u32[]{:S(2)}) collective-permute-start(bf16[1024,1536]{1,0:T(8,128)(2,1)} %fusion.50), channel_id=1, source_target_pairs={{0,1},{1,0},{2,3},{3,2},{4,5},{5,4},{6,7},{7,6}} | collective-permute-start | bytes 9437192 | tf_op jit(solution)/shard_map/ppermute | solution.py:53
  35.7 10.6 collective-permute-start.8
  43.3 78.5 %collective-permute-start.2 = (bf16[384,1792]{1,0:T(8,128)(2,1)}, bf16[384,1792]{1,0:T(8,128)(2,1)}, u32[]{:S(2)}, u32[]{:S(2)}) collective-permute-start(bf16[384,1792]{1,0:T(8,128)(2,1)} %pad_maximum_fusion.12._), channel_id=1, source_target_pairs={{0,2},{2,0},{4,6},{6,4},{1,3},{3,1},{5,7},{7,5}} | collective-permute-start | bytes 4128776 | tf_op jit(solution)/shard_map/ppermute | solution.py:57
  46.4 78.4 %collective-permute-start.3 = (bf16[384,1792]{1,0:T(8,128)(2,1)}, bf16[384,1792]{1,0:T(8,128)(2,1)}, u32[]{:S(2)}, u32[]{:S(2)}) collective-permute-start(bf16[384,1792]{1,0:T(8,128)(2,1)} %pad_maximum_fusion.12._), channel_id=1, source_target_pairs={{0,4},{2,6},{4,0},{6,2},{1,5},{3,7},{5,1},{7,3}} | collective-permute-start | bytes 4128776 | tf_op jit(solution)/shard_map/ppermute | solution.py:57
  123.0 16.6 collective-permute-start.4
  126.0 17.2 collective-permute-start.5
  139.6 77.6 %collective-permute-start.9 = (bf16[384,4480]{1,0:T(8,128)(2,1)}, bf16[384,4480]{1,0:T(8,128)(2,1)}, u32[]{:S(2)}, u32[]{:S(2)}) collective-permute-start(bf16[384,4480]{1,0:T(8,128)(2,1)} %pad_maximum_fusion.10._), channel_id=1, source_target_pairs={{0,2},{2,0},{4,6},{6,4},{1,3},{3,1},{5,7},{7,5}} | collective-permute-start | bytes 10321928 | tf_op jit(solution)/shard_map/ppermute | solution.py:57
  143.2 78.3 %collective-permute-start.10 = (bf16[384,4480]{1,0:T(8,128)(2,1)}, bf16[384,4480]{1,0:T(8,128)(2,1)}, u32[]{:S(2)}, u32[]{:S(2)}) collective-permute-start(bf16[384,4480]{1,0:T(8,128)(2,1)} %pad_maximum_fusion.10._), channel_id=1, source_target_pairs={{0,4},{2,6},{4,0},{6,2},{1,5},{3,7},{5,1},{7,3}} | collective-permute-start | bytes 10321928 | tf_op jit(solution)/shard_map/ppermute | solution.py:57
  178.0 89.1 %collective-permute-start.6 = (f32[1024,1536]{1,0:T(8,128)S(1)}, f32[1024,1536]{1,0:T(8,128)S(1)}, u32[]{:S(2)}, u32[]{:S(2)}) collective-permute-start(f32[1024,1536]{1,0:T(8,128)S(1)} %fusion.73), channel_id=1, source_target_pairs={{0,1},{1,0},{2,3},{3,2},{4,5},{5,4},{6,7},{7,6}} | collective-permute-start | bytes 18874376 | tf_op jit(solution)/shard_map/ppermute | solution.py:53
  186.0 71.5 %collective-permute-start.15 = (bf16[560,1536]{1,0:T(8,128)(2,1)S(1)}, bf16[560,1536]{1,0:T(8,128)(2,1)S(1)}, u32[]{:S(2)}, u32[]{:S(2)}) collective-permute-start(bf16[560,1536]{1,0:T(8,128)(2,1)S(1)} %slice.150), channel_id=1, source_target_pairs={{0,4},{2,6},{4,0},{6,2},{1,5},{3,7},{5,1},{7,3}} | collective-permute-start | bytes 5160968 | tf_op jit(solution)/shard_map/ppermute | solution.py:57
  191.8 260.2 %collective-permute-start.31 = (bf16[1120,1536]{1,0:T(8,128)(2,1)}, bf16[1120,1536]{1,0:T(8,128)(2,1)}, u32[]{:S(2)}, u32[]{:S(2)}) collective-permute-start(bf16[1120,1536]{1,0:T(8,128)(2,1)} %get-tuple-element.106._.down_ref), channel_id=1, source_target_pairs={{0,2},{2,0},{4,6},{6,4},{1,3},{3,1},{5,7},{7,5}} | collective-permute-start | bytes 10321928 | tf_op jit(solution)/shard_map/ppermute | solution.py:57
  217.2 238.9 %collective-permute-start.32 = (bf16[1120,1536]{1,0:T(8,128)(2,1)}, bf16[1120,1536]{1,0:T(8,128)(2,1)}, u32[]{:S(2)}, u32[]{:S(2)}) collective-permute-start(bf16[1120,1536]{1,0:T(8,128)(2,1)} %get-tuple-element.106._.down_ref), channel_id=1, source_target_pairs={{0,4},{2,6},{4,0},{6,2},{1,5},{3,7},{5,1},{7,3}} | collective-permute-start | bytes 10321928 | tf_op jit(solution)/shard_map/ppermute | solution.py:57
  221.5 106.3 %collective-permute-start.16 = (bf16[560,1536]{1,0:T(8,128)(2,1)}, bf16[560,1536]{1,0:T(8,128)(2,1)}, u32[]{:S(2)}, u32[]{:S(2)}) collective-permute-start(bf16[560,1536]{1,0:T(8,128)(2,1)} %slice.151), channel_id=1, source_target_pairs={{0,2},{2,0},{4,6},{6,4},{1,3},{3,1},{5,7},{7,5}} | collective-permute-start | bytes 5160968 | tf_op jit(solution)/shard_map/ppermute | solution.py:57
  257.6 106.4 %collective-permute-start.11 = (bf16[192,4480]{1,0:T(8,128)(2,1)}, bf16[192,4480]{1,0:T(8,128)(2,1)}, u32[]{:S(2)}, u32[]{:S(2)}) collective-permute-start(bf16[192,4480]{1,0:T(8,128)(2,1)} %slice.148), channel_id=1, source_target_pairs={{0,4},{2,6},{4,0},{6,2},{1,5},{3,7},{5,1},{7,3}} | collective-permute-start | bytes 5160968 | tf_op jit(solution)/shard_map/ppermute | solution.py:57
  267.1 99.6 %collective-permute-start.12 = (bf16[192,4480]{1,0:T(8,128)(2,1)}, bf16[192,4480]{1,0:T(8,128)(2,1)}, u32[]{:S(2)}, u32[]{:S(2)}) collective-permute-start(bf16[192,4480]{1,0:T(8,128)(2,1)} %slice.149), channel_id=1, source_target_pairs={{0,2},{2,0},{4,6},{6,4},{1,3},{3,1},{5,7},{7,5}} | collective-permute-start | bytes 5160968 | tf_op jit(solution)/shard_map/ppermute | solution.py:57
  327.8 46.5 %collective-permute-start.7 = (bf16[1024,1536]{1,0:T(8,128)(2,1)S(1)}, bf16[1024,1536]{1,0:T(8,128)(2,1)}, u32[]{:S(2)}, u32[]{:S(2)}) collective-permute-start(bf16[1024,1536]{1,0:T(8,128)(2,1)S(1)} %fusion.34), channel_id=1, source_target_pairs={{0,1},{1,0},{2,3},{3,2},{4,5},{5,4},{6,7},{7,6}} | collective-permute-start | bytes 9437192 | tf_op jit(solution)/shard_map/ppermute | solution.py:53
  374.3 91.8 %collective-permute-start.19 = (bf16[192,1792]{1,0:T(8,128)(2,1)}, bf16[192,1792]{1,0:T(8,128)(2,1)}, u32[]{:S(2)}, u32[]{:S(2)}) collective-permute-start(bf16[192,1792]{1,0:T(8,128)(2,1)} %get-tuple-element.62), channel_id=1, source_target_pairs={{0,1},{1,0},{2,3},{3,2},{4,5},{5,4},{6,7},{7,6}} | collective-permute-start | bytes 2064392 | tf_op jit(solution)/shard_map/ppermute | solution.py:53
  447.5 45.3 %collective-permute-start.17 = (f32[1024,1536]{1,0:T(8,128)}, f32[1024,1536]{1,0:T(8,128)}, u32[]{:S(2)}, u32[]{:S(2)}) collective-permute-start(f32[1024,1536]{1,0:T(8,128)} %fusion.16), channel_id=1, source_target_pairs={{0,1},{1,0},{2,3},{3,2},{4,5},{5,4},{6,7},{7,6}} | collective-permute-start | bytes 18874376 | tf_op jit(solution)/shard_map/ppermute | solution.py:53
  454.7 137.3 %collective-permute-start.33 = (bf16[560,1536]{1,0:T(8,128)(2,1)}, bf16[560,1536]{1,0:T(8,128)(2,1)}, u32[]{:S(2)}, u32[]{:S(2)}) collective-permute-start(bf16[560,1536]{1,0:T(8,128)(2,1)} %slice.160), channel_id=1, source_target_pairs={{0,4},{2,6},{4,0},{6,2},{1,5},{3,7},{5,1},{7,3}} | collective-permute-start | bytes 5160968 | tf_op jit(solution)/shard_map/ppermute | solution.py:57
  458.9 136.4 %collective-permute-start.34 = (bf16[560,1536]{1,0:T(8,128)(2,1)}, bf16[560,1536]{1,0:T(8,128)(2,1)}, u32[]{:S(2)}, u32[]{:S(2)}) collective-permute-start(bf16[560,1536]{1,0:T(8,128)(2,1)} %slice.161), channel_id=1, source_target_pairs={{0,2},{2,0},{4,6},{6,4},{1,3},{3,1},{5,7},{7,5}} | collective-permute-start | bytes 5160968 | tf_op jit(solution)/shard_map/ppermute | solution.py:57
  466.2 33.9 %collective-permute-start.26 = (bf16[192,4480]{1,0:T(8,128)(2,1)}, bf16[192,4480]{1,0:T(8,128)(2,1)}, u32[]{:S(2)}, u32[]{:S(2)}) collective-permute-start(bf16[192,4480]{1,0:T(8,128)(2,1)} %get-tuple-element.64), channel_id=1, source_target_pairs={{0,1},{1,0},{2,3},{3,2},{4,5},{5,4},{6,7},{7,6}} | collective-permute-start | bytes 5160968 | tf_op jit(solution)/shard_map/ppermute | solution.py:53
  468.6 59.2 %collective-permute-start.20 = (bf16[384,1792]{1,0:T(8,128)(2,1)}, bf16[384,1792]{1,0:T(8,128)(2,1)S(1)}, u32[]{:S(2)}, u32[]{:S(2)}) collective-permute-start(bf16[384,1792]{1,0:T(8,128)(2,1)} %pad_maximum_fusion.13._), channel_id=1, source_target_pairs={{0,2},{2,0},{4,6},{6,4},{1,3},{3,1},{5,7},{7,5}} | collective-permute-start | bytes 4128776 | tf_op jit(solution)/shard_map/ppermute | solution.py:57
  492.8 35.7 %collective-permute-start.21 = (bf16[384,1792]{1,0:T(8,128)(2,1)}, bf16[384,1792]{1,0:T(8,128)(2,1)S(1)}, u32[]{:S(2)}, u32[]{:S(2)}) collective-permute-start(bf16[384,1792]{1,0:T(8,128)(2,1)} %pad_maximum_fusion.13._), channel_id=1, source_target_pairs={{0,4},{2,6},{4,0},{6,2},{1,5},{3,7},{5,1},{7,3}} | collective-permute-start | bytes 4128776 | tf_op jit(solution)/shard_map/ppermute | solution.py:57
  500.1 46.3 %collective-permute-start.18 = (bf16[1024,1536]{1,0:T(8,128)(2,1)S(1)}, bf16[1024,1536]{1,0:T(8,128)(2,1)S(1)}, u32[]{:S(2)}, u32[]{:S(2)}) collective-permute-start(bf16[1024,1536]{1,0:T(8,128)(2,1)S(1)} %fusion.38), channel_id=1, source_target_pairs={{0,1},{1,0},{2,3},{3,2},{4,5},{5,4},{6,7},{7,6}} | collective-permute-start | bytes 9437192 | tf_op jit(solution)/shard_map/ppermute | solution.py:53
  527.8 16.2 collective-permute-start.22
  528.6 16.3 collective-permute-start.23
  544.1 74.7 %collective-permute-start.27 = (bf16[384,4480]{1,0:T(8,128)(2,1)}, bf16[384,4480]{1,0:T(8,128)(2,1)}, u32[]{:S(2)}, u32[]{:S(2)}) collective-permute-start(bf16[384,4480]{1,0:T(8,128)(2,1)} %pad_maximum_fusion.11._), channel_id=1, source_target_pairs={{0,2},{2,0},{4,6},{6,4},{1,3},{3,1},{5,7},{7,5}} | collective-permute-start | bytes 10321928 | tf_op jit(solution)/shard_map/ppermute | solution.py:57
  544.8 76.5 %collective-permute-start.28 = (bf16[384,4480]{1,0:T(8,128)(2,1)}, bf16[384,4480]{1,0:T(8,128)(2,1)}, u32[]{:S(2)}, u32[]{:S(2)}) collective-permute-start(bf16[384,4480]{1,0:T(8,128)(2,1)} %pad_maximum_fusion.11._), channel_id=1, source_target_pairs={{0,4},{2,6},{4,0},{6,2},{1,5},{3,7},{5,1},{7,3}} | collective-permute-start | bytes 10321928 | tf_op jit(solution)/shard_map/ppermute | solution.py:57
  584.1 51.4 %collective-permute-start.24 = (f32[1024,1536]{1,0:T(8,128)}, f32[1024,1536]{1,0:T(8,128)}, u32[]{:S(2)}, u32[]{:S(2)}) collective-permute-start(f32[1024,1536]{1,0:T(8,128)} %fusion.68), channel_id=1, source_target_pairs={{0,1},{1,0},{2,3},{3,2},{4,5},{5,4},{6,7},{7,6}} | collective-permute-start | bytes 18874376 | tf_op jit(solution)/shard_map/ppermute | solution.py:53
  592.0 125.3 %collective-permute-start.35 = (bf16[1024,1536]{1,0:T(8,128)(2,1)}, bf16[1024,1536]{1,0:T(8,128)(2,1)}, u32[]{:S(2)}, u32[]{:S(2)}) collective-permute-start(bf16[1024,1536]{1,0:T(8,128)(2,1)} %bitcast.43), channel_id=1, source_target_pairs={{0,1},{1,0},{2,3},{3,2},{4,5},{5,4},{6,7},{7,6}} | collective-permute-start | bytes 9437192 | tf_op jit(solution)/shard_map/ppermute | solution.py:53
  620.3 36.6 %collective-permute-start.29 = (bf16[192,4480]{1,0:T(8,128)(2,1)S(1)}, bf16[192,4480]{1,0:T(8,128)(2,1)S(1)}, u32[]{:S(2)}, u32[]{:S(2)}) collective-permute-start(bf16[192,4480]{1,0:T(8,128)(2,1)S(1)} %slice.158), channel_id=1, source_target_pairs={{0,4},{2,6},{4,0},{6,2},{1,5},{3,7},{5,1},{7,3}} | collective-permute-start | bytes 5160968 | tf_op jit(solution)/shard_map/ppermute | solution.py:57
  624.1 37.0 %collective-permute-start.30 = (bf16[192,4480]{1,0:T(8,128)(2,1)}, bf16[192,4480]{1,0:T(8,128)(2,1)}, u32[]{:S(2)}, u32[]{:S(2)}) collective-permute-start(bf16[192,4480]{1,0:T(8,128)(2,1)} %slice.159), channel_id=1, source_target_pairs={{0,2},{2,0},{4,6},{6,4},{1,3},{3,1},{5,7},{7,5}} | collective-permute-start | bytes 5160968 | tf_op jit(solution)/shard_map/ppermute | solution.py:57
  641.9 22.0 %collective-permute-start.25 = (bf16[1024,1536]{1,0:T(8,128)(2,1)S(1)}, bf16[1024,1536]{1,0:T(8,128)(2,1)S(1)}, u32[]{:S(2)}, u32[]{:S(2)}) collective-permute-start(bf16[1024,1536]{1,0:T(8,128)(2,1)S(1)} %fusion.31), channel_id=1, source_target_pairs={{0,1},{1,0},{2,3},{3,2},{4,5},{5,4},{6,7},{7,6}} | collective-permute-start | bytes 9437192 | tf_op jit(solution)/shard_map/ppermute | solution.py:53
  780.6 19.3 collective-permute-start.36
  804.3 5.7 collective-permute-start.37
  855.9 10.2 collective-permute-start.38
  874.0 27.9 %collective-permute-start.40 = (bf16[1024,1536]{1,0:T(8,128)(2,1)S(1)}, bf16[1024,1536]{1,0:T(8,128)(2,1)}, u32[]{:S(2)}, u32[]{:S(2)}) collective-permute-start(bf16[1024,1536]{1,0:T(8,128)(2,1)S(1)} %fusion.25), channel_id=1, source_target_pairs={{0,1},{1,0},{2,3},{3,2},{4,5},{5,4},{6,7},{7,6}} | collective-permute-start | bytes 9437192 | tf_op jit(solution)/shard_map/ppermute | solution.py:53
  901.9 664.2 %reduce-scatter.3.cloned.1.call-start = ((), (), s32[]{:S(2)}) async-start(), calls=%async_computation.4 | async-start | bytes 13762560 | tf_op jit(solution)/shard_map/reduce_scatter | solution.py:179
  965.5 21.8 %collective-permute-start.41 = (f32[1024,1536]{1,0:T(8,128)}, f32[1024,1536]{1,0:T(8,128)S(1)}, u32[]{:S(2)}, u32[]{:S(2)}) collective-permute-start(f32[1024,1536]{1,0:T(8,128)} %fusion.4), channel_id=1, source_target_pairs={{0,1},{1,0},{2,3},{3,2},{4,5},{5,4},{6,7},{7,6}} | collective-permute-start | bytes 18874376 | tf_op jit(solution)/shard_map/ppermute | solution.py:53
  995.8 7.1 collective-permute-start.42
  1062.4 507.1 %all-gather.5.cloned.1.call-start = ((), (), s32[]{:S(2)}) async-start(), calls=%async_computation.3 | async-start | bytes 56623104 | tf_op jit(solution)/shard_map/all_gather | solution.py:175
  1068.5 642.1 %all-gather.3.cloned.1.call-start = ((), (), s32[]{:S(2)}) async-start(), calls=%async_computation.2 | async-start | bytes 56623104 | tf_op jit(solution)/shard_map/all_gather | solution.py:175
  1086.7 36.2 %collective-permute-start.43 = (f32[1024,1536]{1,0:T(8,128)}, f32[1024,1536]{1,0:T(8,128)}, u32[]{:S(2)}, u32[]{:S(2)}) collective-permute-start(f32[1024,1536]{1,0:T(8,128)} %fusion.58), channel_id=1, source_target_pairs={{0,1},{1,0},{2,3},{3,2},{4,5},{5,4},{6,7},{7,6}} | collective-permute-start | bytes 18874376 | tf_op jit(solution)/shard_map/ppermute | solution.py:53
  1090.9 26.9 %collective-permute-start.45 = (f32[192,1792]{1,0:T(8,128)}, f32[192,1792]{1,0:T(8,128)}, u32[]{:S(2)}, u32[]{:S(2)}) collective-permute-start(f32[192,1792]{1,0:T(8,128)} %get-tuple-element.112), channel_id=1, source_target_pairs={{0,1},{1,0},{2,3},{3,2},{4,5},{5,4},{6,7},{7,6}} | collective-permute-start | bytes 4128776 | tf_op jit(solution)/shard_map/ppermute | solution.py:53
  1569.5 279.6 %collective-permute-start.44 = (f32[192,1792]{1,0:T(8,128)}, f32[192,1792]{1,0:T(8,128)}, u32[]{:S(2)}, u32[]{:S(2)}) collective-permute-start(f32[192,1792]{1,0:T(8,128)} %get-tuple-element.114), channel_id=1, source_target_pairs={{0,1},{1,0},{2,3},{3,2},{4,5},{5,4},{6,7},{7,6}} | collective-permute-start | bytes 4128776 | tf_op jit(solution)/shard_map/ppermute | solution.py:53
  1708.0 142.5 %collective-permute-start.53 = (f32[192,1120]{1,0:T(8,128)}, f32[192,1120]{1,0:T(8,128)S(1)}, u32[]{:S(2)}, u32[]{:S(2)}) collective-permute-start(f32[192,1120]{1,0:T(8,128)} %get-tuple-element.90), channel_id=1, source_target_pairs={{0,1},{1,0},{2,3},{3,2},{4,5},{5,4},{6,7},{7,6}} | collective-permute-start | bytes 2580488 | tf_op jit(solution)/shard_map/ppermute | solution.py:381
  1708.5 165.9 %collective-permute-start.54 = (f32[192,1120]{1,0:T(8,128)}, f32[192,1120]{1,0:T(8,128)}, u32[]{:S(2)}, u32[]{:S(2)}) collective-permute-start(f32[192,1120]{1,0:T(8,128)} %get-tuple-element.91), channel_id=1, source_target_pairs={{0,2},{1,3},{2,0},{3,1},{4,6},{5,7},{6,4},{7,5}} | collective-permute-start | bytes 2580488 | tf_op jit(solution)/shard_map/ppermute | solution.py:381
  1710.0 165.3 %collective-permute-start.55 = (f32[192,1120]{1,0:T(8,128)}, f32[192,1120]{1,0:T(8,128)}, u32[]{:S(2)}, u32[]{:S(2)}) collective-permute-start(f32[192,1120]{1,0:T(8,128)} %get-tuple-element.92), channel_id=1, source_target_pairs={{0,3},{1,2},{2,1},{3,0},{4,7},{5,6},{6,5},{7,4}} | collective-permute-start | bytes 2580488 | tf_op jit(solution)/shard_map/ppermute | solution.py:381
  1710.0 166.0 %collective-permute-start.56 = (f32[192,1120]{1,0:T(8,128)}, f32[192,1120]{1,0:T(8,128)}, u32[]{:S(2)}, u32[]{:S(2)}) collective-permute-start(f32[192,1120]{1,0:T(8,128)} %get-tuple-element.93), channel_id=1, source_target_pairs={{0,4},{1,5},{2,6},{3,7},{4,0},{5,1},{6,2},{7,3}} | collective-permute-start | bytes 2580488 | tf_op jit(solution)/shard_map/ppermute | solution.py:381
  1849.1 59.4 %collective-permute-start.57 = (f32[192,1120]{1,0:T(8,128)}, f32[192,1120]{1,0:T(8,128)S(1)}, u32[]{:S(2)}, u32[]{:S(2)}) collective-permute-start(f32[192,1120]{1,0:T(8,128)} %get-tuple-element.94), channel_id=1, source_target_pairs={{0,5},{1,4},{2,7},{3,6},{4,1},{5,0},{6,3},{7,2}} | collective-permute-start | bytes 2580488 | tf_op jit(solution)/shard_map/ppermute | solution.py:381
  1850.6 60.6 %collective-permute-start.58 = (f32[192,1120]{1,0:T(8,128)}, f32[192,1120]{1,0:T(8,128)S(1)}, u32[]{:S(2)}, u32[]{:S(2)}) collective-permute-start(f32[192,1120]{1,0:T(8,128)} %get-tuple-element.95), channel_id=1, source_target_pairs={{0,6},{1,7},{2,4},{3,5},{4,2},{5,3},{6,0},{7,1}} | collective-permute-start | bytes 2580488 | tf_op jit(solution)/shard_map/ppermute | solution.py:381
  1874.4 47.2 %collective-permute-start.59 = (f32[192,1120]{1,0:T(8,128)}, f32[192,1120]{1,0:T(8,128)S(1)}, u32[]{:S(2)}, u32[]{:S(2)}) collective-permute-start(f32[192,1120]{1,0:T(8,128)} %get-tuple-element.96), channel_id=1, source_target_pairs={{0,7},{1,6},{2,5},{3,4},{4,3},{5,2},{6,1},{7,0}} | collective-permute-start | bytes 2580488 | tf_op jit(solution)/shard_map/ppermute | solution.py:381
  1875.3 56.7 %collective-permute-start.46 = (f32[192,1120]{1,0:T(8,128)}, f32[192,1120]{1,0:T(8,128)S(1)}, u32[]{:S(2)}, u32[]{:S(2)}) collective-permute-start(f32[192,1120]{1,0:T(8,128)} %get-tuple-element.82), channel_id=1, source_target_pairs={{0,1},{1,0},{2,3},{3,2},{4,5},{5,4},{6,7},{7,6}} | collective-permute-start | bytes 2580488 | tf_op jit(solution)/shard_map/ppermute | solution.py:381
  1876.0 56.2 %collective-permute-start.47 = (f32[192,1120]{1,0:T(8,128)}, f32[192,1120]{1,0:T(8,128)S(1)}, u32[]{:S(2)}, u32[]{:S(2)}) collective-permute-start(f32[192,1120]{1,0:T(8,128)} %get-tuple-element.83), channel_id=1, source_target_pairs={{0,2},{1,3},{2,0},{3,1},{4,6},{5,7},{6,4},{7,5}} | collective-permute-start | bytes 2580488 | tf_op jit(solution)/shard_map/ppermute | solution.py:381
  1909.4 25.9 %collective-permute-start.48 = (f32[192,1120]{1,0:T(8,128)}, f32[192,1120]{1,0:T(8,128)S(1)}, u32[]{:S(2)}, u32[]{:S(2)}) collective-permute-start(f32[192,1120]{1,0:T(8,128)} %get-tuple-element.84), channel_id=1, source_target_pairs={{0,3},{1,2},{2,1},{3,0},{4,7},{5,6},{6,5},{7,4}} | collective-permute-start | bytes 2580488 | tf_op jit(solution)/shard_map/ppermute | solution.py:381
  1911.2 107.9 %collective-permute-start.39 = (f32[1024,1536]{1,0:T(8,128)}, f32[1024,1536]{1,0:T(8,128)}, u32[]{:S(2)}, u32[]{:S(2)}) collective-permute-start(f32[1024,1536]{1,0:T(8,128)} %fusion.12), channel_id=1, source_target_pairs={{0,1},{1,0},{2,3},{3,2},{4,5},{5,4},{6,7},{7,6}} | collective-permute-start | bytes 18874376 | tf_op jit(solution)/shard_map/ppermute | solution.py:53
  1930.6 60.7 %collective-permute-start.49 = (f32[192,1120]{1,0:T(8,128)}, f32[192,1120]{1,0:T(8,128)S(1)}, u32[]{:S(2)}, u32[]{:S(2)}) collective-permute-start(f32[192,1120]{1,0:T(8,128)} %get-tuple-element.85), channel_id=1, source_target_pairs={{0,4},{1,5},{2,6},{3,7},{4,0},{5,1},{6,2},{7,3}} | collective-permute-start | bytes 2580488 | tf_op jit(solution)/shard_map/ppermute | solution.py:381
  1932.0 76.7 %collective-permute-start.50 = (f32[192,1120]{1,0:T(8,128)}, f32[192,1120]{1,0:T(8,128)S(1)}, u32[]{:S(2)}, u32[]{:S(2)}) collective-permute-start(f32[192,1120]{1,0:T(8,128)} %get-tuple-element.86), channel_id=1, source_target_pairs={{0,5},{1,4},{2,7},{3,6},{4,1},{5,0},{6,3},{7,2}} | collective-permute-start | bytes 2580488 | tf_op jit(solution)/shard_map/ppermute | solution.py:381
  1932.2 76.5 %collective-permute-start.51 = (f32[192,1120]{1,0:T(8,128)}, f32[192,1120]{1,0:T(8,128)S(1)}, u32[]{:S(2)}, u32[]{:S(2)}) collective-permute-start(f32[192,1120]{1,0:T(8,128)} %get-tuple-element.87), channel_id=1, source_target_pairs={{0,6},{1,7},{2,4},{3,5},{4,2},{5,3},{6,0},{7,1}} | collective-permute-start | bytes 2580488 | tf_op jit(solution)/shard_map/ppermute | solution.py:381
  1935.3 73.4 %collective-permute-start.52 = (f32[192,1120]{1,0:T(8,128)}, f32[192,1120]{1,0:T(8,128)S(1)}, u32[]{:S(2)}, u32[]{:S(2)}) collective-permute-start(f32[192,1120]{1,0:T(8,128)} %get-tuple-element.88), channel_id=1, source_target_pairs={{0,7},{1,6},{2,5},{3,4},{4,3},{5,2},{6,1},{7,0}} | collective-permute-start | bytes 2580488 | tf_op jit(solution)/shard_map/ppermute | solution.py:381
  (67 other events, 1298.2 us)
Sparse Core Ops, SparseCore 0:
  902.0 102.3 reduce-scatter.4
  1062.5 503.4 reduce-scatter.2
Sparse Core Ops, SparseCore 1:
  1068.6 247.6 all-gather.4
  1318.0 236.7 all-gather.2

commit v10 on v9

--- a/solution.py
+++ b/solution.py
@@ -185,8 +185,12 @@
     return own + other
 
 
+def halves_of(value):
+    return value, swap(value)
+
+
 def pair_rows(value):
-    return jnp.concatenate([value, swap(value)], axis=0)
+    return jnp.concatenate(halves_of(value))
 
 
 def causal_blocks(seq):
@@ -253,8 +257,8 @@
 
 
 def attn_forward(x_own, weight, q_width, head, seq):
-    normed = pair_rows(norm_bf16(x_own))
-    qkv = times(normed, weight[:, :q_width + 2 * head]).astype(jnp.bfloat16)
+    normed = halves_of(norm_bf16(x_own))
+    qkv = times(jnp.concatenate(normed), weight[:, :q_width + 2 * head]).astype(jnp.bfloat16)
     o_act = by_sequence(attn_fwd_kernel, seq, q_width, head, (qkv,), q_width, 0,
                   20_000_000_000)
     proj = both_halves(o_act, weight[:, q_width + 2 * head:], x_own.shape[0], times_flipped)
@@ -262,32 +266,33 @@
     return y_own, (x_own, normed, qkv, o_act)
 
 
-def attn_grads_kernel(norm_ref, d_qkv_ref, grad_ref, o_ref, out_ref):
-    width = d_qkv_ref.shape[1]
-    out_ref[:, :width] = dot(norm_ref[...], d_qkv_ref[...], ((0,), (0,)))
-    out_ref[:, width:] = dot(grad_ref[...], o_ref[...], ((0,), (0,)))
+def attn_grads_kernel(n0_ref, n1_ref, d_qkv_ref, g0_ref, g1_ref, o_ref, out_ref):
+    width, rows = d_qkv_ref.shape[1], n0_ref.shape[0]
+    halves = (slice(0, rows), slice(rows, 2 * rows))
+    for cols, lefts, right in ((slice(0, width), (n0_ref, n1_ref), d_qkv_ref), (slice(width, None), (g0_ref, g1_ref), o_ref)):
+        out_ref[:, cols] = sum(dot(left[...], right[half, :], ((0,), (0,))) for left, half in zip(lefts, halves))
 
 
 def attn_grads(normed, d_qkv, grad_y, o_act):
-    rows, width = normed.shape
+    rows, width = normed[0].shape
     cols = d_qkv.shape[1] + o_act.shape[1]
     piece = pl.BlockSpec((rows, WIDTH_TILE), lambda i: (0, i))
     whole = [pl.BlockSpec(arg.shape, lambda i: (0, 0), pipeline_mode=pl.Buffered(1)) for arg in (d_qkv, o_act)]
     return pl.pallas_call(
         attn_grads_kernel,
         grid=(width // WIDTH_TILE,),
-        in_specs=[piece, whole[0], piece, whole[1]],
+        in_specs=[piece, piece, whole[0], piece, piece, whole[1]],
         out_specs=pl.BlockSpec((WIDTH_TILE, cols), lambda i: (i, 0)),
         out_shape=jax.ShapeDtypeStruct((width, cols), jnp.float32),
-        cost_estimate=pl.CostEstimate(flops=2 * rows * width * cols, bytes_accessed=0, transcendentals=0),
+        cost_estimate=pl.CostEstimate(flops=4 * rows * width * cols, bytes_accessed=0, transcendentals=0),
         name="attn_grads",
-    )(normed, d_qkv, grad_y, o_act)
+    )(*normed, d_qkv, *grad_y, o_act)
 
 
 def attn_backward(saved, weight, q_width, head, seq, grad_own):
     x_own, normed, qkv, o_act = saved
-    grad_y = pair_rows(grad_own)
-    d_o = times(grad_y, weight[:, q_width + 2 * head:]).astype(jnp.bfloat16)
+    grad_y = (grad_own, swap(grad_own))
+    d_o = times(jnp.concatenate(grad_y), weight[:, q_width + 2 * head:]).astype(jnp.bfloat16)
     d_qkv = by_sequence(attn_bwd_kernel, seq, q_width, head, (qkv, d_o), qkv.shape[1], 2,
                   40_000_000_000)
     d_norm = both_halves(d_qkv, weight[:, :q_width + 2 * head], grad_own.shape[0], times_flipped)
@@ -345,22 +350,24 @@
                 parts[CORES * i + j][...] = flip_ref[pl.ds(start, rows), :]
 
 
-def mlp_weight_grads(place, layer, pairs, earlier, up_flip, down_block, tokens):
+def mlp_weight_grads(place, layer, pairs, earlier, up_flip, down_block, rows_dev, tokens):
     block, width = down_block.shape
     rows = width // (CHIPS * CORES)
     once = pl.Buffered(1)
     whole = pl.BlockSpec((block, width), lambda i, p: (0, 0), pipeline_mode=once)
-    tiles = tokens.shape[0] // (2 * CHIPS * CORES * TOKEN_TILE)
-    norms, grads = [pl.BlockSpec((TOKEN_TILE, width), lambda i, p, k=k: (2 * tiles * (i // tiles) + k * tiles + i % tiles, 0))
-                    for k in range(2)]
+    tiles, specs = rows_dev // TOKEN_TILE, []
+    for source, place_in in tokens:
+        count = source.shape[0] // (CHIPS * CORES * rows_dev)
+        specs.append(pl.BlockSpec((TOKEN_TILE, width), lambda i, p, count=count, k=place_in:
+                                  (count * tiles * (i // tiles) + k * tiles + i % tiles, 0)))
     part = pl.BlockSpec((rows, block), lambda i, p: (0, 0), pipeline_mode=once)
-    args = [place, up_flip, down_block, tokens, tokens, *earlier]
+    args = [place, up_flip, down_block, *[source for source, _ in tokens], *earlier]
     outs = pl.pallas_call(
         mlp_grads_kernel,
         grid_spec=pltpu.PrefetchScalarGridSpec(
             num_scalar_prefetch=1,
             grid=(tiles * CHIPS * CORES,),
-            in_specs=[whole, whole, norms, grads] + [pl.BlockSpec(memory_space=pl.ANY)] * len(earlier),
+            in_specs=[whole, whole] + specs + [pl.BlockSpec(memory_space=pl.ANY)] * len(earlier),
             out_specs=[pl.BlockSpec((1, block, width), lambda i, p: (layer, 0, 0), pipeline_mode=once)]
             + [part] * (CHIPS * CORES),
             scratch_shapes=[pltpu.VMEM((block, width), jnp.float32), pltpu.VMEM((CORES * rows, block), jnp.float32)],
@@ -369,7 +376,7 @@
         + [jax.ShapeDtypeStruct((rows, block), jnp.float32)] * (CHIPS * CORES),
         input_output_aliases={len(args) - 1: 0} if earlier else {},
         compiler_params=pltpu.CompilerParams(vmem_limit_bytes=60 * 1024 * 1024),
-        cost_estimate=pl.CostEstimate(flops=4 * tokens.shape[0] * block * width, bytes_accessed=0,
+        cost_estimate=pl.CostEstimate(flops=8 * CHIPS * CORES * rows_dev * block * width, bytes_accessed=0,
                                       transcendentals=0),
         name="mlp_grads",
     )(*args)
@@ -493,9 +500,9 @@
         grad_x = grad_out.reshape(seqs * seq, width)
         attn_saved, mlp_saved, d_up, d_down = [], [], [], []
 
-        def weight_grads(layer, n_own, grad_own, d_down):
-            tokens = gather_rows(jnp.concatenate([n_own, grad_own], axis=0))
-            down, parts = mlp_weight_grads(place, layer, pairs, d_down, up_flip[layer], w_down[layer], tokens)
+        def weight_grads(layer, tokens, d_down):
+            down, parts = mlp_weight_grads(place, layer, pairs, d_down, up_flip[layer], w_down[layer],
+                                           seqs * seq, tokens)
             return exchange(parts), [down]
 
         for layer in range(pairs):
@@ -506,17 +513,17 @@
                 gather_weights(layer + 1, *later)
             n_own = norm_bf16(x_own)
             gelu_act, slope = mlp_hidden(pair_rows(n_own), up_full[layer])
-            if layer == pairs - 1:
-                parts, d_down = weight_grads(layer, n_own, grad_x, d_down)
             mlp_saved.append((x_own, n_own, slope))
             if layer < pairs - 1:
                 carry_x = mlp_output(x_own, gelu_act, down_full[layer])
         last = (x_own, gelu_act, down_full[-1])
+        joined = jnp.concatenate([grad_x] + [saved[1] for saved in mlp_saved[::-1]])
+        together = gather_rows(joined)
         d_heads, head_shapes = [], [weight.shape for weight in heads_in]
         for layer in reversed(range(pairs)):
             x_own, n_own, slope = mlp_saved[layer]
-            if layer < pairs - 1:
-                parts, d_down = weight_grads(layer, n_own, grad_x, d_down)
+            grads = (together, 0) if layer == pairs - 1 else (gather_rows(grad_x), 0)
+            parts, d_down = weight_grads(layer, [(together, pairs - layer), grads], d_down)
             d_up = [assemble(place, layer, pairs, d_up, parts)]
             grad_x = mlp_backward(x_own, slope, up_full[layer], down_full[layer], grad_x)
             grad_x, d_attn = attn_backward(attn_saved[layer], attn_full[layer], q_width, head, seq, grad_x)

time: 2050 us -> 2010 us (0.980)
  other arithmetic: 118 us -> 92.9 us
    reduce_scatter x2, waiting for transfers between devices: 437 us -> 379 us  [scatter_sum(): return lax.psum_scatter(grad_full, CHIP, scatter_dimension=0, tiled=True)]
    ppermute x14, waiting for transfers between devices: 84.3 us -> 117 us  [exchange(): lax.ppermute(part, AXES, [(d, d ^ i) for d in devices])]
    concatenate x6 -> x1, other arithmetic: 30.4 us -> 7.47 us  [body(): joined = jnp.concatenate([grad_x] + [saved[1] for saved in mlp_saved[::-1]])]
  transfers between devices with their start and end apart: 64 -> 64, of which waited for: 19 -> 22; matrix products, arithmetic and copies ran while one was open for 28% -> 27% of each run, Pallas kernels for 22% -> 23%
where the time goes in v10:
time: 2010 us; the launch traced here: 2000 us
  waiting for transfers between devices  785 us (39%)
  Pallas kernels  479 us (24%)
  matrix products  451 us (22%)
  local copies, waits for them, and re-layouts  123 us (6%)
  other arithmetic  92.9 us (5%)
  starting transfers between devices  50.2 us (2%)
    dot_general x24, matrix products, dot(): lax.dot_general(left, right, (contract, ((), ())), preferred_element_type...  451 us
    reduce_scatter x2, waiting for transfers between devices, scatter_sum(): return lax.psum_scatter(grad_full, CHIP, scatter_dimension=0, tiled=True)  379 us
    pallas_call x2, Pallas kernels, mlp_weight_grads(): pl.pallas_call(mlp_grads_kernel, grid_spec=pltpu.PrefetchScalarGridSpec(n...  278 us
    ppermute x24, waiting for transfers between devices, hop(): lax.ppermute(value, CHIP, [(chip, chip ^ step) for chip in range(CHIPS)])  273 us
    ppermute x14, waiting for transfers between devices, exchange(): lax.ppermute(part, AXES, [(d, d ^ i) for d in devices])  117 us
    pallas_call x4, Pallas kernels, by_sequence(): pl.pallas_call(functools.partial(kernel, q_width, head), grid=(rows // se...  90 us
    dynamic_update_slice x26, local copies, waits for them, and re-layouts, gather_weight(): full = lax.dynamic_update_slice(full, part[None], (chip ^ step, row, 0))  67.8 us
  transfers between devices with their start and end apart: 64, of which 22 were waited for; matrix products, arithmetic and copies ran while one was open for 27% of the time, Pallas kernels for 23%

profile of v10, /device:TPU:0, one launch (start us, length us, event | category | flops | bytes accessed | tf_op | source)
XLA Modules:
  0.0 1998.9 jit_solution(11932451523294838013)
XLA Ops:
  8.0 6.5 slice_bitcast_fusion
  29.4 6.5 split.2
  56.5 65.5 %collective-permute-done.2 = bf16[384,1792]{1,0:T(8,128)(2,1)} collective-permute-done((bf16[384,1792]{1,0:T(8,128)(2,1)}, bf16[384,1792]{1,0:T(8,128)(2,1)}, u32[]{:S(2)}, u32[]{:S(2)}) %collective-permute-start.2) | collective-permute-done | bytes 1376288 | tf_op jit(solution)/shard_map/ppermute | solution.py:57
  132.7 7.1 collective-permute-done.4
  144.6 11.6 fusion.76.qkv_ref
  156.2 17.0 shard_map.143.o_ref
  178.3 6.4 fusion.107
  200.4 17.0 collective-permute-done.9
  226.0 31.8 %collective-permute-done.15 = bf16[560,1536]{1,0:T(8,128)(2,1)S(1)} collective-permute-done((bf16[560,1536]{1,0:T(8,128)(2,1)S(1)}, bf16[560,1536]{1,0:T(8,128)(2,1)S(1)}, u32[]{:S(2)}, u32[]{:S(2)}) %collective-permute-start.15) | collective-permute-done | bytes 1720352 | tf_op jit(solution)/shard_map/ppermute | solution.py:57
  275.6 52.4 %collective-permute-done.16 = bf16[560,1536]{1,0:T(8,128)(2,1)} collective-permute-done((bf16[560,1536]{1,0:T(8,128)(2,1)}, bf16[560,1536]{1,0:T(8,128)(2,1)}, u32[]{:S(2)}, u32[]{:S(2)}) %collective-permute-start.16) | collective-permute-done | bytes 1720352 | tf_op jit(solution)/shard_map/ppermute | solution.py:57
  330.8 33.3 %collective-permute-done.11 = bf16[192,4480]{1,0:T(8,128)(2,1)} collective-permute-done((bf16[192,4480]{1,0:T(8,128)(2,1)}, bf16[192,4480]{1,0:T(8,128)(2,1)}, u32[]{:S(2)}, u32[]{:S(2)}) %collective-permute-start.11) | collective-permute-done | bytes 1720352 | tf_op jit(solution)/shard_map/ppermute | solution.py:57
  374.5 51.8 %multiply_add_fusion.2 = (f32[2048,4480]{1,0:T(8,128)}, bf16[2048,4480]{1,0:T(8,128)(2,1)}) fusion(bf16[1536,4480]{1,0:T(8,128)(2,1)} %bitcast.127, bf16[1024,1536]{1,0:T(8,128)(2,1)} %collective-permute-done.7, bf16[1024,1536]{1,0:T(8,128)(2,1)S(1)} %fusion.32), kind=kOutput, calls=%fused_computation.6 | convolution fusion | flops 28326756352 | bytes 75104256 | tf_op jit(solution)/shard_map/dot_general | solution.py:41
  426.3 21.5 %fusion.16 = f32[1024,1536]{1,0:T(8,128)} fusion(bf16[4480,1536]{1,0:T(8,128)(2,1)} %bitcast.120, bf16[2048,4480]{1,0:T(8,128)(2,1)} %get-tuple-element.58), kind=kOutput, calls=%fused_computation.41 | convolution fusion | flops 14092861440 | bytes 29229056 | tf_op jit(solution)/shard_map/dot_general | solution.py:41
  459.8 6.7 split.3
  471.6 21.7 %fusion.18 = f32[1024,1536]{1,0:T(8,128)} fusion(bf16[4480,1536]{1,0:T(8,128)(2,1)} %bitcast.121, bf16[2048,4480]{1,0:T(8,128)(2,1)} %get-tuple-element.58), kind=kOutput, calls=%fused_computation.43 | convolution fusion | flops 14092861440 | bytes 29229056 | tf_op jit(solution)/shard_map/dot_general | solution.py:41
  493.8 6.0 fusion.35
  506.6 21.5 %collective-permute-done.20 = bf16[384,1792]{1,0:T(8,128)(2,1)S(1)} collective-permute-done((bf16[384,1792]{1,0:T(8,128)(2,1)}, bf16[384,1792]{1,0:T(8,128)(2,1)S(1)}, u32[]{:S(2)}, u32[]{:S(2)}) %collective-permute-start.20) | collective-permute-done | bytes 1376288 | tf_op jit(solution)/shard_map/ppermute | solution.py:57
  530.6 13.8 collective-permute-done.22
  550.1 9.6 fusion.73.qkv_ref
  559.7 17.3 shard_map.144.o_ref
  577.0 7.4 fusion.100
  602.3 16.8 collective-permute-done.27
  629.5 6.1 fusion.102
  635.6 5.8 fusion.28
  642.1 5.5 bitcast_dynamic-update-slice_fusion.3
  647.6 9.8 collective-permute-done.29
  666.1 51.6 %multiply_add_fusion = (f32[2048,4480]{1,0:T(8,128)}, bf16[2048,4480]{1,0:T(8,128)(2,1)}) fusion(bf16[1536,4480]{1,0:T(8,128)(2,1)} %bitcast.123, bf16[1024,1536]{1,0:T(8,128)(2,1)} %copy-done.58, bf16[1024,1536]{1,0:T(8,128)(2,1)S(1)} %fusion.29), kind=kOutput, calls=%fused_computation.2 | convolution fusion | flops 28326756352 | bytes 75104256 | tf_op jit(solution)/shard_map/dot_general | solution.py:41
  717.7 41.7 %multiply_convert_fusion.1 = bf16[2048,4480]{1,0:T(8,128)(2,1)} fusion(f32[2048,4480]{1,0:T(8,128)} %get-tuple-element.66, bf16[4480,1536]{1,0:T(8,128)(2,1)} %bitcast.42, bf16[1024,1536]{1,0:T(8,128)(2,1)} %collective-permute-done.35, bf16[1024,1536]{1,0:T(8,128)(2,1)} %bitcast.43), kind=kOutput, calls=%fused_computation.1 | convolution fusion | flops 28216655872 | bytes 75104256 | tf_op jit(solution)/shard_map/dot_general | solution.py:41
  759.4 21.6 %fusion.8 = f32[1024,1536]{1,0:T(8,128)} fusion(bf16[1536,4480]{1,0:T(8,128)(2,1)} %bitcast.124, bf16[2048,4480]{1,0:T(8,128)(2,1)} %multiply_convert_fusion.1), kind=kOutput, calls=%fused_computation.33 | convolution fusion | flops 14092861440 | bytes 29229056 | tf_op jit(solution)/shard_map/dot_general | solution.py:41
  781.0 19.2 fusion.10
  805.1 5.3 collective-permute-done.37.g1_ref
  812.1 10.0 fusion.82.d_o_ref
  822.1 28.1 %shard_map.145.d_qkv_ref = bf16[2048,1024]{1,0:T(8,128)(2,1)} custom-call(bf16[2048,1024]{1,0:T(8,128)(2,1)} %fusion.73.qkv_ref, bf16[2048,768]{1,0:T(8,128)(2,1)} %fusion.82.d_o_ref), custom_call_target="tpu_custom_call" | custom-call | flops 40000000000 | tf_op jit(solution)/shard_map/pallas_call | solution.py:248
  850.2 6.1 fusion.85
  856.7 5.5 fusion.87
  872.8 19.3 attn_grads.3
  892.2 41.7 %multiply_convert_fusion = bf16[2048,4480]{1,0:T(8,128)(2,1)} fusion(f32[2048,4480]{1,0:T(8,128)} %get-tuple-element.72, bf16[4480,1536]{1,0:T(8,128)(2,1)} %bitcast.122, bf16[1024,1536]{1,0:T(8,128)(2,1)} %collective-permute-done.40, bf16[1024,1536]{1,0:T(8,128)(2,1)S(1)} %fusion.23), kind=kOutput, calls=%fused_computation | convolution fusion | flops 28216655872 | bytes 75104256 | tf_op jit(solution)/shard_map/dot_general | solution.py:41
  933.8 21.9 %fusion.4 = f32[1024,1536]{1,0:T(8,128)} fusion(bf16[1536,4480]{1,0:T(8,128)(2,1)} %bitcast.128, bf16[2048,4480]{1,0:T(8,128)(2,1)} %multiply_convert_fusion), kind=kOutput, calls=%fused_computation.29 | convolution fusion | flops 14092861440 | bytes 29229056 | tf_op jit(solution)/shard_map/dot_general | solution.py:41
  956.2 22.1 %fusion.6 = f32[1024,1536]{1,0:T(8,128)} fusion(bf16[1536,4480]{1,0:T(8,128)(2,1)} %bitcast.129, bf16[2048,4480]{1,0:T(8,128)(2,1)} %multiply_convert_fusion), kind=kOutput, calls=%fused_computation.31 | convolution fusion | flops 14092861440 | bytes 29229056 | tf_op jit(solution)/shard_map/dot_general | solution.py:41
  987.3 5.6 collective-permute-done.42.g1_ref
  993.0 11.2 fusion.79.d_o_ref
  1004.2 27.6 %shard_map.146.d_qkv_ref = bf16[2048,1024]{1,0:T(8,128)(2,1)} custom-call(bf16[2048,1024]{1,0:T(8,128)(2,1)} %fusion.76.qkv_ref, bf16[2048,768]{1,0:T(8,128)(2,1)} %fusion.79.d_o_ref), custom_call_target="tpu_custom_call" | custom-call | flops 40000000000 | tf_op jit(solution)/shard_map/pallas_call | solution.py:248
  1031.8 19.1 attn_grads.2
  1052.8 7.5 pad_maximum_fusion
  1060.9 13.8 flip.2.up_ref
  1074.7 11.3 flip.3.up_ref
  1089.4 8.7 fusion.92
  1098.1 5.4 fusion.90
  1110.5 379.0 %reduce-scatter.3.cloned.1.call-done = f32[384,1792]{1,0:T(8,128)} async-done(((f32[1536,1792]{1,0:T(8,128)}), f32[384,1792]{1,0:T(8,128)}) %reduce-scatter.3.cloned.1.call-update) | async-done | bytes 2752528 | tf_op jit(solution)/shard_map/reduce_scatter | solution.py:179
  1493.0 138.5 %mlp_grads.2 = (f32[2,1120,1536]{2,1,0:T(8,128)}, f32[192,1120]{1,0:T(8,128)}, f32[192,1120]{1,0:T(8,128)}, f32[192,1120]{1,0:T(8,128)}, f32[192,1120]{1,0:T(8,1...) custom-call(s32[2]{0:T(128)} %pad_add_fusion.place_ref, ...), custom_call_target="tpu_custom_call" | custom-call | flops 112742891520 | tf_op jit(solution)/shard_map/mlp_grads/pallas_call | solution.py:365
  1631.4 139.1 %mlp_grads.3 = (f32[2,1120,1536]{2,1,0:T(8,128)}, f32[192,1120]{1,0:T(8,128)}, f32[192,1120]{1,0:T(8,128)}, f32[192,1120]{1,0:T(8,128)}, f32[192,1120]{1,0:T(8,1...) custom-call(s32[2]{0:T(128)} %pad_add_fusion.place_ref, ...), custom_call_target="tpu_custom_call", output_to_operand_aliasing={{0}: (5, {})} | custom-call | flops 112742891520 | tf_op jit(solution)/shard_map/mlp_grads/pallas_call | solution.py:365
  1771.2 5.8 fusion.72
  1781.7 21.6 %fusion.12 = f32[1024,1536]{1,0:T(8,128)} fusion(bf16[4480,1536]{1,0:T(8,128)(2,1)} %bitcast.42, bf16[2048,4480]{1,0:T(8,128)(2,1)} %get-tuple-element.70), kind=kOutput, calls=%fused_computation.37 | convolution fusion | flops 14092861440 | bytes 29229056 | tf_op jit(solution)/shard_map/dot_general | solution.py:41
  1804.2 13.3 collective-permute-done.48.refs_3_
  1819.7 17.8 collective-permute-done.54.refs_2_
  1839.0 16.5 collective-permute-done.55.refs_3_
  1857.8 5.5 fusion.27
  1869.6 27.3 %collective-permute-done.57.refs_5_ = f32[192,1120]{1,0:T(8,128)} collective-permute-done((f32[192,1120]{1,0:T(8,128)}, f32[192,1120]{1,0:T(8,128)}, u32[]{:S(2)}, u32[]{:S(2)}) %collective-permute-start.57) | collective-permute-done | bytes 860192 | tf_op jit(solution)/shard_map/ppermute | solution.py:388
  1900.9 21.4 %fusion.14 = f32[1024,1536]{1,0:T(8,128)} fusion(bf16[4480,1536]{1,0:T(8,128)(2,1)} %bitcast.42, bf16[2048,4480]{1,0:T(8,128)(2,1)} %get-tuple-element.70), kind=kOutput, calls=%fused_computation.39 | convolution fusion | flops 14092861440 | bytes 29229056 | tf_op jit(solution)/shard_map/dot_general | solution.py:41
  1922.3 7.9 assemble.2.refs_8_
  1930.2 23.8 %collective-permute-done.49.refs_4_ = f32[192,1120]{1,0:T(8,128)S(1)} collective-permute-done((f32[192,1120]{1,0:T(8,128)}, f32[192,1120]{1,0:T(8,128)S(1)}, u32[]{:S(2)}, u32[]{:S(2)}) %collective-permute-start.49) | collective-permute-done | bytes 860192 | tf_op jit(solution)/shard_map/ppermute | solution.py:388
  1954.0 18.7 collective-permute-done.50.refs_5_
  1974.9 8.1 assemble.3
  1983.0 8.1 add_convert_fusion
  (354 shorter events, 248.6 us)
Async XLA Ops:
  8.0 1078.0 %reduce-scatter.5.cloned.1.call-start = ((), (), s32[]{:S(2)}) async-start(), calls=%async_computation.5 | async-start | bytes 13762560 | tf_op jit(solution)/shard_map/reduce_scatter | solution.py:179
  14.5 170.2 %collective-permute-start.13 = (bf16[1120,1536]{1,0:T(8,128)(2,1)}, bf16[1120,1536]{1,0:T(8,128)(2,1)}, u32[]{:S(2)}, u32[]{:S(2)}) collective-permute-start(bf16[1120,1536]{1,0:T(8,128)(2,1)} %get-tuple-element.107._.down_ref), channel_id=1, source_target_pairs={{0,2},{2,0},{4,6},{6,4},{1,3},{3,1},{5,7},{7,5}} | collective-permute-start | bytes 10321928 | tf_op jit(solution)/shard_map/ppermute | solution.py:57
  17.8 174.1 %collective-permute-start.14 = (bf16[1120,1536]{1,0:T(8,128)(2,1)}, bf16[1120,1536]{1,0:T(8,128)(2,1)}, u32[]{:S(2)}, u32[]{:S(2)}) collective-permute-start(bf16[1120,1536]{1,0:T(8,128)(2,1)} %get-tuple-element.107._.down_ref), channel_id=1, source_target_pairs={{0,4},{2,6},{4,0},{6,2},{1,5},{3,7},{5,1},{7,3}} | collective-permute-start | bytes 10321928 | tf_op jit(solution)/shard_map/ppermute | solution.py:57
  24.7 15.2 collective-permute-start.1
  28.9 115.8 %collective-permute-start = (bf16[1024,1536]{1,0:T(8,128)(2,1)}, bf16[1024,1536]{1,0:T(8,128)(2,1)}, u32[]{:S(2)}, u32[]{:S(2)}) collective-permute-start(bf16[1024,1536]{1,0:T(8,128)(2,1)} %fusion.70.n0_ref), channel_id=1, source_target_pairs={{0,1},{1,0},{2,3},{3,2},{4,5},{5,4},{6,7},{7,6}} | collective-permute-start | bytes 9437192 | tf_op jit(solution)/shard_map/ppermute | solution.py:53
  35.9 10.6 collective-permute-start.8
  43.4 78.6 %collective-permute-start.2 = (bf16[384,1792]{1,0:T(8,128)(2,1)}, bf16[384,1792]{1,0:T(8,128)(2,1)}, u32[]{:S(2)}, u32[]{:S(2)}) collective-permute-start(bf16[384,1792]{1,0:T(8,128)(2,1)} %pad_maximum_fusion.3._), channel_id=1, source_target_pairs={{0,2},{2,0},{4,6},{6,4},{1,3},{3,1},{5,7},{7,5}} | collective-permute-start | bytes 4128776 | tf_op jit(solution)/shard_map/ppermute | solution.py:57
  46.5 78.5 %collective-permute-start.3 = (bf16[384,1792]{1,0:T(8,128)(2,1)}, bf16[384,1792]{1,0:T(8,128)(2,1)}, u32[]{:S(2)}, u32[]{:S(2)}) collective-permute-start(bf16[384,1792]{1,0:T(8,128)(2,1)} %pad_maximum_fusion.3._), channel_id=1, source_target_pairs={{0,4},{2,6},{4,0},{6,2},{1,5},{3,7},{5,1},{7,3}} | collective-permute-start | bytes 4128776 | tf_op jit(solution)/shard_map/ppermute | solution.py:57
  123.2 16.6 collective-permute-start.4
  126.1 17.2 collective-permute-start.5
  139.8 77.6 %collective-permute-start.9 = (bf16[384,4480]{1,0:T(8,128)(2,1)}, bf16[384,4480]{1,0:T(8,128)(2,1)}, u32[]{:S(2)}, u32[]{:S(2)}) collective-permute-start(bf16[384,4480]{1,0:T(8,128)(2,1)} %pad_maximum_fusion.1._), channel_id=1, source_target_pairs={{0,2},{2,0},{4,6},{6,4},{1,3},{3,1},{5,7},{7,5}} | collective-permute-start | bytes 10321928 | tf_op jit(solution)/shard_map/ppermute | solution.py:57
  143.4 78.3 %collective-permute-start.10 = (bf16[384,4480]{1,0:T(8,128)(2,1)}, bf16[384,4480]{1,0:T(8,128)(2,1)}, u32[]{:S(2)}, u32[]{:S(2)}) collective-permute-start(bf16[384,4480]{1,0:T(8,128)(2,1)} %pad_maximum_fusion.1._), channel_id=1, source_target_pairs={{0,4},{2,6},{4,0},{6,2},{1,5},{3,7},{5,1},{7,3}} | collective-permute-start | bytes 10321928 | tf_op jit(solution)/shard_map/ppermute | solution.py:57
  178.2 89.1 %collective-permute-start.6 = (f32[1024,1536]{1,0:T(8,128)S(1)}, f32[1024,1536]{1,0:T(8,128)S(1)}, u32[]{:S(2)}, u32[]{:S(2)}) collective-permute-start(f32[1024,1536]{1,0:T(8,128)S(1)} %fusion.105), channel_id=1, source_target_pairs={{0,1},{1,0},{2,3},{3,2},{4,5},{5,4},{6,7},{7,6}} | collective-permute-start | bytes 18874376 | tf_op jit(solution)/shard_map/ppermute | solution.py:53
  186.2 71.5 %collective-permute-start.15 = (bf16[560,1536]{1,0:T(8,128)(2,1)S(1)}, bf16[560,1536]{1,0:T(8,128)(2,1)S(1)}, u32[]{:S(2)}, u32[]{:S(2)}) collective-permute-start(bf16[560,1536]{1,0:T(8,128)(2,1)S(1)} %slice.150), channel_id=1, source_target_pairs={{0,4},{2,6},{4,0},{6,2},{1,5},{3,7},{5,1},{7,3}} | collective-permute-start | bytes 5160968 | tf_op jit(solution)/shard_map/ppermute | solution.py:57
  191.9 260.3 %collective-permute-start.31 = (bf16[1120,1536]{1,0:T(8,128)(2,1)}, bf16[1120,1536]{1,0:T(8,128)(2,1)}, u32[]{:S(2)}, u32[]{:S(2)}) collective-permute-start(bf16[1120,1536]{1,0:T(8,128)(2,1)} %get-tuple-element.106._.down_ref), channel_id=1, source_target_pairs={{0,2},{2,0},{4,6},{6,4},{1,3},{3,1},{5,7},{7,5}} | collective-permute-start | bytes 10321928 | tf_op jit(solution)/shard_map/ppermute | solution.py:57
  217.4 239.1 %collective-permute-start.32 = (bf16[1120,1536]{1,0:T(8,128)(2,1)}, bf16[1120,1536]{1,0:T(8,128)(2,1)}, u32[]{:S(2)}, u32[]{:S(2)}) collective-permute-start(bf16[1120,1536]{1,0:T(8,128)(2,1)} %get-tuple-element.106._.down_ref), channel_id=1, source_target_pairs={{0,4},{2,6},{4,0},{6,2},{1,5},{3,7},{5,1},{7,3}} | collective-permute-start | bytes 10321928 | tf_op jit(solution)/shard_map/ppermute | solution.py:57
  221.7 106.3 %collective-permute-start.16 = (bf16[560,1536]{1,0:T(8,128)(2,1)}, bf16[560,1536]{1,0:T(8,128)(2,1)}, u32[]{:S(2)}, u32[]{:S(2)}) collective-permute-start(bf16[560,1536]{1,0:T(8,128)(2,1)} %slice.151), channel_id=1, source_target_pairs={{0,2},{2,0},{4,6},{6,4},{1,3},{3,1},{5,7},{7,5}} | collective-permute-start | bytes 5160968 | tf_op jit(solution)/shard_map/ppermute | solution.py:57
  257.7 106.4 %collective-permute-start.11 = (bf16[192,4480]{1,0:T(8,128)(2,1)}, bf16[192,4480]{1,0:T(8,128)(2,1)}, u32[]{:S(2)}, u32[]{:S(2)}) collective-permute-start(bf16[192,4480]{1,0:T(8,128)(2,1)} %slice.148), channel_id=1, source_target_pairs={{0,4},{2,6},{4,0},{6,2},{1,5},{3,7},{5,1},{7,3}} | collective-permute-start | bytes 5160968 | tf_op jit(solution)/shard_map/ppermute | solution.py:57
  267.3 99.6 %collective-permute-start.12 = (bf16[192,4480]{1,0:T(8,128)(2,1)}, bf16[192,4480]{1,0:T(8,128)(2,1)}, u32[]{:S(2)}, u32[]{:S(2)}) collective-permute-start(bf16[192,4480]{1,0:T(8,128)(2,1)} %slice.149), channel_id=1, source_target_pairs={{0,2},{2,0},{4,6},{6,4},{1,3},{3,1},{5,7},{7,5}} | collective-permute-start | bytes 5160968 | tf_op jit(solution)/shard_map/ppermute | solution.py:57
  328.0 46.5 %collective-permute-start.7 = (bf16[1024,1536]{1,0:T(8,128)(2,1)S(1)}, bf16[1024,1536]{1,0:T(8,128)(2,1)}, u32[]{:S(2)}, u32[]{:S(2)}) collective-permute-start(bf16[1024,1536]{1,0:T(8,128)(2,1)S(1)} %fusion.32), channel_id=1, source_target_pairs={{0,1},{1,0},{2,3},{3,2},{4,5},{5,4},{6,7},{7,6}} | collective-permute-start | bytes 9437192 | tf_op jit(solution)/shard_map/ppermute | solution.py:53
  374.5 92.0 %collective-permute-start.19 = (bf16[192,1792]{1,0:T(8,128)(2,1)}, bf16[192,1792]{1,0:T(8,128)(2,1)}, u32[]{:S(2)}, u32[]{:S(2)}) collective-permute-start(bf16[192,1792]{1,0:T(8,128)(2,1)} %get-tuple-element.62), channel_id=1, source_target_pairs={{0,1},{1,0},{2,3},{3,2},{4,5},{5,4},{6,7},{7,6}} | collective-permute-start | bytes 2064392 | tf_op jit(solution)/shard_map/ppermute | solution.py:53
  447.8 45.5 %collective-permute-start.17 = (f32[1024,1536]{1,0:T(8,128)}, f32[1024,1536]{1,0:T(8,128)}, u32[]{:S(2)}, u32[]{:S(2)}) collective-permute-start(f32[1024,1536]{1,0:T(8,128)} %fusion.16), channel_id=1, source_target_pairs={{0,1},{1,0},{2,3},{3,2},{4,5},{5,4},{6,7},{7,6}} | collective-permute-start | bytes 18874376 | tf_op jit(solution)/shard_map/ppermute | solution.py:53
  455.0 137.3 %collective-permute-start.33 = (bf16[560,1536]{1,0:T(8,128)(2,1)}, bf16[560,1536]{1,0:T(8,128)(2,1)}, u32[]{:S(2)}, u32[]{:S(2)}) collective-permute-start(bf16[560,1536]{1,0:T(8,128)(2,1)} %slice.160), channel_id=1, source_target_pairs={{0,4},{2,6},{4,0},{6,2},{1,5},{3,7},{5,1},{7,3}} | collective-permute-start | bytes 5160968 | tf_op jit(solution)/shard_map/ppermute | solution.py:57
  459.3 136.3 %collective-permute-start.34 = (bf16[560,1536]{1,0:T(8,128)(2,1)}, bf16[560,1536]{1,0:T(8,128)(2,1)}, u32[]{:S(2)}, u32[]{:S(2)}) collective-permute-start(bf16[560,1536]{1,0:T(8,128)(2,1)} %slice.161), channel_id=1, source_target_pairs={{0,2},{2,0},{4,6},{6,4},{1,3},{3,1},{5,7},{7,5}} | collective-permute-start | bytes 5160968 | tf_op jit(solution)/shard_map/ppermute | solution.py:57
  466.5 33.9 %collective-permute-start.26 = (bf16[192,4480]{1,0:T(8,128)(2,1)}, bf16[192,4480]{1,0:T(8,128)(2,1)}, u32[]{:S(2)}, u32[]{:S(2)}) collective-permute-start(bf16[192,4480]{1,0:T(8,128)(2,1)} %get-tuple-element.64), channel_id=1, source_target_pairs={{0,1},{1,0},{2,3},{3,2},{4,5},{5,4},{6,7},{7,6}} | collective-permute-start | bytes 5160968 | tf_op jit(solution)/shard_map/ppermute | solution.py:53
  468.9 59.2 %collective-permute-start.20 = (bf16[384,1792]{1,0:T(8,128)(2,1)}, bf16[384,1792]{1,0:T(8,128)(2,1)S(1)}, u32[]{:S(2)}, u32[]{:S(2)}) collective-permute-start(bf16[384,1792]{1,0:T(8,128)(2,1)} %pad_maximum_fusion.4._), channel_id=1, source_target_pairs={{0,2},{2,0},{4,6},{6,4},{1,3},{3,1},{5,7},{7,5}} | collective-permute-start | bytes 4128776 | tf_op jit(solution)/shard_map/ppermute | solution.py:57
  493.3 35.5 %collective-permute-start.21 = (bf16[384,1792]{1,0:T(8,128)(2,1)}, bf16[384,1792]{1,0:T(8,128)(2,1)S(1)}, u32[]{:S(2)}, u32[]{:S(2)}) collective-permute-start(bf16[384,1792]{1,0:T(8,128)(2,1)} %pad_maximum_fusion.4._), channel_id=1, source_target_pairs={{0,4},{2,6},{4,0},{6,2},{1,5},{3,7},{5,1},{7,3}} | collective-permute-start | bytes 4128776 | tf_op jit(solution)/shard_map/ppermute | solution.py:57
  500.4 46.3 %collective-permute-start.18 = (bf16[1024,1536]{1,0:T(8,128)(2,1)S(1)}, bf16[1024,1536]{1,0:T(8,128)(2,1)S(1)}, u32[]{:S(2)}, u32[]{:S(2)}) collective-permute-start(bf16[1024,1536]{1,0:T(8,128)(2,1)S(1)} %fusion.36.n0_ref), channel_id=1, source_target_pairs={{0,1},{1,0},{2,3},{3,2},{4,5},{5,4},{6,7},{7,6}} | collective-permute-start | bytes 9437192 | tf_op jit(solution)/shard_map/ppermute | solution.py:53
  528.2 16.2 collective-permute-start.22
  528.8 16.2 collective-permute-start.23
  544.5 74.7 %collective-permute-start.27 = (bf16[384,4480]{1,0:T(8,128)(2,1)}, bf16[384,4480]{1,0:T(8,128)(2,1)}, u32[]{:S(2)}, u32[]{:S(2)}) collective-permute-start(bf16[384,4480]{1,0:T(8,128)(2,1)} %pad_maximum_fusion.2._), channel_id=1, source_target_pairs={{0,2},{2,0},{4,6},{6,4},{1,3},{3,1},{5,7},{7,5}} | collective-permute-start | bytes 10321928 | tf_op jit(solution)/shard_map/ppermute | solution.py:57
  545.1 76.7 %collective-permute-start.28 = (bf16[384,4480]{1,0:T(8,128)(2,1)}, bf16[384,4480]{1,0:T(8,128)(2,1)}, u32[]{:S(2)}, u32[]{:S(2)}) collective-permute-start(bf16[384,4480]{1,0:T(8,128)(2,1)} %pad_maximum_fusion.2._), channel_id=1, source_target_pairs={{0,4},{2,6},{4,0},{6,2},{1,5},{3,7},{5,1},{7,3}} | collective-permute-start | bytes 10321928 | tf_op jit(solution)/shard_map/ppermute | solution.py:57
  584.4 51.2 %collective-permute-start.24 = (f32[1024,1536]{1,0:T(8,128)}, f32[1024,1536]{1,0:T(8,128)}, u32[]{:S(2)}, u32[]{:S(2)}) collective-permute-start(f32[1024,1536]{1,0:T(8,128)} %fusion.100), channel_id=1, source_target_pairs={{0,1},{1,0},{2,3},{3,2},{4,5},{5,4},{6,7},{7,6}} | collective-permute-start | bytes 18874376 | tf_op jit(solution)/shard_map/ppermute | solution.py:53
  592.3 125.4 %collective-permute-start.35 = (bf16[1024,1536]{1,0:T(8,128)(2,1)}, bf16[1024,1536]{1,0:T(8,128)(2,1)}, u32[]{:S(2)}, u32[]{:S(2)}) collective-permute-start(bf16[1024,1536]{1,0:T(8,128)(2,1)} %bitcast.43), channel_id=1, source_target_pairs={{0,1},{1,0},{2,3},{3,2},{4,5},{5,4},{6,7},{7,6}} | collective-permute-start | bytes 9437192 | tf_op jit(solution)/shard_map/ppermute | solution.py:53
  620.7 36.7 %collective-permute-start.29 = (bf16[192,4480]{1,0:T(8,128)(2,1)S(1)}, bf16[192,4480]{1,0:T(8,128)(2,1)S(1)}, u32[]{:S(2)}, u32[]{:S(2)}) collective-permute-start(bf16[192,4480]{1,0:T(8,128)(2,1)S(1)} %slice.158), channel_id=1, source_target_pairs={{0,4},{2,6},{4,0},{6,2},{1,5},{3,7},{5,1},{7,3}} | collective-permute-start | bytes 5160968 | tf_op jit(solution)/shard_map/ppermute | solution.py:57
  624.5 37.1 %collective-permute-start.30 = (bf16[192,4480]{1,0:T(8,128)(2,1)}, bf16[192,4480]{1,0:T(8,128)(2,1)}, u32[]{:S(2)}, u32[]{:S(2)}) collective-permute-start(bf16[192,4480]{1,0:T(8,128)(2,1)} %slice.159), channel_id=1, source_target_pairs={{0,2},{2,0},{4,6},{6,4},{1,3},{3,1},{5,7},{7,5}} | collective-permute-start | bytes 5160968 | tf_op jit(solution)/shard_map/ppermute | solution.py:57
  642.0 22.3 %collective-permute-start.25 = (bf16[1024,1536]{1,0:T(8,128)(2,1)S(1)}, bf16[1024,1536]{1,0:T(8,128)(2,1)S(1)}, u32[]{:S(2)}, u32[]{:S(2)}) collective-permute-start(bf16[1024,1536]{1,0:T(8,128)(2,1)S(1)} %fusion.29), channel_id=1, source_target_pairs={{0,1},{1,0},{2,3},{3,2},{4,5},{5,4},{6,7},{7,6}} | collective-permute-start | bytes 9437192 | tf_op jit(solution)/shard_map/ppermute | solution.py:53
  781.0 19.3 collective-permute-start.36
  804.8 5.7 collective-permute-start.37
  856.3 10.2 collective-permute-start.38
  872.4 19.8 collective-permute-start.40
  892.1 597.4 %reduce-scatter.3.cloned.1.call-start = ((), (), s32[]{:S(2)}) async-start(), calls=%async_computation.4 | async-start | bytes 13762560 | tf_op jit(solution)/shard_map/reduce_scatter | solution.py:179
  955.8 22.5 %collective-permute-start.41 = (f32[1024,1536]{1,0:T(8,128)}, f32[1024,1536]{1,0:T(8,128)S(1)}, u32[]{:S(2)}, u32[]{:S(2)}) collective-permute-start(f32[1024,1536]{1,0:T(8,128)} %fusion.4), channel_id=1, source_target_pairs={{0,1},{1,0},{2,3},{3,2},{4,5},{5,4},{6,7},{7,6}} | collective-permute-start | bytes 18874376 | tf_op jit(solution)/shard_map/ppermute | solution.py:53
  987.3 5.7 collective-permute-start.42
  1051.0 442.0 %all-gather.3.cloned.1.call-start = ((), (), s32[]{:S(2)}) async-start(), calls=%async_computation.2 | async-start | bytes 84934656 | tf_op jit(solution)/shard_map/all_gather | solution.py:175
  1060.3 571.1 %all-gather.5.cloned.1.call-start = ((), (), s32[]{:S(2)}) async-start(), calls=%async_computation.3 | async-start | bytes 28311552 | tf_op jit(solution)/shard_map/all_gather | solution.py:175
  1089.3 15.3 collective-permute-start.45
  1103.5 667.7 %collective-permute-start.43 = (f32[1024,1536]{1,0:T(8,128)}, f32[1024,1536]{1,0:T(8,128)}, u32[]{:S(2)}, u32[]{:S(2)}) collective-permute-start(f32[1024,1536]{1,0:T(8,128)} %fusion.90), channel_id=1, source_target_pairs={{0,1},{1,0},{2,3},{3,2},{4,5},{5,4},{6,7},{7,6}} | collective-permute-start | bytes 18874376 | tf_op jit(solution)/shard_map/ppermute | solution.py:53
  1493.0 286.2 %collective-permute-start.44 = (f32[192,1792]{1,0:T(8,128)}, f32[192,1792]{1,0:T(8,128)}, u32[]{:S(2)}, u32[]{:S(2)}) collective-permute-start(f32[192,1792]{1,0:T(8,128)} %get-tuple-element.114), channel_id=1, source_target_pairs={{0,1},{1,0},{2,3},{3,2},{4,5},{5,4},{6,7},{7,6}} | collective-permute-start | bytes 4128776 | tf_op jit(solution)/shard_map/ppermute | solution.py:53
  1770.6 10.1 collective-permute-start.46
  1777.0 26.2 %collective-permute-start.47 = (f32[192,1120]{1,0:T(8,128)S(1)}, f32[192,1120]{1,0:T(8,128)S(1)}, u32[]{:S(2)}, u32[]{:S(2)}) collective-permute-start(f32[192,1120]{1,0:T(8,128)S(1)} %copy-done.65), channel_id=1, source_target_pairs={{0,2},{1,3},{2,0},{3,1},{4,6},{5,7},{6,4},{7,5}} | collective-permute-start | bytes 2580488 | tf_op jit(solution)/shard_map/ppermute | solution.py:388
  1778.5 39.0 %collective-permute-start.48 = (f32[192,1120]{1,0:T(8,128)S(1)}, f32[192,1120]{1,0:T(8,128)S(1)}, u32[]{:S(2)}, u32[]{:S(2)}) collective-permute-start(f32[192,1120]{1,0:T(8,128)S(1)} %copy-done.64), channel_id=1, source_target_pairs={{0,3},{1,2},{2,1},{3,0},{4,7},{5,6},{6,5},{7,4}} | collective-permute-start | bytes 2580488 | tf_op jit(solution)/shard_map/ppermute | solution.py:388
  1778.5 39.6 %collective-permute-start.53 = (f32[192,1120]{1,0:T(8,128)S(1)}, f32[192,1120]{1,0:T(8,128)S(1)}, u32[]{:S(2)}, u32[]{:S(2)}) collective-permute-start(f32[192,1120]{1,0:T(8,128)S(1)} %copy-done.63), channel_id=1, source_target_pairs={{0,1},{1,0},{2,3},{3,2},{4,5},{5,4},{6,7},{7,6}} | collective-permute-start | bytes 2580488 | tf_op jit(solution)/shard_map/ppermute | solution.py:388
  1779.2 58.3 %collective-permute-start.54 = (f32[192,1120]{1,0:T(8,128)S(1)}, f32[192,1120]{1,0:T(8,128)S(1)}, u32[]{:S(2)}, u32[]{:S(2)}) collective-permute-start(f32[192,1120]{1,0:T(8,128)S(1)} %copy-done.62), channel_id=1, source_target_pairs={{0,2},{1,3},{2,0},{3,1},{4,6},{5,7},{6,4},{7,5}} | collective-permute-start | bytes 2580488 | tf_op jit(solution)/shard_map/ppermute | solution.py:388
  1781.6 73.8 %collective-permute-start.55 = (f32[192,1120]{1,0:T(8,128)S(1)}, f32[192,1120]{1,0:T(8,128)S(1)}, u32[]{:S(2)}, u32[]{:S(2)}) collective-permute-start(f32[192,1120]{1,0:T(8,128)S(1)} %copy-done.61), channel_id=1, source_target_pairs={{0,3},{1,2},{2,1},{3,0},{4,7},{5,6},{6,5},{7,4}} | collective-permute-start | bytes 2580488 | tf_op jit(solution)/shard_map/ppermute | solution.py:388
  1803.3 179.7 %collective-permute-start.39 = (f32[1024,1536]{1,0:T(8,128)}, f32[1024,1536]{1,0:T(8,128)}, u32[]{:S(2)}, u32[]{:S(2)}) collective-permute-start(f32[1024,1536]{1,0:T(8,128)} %fusion.12), channel_id=1, source_target_pairs={{0,1},{1,0},{2,3},{3,2},{4,5},{5,4},{6,7},{7,6}} | collective-permute-start | bytes 18874376 | tf_op jit(solution)/shard_map/ppermute | solution.py:53
  1817.5 50.6 %collective-permute-start.56 = (f32[192,1120]{1,0:T(8,128)}, f32[192,1120]{1,0:T(8,128)S(1)}, u32[]{:S(2)}, u32[]{:S(2)}) collective-permute-start(f32[192,1120]{1,0:T(8,128)} %get-tuple-element.93), channel_id=1, source_target_pairs={{0,4},{1,5},{2,6},{3,7},{4,0},{5,1},{6,2},{7,3}} | collective-permute-start | bytes 2580488 | tf_op jit(solution)/shard_map/ppermute | solution.py:388
  1818.1 78.9 %collective-permute-start.57 = (f32[192,1120]{1,0:T(8,128)}, f32[192,1120]{1,0:T(8,128)}, u32[]{:S(2)}, u32[]{:S(2)}) collective-permute-start(f32[192,1120]{1,0:T(8,128)} %get-tuple-element.94), channel_id=1, source_target_pairs={{0,5},{1,4},{2,7},{3,6},{4,1},{5,0},{6,3},{7,2}} | collective-permute-start | bytes 2580488 | tf_op jit(solution)/shard_map/ppermute | solution.py:388
  1837.5 59.5 %collective-permute-start.58 = (f32[192,1120]{1,0:T(8,128)}, f32[192,1120]{1,0:T(8,128)}, u32[]{:S(2)}, u32[]{:S(2)}) collective-permute-start(f32[192,1120]{1,0:T(8,128)} %get-tuple-element.95), channel_id=1, source_target_pairs={{0,6},{1,7},{2,4},{3,5},{4,2},{5,3},{6,0},{7,1}} | collective-permute-start | bytes 2580488 | tf_op jit(solution)/shard_map/ppermute | solution.py:388
  1855.4 43.1 %collective-permute-start.59 = (f32[192,1120]{1,0:T(8,128)}, f32[192,1120]{1,0:T(8,128)}, u32[]{:S(2)}, u32[]{:S(2)}) collective-permute-start(f32[192,1120]{1,0:T(8,128)} %get-tuple-element.96), channel_id=1, source_target_pairs={{0,7},{1,6},{2,5},{3,4},{4,3},{5,2},{6,1},{7,0}} | collective-permute-start | bytes 2580488 | tf_op jit(solution)/shard_map/ppermute | solution.py:388
  1868.1 85.9 %collective-permute-start.49 = (f32[192,1120]{1,0:T(8,128)}, f32[192,1120]{1,0:T(8,128)S(1)}, u32[]{:S(2)}, u32[]{:S(2)}) collective-permute-start(f32[192,1120]{1,0:T(8,128)} %get-tuple-element.85), channel_id=1, source_target_pairs={{0,4},{1,5},{2,6},{3,7},{4,0},{5,1},{6,2},{7,3}} | collective-permute-start | bytes 2580488 | tf_op jit(solution)/shard_map/ppermute | solution.py:388
  1897.0 75.7 %collective-permute-start.50 = (f32[192,1120]{1,0:T(8,128)}, f32[192,1120]{1,0:T(8,128)S(1)}, u32[]{:S(2)}, u32[]{:S(2)}) collective-permute-start(f32[192,1120]{1,0:T(8,128)} %get-tuple-element.86), channel_id=1, source_target_pairs={{0,5},{1,4},{2,7},{3,6},{4,1},{5,0},{6,3},{7,2}} | collective-permute-start | bytes 2580488 | tf_op jit(solution)/shard_map/ppermute | solution.py:388
  1897.0 75.7 %collective-permute-start.51 = (f32[192,1120]{1,0:T(8,128)}, f32[192,1120]{1,0:T(8,128)S(1)}, u32[]{:S(2)}, u32[]{:S(2)}) collective-permute-start(f32[192,1120]{1,0:T(8,128)} %get-tuple-element.87), channel_id=1, source_target_pairs={{0,6},{1,7},{2,4},{3,5},{4,2},{5,3},{6,0},{7,1}} | collective-permute-start | bytes 2580488 | tf_op jit(solution)/shard_map/ppermute | solution.py:388
  1898.5 74.2 %collective-permute-start.52 = (f32[192,1120]{1,0:T(8,128)}, f32[192,1120]{1,0:T(8,128)S(1)}, u32[]{:S(2)}, u32[]{:S(2)}) collective-permute-start(f32[192,1120]{1,0:T(8,128)} %get-tuple-element.88), channel_id=1, source_target_pairs={{0,7},{1,6},{2,5},{3,4},{4,3},{5,2},{6,1},{7,0}} | collective-permute-start | bytes 2580488 | tf_op jit(solution)/shard_map/ppermute | solution.py:388
  (76 other events, 1666.4 us)
Sparse Core Ops, SparseCore 0:
  892.2 102.1 reduce-scatter.4
  1051.1 438.3 reduce-scatter.2
Sparse Core Ops, SparseCore 1:
  1060.4 353.2 all-gather.2
  1415.4 142.5 all-gather.4
